TPU v7x, 256 devices: a whole 4x4x8 slice. The times are simulated.
256 devices in a mesh: pts: 32 (over x, y, core), med: 8 (over z).
Axes of the slice: x: 4, y: 4, z: 8, core: 2. Of those that a mesh axis runs over, the one named last changes fastest.
Arguments:
- sketches: bfloat16 [32768, 4096], P('pts'), may hold values from -12 to 12
- assignment: int32 [32768], P('pts'), may hold values from 0 to 4095
- medoid_ids: int32 [4096], P('med'), may hold values from 0 to 32767, as said below
Outputs:
- gap: float32 [32768], P('pts')
- coverage: float32 [], replicated
- weights: float32 [4096], P('med')
- gradient_sums: float32 [4096, 4096], P('pts', 'med')
Inputs may be any that keep to these rules, and one draw needn't show every extreme that they name: `medoid_ids`: the 4096 medoid ids are distinct point indices.
All inputs are finite; a program needn't handle non-finite values.
Results may differ from a plain program's by a relative error of at most 0.0003.
Values may be sent and summed in bfloat16 or wider, within the bound.
No kernel may reach another device: no remote copies, remote signals or barrier semaphores. Data moves between devices by JAX's collectives and lax.ppermute only.
A program may use at most 64 MiB of HBM per device.

v0:
```python
import jax
import jax.numpy as jnp
from jax import lax
from jax.sharding import PartitionSpec as P


def from_everyone(array, axis):
    size = lax.axis_size(axis)
    return lax.all_to_all(
        jnp.broadcast_to(array[None], (size, *array.shape)), axis, 0, 0, tiled=True
    )


def over_copies(array, axis):
    return from_everyone(array, axis).sum(axis=0)


def together(arrays, axis):
    line, at, done = (jnp.concatenate([a.reshape(-1) for a in arrays]), 0, [])
    running = over_copies(line, axis)
    for a in arrays:
        done.append(running[at : at + a.size].reshape(a.shape))
        at += a.size
    return tuple(done)


def shards(sketches, assignment, medoid_ids):
    row_count, feat_width = sketches.shape
    medoid_count = medoid_ids.shape[0]
    pts_count = lax.axis_size("pts")
    pts_index = lax.axis_index("pts")
    med_index = lax.axis_index("med")
    medoid_iota = jnp.arange(medoid_count, dtype=jnp.int32)
    local_assign = assignment - med_index * medoid_count
    one_hot = (local_assign[:, None] == medoid_iota[None, :]).astype(jnp.bfloat16)
    offsets = medoid_ids - pts_index * row_count
    inside = (offsets >= 0) & (offsets < row_count)
    picked = jnp.take(sketches, jnp.clip(offsets, 0, row_count - 1), axis=0)
    fetch_terms = jnp.where(inside[:, None], picked, jnp.zeros_like(picked))
    medoid_slice = (
        lax.psum_scatter(fetch_terms, "pts", scatter_dimension=1, tiled=True)
        .astype(jnp.float32)
        .astype(jnp.bfloat16)
    )
    gradient_sums = lax.psum_scatter(
        lax.dot_general(
            sketches, one_hot, (((0,), (0,)), ((), ())), preferred_element_type=jnp.float32
        ),
        "pts",
        scatter_dimension=0,
        tiled=True,
    )
    count_terms = jnp.sum(one_hot.astype(jnp.float32), axis=0)
    raw_scores = lax.dot_general(
        sketches,
        lax.all_gather(medoid_slice, "pts", axis=1, tiled=True),
        (((1,), (1,)), ((), ())),
        preferred_element_type=jnp.float32,
    )
    scores = raw_scores * (1.0 / feat_width)
    best_local = jnp.max(scores, axis=1)
    in_shard = (local_assign >= 0) & (local_assign < medoid_count)
    taken = jnp.take_along_axis(
        scores, jnp.clip(local_assign, 0, medoid_count - 1)[:, None], axis=1
    )[:, 0]
    assigned_local = jnp.where(in_shard, taken, -1e30)
    best_score, assigned = lax.pmax((best_local, assigned_local), "med")
    gap = best_score - assigned
    weights, cover_total = together((count_terms, jnp.sum(best_score)), "pts")
    coverage = cover_total / (row_count * pts_count)
    return (gap, coverage, weights, gradient_sums)


def solution(mesh):
    in_specs = (P("pts", None), P("pts"), P("med"))
    out_specs = (P("pts"), P(), P("med"), P("pts", "med"))
    return jax.shard_map(shards, mesh=mesh, in_specs=in_specs, out_specs=out_specs, check_vma=False)
```

profile of v0, /device:TPU:2, one launch (start us, length us, event | category | flops | bytes accessed | tf_op | source)
XLA Modules:
  0.0 295.6 jit_solution(7401411365770368771)
XLA Ops:
  7.2 0.0 reduce-scatter.7.cloned.1.call-start
  7.2 0.7 compare_and_fusion
  7.9 13.1 %gather_fusion = bf16[512,4096]{1,0:T(8,128)(2,1)} fusion(bf16[1024,4096]{1,0:T(8,128)(2,1)} %param.3, s32[1024]{0:T(1024)S(1)} %pad_clamp_fusion), kind=kCustom, calls=%fused_computation | custom fusion | bytes 8390656 | tf_op jit(solution)/shard_map/jit(_take)/gather | solution.py:38
  21.0 4.0 %select_select_fusion = bf16[512,4096]{1,0:T(8,128)(2,1)} fusion(bf16[512,4096]{1,0:T(8,128)(2,1)} %gather_fusion, pred[512]{0:T(512)(128)(4,1)S(1)} %get-tuple-element.28, pred[512]{0:T(512)(128)(4,1)S(1)} %get-tuple-element.34), kind=kLoop, calls=%fused_computation.3 | loop fusion | flops 4194304 | bytes 8389632 | tf_op jit(solution)/shard_map/jit(_where)/select_n | solution.py:39
  25.0 6.5 %copy.13 = bf16[512,4096]{0,1:T(8,128)(2,1)} copy(bf16[512,4096]{1,0:T(8,128)(2,1)} %select_select_fusion) | data formatting | bytes 8388608
  31.4 0.0 copy-start
  31.4 0.0 reduce-scatter.7.cloned.1.call-update
  31.5 0.0 all-gather.2.cloned.1.call-start
  31.5 92.7 %reduce-scatter.7.cloned.1.call-done = bf16[128,512]{1,0:T(8,128)(2,1)} async-done(((bf16[4096,512]{1,0:T(8,128)(2,1)}), bf16[128,512]{1,0:T(8,128)(2,1)}) %reduce-scatter.7.cloned.1.call-update) | async-done | bytes 131088
  124.2 1.7 copy.14
  125.9 0.0 all-gather.2.cloned.1.call-update
  125.9 0.0 reduce-scatter.5.cloned.1.call-start
  126.0 0.0 copy-done
  126.0 10.4 %convolution_bitcast_fusion = f32[4096,512]{0,1:T(8,128)} fusion(bf16[1024,4096]{1,0:T(8,128)(2,1)} %param.3, s32[1024]{0:T(1024)S(1)} %get-tuple-element.27), kind=kOutput, calls=%fused_computation.2 | convolution fusion | flops 4295491584 | bytes 16781312 | tf_op jit(solution)/shard_map/dot_general | solution.py:46
  136.4 0.0 reduce-scatter.5.cloned.1.call-update
  136.4 0.3 convert_reduce_fusion
  136.7 43.6 %all-gather.2.cloned.1.call-done = bf16[512,4096]{1,0:T(8,128)(2,1)} async-done(((bf16[512,128]{1,0:T(8,128)(2,1)}), bf16[512,4096]{1,0:T(8,128)(2,1)}) %all-gather.2.cloned.1.call-update) | async-done | bytes 4194320 | tf_op jit(solution)/shard_map/all_gather | solution.py:56
  180.3 8.3 %multiply_bitcast_fusion = (f32[1024,512]{0,1:T(8,128)S(1)}, f32[1024]{0:T(1024)S(1)}) fusion(bf16[512,4096]{1,0:T(8,128)(2,1)} %all-gather.2.cloned.1.call-done, bf16[1024,4096]{1,0:T(8,128)(2,1)} %param.3), kind=kOutput, calls=%fused_computation.7 | convolution fusion | flops 4296014848 | bytes 14684160 | tf_op jit(solution)/shard_map/dot_general | solution.py:54
  188.6 8.6 %gather_fusion.1 = f32[1024]{0:T(1024)S(1)} fusion(f32[1024,512]{0,1:T(8,128)S(1)} %get-tuple-element.30, s32[1024]{0:T(1024)S(1)} %bitcast.15), kind=kCustom, calls=%fused_computation.1 | custom fusion | bytes 16384 | tf_op jit(solution)/shard_map/jit(take_along_axis)/gather | solution.py:63
  197.2 17.7 %all-reduce = (f32[1024]{0:T(1024)S(1)}, f32[1024]{0:T(1024)S(1)}) all-reduce(f32[1024]{0:T(1024)S(1)} %get-tuple-element.31, f32[1024]{0:T(1024)S(1)} %select_select_fusion.1), channel_id=1, replica_groups=mesh['pts'=32,'med'=8] {'med'}, use_global_device_ids=true, to_apply=%region_2.3 | all-reduce | flops 2048 | bytes 16384 | tf_op jit(solution)/shard_map/pmax | solution.py:67
  215.0 1.2 fusion.5
  216.2 0.7 pad_maximum_fusion
  216.8 0.7 broadcast_in_dim.48
  217.5 6.0 %all-to-all-start = ((f32[32,1,513]{2,1,0:T(1,128)}), f32[32,1,513]{2,1,0:T(1,128)S(1)}, u32[]{:S(2)}, u32[]{:S(2)}) async-start(f32[32,1,513]{2,1,0:T(1,128)} %broadcast_in_dim.48), calls=%async_computation | async-start | bytes 163840 | tf_op jit(solution)/shard_map/all_to_all | solution.py:9
  223.5 60.8 %reduce-scatter.5.cloned.1.call-done = f32[128,512]{0,1:T(8,128)} async-done(((f32[4096,512]{0,1:T(8,128)}), f32[128,512]{0,1:T(8,128)}) %reduce-scatter.5.cloned.1.call-update) | async-done | bytes 262160 | tf_op jit(solution)/shard_map/reduce_scatter | solution.py:45
  284.3 1.8 copy.12
  286.1 0.0 all-to-all-done
  286.1 0.1 reduce_sum.29
  286.2 0.5 slice.6
  286.7 0.6 slice.7
  (6 shorter events, 0.1 us)
Async XLA Ops:
  7.2 117.1 %reduce-scatter.7.cloned.1.call-start = ((), (), s32[]{:S(2)}) async-start(), calls=%async_computation.5 | async-start | bytes 4325376
  31.4 94.5 %copy-start = (s32[1024]{0:T(1024)S(1)}, s32[1024]{0:T(1024)}, u32[]{:S(2)}) copy-start(s32[1024]{0:T(1024)} %param.4) | copy-start | bytes 12292
  31.5 148.8 %all-gather.2.cloned.1.call-start = ((), (), s32[]{:S(2)}) async-start(), calls=%async_computation.3 | async-start | bytes 4325376 | tf_op jit(solution)/shard_map/all_gather | solution.py:56
  125.9 158.4 %reduce-scatter.5.cloned.1.call-start = ((), (), s32[]{:S(2)}) async-start(), calls=%async_computation.4 | async-start | bytes 8650752 | tf_op jit(solution)/shard_map/reduce_scatter | solution.py:45
  217.5 68.6 %all-to-all-start = ((f32[32,1,513]{2,1,0:T(1,128)}), f32[32,1,513]{2,1,0:T(1,128)S(1)}, u32[]{:S(2)}, u32[]{:S(2)}) async-start(f32[32,1,513]{2,1,0:T(1,128)} %broadcast_in_dim.48), calls=%async_computation | async-start | bytes 163840 | tf_op jit(solution)/shard_map/all_to_all | solution.py:9
Sparse Core Ops, SparseCore 0:
  31.6 92.5 reduce-scatter.6
  127.3 52.9 all-gather.1
  184.3 99.9 reduce-scatter.4
where the time goes:
time: 296 us
  waiting for transfers between devices  197 us (67%)
  local copies, waits for them, and re-layouts  33.4 us (11%)
  matrix products  18.6 us (6%)
  blocking collectives  17.7 us (6%)
  between operations  15.6 us (5%)
  other arithmetic  6.93 us (2%)
  starting transfers between devices  6.15 us (2%)
    unnamed x4, waiting for transfers between devices  92.8 us
    reduce_scatter x1, waiting for transfers between devices, shards(): lax.psum_scatter(lax.dot_general(sketches, one_hot, (((0,), (0,)), ((), (...  60.8 us
    all_gather x1, waiting for transfers between devices, shards(): lax.all_gather(medoid_slice, 'pts', axis=1, tiled=True)  43.6 us
    pmax x1, blocking collectives, shards(): best_score, assigned = lax.pmax((best_local, assigned_local), 'med')  17.7 us
    gather x1, local copies, waits for them, and re-layouts, shards(): picked = jnp.take(sketches, jnp.clip(offsets, 0, row_count - 1), axis=0)  13.1 us
    dot_general x1, matrix products, shards(): lax.dot_general(sketches, one_hot, (((0,), (0,)), ((), ())), preferred_el...  10.4 us
    unnamed x6, local copies, waits for them, and re-layouts  9.92 us
    gather x1, local copies, waits for them, and re-layouts, shards(): jnp.take_along_axis(scores, jnp.clip(local_assign, 0, medoid_count - 1)[:...  8.65 us
  transfers between devices with their start and end apart: 4, of which 3 were waited for; matrix products, arithmetic and copies ran while one was open for 11% of the time, Pallas kernels for 0%

commit v1 on v0

v1 whole, which is shorter than its diff:
```python
import functools

import jax
import jax.numpy as jnp
from jax import lax
from jax.experimental import pallas as pl
from jax.experimental.pallas import tpu as pltpu
from jax.sharding import PartitionSpec as P

BF = jnp.bfloat16
F32 = jnp.float32
I32 = jnp.int32
LANES = 128
GRAD_ROWS = 192
GRAD_SLOTS = 176
MED_ROWS = 32
MED_SLOTS = 24
SEL = GRAD_ROWS + 2 * MED_ROWS
NONE = -1e30


def contract_last(a, b):
    return lax.dot_general(a, b, (((1,), (1,)), ((), ())), preferred_element_type=F32)


def pick_kernel(where_ref, assign_ref, ids_ref, sk_ref, med_ref, grad_ref, over_ref, sel, code):
    step = pl.program_id(0)

    @pl.when(step == 0)
    def _():
        base = where_ref[0]
        plane = where_ref[1]
        groups = assign_ref.shape[0]
        half = ids_ref.shape[1] // 2
        off = ids_ref[...] - base
        inside = (off >= 0) & (off < groups * LANES)
        hi = jnp.where(inside, off >> 7, -1)
        lo = off & (LANES - 1)
        j = lax.broadcasted_iota(I32, (1, 2 * half), 1)
        first = j < half
        number = (jnp.where(first, j, j - half) + 1).astype(F32)
        row = lax.broadcasted_iota(I32, (2 * groups, 2 * half), 0)
        wanted = jnp.where(first, hi, hi + groups)
        wanted = jnp.where(hi >= 0, wanted, -1)
        table = jnp.where(wanted == row, number, 0.0).astype(BF)
        lane_hot = (lo == lax.broadcasted_iota(I32, (LANES, 2 * half), 0)).astype(F32).astype(BF)
        medoid = contract_last(table, lane_hot)
        med0, med1 = medoid[:groups], medoid[groups:]
        local = assign_ref[...] - plane * (2 * half)
        mine = (local >= 0) & (local < 2 * half)
        local_lo = jnp.where(mine, (local & 255) + 1, 0).astype(F32)
        local_hi = jnp.where(mine, local >> 8, 0).astype(F32)
        flags = jnp.concatenate(
            [mine.astype(F32), (med0 > 0).astype(F32), (med1 > 0).astype(F32)], axis=0
        ).astype(BF)
        k = lax.broadcasted_iota(I32, (LANES, LANES), 0)
        b = lax.broadcasted_iota(I32, (LANES, LANES), 1)
        before = jnp.dot(flags, (k < b).astype(F32).astype(BF), preferred_element_type=F32)
        total = jnp.dot(flags, jnp.ones((LANES, LANES), BF), preferred_element_type=F32)
        slots, over = [], jnp.zeros((1, LANES), F32)
        for kind, limit in enumerate((GRAD_SLOTS, MED_SLOTS, MED_SLOTS)):
            run = jnp.zeros((1, LANES), F32)
            rows = []
            for g in range(groups):
                at = kind * groups + g
                rows.append(before[at : at + 1] + run)
                run = run + total[at : at + 1]
            over = over + jnp.where(run > limit, 1.0, 0.0)
            position = jnp.concatenate(rows, axis=0).astype(I32)
            flag = (mine, med0 > 0, med1 > 0)[kind] & (position < limit)
            slots.append(jnp.where(flag, position, -1))
        over_ref[...] = jnp.broadcast_to(over, over_ref.shape)
        slot_g = slots[0]
        slot_m = jnp.where(slots[1] >= 0, slots[1], -1)
        slot_n = jnp.where(slots[2] >= 0, slots[2] + MED_ROWS, -1)
        grad_iota = lax.broadcasted_iota(I32, (GRAD_ROWS, LANES), 0)
        med_iota = lax.broadcasted_iota(I32, (2 * MED_ROWS, LANES), 0)
        codes = jnp.zeros((8, SEL), F32)
        zeros = jnp.zeros((5, LANES), F32)
        either = med0 + med1
        for g in range(groups):
            at = slice(g, g + 1)
            top = (slot_g[at] == grad_iota).astype(F32)
            low = ((slot_m[at] == med_iota) | (slot_n[at] == med_iota)).astype(F32)
            block = jnp.concatenate([top, low], axis=0).astype(BF)
            sel[:, g * LANES : (g + 1) * LANES] = block
            fields = jnp.concatenate(
                [either[at], local_lo[at], local_hi[at], zeros], axis=0
            ).astype(BF)
            codes = codes + contract_last(fields, block)
        code[...] = codes.astype(BF)

    rows = jnp.dot(sel[...], sk_ref[...], preferred_element_type=F32).astype(BF)
    codes = code[...]
    for c in range(2):
        grad_ref[c, :GRAD_SLOTS, :] = rows[:GRAD_SLOTS, c * LANES : (c + 1) * LANES]
        grad_ref[c, GRAD_SLOTS:, :] = jnp.concatenate(
            [codes[:, :LANES], codes[:, LANES:]], axis=0
        )
        at = GRAD_ROWS + c * MED_ROWS
        med_ref[c, :, :] = jnp.concatenate([rows[at : at + MED_SLOTS], codes], axis=0)


def pick(where, assignment, medoid_ids, sketches, pts_count):
    rows, feats = sketches.shape
    wide = 2 * LANES
    return pl.pallas_call(
        pick_kernel,
        grid_spec=pltpu.PrefetchScalarGridSpec(
            num_scalar_prefetch=1,
            grid=(feats // wide,),
            in_specs=[
                pl.BlockSpec((rows // LANES, LANES), lambda i, w: (0, 0)),
                pl.BlockSpec((1, medoid_ids.shape[0]), lambda i, w: (0, 0)),
                pl.BlockSpec((rows, wide), lambda i, w: (0, i)),
            ],
            out_specs=[
                pl.BlockSpec((2, MED_ROWS, wide), lambda i, w: (i, 0, 0)),
                pl.BlockSpec((2, GRAD_ROWS, LANES), lambda i, w: (i, 0, 0)),
                pl.BlockSpec((8, LANES), lambda i, w: (0, 0)),
            ],
            scratch_shapes=[pltpu.VMEM((SEL, rows), BF), pltpu.VMEM((8, SEL), BF)],
        ),
        out_shape=[
            jax.ShapeDtypeStruct((pts_count, MED_ROWS, wide), BF),
            jax.ShapeDtypeStruct((pts_count, GRAD_ROWS, LANES), BF),
            jax.ShapeDtypeStruct((8, LANES), F32),
        ],
        compiler_params=pltpu.CompilerParams(vmem_limit_bytes=24 * 2**20),
        cost_estimate=pl.CostEstimate(
            flops=2 * SEL * rows * feats, bytes_accessed=rows * feats * 2, transcendentals=0
        ),
        name="pick",
    )(where, assignment.reshape(-1, LANES), medoid_ids[None, :], sketches)


def place_kernel(where_ref, got_ref, out_ref):
    core = where_ref[2]
    sources = got_ref.shape[0]
    count = out_ref.shape[0]
    total = jnp.zeros(out_ref.shape, F32)
    per = 2 * LANES // MED_ROWS
    iota = lax.broadcasted_iota(I32, (count, per * MED_ROWS), 0)
    for g in range(sources // per):
        numbers = []
        for q in range(g * per, (g + 1) * per):
            line = got_ref[q, MED_SLOTS : MED_SLOTS + 8, :].astype(F32)[0:1]
            a = line[:, GRAD_ROWS : GRAD_ROWS + MED_ROWS]
            b = line[:, GRAD_ROWS + MED_ROWS :]
            numbers.append(jnp.where(core == 0, a, b))
        number = jnp.concatenate(numbers, axis=1).astype(I32) - 1
        hot = (number == iota).astype(F32).astype(BF)
        block = got_ref[g * per : (g + 1) * per].reshape(per * MED_ROWS, got_ref.shape[2])
        total = total + jnp.dot(hot, block, preferred_element_type=F32)
    out_ref[...] = total.astype(BF)


def place(where, got, count):
    return pl.pallas_call(
        place_kernel,
        in_specs=[
            pl.BlockSpec(memory_space=pltpu.SMEM),
            pl.BlockSpec(memory_space=pltpu.VMEM),
        ],
        out_specs=pl.BlockSpec(memory_space=pltpu.VMEM),
        out_shape=jax.ShapeDtypeStruct((count, got.shape[2]), BF),
        compiler_params=pltpu.CompilerParams(vmem_limit_bytes=8 * 2**20),
        cost_estimate=pl.CostEstimate(
            flops=2 * count * got.size, bytes_accessed=2 * got.size, transcendentals=0
        ),
        name="place",
    )(where, got)


def sums_kernel(got_ref, sums_ref, count_ref):
    feats = got_ref.shape[2]
    medoids = sums_ref.shape[1]
    tail = GRAD_ROWS - LANES
    iota_a = lax.broadcasted_iota(I32, (medoids, LANES), 0)
    iota_b = lax.broadcasted_iota(I32, (medoids, tail), 0)
    ones = jnp.ones((GRAD_ROWS, LANES), BF)

    def body(q, total):
        codes = got_ref[q, GRAD_SLOTS:, :].astype(F32).astype(I32)
        a = codes[1:2] - 1 + codes[2:3] * 256
        b = (codes[9:10] - 1 + codes[10:11] * 256)[:, :tail]
        hot = jnp.concatenate(
            [(a == iota_a).astype(F32), (b == iota_b).astype(F32)], axis=1
        ).astype(BF)
        block = jnp.concatenate([got_ref[q], ones], axis=1)
        return total + jnp.dot(hot, block, preferred_element_type=F32)

    total = lax.fori_loop(
        0, got_ref.shape[0], body, jnp.zeros((medoids, feats + LANES), F32)
    )
    sums_ref[...] = total[:, :feats].T
    count_ref[...] = total[:, feats:].T[:8]


def sums(got, medoids):
    return pl.pallas_call(
        sums_kernel,
        in_specs=[pl.BlockSpec(memory_space=pltpu.VMEM)],
        out_specs=[pl.BlockSpec(memory_space=pltpu.VMEM)] * 2,
        out_shape=[
            jax.ShapeDtypeStruct((got.shape[2], medoids), F32),
            jax.ShapeDtypeStruct((8, medoids), F32),
        ],
        compiler_params=pltpu.CompilerParams(vmem_limit_bytes=16 * 2**20),
        cost_estimate=pl.CostEstimate(
            flops=4 * medoids * got.size, bytes_accessed=2 * got.size, transcendentals=0
        ),
        name="sums",
    )(got)


def score_kernel(scale, where_ref, assign_ref, prior_ref, sk_ref, *refs):
    parts, out_ref = refs[:-1], refs[-1]
    medoids = 2 * parts[0].shape[1]
    x, y, first = where_ref[3], where_ref[4], where_ref[5]
    points = sk_ref.shape[0]
    total = jnp.zeros((medoids, points), F32)
    for kx in range(4):
        for ky in range(4):
            block = ((x + 4 - kx) & 3) * 4 + ((y + 4 - ky) & 3)
            at = pl.multiple_of(block * 2 * LANES, 2 * LANES)
            if len(parts) == 8:
                a, b = parts[ky][kx], parts[4 + kx][ky]
            else:
                a, b = parts[0][ky * 4 + kx], parts[0][16 + kx * 4 + ky]
            total = total + contract_last(
                jnp.concatenate([a, b], axis=0), sk_ref[:, pl.ds(at, 2 * LANES)]
            )
    scores = total * scale
    best = jnp.max(scores, axis=0, keepdims=True)
    row = lax.broadcasted_iota(I32, scores.shape, 0)
    local = assign_ref[...] - first
    chosen = jnp.max(jnp.where(local == row, scores, NONE), axis=0, keepdims=True)
    prior = prior_ref[...]
    best = jnp.maximum(best, prior[0:1])
    chosen = jnp.maximum(chosen, prior[1:2])
    out_ref[...] = jnp.concatenate([best, chosen, prior[2:]], axis=0)


def scored(where, assignment, prior, sketches, parts):
    rows, feats = sketches.shape
    tile = 2 * LANES
    whole = lambda a: pl.BlockSpec(a.shape, lambda i, w: (0,) * a.ndim)
    return pl.pallas_call(
        functools.partial(score_kernel, 1.0 / feats),
        grid_spec=pltpu.PrefetchScalarGridSpec(
            num_scalar_prefetch=1,
            grid=(rows // tile,),
            in_specs=[
                pl.BlockSpec((1, tile), lambda i, w: (0, i)),
                pl.BlockSpec((8, tile), lambda i, w: (0, i)),
                pl.BlockSpec((tile, feats), lambda i, w: (i, 0)),
            ]
            + [whole(a) for a in parts],
            out_specs=pl.BlockSpec((8, tile), lambda i, w: (0, i)),
        ),
        out_shape=jax.ShapeDtypeStruct((8, rows), F32),
        compiler_params=pltpu.CompilerParams(vmem_limit_bytes=24 * 2**20),
        cost_estimate=pl.CostEstimate(
            flops=2 * rows * feats * 256, bytes_accessed=rows * feats * 2, transcendentals=0
        ),
        name="scored",
    )(where, assignment[None, :], prior, sketches, *parts)


def from_everyone(array, axis):
    size = lax.axis_size(axis)
    return lax.all_to_all(
        jnp.broadcast_to(array[None], (size, *array.shape)), axis, 0, 0, tiled=True
    )


def chip_of(p):
    return p // 8, (p // 2) % 4, p % 2


def shifted(array, dx, dy, dc):
    pairs = []
    for p in range(32):
        x, y, c = chip_of(p)
        pairs.append((p, (((x + dx) % 4) * 4 + (y + dy) % 4) * 2 + (c ^ dc)))
    return lax.ppermute(array, "pts", pairs)


def general(sketches, assignment, medoid_ids):
    row_count, feat_width = sketches.shape
    medoid_count = medoid_ids.shape[0]
    pts_count = lax.axis_size("pts")
    part = feat_width // pts_count
    pts_index = lax.axis_index("pts")
    med_index = lax.axis_index("med")
    local_assign = assignment - med_index * medoid_count
    one_hot = (
        local_assign[:, None] == jnp.arange(medoid_count, dtype=I32)[None, :]
    ).astype(BF)
    offsets = medoid_ids - pts_index * row_count
    inside = (offsets >= 0) & (offsets < row_count)
    picked = jnp.take(sketches, jnp.clip(offsets, 0, row_count - 1), axis=0)
    terms = jnp.where(inside[:, None], picked, jnp.zeros_like(picked))
    terms = terms.reshape(medoid_count, pts_count, part).swapaxes(0, 1)
    piece = (
        lax.all_to_all(terms, "pts", 0, 0, tiled=True).astype(F32).sum(axis=0).astype(BF)
    )
    everything = from_everyone(piece, "pts").swapaxes(0, 1).reshape(medoid_count, feat_width)
    partial = lax.dot_general(
        sketches, one_hot, (((0,), (0,)), ((), ())), preferred_element_type=F32
    ).reshape(pts_count, part, medoid_count)
    gradient_sums = lax.all_to_all(partial, "pts", 0, 0, tiled=True).sum(axis=0)
    counts = from_everyone(jnp.sum(one_hot.astype(F32), axis=0), "pts").sum(axis=0)
    scores = contract_last(sketches, everything) * (1.0 / feat_width)
    best = jnp.max(scores, axis=1)
    here = (local_assign >= 0) & (local_assign < medoid_count)
    taken = jnp.take_along_axis(
        scores, jnp.clip(local_assign, 0, medoid_count - 1)[:, None], axis=1
    )[:, 0]
    both = from_everyone(jnp.stack([best, jnp.where(here, taken, NONE)]), "med").max(axis=0)
    cover = from_everyone(jnp.sum(both[0])[None], "pts").sum()
    return both[0] - both[1], cover / (row_count * pts_count), counts, gradient_sums


def shards(sketches, assignment, medoid_ids):
    row_count, feat_width = sketches.shape
    medoid_count = medoid_ids.shape[0]
    half = medoid_count // 2
    pts_count = lax.axis_size("pts")
    p = lax.axis_index("pts")
    m = lax.axis_index("med")
    core = p % 2
    own = m * medoid_count + core * half
    other = m * medoid_count + (1 - core) * half
    where = jnp.stack(
        [p * row_count, m, core, p // 8, (p // 2) % 4, own, other, other]
    ).astype(I32)
    where_other = jnp.stack(
        [p * row_count, m, core, p // 8, (p // 2) % 4, other, own, own]
    ).astype(I32)

    med_send, grad_send, over = pick(where, assignment, medoid_ids, sketches, pts_count)
    med_got = lax.all_to_all(med_send, "pts", 0, 0, tiled=True)
    piece = place(where, med_got, half)
    a, b = piece[: half // 2], piece[half // 2 :]
    pa = jnp.stack([a] + [shifted(a, k, 0, 0) for k in (1, 2, 3)])
    pb = jnp.stack([b] + [shifted(b, 0, k, 0) for k in (1, 2, 3)])
    qa = [pa] + [shifted(pa, 0, k, 0) for k in (1, 2, 3)]
    qb = [pb] + [shifted(pb, k, 0, 0) for k in (1, 2, 3)]
    mine = jnp.concatenate(qa + qb, axis=0)
    theirs = shifted(mine, 0, 0, 1)

    grad_got = lax.all_to_all(grad_send, "pts", 0, 0, tiled=True)
    gradient_sums, counts = sums(grad_got, medoid_count)

    prior = jnp.full((8, row_count), NONE, F32)
    stats = scored(where, assignment, prior, sketches, qa + qb)
    stats = scored(where_other, assignment, stats, sketches, [theirs])
    flag = jnp.broadcast_to(over[0:1, 0:1], (1, row_count))
    packed = jnp.concatenate([stats[:2], flag], axis=0)
    both = from_everyone(packed, "med").max(axis=0)
    gap = both[0] - both[1]
    last = from_everyone(jnp.stack([jnp.sum(both[0]), both[2, 0]]), "pts")
    cover = jnp.sum(last[:, 0])
    full = jnp.max(last[:, 1]) > 0.0
    fast = (gap, cover / (row_count * pts_count), counts[0], gradient_sums)
    return lax.cond(
        full, lambda: general(sketches, assignment, medoid_ids), lambda: fast
    )


def solution(mesh):
    in_specs = (P("pts", None), P("pts"), P("med"))
    out_specs = (P("pts"), P(), P("med"), P("pts", "med"))
    return jax.shard_map(shards, mesh=mesh, in_specs=in_specs, out_specs=out_specs, check_vma=False)
```

time: 296 us -> 151 us (0.51)
  waiting for transfers between devices: 197 us -> 29.2 us
  Pallas kernels: 0 us -> 33.6 us
  starting transfers between devices: 6.15 us -> 28.4 us
  matrix products: 18.6 us -> 0 us
  local copies, waits for them, and re-layouts: 33.4 us -> 14.9 us
  blocking collectives: 17.7 us -> 35.2 us
  between operations: 15.6 us -> 2.64 us
    unnamed x4 -> x0, waiting for transfers between devices: 92.8 us -> none
    reduce_scatter x1 -> x0, waiting for transfers between devices: 60.8 us -> none  [shards(): lax.psum_scatter(lax.dot_general(sketches, one_hot, (((0,), (0,)), ((), (...]
    all_gather x1 -> x0, waiting for transfers between devices: 43.6 us -> none  [shards(): lax.all_gather(medoid_slice, 'pts', axis=1, tiled=True)]
    all_to_all x0 -> x2, blocking collectives: none -> 35.2 us  [the longest x1 18 us: from_everyone(): lax.all_to_all(jnp.broadcast_to(array[None], (size, *array.shape)), axis,...]
    pallas_call x0 -> x5, Pallas kernels: none -> 33.6 us  [the longest x1 12.7 us: pick(): pl.pallas_call(pick_kernel, grid_spec=pltpu.PrefetchScalarGridSpec(num_sc...]
    gather x2 -> x0, local copies, waits for them, and re-layouts: 21.7 us -> none  [the longest x1 13.1 us: shards(): picked = jnp.take(sketches, jnp.clip(offsets, 0, row_count - 1), axis=0)]
    dot_general x2 -> x0, matrix products: 18.6 us -> none  [the longest x1 10.4 us: shards(): lax.dot_general(sketches, one_hot, (((0,), (0,)), ((), ())), preferred_el...]
    pmax x1 -> x0, blocking collectives: 17.7 us -> none  [shards(): best_score, assigned = lax.pmax((best_local, assigned_local), 'med')]
  transfers between devices with their start and end apart: 4 -> 15, of which waited for: 3 -> 4; matrix products, arithmetic and copies ran while one was open for 11% -> 8% of each run, Pallas kernels for 0% -> 11%
where the time goes in v1:
time: 151 us; the launch traced here: 149 us
  blocking collectives  35.2 us (23%)
  Pallas kernels  33.6 us (22%)
  waiting for transfers between devices  29.2 us (19%)
  starting transfers between devices  28.4 us (19%)
  local copies, waits for them, and re-layouts  14.9 us (10%)
  other arithmetic  4.61 us (3%)
  between operations  2.64 us (2%)
    all_to_all x1, blocking collectives, from_everyone(): lax.all_to_all(jnp.broadcast_to(array[None], (size, *array.shape)), axis,...  18 us
    all_to_all x1, waiting for transfers between devices, shards(): grad_got = lax.all_to_all(grad_send, 'pts', 0, 0, tiled=True)  17.7 us
    all_to_all x1, blocking collectives, shards(): med_got = lax.all_to_all(med_send, 'pts', 0, 0, tiled=True)  17.2 us
    ppermute x13, starting transfers between devices, shifted(): return lax.ppermute(array, 'pts', pairs)  15.2 us
    pallas_call x1, Pallas kernels, pick(): pl.pallas_call(pick_kernel, grid_spec=pltpu.PrefetchScalarGridSpec(num_sc...  12.7 us
    unnamed x35, local copies, waits for them, and re-layouts  11.6 us
    ppermute x13, waiting for transfers between devices, shifted(): return lax.ppermute(array, 'pts', pairs)  11.5 us
    pallas_call x2, Pallas kernels, scored(): pl.pallas_call(functools.partial(score_kernel, 1.0 / feats), grid_spec=pl...  10.4 us
  transfers between devices with their start and end apart: 15, of which 4 were waited for; matrix products, arithmetic and copies ran while one was open for 8% of the time, Pallas kernels for 11%

profile of v1, /device:TPU:2, one launch (start us, length us, event | category | flops | bytes accessed | tf_op | source)
XLA Modules:
  0.0 149.2 jit_solution(4113524795955776750)
XLA Ops:
  0.8 12.7 %pick.1 = (bf16[32,32,256]{2,1,0:T(8,128)(2,1)S(1)}, bf16[32,192,128]{2,1,0:T(8,128)(2,1)S(1)}, f32[8,128]{1,0:T(8,128)S(1)}) custom-call(s32[8]{0:T(128)S(1)} %stack.89.where_ref, s32[8,128]{1,0:T(8,128)} %bitcast.74, s32[1,512]{1,0:T(1,128)} %bitcast.79, bf16[1024,4096]{1,0:T(8,128)(2,1)} %sk_ref.5), custom_call_target="tpu_custom_call" | custom-call | flops 2147483648 | bytes 8388608 | tf_op jit(solution)/shard_map/pick/pallas_call | solution.py:107
  13.5 17.2 %all_to_all.51.got_ref = bf16[32,32,256]{2,1,0:T(8,128)(2,1)S(1)} all-to-all(bf16[32,32,256]{2,1,0:T(8,128)(2,1)S(1)} %get-tuple-element.48), channel_id=1, replica_groups=mesh['pts'=32,'med'=8] {'pts'}, dimensions={0} | all-to-all | bytes 1048576 | tf_op jit(solution)/shard_map/all_to_all | solution.py:344
  30.7 1.0 place.1
  31.7 2.1 %collective-permute-start.7 = (bf16[128,256]{1,0:T(8,128)(2,1)S(1)}, bf16[128,256]{1,0:T(8,128)(2,1)S(1)}, u32[]{:S(2)}, u32[]{:S(2)}) collective-permute-start(bf16[128,256]{1,0:T(8,128)(2,1)S(1)} %get-tuple-element.95), channel_id=1, source_target_pairs={{0,32},{8,40},{16,48},{24,56},{32,0},{40,8},{48,16},{56,24},{64,96... | collective-permute-start | bytes 196616 | tf_op jit(solution)/shard_map/ppermute | solution.py:287
  34.4 2.7 %collective-permute-start.8 = (bf16[128,256]{1,0:T(8,128)(2,1)S(1)}, bf16[128,256]{1,0:T(8,128)(2,1)S(1)}, u32[]{:S(2)}, u32[]{:S(2)}) collective-permute-start(bf16[128,256]{1,0:T(8,128)(2,1)S(1)} %get-tuple-element.95), channel_id=1, source_target_pairs={{0,48},{8,56},{16,0},{24,8},{32,16},{40,24},{48,32},{56,40},{64,11... | collective-permute-start | bytes 196616 | tf_op jit(solution)/shard_map/ppermute | solution.py:287
  37.1 1.4 collective-permute-start.1
  38.5 1.5 collective-permute-start
  39.9 0.6 constant_dynamic-update-slice_fusion.13
  41.2 2.2 %collective-permute-start.11 = (bf16[4,128,256]{2,1,0:T(8,128)(2,1)S(1)}, bf16[4,128,256]{2,1,0:T(8,128)(2,1)S(1)}, u32[]{:S(2)}, u32[]{:S(2)}) collective-permute-start(bf16[4,128,256]{2,1,0:T(8,128)(2,1)S(1)} %pad_maximum_fusion.2.refs_4_), channel_id=1, source_target_pairs={{0,192},{8,200},{16,208},{24,216},{32,224},{40,232},{48,240},{56,2... | collective-permute-start | bytes 786440 | tf_op jit(solution)/shard_map/ppermute | solution.py:287
  43.4 0.8 collective-permute-start.10
  44.2 1.3 collective-permute-done.2
  46.0 1.1 collective-permute-start.4
  47.1 0.6 collective-permute-start.3
  47.7 0.6 constant_dynamic-update-slice_fusion.12
  48.3 0.6 constant_dynamic-update-slice_fusion.11
  48.9 0.6 constant_dynamic-update-slice_fusion.10
  49.6 9.1 %collective-permute-done.3.refs_1_ = bf16[4,128,256]{2,1,0:T(8,128)(2,1)S(1)} collective-permute-done((bf16[4,128,256]{2,1,0:T(8,128)(2,1)S(1)}, bf16[4,128,256]{2,1,0:T(8,128)(2,1)S(1)}, u32[]{:S(2)}, u32[]{:S(2)}) %collective-permute-start.3) | collective-permute-done | bytes 262176 | tf_op jit(solution)/shard_map/ppermute | solution.py:287
  58.7 1.3 collective-permute-start.9
  59.9 0.7 constant_dynamic-update-slice_fusion.9
  60.7 0.8 constant_dynamic-update-slice_fusion.8
  61.4 0.7 constant_dynamic-update-slice_fusion.7
  62.2 0.6 constant_dynamic-update-slice_fusion.6
  62.8 0.6 constant_dynamic-update-slice_fusion.5
  63.4 0.6 constant_dynamic-update-slice_fusion.4
  64.1 0.6 constant_dynamic-update-slice_fusion.3
  64.7 1.0 collective-permute-done.9.refs_5_
  65.7 0.8 constant_dynamic-update-slice_fusion.2
  66.5 0.7 constant_dynamic-update-slice_fusion.1
  67.2 0.8 constant_dynamic-update-slice_fusion
  68.6 0.9 copy-done.2
  69.6 0.9 copy-done.4
  70.5 0.9 copy-done.6
  71.5 6.7 %scored.2.prior_ref = f32[8,1024]{1,0:T(8,128)S(1)} custom-call(s32[8]{0:T(128)S(1)} %stack.89.where_ref, s32[1,1024]{1,0:T(1,128)S(1)} %bitcast.75, f32[8,1024]{1,0:T(8,128)S(1)} %broadcast_in_dim.49.prior_ref, bf16[1024,4096]{1,0:T(8,128)(2,1)} %sk_ref.5, bf16[4,128,256]{2,1,0:T(8,128)(2,1)S(1)} %pad_maximum_fusion.1.refs_0_, ...), custom_call_target="tpu_custom_call" | custom-call | flops 2147483648 | bytes 8388608 | tf_op jit(solution)/shard_map/scored/pallas_call | solution.py:249
  78.2 3.7 %scored.3 = f32[8,1024]{1,0:T(8,128)S(1)} custom-call(s32[8]{0:T(128)S(1)} %stack.88.where_ref, s32[1,1024]{1,0:T(1,128)S(1)} %bitcast.76, f32[8,1024]{1,0:T(8,128)S(1)} %scored.2.prior_ref, bf16[1024,4096]{1,0:T(8,128)(2,1)S(1)} %copy-done.7, bf16[32,128,256]{2,1,0:T(8,128)(2,1)S(1)} %collective-permute-done.12.refs_0_), custom_call_target="tpu_custom_call" | custom-call | flops 2147483648 | bytes 8388608 | tf_op jit(solution)/shard_map/scored/pallas_call | solution.py:249
  81.9 0.7 slice_select_fusion
  82.7 18.0 %all_to_all.52 = f32[8,3,1024]{2,1,0:T(4,128)S(1)} all-to-all(f32[8,3,1024]{2,1,0:T(4,128)S(1)} %broadcast_in_dim.87), channel_id=1, replica_groups=mesh['pts'=32,'med'=8] {'med'}, dimensions={0} | all-to-all | bytes 196608 | tf_op jit(solution)/shard_map/all_to_all | solution.py:273
  100.7 6.7 %all-to-all-start.9 = ((bf16[32,192,128]{2,1,0:T(8,128)(2,1)}), bf16[32,192,128]{2,1,0:T(8,128)(2,1)S(1)}, u32[]{:S(2)}, u32[]{:S(2)}) async-start(bf16[32,192,128]{2,1,0:T(8,128)(2,1)} %copy-done), calls=%async_computation.9 | async-start | bytes 3145728 | tf_op jit(solution)/shard_map/all_to_all | solution.py:354
  107.9 0.6 fusion.7
  108.5 1.4 pad_maximum_fusion.3
  109.9 17.7 %all-to-all-done.9.got_ref = bf16[32,192,128]{2,1,0:T(8,128)(2,1)S(1)} async-done(((bf16[32,192,128]{2,1,0:T(8,128)(2,1)}), bf16[32,192,128]{2,1,0:T(8,128)(2,1)S(1)}, u32[]{:S(2)}, u32[]{:S(2)}) %all-to-all-start.9) | async-done | bytes 1572896 | tf_op jit(solution)/shard_map/all_to_all | solution.py:354
  127.6 0.6 broadcast_in_dim.88
  128.2 6.5 %all-to-all-start.8 = ((f32[32,1,2]{2,1,0:T(1,128)}), f32[32,1,2]{2,1,0:T(1,128)S(1)}, u32[]{:S(2)}, u32[]{:S(2)}) async-start(f32[32,1,2]{2,1,0:T(1,128)} %broadcast_in_dim.88), calls=%async_computation.8 | async-start | bytes 32768 | tf_op jit(solution)/shard_map/all_to_all | solution.py:273
  134.7 9.5 %sums.1 = (f32[128,512]{1,0:T(8,128)}, f32[8,512]{1,0:T(8,128)S(1)}) custom-call(bf16[32,192,128]{2,1,0:T(8,128)(2,1)S(1)} %all-to-all-done.9.got_ref), custom_call_target="tpu_custom_call" | custom-call | flops 1610612736 | bytes 1572864 | tf_op jit(solution)/shard_map/sums/pallas_call | solution.py:201
  144.4 0.6 slice_reduce_fusion.2
  145.6 2.4 %conditional.1 = (f32[1024]{0:T(1024)}, f32[]{:T(128)}, f32[512]{0:T(512)}, f32[128,512]{1,0:T(8,128)}) conditional(s32[]{:T(128)} %convert_element_type.11, (f32[3,1024]{1,0:T(4,128)S(1)}, f32[1,1024]{1,0:T(1,128)S(1)}, f32[32,2]{0,1:T(2,128)S(1)}, f32[8,512]{1,0:T(8,128)S(1)}, f32[128,512]{1,0:T(8,128)}) %tuple.49, (s32[512]{0:T(512)S(1)}, ...), branch_computations={%region_3.5_spmd, %region_5.14_spmd} | conditional | flops 8601925632 | bytes 130077376 | solution.py:368
  145.6 0.6 slice_reduce_fusion
  146.9 0.6 slice.32
  147.5 0.6 slice_subtract_fusion
  (45 shorter events, 3.0 us)
Async XLA Ops:
  13.5 47.2 %copy-start = (bf16[32,192,128]{2,1,0:T(8,128)(2,1)}, bf16[32,192,128]{2,1,0:T(8,128)(2,1)S(1)}, u32[]{:S(2)}) copy-start(bf16[32,192,128]{2,1,0:T(8,128)(2,1)S(1)} %get-tuple-element.50) | copy-start | bytes 4718596
  31.7 8.8 %collective-permute-start.7 = (bf16[128,256]{1,0:T(8,128)(2,1)S(1)}, bf16[128,256]{1,0:T(8,128)(2,1)S(1)}, u32[]{:S(2)}, u32[]{:S(2)}) collective-permute-start(bf16[128,256]{1,0:T(8,128)(2,1)S(1)} %get-tuple-element.95), channel_id=1, source_target_pairs={{0,32},{8,40},{16,48},{24,56},{32,0},{40,8},{48,16},{56,24},{64,96... | collective-permute-start | bytes 196616 | tf_op jit(solution)/shard_map/ppermute | solution.py:287
  33.8 7.3 %collective-permute-start.6 = (bf16[128,256]{1,0:T(8,128)(2,1)S(1)}, bf16[128,256]{1,0:T(8,128)(2,1)S(1)}, u32[]{:S(2)}, u32[]{:S(2)}) collective-permute-start(bf16[128,256]{1,0:T(8,128)(2,1)S(1)} %get-tuple-element.95), channel_id=1, source_target_pairs={{0,16},{8,24},{16,32},{24,40},{32,48},{40,56},{48,0},{56,8},{64,80... | collective-permute-start | bytes 196616 | tf_op jit(solution)/shard_map/ppermute | solution.py:287
  34.4 6.7 %collective-permute-start.8 = (bf16[128,256]{1,0:T(8,128)(2,1)S(1)}, bf16[128,256]{1,0:T(8,128)(2,1)S(1)}, u32[]{:S(2)}, u32[]{:S(2)}) collective-permute-start(bf16[128,256]{1,0:T(8,128)(2,1)S(1)} %get-tuple-element.95), channel_id=1, source_target_pairs={{0,48},{8,56},{16,0},{24,8},{32,16},{40,24},{48,32},{56,40},{64,11... | collective-permute-start | bytes 196616 | tf_op jit(solution)/shard_map/ppermute | solution.py:287
  37.1 7.1 %collective-permute-start.1 = (bf16[128,256]{1,0:T(8,128)(2,1)S(1)}, bf16[128,256]{1,0:T(8,128)(2,1)S(1)}, u32[]{:S(2)}, u32[]{:S(2)}) collective-permute-start(bf16[128,256]{1,0:T(8,128)(2,1)S(1)} %get-tuple-element.96), channel_id=1, source_target_pairs={{0,128},{8,136},{16,144},{24,152},{32,160},{40,168},{48,176},{56,1... | collective-permute-start | bytes 196616 | tf_op jit(solution)/shard_map/ppermute | solution.py:287
  38.5 5.7 %collective-permute-start = (bf16[128,256]{1,0:T(8,128)(2,1)S(1)}, bf16[128,256]{1,0:T(8,128)(2,1)S(1)}, u32[]{:S(2)}, u32[]{:S(2)}) collective-permute-start(bf16[128,256]{1,0:T(8,128)(2,1)S(1)} %get-tuple-element.96), channel_id=1, source_target_pairs={{0,64},{8,72},{16,80},{24,88},{32,96},{40,104},{48,112},{56,120},{... | collective-permute-start | bytes 196616 | tf_op jit(solution)/shard_map/ppermute | solution.py:287
  40.6 5.0 %collective-permute-start.2 = (bf16[128,256]{1,0:T(8,128)(2,1)S(1)}, bf16[128,256]{1,0:T(8,128)(2,1)S(1)}, u32[]{:S(2)}, u32[]{:S(2)}) collective-permute-start(bf16[128,256]{1,0:T(8,128)(2,1)S(1)} %get-tuple-element.96), channel_id=1, source_target_pairs={{0,192},{8,200},{16,208},{24,216},{32,224},{40,232},{48,240},{56,2... | collective-permute-start | bytes 196616 | tf_op jit(solution)/shard_map/ppermute | solution.py:287
  41.2 26.1 %collective-permute-start.11 = (bf16[4,128,256]{2,1,0:T(8,128)(2,1)S(1)}, bf16[4,128,256]{2,1,0:T(8,128)(2,1)S(1)}, u32[]{:S(2)}, u32[]{:S(2)}) collective-permute-start(bf16[4,128,256]{2,1,0:T(8,128)(2,1)S(1)} %pad_maximum_fusion.2.refs_4_), channel_id=1, source_target_pairs={{0,192},{8,200},{16,208},{24,216},{32,224},{40,232},{48,240},{56,2... | collective-permute-start | bytes 786440 | tf_op jit(solution)/shard_map/ppermute | solution.py:287
  43.4 23.1 %collective-permute-start.10 = (bf16[4,128,256]{2,1,0:T(8,128)(2,1)S(1)}, bf16[4,128,256]{2,1,0:T(8,128)(2,1)S(1)}, u32[]{:S(2)}, u32[]{:S(2)}) collective-permute-start(bf16[4,128,256]{2,1,0:T(8,128)(2,1)S(1)} %pad_maximum_fusion.2.refs_4_), channel_id=1, source_target_pairs={{0,128},{8,136},{16,144},{24,152},{32,160},{40,168},{48,176},{56,1... | collective-permute-start | bytes 786440 | tf_op jit(solution)/shard_map/ppermute | solution.py:287
  45.6 23.0 %copy-start.8 = (s32[1024]{0:T(1024)S(1)}, s32[1024]{0:T(1024)}, u32[]{:S(2)}) copy-start(s32[1024]{0:T(1024)} %param.6) | copy-start | bytes 12292
  45.6 15.8 %collective-permute-start.5 = (bf16[4,128,256]{2,1,0:T(8,128)(2,1)S(1)}, bf16[4,128,256]{2,1,0:T(8,128)(2,1)S(1)}, u32[]{:S(2)}, u32[]{:S(2)}) collective-permute-start(bf16[4,128,256]{2,1,0:T(8,128)(2,1)S(1)} %pad_maximum_fusion.1.refs_0_), channel_id=1, source_target_pairs={{0,48},{8,56},{16,0},{24,8},{32,16},{40,24},{48,32},{56,40},{64,11... | collective-permute-start | bytes 786440 | tf_op jit(solution)/shard_map/ppermute | solution.py:287
  46.0 14.7 %collective-permute-start.4 = (bf16[4,128,256]{2,1,0:T(8,128)(2,1)S(1)}, bf16[4,128,256]{2,1,0:T(8,128)(2,1)S(1)}, u32[]{:S(2)}, u32[]{:S(2)}) collective-permute-start(bf16[4,128,256]{2,1,0:T(8,128)(2,1)S(1)} %pad_maximum_fusion.1.refs_0_), channel_id=1, source_target_pairs={{0,32},{8,40},{16,48},{24,56},{32,0},{40,8},{48,16},{56,24},{64,96... | collective-permute-start | bytes 786440 | tf_op jit(solution)/shard_map/ppermute | solution.py:287
  47.1 11.5 %collective-permute-start.3 = (bf16[4,128,256]{2,1,0:T(8,128)(2,1)S(1)}, bf16[4,128,256]{2,1,0:T(8,128)(2,1)S(1)}, u32[]{:S(2)}, u32[]{:S(2)}) collective-permute-start(bf16[4,128,256]{2,1,0:T(8,128)(2,1)S(1)} %pad_maximum_fusion.1.refs_0_), channel_id=1, source_target_pairs={{0,16},{8,24},{16,32},{24,40},{32,48},{40,56},{48,0},{56,8},{64,80... | collective-permute-start | bytes 786440 | tf_op jit(solution)/shard_map/ppermute | solution.py:287
  58.7 9.3 %copy-start.3 = (bf16[4,128,256]{2,1,0:T(8,128)(2,1)}, bf16[4,128,256]{2,1,0:T(8,128)(2,1)S(1)}, u32[]{:S(2)}) copy-start(bf16[4,128,256]{2,1,0:T(8,128)(2,1)S(1)} %collective-permute-done.3.refs_1_) | copy-start | bytes 786436
  58.7 7.1 %collective-permute-start.9 = (bf16[4,128,256]{2,1,0:T(8,128)(2,1)S(1)}, bf16[4,128,256]{2,1,0:T(8,128)(2,1)S(1)}, u32[]{:S(2)}, u32[]{:S(2)}) collective-permute-start(bf16[4,128,256]{2,1,0:T(8,128)(2,1)S(1)} %pad_maximum_fusion.2.refs_4_), channel_id=1, source_target_pairs={{0,64},{8,72},{16,80},{24,88},{32,96},{40,104},{48,112},{56,120},{... | collective-permute-start | bytes 786440 | tf_op jit(solution)/shard_map/ppermute | solution.py:287
  60.7 6.6 %copy-start.1 = (bf16[4,128,256]{2,1,0:T(8,128)(2,1)}, bf16[4,128,256]{2,1,0:T(8,128)(2,1)S(1)}, u32[]{:S(2)}) copy-start(bf16[4,128,256]{2,1,0:T(8,128)(2,1)S(1)} %collective-permute-done.4.refs_2_) | copy-start | bytes 786436
  65.7 2.3 %copy-start.5 = (bf16[4,128,256]{2,1,0:T(8,128)(2,1)}, bf16[4,128,256]{2,1,0:T(8,128)(2,1)S(1)}, u32[]{:S(2)}) copy-start(bf16[4,128,256]{2,1,0:T(8,128)(2,1)S(1)} %collective-permute-done.9.refs_5_) | copy-start | bytes 786436
  68.0 10.2 %collective-permute-start.12 = (bf16[32,128,256]{2,1,0:T(8,128)(2,1)}, bf16[32,128,256]{2,1,0:T(8,128)(2,1)S(1)}, u32[]{:S(2)}, u32[]{:S(2)}) collective-permute-start(bf16[32,128,256]{2,1,0:T(8,128)(2,1)} %constant_dynamic-update-slice_fusion), channel_id=1, source_target_pairs={{0,8},{8,0},{16,24},{24,16},{32,40},{40,32},{48,56},{56,48},{64,72... | collective-permute-start | bytes 6291464 | tf_op jit(solution)/shard_map/ppermute | solution.py:287
  68.6 1.0 copy-start.2
  69.6 0.9 copy-start.4
  70.5 0.9 copy-start.6
  71.5 6.8 %copy-start.7 = (bf16[1024,4096]{1,0:T(8,128)(2,1)S(1)}, bf16[1024,4096]{1,0:T(8,128)(2,1)}, u32[]{:S(2)}) copy-start(bf16[1024,4096]{1,0:T(8,128)(2,1)} %sk_ref.5) | copy-start | bytes 25165828
  78.2 3.7 %copy-start.10 = (pred[3]{0:T(512)(128)(4,1)S(1)}, pred[3]{0:T(512)(128)(4,1)}, u32[]{:S(2)}) copy-start(pred[3]{0:T(512)(128)(4,1)} %constant.125.clone.1) | copy-start | bytes 13
  100.7 26.9 %all-to-all-start.9 = ((bf16[32,192,128]{2,1,0:T(8,128)(2,1)}), bf16[32,192,128]{2,1,0:T(8,128)(2,1)S(1)}, u32[]{:S(2)}, u32[]{:S(2)}) async-start(bf16[32,192,128]{2,1,0:T(8,128)(2,1)} %copy-done), calls=%async_computation.9 | async-start | bytes 3145728 | tf_op jit(solution)/shard_map/all_to_all | solution.py:354
  128.2 16.1 %all-to-all-start.8 = ((f32[32,1,2]{2,1,0:T(1,128)}), f32[32,1,2]{2,1,0:T(1,128)S(1)}, u32[]{:S(2)}, u32[]{:S(2)}) async-start(f32[32,1,2]{2,1,0:T(1,128)} %broadcast_in_dim.88), calls=%async_computation.8 | async-start | bytes 32768 | tf_op jit(solution)/shard_map/all_to_all | solution.py:273
  134.7 10.9 %copy-start.9 = (s32[512]{0:T(512)S(1)}, s32[512]{0:T(512)}, u32[]{:S(2)}) copy-start(s32[512]{0:T(512)} %param.7) | copy-start | bytes 6148

commit v2 on v1

--- a/solution.py
+++ b/solution.py
@@ -6,6 +6,7 @@
 from jax.experimental import pallas as pl
 from jax.experimental.pallas import tpu as pltpu
 from jax.sharding import PartitionSpec as P
+
 
 BF = jnp.bfloat16
 F32 = jnp.float32
@@ -214,6 +215,28 @@
     )(got)
 
 
+def joined_kernel(*refs):
+    parts, out_ref = refs[:-1], refs[-1]
+    size = parts[0].shape[0]
+    for i, part in enumerate(parts):
+        out_ref[i * size : (i + 1) * size] = part[...]
+
+
+def joined(parts):
+    size, *rest = parts[0].shape
+    return pl.pallas_call(
+        joined_kernel,
+        in_specs=[pl.BlockSpec(memory_space=pltpu.VMEM)] * len(parts),
+        out_specs=pl.BlockSpec(memory_space=pltpu.VMEM),
+        out_shape=jax.ShapeDtypeStruct((size * len(parts), *rest), parts[0].dtype),
+        compiler_params=pltpu.CompilerParams(vmem_limit_bytes=8 * 2**20),
+        cost_estimate=pl.CostEstimate(
+            flops=0, bytes_accessed=4 * len(parts) * parts[0].size, transcendentals=0
+        ),
+        name="joined",
+    )(*parts)
+
+
 def score_kernel(scale, where_ref, assign_ref, prior_ref, sk_ref, *refs):
     parts, out_ref = refs[:-1], refs[-1]
     medoids = 2 * parts[0].shape[1]
@@ -324,7 +347,7 @@
 
 
 def shards(sketches, assignment, medoid_ids):
-    row_count, feat_width = sketches.shape
+    row_count, _ = sketches.shape
     medoid_count = medoid_ids.shape[0]
     half = medoid_count // 2
     pts_count = lax.axis_size("pts")
@@ -340,26 +363,28 @@
         [p * row_count, m, core, p // 8, (p // 2) % 4, other, own, own]
     ).astype(I32)
 
-    med_send, grad_send, over = pick(where, assignment, medoid_ids, sketches, pts_count)
+    med_send, grad_send, over = pick(
+        where, assignment, medoid_ids, sketches, pts_count
+    )
     med_got = lax.all_to_all(med_send, "pts", 0, 0, tiled=True)
+    grad_got = lax.all_to_all(grad_send, "pts", 0, 0, tiled=True)
     piece = place(where, med_got, half)
     a, b = piece[: half // 2], piece[half // 2 :]
     pa = jnp.stack([a] + [shifted(a, k, 0, 0) for k in (1, 2, 3)])
     pb = jnp.stack([b] + [shifted(b, 0, k, 0) for k in (1, 2, 3)])
     qa = [pa] + [shifted(pa, 0, k, 0) for k in (1, 2, 3)]
     qb = [pb] + [shifted(pb, k, 0, 0) for k in (1, 2, 3)]
-    mine = jnp.concatenate(qa + qb, axis=0)
+    mine = joined(qa + qb)
     theirs = shifted(mine, 0, 0, 1)
 
-    grad_got = lax.all_to_all(grad_send, "pts", 0, 0, tiled=True)
-    gradient_sums, counts = sums(grad_got, medoid_count)
-
     prior = jnp.full((8, row_count), NONE, F32)
-    stats = scored(where, assignment, prior, sketches, qa + qb)
+    stats = scored(where, assignment, prior, sketches, [mine])
     stats = scored(where_other, assignment, stats, sketches, [theirs])
     flag = jnp.broadcast_to(over[0:1, 0:1], (1, row_count))
     packed = jnp.concatenate([stats[:2], flag], axis=0)
-    both = from_everyone(packed, "med").max(axis=0)
+    both = from_everyone(packed, "med")
+    gradient_sums, counts = sums(grad_got, medoid_count)
+    both = both.max(axis=0)
     gap = both[0] - both[1]
     last = from_everyone(jnp.stack([jnp.sum(both[0]), both[2, 0]]), "pts")
     cover = jnp.sum(last[:, 0])
@@ -373,4 +398,6 @@
 def solution(mesh):
     in_specs = (P("pts", None), P("pts"), P("med"))
     out_specs = (P("pts"), P(), P("med"), P("pts", "med"))
-    return jax.shard_map(shards, mesh=mesh, in_specs=in_specs, out_specs=out_specs, check_vma=False)
+    return jax.shard_map(
+        shards, mesh=mesh, in_specs=in_specs, out_specs=out_specs, check_vma=False
+    )

time: 151 us -> 150 us (level)
  local copies, waits for them, and re-layouts: 14.9 us -> 2.52 us
  starting transfers between devices: 28.4 us -> 35.4 us
  Pallas kernels: 33.6 us -> 37.4 us
    unnamed x35 -> x6, local copies, waits for them, and re-layouts: 11.6 us -> 0.01 us
    ppermute x13, starting transfers between devices: 15.2 us -> 21.1 us  [shifted(): return lax.ppermute(array, 'pts', pairs)]
    pallas_call x2, Pallas kernels: 10.4 us -> 13 us  [scored(): pl.pallas_call(functools.partial(score_kernel, 1.0 / feats), grid_spec=pl...]
  transfers between devices with their start and end apart: 15 -> 15, of which waited for: 4 -> 10; matrix products, arithmetic and copies ran while one was open for 8% -> 2% of each run, Pallas kernels for 11% -> 11%
where the time goes in v2:
time: 150 us; the launch traced here: 148 us
  Pallas kernels  37.4 us (25%)
  starting transfers between devices  35.4 us (24%)
  blocking collectives  35.3 us (24%)
  waiting for transfers between devices  29.7 us (20%)
  other arithmetic  4.61 us (3%)
  between operations  2.59 us (2%)
  local copies, waits for them, and re-layouts  2.52 us (2%)
    ppermute x13, starting transfers between devices, shifted(): return lax.ppermute(array, 'pts', pairs)  21.1 us
    all_to_all x1, blocking collectives, from_everyone(): lax.all_to_all(jnp.broadcast_to(array[None], (size, *array.shape)), axis,...  18 us
    all_to_all x1, waiting for transfers between devices, shards(): grad_got = lax.all_to_all(grad_send, 'pts', 0, 0, tiled=True)  17.6 us
    all_to_all x1, blocking collectives, shards(): med_got = lax.all_to_all(med_send, 'pts', 0, 0, tiled=True)  17.3 us
    pallas_call x1, Pallas kernels, pick(): pl.pallas_call(pick_kernel, grid_spec=pltpu.PrefetchScalarGridSpec(num_sc...  13.7 us
    pallas_call x2, Pallas kernels, scored(): pl.pallas_call(functools.partial(score_kernel, 1.0 / feats), grid_spec=pl...  13 us
    ppermute x13, waiting for transfers between devices, shifted(): return lax.ppermute(array, 'pts', pairs)  12.1 us
    pallas_call x1, Pallas kernels, sums(): pl.pallas_call(sums_kernel, in_specs=[pl.BlockSpec(memory_space=pltpu.VME...  9.53 us
  transfers between devices with their start and end apart: 15, of which 10 were waited for; matrix products, arithmetic and copies ran while one was open for 2% of the time, Pallas kernels for 11%

profile of v2, /device:TPU:2, one launch (start us, length us, event | category | flops | bytes accessed | tf_op | source)
XLA Modules:
  0.0 148.2 jit_solution(11067062655050141538)
XLA Ops:
  0.7 0.1 stack.89.where_ref
  0.8 13.7 %pick.1 = (bf16[32,32,256]{2,1,0:T(8,128)(2,1)S(1)}, bf16[32,192,128]{2,1,0:T(8,128)(2,1)}, f32[8,128]{1,0:T(8,128)S(1)}) custom-call(s32[8]{0:T(128)S(1)} %stack.89.where_ref, s32[8,128]{1,0:T(8,128)} %bitcast.60, s32[1,512]{1,0:T(1,128)} %bitcast.71, bf16[1024,4096]{1,0:T(8,128)(2,1)} %sk_ref.5), custom_call_target="tpu_custom_call" | custom-call | flops 2147483648 | bytes 8388608 | tf_op jit(solution)/shard_map/pick/pallas_call | solution.py:108
  14.5 17.3 %all_to_all.51.got_ref = bf16[32,32,256]{2,1,0:T(8,128)(2,1)S(1)} all-to-all(bf16[32,32,256]{2,1,0:T(8,128)(2,1)S(1)} %get-tuple-element.48), channel_id=1, replica_groups=mesh['pts'=32,'med'=8] {'pts'}, dimensions={0} | all-to-all | bytes 1048576 | tf_op jit(solution)/shard_map/all_to_all | solution.py:369
  31.8 1.0 place.1
  32.9 1.7 %collective-permute-start.1 = (bf16[128,256]{1,0:T(8,128)(2,1)S(1)}, bf16[128,256]{1,0:T(8,128)(2,1)S(1)}, u32[]{:S(2)}, u32[]{:S(2)}) collective-permute-start(bf16[128,256]{1,0:T(8,128)(2,1)S(1)} %get-tuple-element.96), channel_id=1, source_target_pairs={{0,128},{8,136},{16,144},{24,152},{32,160},{40,168},{48,176},{56,1... | collective-permute-start | bytes 196616 | tf_op jit(solution)/shard_map/ppermute | solution.py:310
  34.6 1.4 collective-permute-start
  35.9 0.6 collective-permute-start.2
  36.6 2.6 %collective-permute-done.1 = bf16[128,256]{1,0:T(8,128)(2,1)S(1)} collective-permute-done((bf16[128,256]{1,0:T(8,128)(2,1)S(1)}, bf16[128,256]{1,0:T(8,128)(2,1)S(1)}, u32[]{:S(2)}, u32[]{:S(2)}) %collective-permute-start.1) | collective-permute-done | bytes 65568 | tf_op jit(solution)/shard_map/ppermute | solution.py:310
  39.2 0.8 collective-permute-done
  40.0 0.5 collective-permute-done.2
  40.6 1.6 %collective-permute-start.5 = (bf16[4,128,256]{2,1,0:T(8,128)(2,1)S(1)}, bf16[4,128,256]{2,1,0:T(8,128)(2,1)S(1)}, u32[]{:S(2)}, u32[]{:S(2)}) collective-permute-start(bf16[4,128,256]{2,1,0:T(8,128)(2,1)S(1)} %pad_maximum_fusion.1.refs_0_), channel_id=1, source_target_pairs={{0,48},{8,56},{16,0},{24,8},{32,16},{40,24},{48,32},{56,40},{64,11... | collective-permute-start | bytes 786440 | tf_op jit(solution)/shard_map/ppermute | solution.py:310
  42.2 1.3 collective-permute-start.7
  43.5 0.1 collective-permute-start.6
  43.6 3.1 %collective-permute-start.8 = (bf16[128,256]{1,0:T(8,128)(2,1)S(1)}, bf16[128,256]{1,0:T(8,128)(2,1)S(1)}, u32[]{:S(2)}, u32[]{:S(2)}) collective-permute-start(bf16[128,256]{1,0:T(8,128)(2,1)S(1)} %get-tuple-element.95), channel_id=1, source_target_pairs={{0,48},{8,56},{16,0},{24,8},{32,16},{40,24},{48,32},{56,40},{64,11... | collective-permute-start | bytes 196616 | tf_op jit(solution)/shard_map/ppermute | solution.py:310
  46.7 1.0 collective-permute-start.4
  47.8 0.3 collective-permute-done.7
  48.1 4.2 %collective-permute-start.3 = (bf16[4,128,256]{2,1,0:T(8,128)(2,1)S(1)}, bf16[4,128,256]{2,1,0:T(8,128)(2,1)S(1)}, u32[]{:S(2)}, u32[]{:S(2)}) collective-permute-start(bf16[4,128,256]{2,1,0:T(8,128)(2,1)S(1)} %pad_maximum_fusion.1.refs_0_), channel_id=1, source_target_pairs={{0,16},{8,24},{16,32},{24,40},{32,48},{40,56},{48,0},{56,8},{64,80... | collective-permute-start | bytes 786440 | tf_op jit(solution)/shard_map/ppermute | solution.py:310
  52.3 0.4 collective-permute-done.8
  52.7 1.6 %collective-permute-start.11 = (bf16[4,128,256]{2,1,0:T(8,128)(2,1)S(1)}, bf16[4,128,256]{2,1,0:T(8,128)(2,1)S(1)}, u32[]{:S(2)}, u32[]{:S(2)}) collective-permute-start(bf16[4,128,256]{2,1,0:T(8,128)(2,1)S(1)} %pad_maximum_fusion.2.refs_4_), channel_id=1, source_target_pairs={{0,192},{8,200},{16,208},{24,216},{32,224},{40,232},{48,240},{56,2... | collective-permute-start | bytes 786440 | tf_op jit(solution)/shard_map/ppermute | solution.py:310
  54.4 1.7 %collective-permute-start.10 = (bf16[4,128,256]{2,1,0:T(8,128)(2,1)S(1)}, bf16[4,128,256]{2,1,0:T(8,128)(2,1)S(1)}, u32[]{:S(2)}, u32[]{:S(2)}) collective-permute-start(bf16[4,128,256]{2,1,0:T(8,128)(2,1)S(1)} %pad_maximum_fusion.2.refs_4_), channel_id=1, source_target_pairs={{0,128},{8,136},{16,144},{24,152},{32,160},{40,168},{48,176},{56,1... | collective-permute-start | bytes 786440 | tf_op jit(solution)/shard_map/ppermute | solution.py:310
  56.1 2.5 %collective-permute-start.9 = (bf16[4,128,256]{2,1,0:T(8,128)(2,1)S(1)}, bf16[4,128,256]{2,1,0:T(8,128)(2,1)S(1)}, u32[]{:S(2)}, u32[]{:S(2)}) collective-permute-start(bf16[4,128,256]{2,1,0:T(8,128)(2,1)S(1)} %pad_maximum_fusion.2.refs_4_), channel_id=1, source_target_pairs={{0,64},{8,72},{16,80},{24,88},{32,96},{40,104},{48,112},{56,120},{... | collective-permute-start | bytes 786440 | tf_op jit(solution)/shard_map/ppermute | solution.py:310
  58.7 2.1 %collective-permute-done.3.refs_1_ = bf16[4,128,256]{2,1,0:T(8,128)(2,1)S(1)} collective-permute-done((bf16[4,128,256]{2,1,0:T(8,128)(2,1)S(1)}, bf16[4,128,256]{2,1,0:T(8,128)(2,1)S(1)}, u32[]{:S(2)}, u32[]{:S(2)}) %collective-permute-start.3) | collective-permute-done | bytes 262176 | tf_op jit(solution)/shard_map/ppermute | solution.py:310
  60.7 1.3 collective-permute-done.11.refs_7_
  62.0 3.1 %collective-permute-done.10.refs_6_ = bf16[4,128,256]{2,1,0:T(8,128)(2,1)S(1)} collective-permute-done((bf16[4,128,256]{2,1,0:T(8,128)(2,1)S(1)}, bf16[4,128,256]{2,1,0:T(8,128)(2,1)S(1)}, u32[]{:S(2)}, u32[]{:S(2)}) %collective-permute-start.10) | collective-permute-done | bytes 262176 | tf_op jit(solution)/shard_map/ppermute | solution.py:310
  65.1 0.9 collective-permute-done.9.refs_5_
  66.0 0.1 joined.1.refs_0_
  66.1 0.1 collective-permute-start.12
  66.2 0.1 stack.88.where_ref
  66.3 0.5 slice.45
  66.8 6.2 %scored.2.prior_ref = f32[8,1024]{1,0:T(8,128)S(1)} custom-call(s32[8]{0:T(128)S(1)} %stack.89.where_ref, s32[1,1024]{1,0:T(1,128)S(1)} %bitcast.61, f32[8,1024]{1,0:T(8,128)S(1)} %broadcast_in_dim.49.prior_ref, bf16[1024,4096]{1,0:T(8,128)(2,1)} %sk_ref.5, bf16[32,128,256]{2,1,0:T(8,128)(2,1)S(1)} %joined.1.refs_0_), custom_call_target="tpu_custom_call" | custom-call | flops 2147483648 | bytes 8388608 | tf_op jit(solution)/shard_map/scored/pallas_call | solution.py:272
  73.0 0.0 copy-start.2
  73.1 6.8 %scored.3 = f32[8,1024]{1,0:T(8,128)S(1)} custom-call(s32[8]{0:T(128)S(1)} %stack.88.where_ref, s32[1,1024]{1,0:T(1,128)S(1)} %bitcast.62, f32[8,1024]{1,0:T(8,128)S(1)} %scored.2.prior_ref, bf16[1024,4096]{1,0:T(8,128)(2,1)} %sk_ref.5, bf16[32,128,256]{2,1,0:T(8,128)(2,1)} %collective-permute-done.12.refs_0_), custom_call_target="tpu_custom_call" | custom-call | flops 2147483648 | bytes 8388608 | tf_op jit(solution)/shard_map/scored/pallas_call | solution.py:272
  79.9 0.7 slice_select_fusion
  80.7 18.0 %all_to_all.52 = f32[8,3,1024]{2,1,0:T(4,128)S(1)} all-to-all(f32[8,3,1024]{2,1,0:T(4,128)S(1)} %broadcast_in_dim.87), channel_id=1, replica_groups=mesh['pts'=32,'med'=8] {'med'}, dimensions={0} | all-to-all | bytes 196608 | tf_op jit(solution)/shard_map/all_to_all | solution.py:296
  98.7 7.8 %all-to-all-start.9 = ((bf16[32,192,128]{2,1,0:T(8,128)(2,1)}), bf16[32,192,128]{2,1,0:T(8,128)(2,1)S(1)}, u32[]{:S(2)}, u32[]{:S(2)}) async-start(bf16[32,192,128]{2,1,0:T(8,128)(2,1)} %get-tuple-element.50), calls=%async_computation.9 | async-start | bytes 3145728 | tf_op jit(solution)/shard_map/all_to_all | solution.py:370
  106.5 0.5 slice.61
  107.0 0.6 fusion.7
  107.6 1.4 pad_maximum_fusion.3
  109.0 17.6 %all-to-all-done.9.got_ref = bf16[32,192,128]{2,1,0:T(8,128)(2,1)S(1)} async-done(((bf16[32,192,128]{2,1,0:T(8,128)(2,1)}), bf16[32,192,128]{2,1,0:T(8,128)(2,1)S(1)}, u32[]{:S(2)}, u32[]{:S(2)}) %all-to-all-start.9) | async-done | bytes 1572896 | tf_op jit(solution)/shard_map/all_to_all | solution.py:370
  126.6 0.6 broadcast_in_dim.88
  127.2 6.6 %all-to-all-start.8 = ((f32[32,1,2]{2,1,0:T(1,128)}), f32[32,1,2]{2,1,0:T(1,128)S(1)}, u32[]{:S(2)}, u32[]{:S(2)}) async-start(f32[32,1,2]{2,1,0:T(1,128)} %broadcast_in_dim.88), calls=%async_computation.8 | async-start | bytes 32768 | tf_op jit(solution)/shard_map/all_to_all | solution.py:296
  133.7 9.5 %sums.1 = (f32[128,512]{1,0:T(8,128)}, f32[8,512]{1,0:T(8,128)S(1)}) custom-call(bf16[32,192,128]{2,1,0:T(8,128)(2,1)S(1)} %all-to-all-done.9.got_ref), custom_call_target="tpu_custom_call" | custom-call | flops 1610612736 | bytes 1572864 | tf_op jit(solution)/shard_map/sums/pallas_call | solution.py:202
  143.3 0.1 copy.38
  143.3 0.6 slice_reduce_fusion.2
  144.6 2.4 %conditional.1 = (f32[1024]{0:T(1024)}, f32[]{:T(128)}, f32[512]{0:T(512)}, f32[128,512]{1,0:T(8,128)}) conditional(s32[]{:T(128)} %convert_element_type.11, (f32[3,1024]{1,0:T(4,128)S(1)}, f32[1,1024]{1,0:T(1,128)S(1)}, f32[32,2]{0,1:T(2,128)S(1)}, f32[8,512]{1,0:T(8,128)S(1)}, f32[128,512]{1,0:T(8,128)}) %tuple.49, (s32[512]{0:T(512)S(1)}, ...), branch_computations={%region_3.5_spmd, %region_5.14_spmd} | conditional | flops 8601925632 | bytes 130077376 | solution.py:393
  144.6 0.6 slice_reduce_fusion
  145.9 0.6 slice.32
  146.5 0.6 slice_subtract_fusion
  (16 shorter events, 0.2 us)
Async XLA Ops:
  14.5 52.3 %copy-start = (s32[1024]{0:T(1024)S(1)}, s32[1024]{0:T(1024)}, u32[]{:S(2)}) copy-start(s32[1024]{0:T(1024)} %param.6) | copy-start | bytes 12292
  32.9 6.4 %collective-permute-start.1 = (bf16[128,256]{1,0:T(8,128)(2,1)S(1)}, bf16[128,256]{1,0:T(8,128)(2,1)S(1)}, u32[]{:S(2)}, u32[]{:S(2)}) collective-permute-start(bf16[128,256]{1,0:T(8,128)(2,1)S(1)} %get-tuple-element.96), channel_id=1, source_target_pairs={{0,128},{8,136},{16,144},{24,152},{32,160},{40,168},{48,176},{56,1... | collective-permute-start | bytes 196616 | tf_op jit(solution)/shard_map/ppermute | solution.py:310
  34.6 5.5 %collective-permute-start = (bf16[128,256]{1,0:T(8,128)(2,1)S(1)}, bf16[128,256]{1,0:T(8,128)(2,1)S(1)}, u32[]{:S(2)}, u32[]{:S(2)}) collective-permute-start(bf16[128,256]{1,0:T(8,128)(2,1)S(1)} %get-tuple-element.96), channel_id=1, source_target_pairs={{0,64},{8,72},{16,80},{24,88},{32,96},{40,104},{48,112},{56,120},{... | collective-permute-start | bytes 196616 | tf_op jit(solution)/shard_map/ppermute | solution.py:310
  35.9 4.7 %collective-permute-start.2 = (bf16[128,256]{1,0:T(8,128)(2,1)S(1)}, bf16[128,256]{1,0:T(8,128)(2,1)S(1)}, u32[]{:S(2)}, u32[]{:S(2)}) collective-permute-start(bf16[128,256]{1,0:T(8,128)(2,1)S(1)} %get-tuple-element.96), channel_id=1, source_target_pairs={{0,192},{8,200},{16,208},{24,216},{32,224},{40,232},{48,240},{56,2... | collective-permute-start | bytes 196616 | tf_op jit(solution)/shard_map/ppermute | solution.py:310
  40.6 15.5 %collective-permute-start.5 = (bf16[4,128,256]{2,1,0:T(8,128)(2,1)S(1)}, bf16[4,128,256]{2,1,0:T(8,128)(2,1)S(1)}, u32[]{:S(2)}, u32[]{:S(2)}) collective-permute-start(bf16[4,128,256]{2,1,0:T(8,128)(2,1)S(1)} %pad_maximum_fusion.1.refs_0_), channel_id=1, source_target_pairs={{0,48},{8,56},{16,0},{24,8},{32,16},{40,24},{48,32},{56,40},{64,11... | collective-permute-start | bytes 786440 | tf_op jit(solution)/shard_map/ppermute | solution.py:310
  42.2 5.9 %collective-permute-start.7 = (bf16[128,256]{1,0:T(8,128)(2,1)S(1)}, bf16[128,256]{1,0:T(8,128)(2,1)S(1)}, u32[]{:S(2)}, u32[]{:S(2)}) collective-permute-start(bf16[128,256]{1,0:T(8,128)(2,1)S(1)} %get-tuple-element.95), channel_id=1, source_target_pairs={{0,32},{8,40},{16,48},{24,56},{32,0},{40,8},{48,16},{56,24},{64,96... | collective-permute-start | bytes 196616 | tf_op jit(solution)/shard_map/ppermute | solution.py:310
  43.5 8.8 %collective-permute-start.6 = (bf16[128,256]{1,0:T(8,128)(2,1)S(1)}, bf16[128,256]{1,0:T(8,128)(2,1)S(1)}, u32[]{:S(2)}, u32[]{:S(2)}) collective-permute-start(bf16[128,256]{1,0:T(8,128)(2,1)S(1)} %get-tuple-element.95), channel_id=1, source_target_pairs={{0,16},{8,24},{16,32},{24,40},{32,48},{40,56},{48,0},{56,8},{64,80... | collective-permute-start | bytes 196616 | tf_op jit(solution)/shard_map/ppermute | solution.py:310
  43.6 9.1 %collective-permute-start.8 = (bf16[128,256]{1,0:T(8,128)(2,1)S(1)}, bf16[128,256]{1,0:T(8,128)(2,1)S(1)}, u32[]{:S(2)}, u32[]{:S(2)}) collective-permute-start(bf16[128,256]{1,0:T(8,128)(2,1)S(1)} %get-tuple-element.95), channel_id=1, source_target_pairs={{0,48},{8,56},{16,0},{24,8},{32,16},{40,24},{48,32},{56,40},{64,11... | collective-permute-start | bytes 196616 | tf_op jit(solution)/shard_map/ppermute | solution.py:310
  46.7 11.9 %collective-permute-start.4 = (bf16[4,128,256]{2,1,0:T(8,128)(2,1)S(1)}, bf16[4,128,256]{2,1,0:T(8,128)(2,1)S(1)}, u32[]{:S(2)}, u32[]{:S(2)}) collective-permute-start(bf16[4,128,256]{2,1,0:T(8,128)(2,1)S(1)} %pad_maximum_fusion.1.refs_0_), channel_id=1, source_target_pairs={{0,32},{8,40},{16,48},{24,56},{32,0},{40,8},{48,16},{56,24},{64,96... | collective-permute-start | bytes 786440 | tf_op jit(solution)/shard_map/ppermute | solution.py:310
  48.1 12.7 %collective-permute-start.3 = (bf16[4,128,256]{2,1,0:T(8,128)(2,1)S(1)}, bf16[4,128,256]{2,1,0:T(8,128)(2,1)S(1)}, u32[]{:S(2)}, u32[]{:S(2)}) collective-permute-start(bf16[4,128,256]{2,1,0:T(8,128)(2,1)S(1)} %pad_maximum_fusion.1.refs_0_), channel_id=1, source_target_pairs={{0,16},{8,24},{16,32},{24,40},{32,48},{40,56},{48,0},{56,8},{64,80... | collective-permute-start | bytes 786440 | tf_op jit(solution)/shard_map/ppermute | solution.py:310
  52.7 9.3 %collective-permute-start.11 = (bf16[4,128,256]{2,1,0:T(8,128)(2,1)S(1)}, bf16[4,128,256]{2,1,0:T(8,128)(2,1)S(1)}, u32[]{:S(2)}, u32[]{:S(2)}) collective-permute-start(bf16[4,128,256]{2,1,0:T(8,128)(2,1)S(1)} %pad_maximum_fusion.2.refs_4_), channel_id=1, source_target_pairs={{0,192},{8,200},{16,208},{24,216},{32,224},{40,232},{48,240},{56,2... | collective-permute-start | bytes 786440 | tf_op jit(solution)/shard_map/ppermute | solution.py:310
  54.4 10.7 %collective-permute-start.10 = (bf16[4,128,256]{2,1,0:T(8,128)(2,1)S(1)}, bf16[4,128,256]{2,1,0:T(8,128)(2,1)S(1)}, u32[]{:S(2)}, u32[]{:S(2)}) collective-permute-start(bf16[4,128,256]{2,1,0:T(8,128)(2,1)S(1)} %pad_maximum_fusion.2.refs_4_), channel_id=1, source_target_pairs={{0,128},{8,136},{16,144},{24,152},{32,160},{40,168},{48,176},{56,1... | collective-permute-start | bytes 786440 | tf_op jit(solution)/shard_map/ppermute | solution.py:310
  56.1 9.9 %collective-permute-start.9 = (bf16[4,128,256]{2,1,0:T(8,128)(2,1)S(1)}, bf16[4,128,256]{2,1,0:T(8,128)(2,1)S(1)}, u32[]{:S(2)}, u32[]{:S(2)}) collective-permute-start(bf16[4,128,256]{2,1,0:T(8,128)(2,1)S(1)} %pad_maximum_fusion.2.refs_4_), channel_id=1, source_target_pairs={{0,64},{8,72},{16,80},{24,88},{32,96},{40,104},{48,112},{56,120},{... | collective-permute-start | bytes 786440 | tf_op jit(solution)/shard_map/ppermute | solution.py:310
  66.1 6.9 %collective-permute-start.12 = (bf16[32,128,256]{2,1,0:T(8,128)(2,1)S(1)}, bf16[32,128,256]{2,1,0:T(8,128)(2,1)}, u32[]{:S(2)}, u32[]{:S(2)}) collective-permute-start(bf16[32,128,256]{2,1,0:T(8,128)(2,1)S(1)} %joined.1.refs_0_), channel_id=1, source_target_pairs={{0,8},{8,0},{16,24},{24,16},{32,40},{40,32},{48,56},{56,48},{64,72... | collective-permute-start | bytes 6291464 | tf_op jit(solution)/shard_map/ppermute | solution.py:310
  73.0 6.9 %copy-start.2 = (pred[3]{0:T(512)(128)(4,1)S(1)}, pred[3]{0:T(512)(128)(4,1)}, u32[]{:S(2)}) copy-start(pred[3]{0:T(512)(128)(4,1)} %constant.125.clone.1) | copy-start | bytes 13
  98.7 45.9 %copy-start.1 = (s32[512]{0:T(512)S(1)}, s32[512]{0:T(512)}, u32[]{:S(2)}) copy-start(s32[512]{0:T(512)} %param.7) | copy-start | bytes 6148
  98.7 27.9 %all-to-all-start.9 = ((bf16[32,192,128]{2,1,0:T(8,128)(2,1)}), bf16[32,192,128]{2,1,0:T(8,128)(2,1)S(1)}, u32[]{:S(2)}, u32[]{:S(2)}) async-start(bf16[32,192,128]{2,1,0:T(8,128)(2,1)} %get-tuple-element.50), calls=%async_computation.9 | async-start | bytes 3145728 | tf_op jit(solution)/shard_map/all_to_all | solution.py:370
  127.2 16.1 %all-to-all-start.8 = ((f32[32,1,2]{2,1,0:T(1,128)}), f32[32,1,2]{2,1,0:T(1,128)S(1)}, u32[]{:S(2)}, u32[]{:S(2)}) async-start(f32[32,1,2]{2,1,0:T(1,128)} %broadcast_in_dim.88), calls=%async_computation.8 | async-start | bytes 32768 | tf_op jit(solution)/shard_map/all_to_all | solution.py:296

commit v3 on v2

--- a/solution.py
+++ b/solution.py
@@ -18,13 +18,14 @@
 MED_SLOTS = 24
 SEL = GRAD_ROWS + 2 * MED_ROWS
 NONE = -1e30
+CHIPS = 4
 
 
 def contract_last(a, b):
     return lax.dot_general(a, b, (((1,), (1,)), ((), ())), preferred_element_type=F32)
 
 
-def pick_kernel(where_ref, assign_ref, ids_ref, sk_ref, med_ref, grad_ref, over_ref, sel, code):
+def pick_kernel(where_ref, assign_ref, ids_ref, sk_ref, med_ref, grad_ref, sel, code):
     step = pl.program_id(0)
 
     @pl.when(step == 0)
@@ -70,7 +71,6 @@
             position = jnp.concatenate(rows, axis=0).astype(I32)
             flag = (mine, med0 > 0, med1 > 0)[kind] & (position < limit)
             slots.append(jnp.where(flag, position, -1))
-        over_ref[...] = jnp.broadcast_to(over, over_ref.shape)
         slot_g = slots[0]
         slot_m = jnp.where(slots[1] >= 0, slots[1], -1)
         slot_n = jnp.where(slots[2] >= 0, slots[2] + MED_ROWS, -1)
@@ -89,22 +89,26 @@
                 [either[at], local_lo[at], local_hi[at], zeros], axis=0
             ).astype(BF)
             codes = codes + contract_last(fields, block)
-        code[...] = codes.astype(BF)
-
-    rows = jnp.dot(sel[...], sk_ref[...], preferred_element_type=F32).astype(BF)
+        marks = jnp.broadcast_to(jnp.concatenate([over, over], axis=1), (8, SEL))
+        third = lax.broadcasted_iota(I32, (8, SEL), 0) == 3
+        code[...] = jnp.where(third, marks, codes).astype(BF)
+
     codes = code[...]
-    for c in range(2):
-        grad_ref[c, :GRAD_SLOTS, :] = rows[:GRAD_SLOTS, c * LANES : (c + 1) * LANES]
-        grad_ref[c, GRAD_SLOTS:, :] = jnp.concatenate(
-            [codes[:, :LANES], codes[:, LANES:]], axis=0
-        )
-        at = GRAD_ROWS + c * MED_ROWS
-        med_ref[c, :, :] = jnp.concatenate([rows[at : at + MED_SLOTS], codes], axis=0)
+    lines = jnp.concatenate([codes[:, :LANES], codes[:, LANES:]], axis=0)
+    for chip in range(sk_ref.shape[1] // SEL):
+        block = sk_ref[:, chip * SEL : (chip + 1) * SEL]
+        rows = jnp.dot(sel[...], block, preferred_element_type=F32).astype(BF)
+        for c in range(2):
+            to = 2 * chip + c
+            grad_ref[to, :GRAD_SLOTS, :] = rows[:GRAD_SLOTS, c * LANES : (c + 1) * LANES]
+            grad_ref[to, GRAD_SLOTS:, :] = lines
+            at = GRAD_ROWS + c * MED_ROWS
+            med_ref[to, :, :] = jnp.concatenate([rows[at : at + MED_SLOTS], codes], axis=0)
 
 
 def pick(where, assignment, medoid_ids, sketches, pts_count):
     rows, feats = sketches.shape
-    wide = 2 * LANES
+    wide = CHIPS * 2 * LANES
     return pl.pallas_call(
         pick_kernel,
         grid_spec=pltpu.PrefetchScalarGridSpec(
@@ -116,16 +120,14 @@
                 pl.BlockSpec((rows, wide), lambda i, w: (0, i)),
             ],
             out_specs=[
-                pl.BlockSpec((2, MED_ROWS, wide), lambda i, w: (i, 0, 0)),
-                pl.BlockSpec((2, GRAD_ROWS, LANES), lambda i, w: (i, 0, 0)),
-                pl.BlockSpec((8, LANES), lambda i, w: (0, 0)),
+                pl.BlockSpec((2 * CHIPS, MED_ROWS, 2 * LANES), lambda i, w: (i, 0, 0)),
+                pl.BlockSpec((2 * CHIPS, GRAD_ROWS, LANES), lambda i, w: (i, 0, 0)),
             ],
             scratch_shapes=[pltpu.VMEM((SEL, rows), BF), pltpu.VMEM((8, SEL), BF)],
         ),
         out_shape=[
-            jax.ShapeDtypeStruct((pts_count, MED_ROWS, wide), BF),
+            jax.ShapeDtypeStruct((pts_count, MED_ROWS, 2 * LANES), BF),
             jax.ShapeDtypeStruct((pts_count, GRAD_ROWS, LANES), BF),
-            jax.ShapeDtypeStruct((8, LANES), F32),
         ],
         compiler_params=pltpu.CompilerParams(vmem_limit_bytes=24 * 2**20),
         cost_estimate=pl.CostEstimate(
@@ -135,17 +137,20 @@
     )(where, assignment.reshape(-1, LANES), medoid_ids[None, :], sketches)
 
 
-def place_kernel(where_ref, got_ref, out_ref):
+def place_kernel(where_ref, got_ref, a_ref, b_ref, flag_ref):
     core = where_ref[2]
     sources = got_ref.shape[0]
-    count = out_ref.shape[0]
-    total = jnp.zeros(out_ref.shape, F32)
+    count = 2 * a_ref.shape[0]
+    total = jnp.zeros((count, got_ref.shape[2]), F32)
+    marks = jnp.zeros((1, LANES), F32)
     per = 2 * LANES // MED_ROWS
     iota = lax.broadcasted_iota(I32, (count, per * MED_ROWS), 0)
     for g in range(sources // per):
         numbers = []
         for q in range(g * per, (g + 1) * per):
-            line = got_ref[q, MED_SLOTS : MED_SLOTS + 8, :].astype(F32)[0:1]
+            lines = got_ref[q, MED_SLOTS : MED_SLOTS + 8, :].astype(F32)
+            line = lines[0:1]
+            marks = marks + lines[3:4, :LANES]
             a = line[:, GRAD_ROWS : GRAD_ROWS + MED_ROWS]
             b = line[:, GRAD_ROWS + MED_ROWS :]
             numbers.append(jnp.where(core == 0, a, b))
@@ -153,7 +158,9 @@
         hot = (number == iota).astype(F32).astype(BF)
         block = got_ref[g * per : (g + 1) * per].reshape(per * MED_ROWS, got_ref.shape[2])
         total = total + jnp.dot(hot, block, preferred_element_type=F32)
-    out_ref[...] = total.astype(BF)
+    a_ref[...] = total[: count // 2].astype(BF)
+    b_ref[...] = total[count // 2 :].astype(BF)
+    flag_ref[...] = jnp.concatenate([marks, marks], axis=1)
 
 
 def place(where, got, count):
@@ -163,8 +170,12 @@
             pl.BlockSpec(memory_space=pltpu.SMEM),
             pl.BlockSpec(memory_space=pltpu.VMEM),
         ],
-        out_specs=pl.BlockSpec(memory_space=pltpu.VMEM),
-        out_shape=jax.ShapeDtypeStruct((count, got.shape[2]), BF),
+        out_specs=[pl.BlockSpec(memory_space=pltpu.VMEM)] * 3,
+        out_shape=[
+            jax.ShapeDtypeStruct((count // 2, got.shape[2]), BF),
+            jax.ShapeDtypeStruct((count // 2, got.shape[2]), BF),
+            jax.ShapeDtypeStruct((1, 2 * LANES), F32),
+        ],
         compiler_params=pltpu.CompilerParams(vmem_limit_bytes=8 * 2**20),
         cost_estimate=pl.CostEstimate(
             flops=2 * count * got.size, bytes_accessed=2 * got.size, transcendentals=0
@@ -181,18 +192,25 @@
     iota_b = lax.broadcasted_iota(I32, (medoids, tail), 0)
     ones = jnp.ones((GRAD_ROWS, LANES), BF)
 
-    def body(q, total):
-        codes = got_ref[q, GRAD_SLOTS:, :].astype(F32).astype(I32)
-        a = codes[1:2] - 1 + codes[2:3] * 256
-        b = (codes[9:10] - 1 + codes[10:11] * 256)[:, :tail]
-        hot = jnp.concatenate(
-            [(a == iota_a).astype(F32), (b == iota_b).astype(F32)], axis=1
-        ).astype(BF)
-        block = jnp.concatenate([got_ref[q], ones], axis=1)
-        return total + jnp.dot(hot, block, preferred_element_type=F32)
+    per = 4
+
+    def body(step, total):
+        hots, blocks = [], []
+        for k in range(per):
+            q = step * per + k
+            codes = got_ref[q, GRAD_SLOTS:, :].astype(F32).astype(I32)
+            a = codes[1:2] - 1 + codes[2:3] * 256
+            b = (codes[9:10] - 1 + codes[10:11] * 256)[:, :tail]
+            hots.append((a == iota_a).astype(F32))
+            hots.append((b == iota_b).astype(F32))
+            blocks.append(jnp.concatenate([got_ref[q], ones], axis=1))
+        hot = jnp.concatenate(hots, axis=1).astype(BF)
+        return total + jnp.dot(
+            hot, jnp.concatenate(blocks, axis=0), preferred_element_type=F32
+        )
 
     total = lax.fori_loop(
-        0, got_ref.shape[0], body, jnp.zeros((medoids, feats + LANES), F32)
+        0, got_ref.shape[0] // per, body, jnp.zeros((medoids, feats + LANES), F32)
     )
     sums_ref[...] = total[:, :feats].T
     count_ref[...] = total[:, feats:].T[:8]
@@ -237,35 +255,32 @@
     )(*parts)
 
 
-def score_kernel(scale, where_ref, assign_ref, prior_ref, sk_ref, *refs):
-    parts, out_ref = refs[:-1], refs[-1]
-    medoids = 2 * parts[0].shape[1]
-    x, y, first = where_ref[3], where_ref[4], where_ref[5]
+def score_kernel(scale, where_ref, assign_ref, mark_ref, sk_ref, own_ref, other_ref, out_ref):
+    quarter, wide = own_ref.shape[1:]
+    half = 2 * quarter
+    core, x, y, base = where_ref[2], where_ref[3], where_ref[4], where_ref[5]
     points = sk_ref.shape[0]
-    total = jnp.zeros((medoids, points), F32)
+    total = jnp.zeros((2 * half, points), F32)
     for kx in range(4):
         for ky in range(4):
             block = ((x + 4 - kx) & 3) * 4 + ((y + 4 - ky) & 3)
-            at = pl.multiple_of(block * 2 * LANES, 2 * LANES)
-            if len(parts) == 8:
-                a, b = parts[ky][kx], parts[4 + kx][ky]
-            else:
-                a, b = parts[0][ky * 4 + kx], parts[0][16 + kx * 4 + ky]
+            at = pl.multiple_of(block * wide, wide)
+            a, b = ky * 4 + kx, 16 + kx * 4 + ky
             total = total + contract_last(
-                jnp.concatenate([a, b], axis=0), sk_ref[:, pl.ds(at, 2 * LANES)]
+                jnp.concatenate([own_ref[a], own_ref[b], other_ref[a], other_ref[b]], axis=0),
+                sk_ref[:, pl.ds(at, wide)],
             )
     scores = total * scale
     best = jnp.max(scores, axis=0, keepdims=True)
     row = lax.broadcasted_iota(I32, scores.shape, 0)
-    local = assign_ref[...] - first
+    local = assign_ref[...] - base
+    here = (local >= 0) & (local < 2 * half)
+    local = jnp.where(here, local ^ (core * half), -1)
     chosen = jnp.max(jnp.where(local == row, scores, NONE), axis=0, keepdims=True)
-    prior = prior_ref[...]
-    best = jnp.maximum(best, prior[0:1])
-    chosen = jnp.maximum(chosen, prior[1:2])
-    out_ref[...] = jnp.concatenate([best, chosen, prior[2:]], axis=0)
-
-
-def scored(where, assignment, prior, sketches, parts):
+    out_ref[...] = jnp.concatenate([best, chosen, mark_ref[...]], axis=0)
+
+
+def scored(where, assignment, marks, sketches, own, other):
     rows, feats = sketches.shape
     tile = 2 * LANES
     whole = lambda a: pl.BlockSpec(a.shape, lambda i, w: (0,) * a.ndim)
@@ -276,19 +291,51 @@
             grid=(rows // tile,),
             in_specs=[
                 pl.BlockSpec((1, tile), lambda i, w: (0, i)),
-                pl.BlockSpec((8, tile), lambda i, w: (0, i)),
+                pl.BlockSpec((1, tile), lambda i, w: (0, 0)),
                 pl.BlockSpec((tile, feats), lambda i, w: (i, 0)),
-            ]
-            + [whole(a) for a in parts],
-            out_specs=pl.BlockSpec((8, tile), lambda i, w: (0, i)),
-        ),
-        out_shape=jax.ShapeDtypeStruct((8, rows), F32),
+                whole(own),
+                whole(other),
+            ],
+            out_specs=pl.BlockSpec((3, tile), lambda i, w: (0, i)),
+        ),
+        out_shape=jax.ShapeDtypeStruct((3, rows), F32),
         compiler_params=pltpu.CompilerParams(vmem_limit_bytes=24 * 2**20),
         cost_estimate=pl.CostEstimate(
-            flops=2 * rows * feats * 256, bytes_accessed=rows * feats * 2, transcendentals=0
+            flops=2 * rows * feats * 512, bytes_accessed=rows * feats * 2, transcendentals=0
         ),
         name="scored",
-    )(where, assignment[None, :], prior, sketches, *parts)
+    )(where, assignment[None, :], marks, sketches, own, other)
+
+
+def closing_kernel(a_ref, b_ref, gap_ref, send_ref, mark_ref):
+    both = jnp.maximum(a_ref[...], b_ref[...])
+    gap_ref[...] = both[0:1] - both[1:2]
+    mark_ref[0, 0] = jnp.max(both[2:3, :LANES]).astype(I32)
+    total = jnp.broadcast_to(jnp.sum(both[0:1], axis=1, keepdims=True), (1, LANES))
+    for i in range(send_ref.shape[0]):
+        send_ref[i] = total
+
+
+def closing(a, b, pts_count):
+    return pl.pallas_call(
+        closing_kernel,
+        in_specs=[pl.BlockSpec(memory_space=pltpu.VMEM)] * 2,
+        out_specs=[
+            pl.BlockSpec(memory_space=pltpu.VMEM),
+            pl.BlockSpec(memory_space=pltpu.VMEM),
+            pl.BlockSpec(memory_space=pltpu.SMEM),
+        ],
+        out_shape=[
+            jax.ShapeDtypeStruct((1, a.shape[1]), F32),
+            jax.ShapeDtypeStruct((pts_count, 1, LANES), F32),
+            jax.ShapeDtypeStruct((1, 1), I32),
+        ],
+        compiler_params=pltpu.CompilerParams(vmem_limit_bytes=4 * 2**20),
+        cost_estimate=pl.CostEstimate(
+            flops=a.size, bytes_accessed=8 * a.size, transcendentals=0
+        ),
+        name="closing",
+    )(a, b)
 
 
 def from_everyone(array, axis):
@@ -308,6 +355,10 @@
         x, y, c = chip_of(p)
         pairs.append((p, (((x + dx) % 4) * 4 + (y + dy) % 4) * 2 + (c ^ dc)))
     return lax.ppermute(array, "pts", pairs)
+
+
+def across(array, step, planes):
+    return lax.ppermute(array, "med", [(z, z ^ step) for z in range(planes)])
 
 
 def general(sketches, assignment, medoid_ids):
@@ -354,45 +405,37 @@
     p = lax.axis_index("pts")
     m = lax.axis_index("med")
     core = p % 2
-    own = m * medoid_count + core * half
-    other = m * medoid_count + (1 - core) * half
+    planes = lax.axis_size("med")
     where = jnp.stack(
-        [p * row_count, m, core, p // 8, (p // 2) % 4, own, other, other]
+        [p * row_count, m, core, p // 8, (p // 2) % 4, m * medoid_count, m, m]
     ).astype(I32)
-    where_other = jnp.stack(
-        [p * row_count, m, core, p // 8, (p // 2) % 4, other, own, own]
-    ).astype(I32)
-
-    med_send, grad_send, over = pick(
+
+    med_send, grad_send = pick(
         where, assignment, medoid_ids, sketches, pts_count
     )
     med_got = lax.all_to_all(med_send, "pts", 0, 0, tiled=True)
-    grad_got = lax.all_to_all(grad_send, "pts", 0, 0, tiled=True)
-    piece = place(where, med_got, half)
-    a, b = piece[: half // 2], piece[half // 2 :]
+    a, b, marks = place(where, med_got, half)
     pa = jnp.stack([a] + [shifted(a, k, 0, 0) for k in (1, 2, 3)])
     pb = jnp.stack([b] + [shifted(b, 0, k, 0) for k in (1, 2, 3)])
     qa = [pa] + [shifted(pa, 0, k, 0) for k in (1, 2, 3)]
     qb = [pb] + [shifted(pb, k, 0, 0) for k in (1, 2, 3)]
-    mine = joined(qa + qb)
-    theirs = shifted(mine, 0, 0, 1)
-
-    prior = jnp.full((8, row_count), NONE, F32)
-    stats = scored(where, assignment, prior, sketches, [mine])
-    stats = scored(where_other, assignment, stats, sketches, [theirs])
-    flag = jnp.broadcast_to(over[0:1, 0:1], (1, row_count))
-    packed = jnp.concatenate([stats[:2], flag], axis=0)
-    both = from_everyone(packed, "med")
-    gradient_sums, counts = sums(grad_got, medoid_count)
-    both = both.max(axis=0)
-    gap = both[0] - both[1]
-    last = from_everyone(jnp.stack([jnp.sum(both[0]), both[2, 0]]), "pts")
-    cover = jnp.sum(last[:, 0])
-    full = jnp.max(last[:, 1]) > 0.0
-    fast = (gap, cover / (row_count * pts_count), counts[0], gradient_sums)
-    return lax.cond(
-        full, lambda: general(sketches, assignment, medoid_ids), lambda: fast
-    )
+    own = joined(qa + qb)
+    other = shifted(own, 0, 0, 1)
+    grad_got = lax.all_to_all(grad_send, "pts", 0, 0, tiled=True)
+    stats = scored(where, assignment, marks, sketches, own, other)
+    for step in (1, 2):
+        stats = jnp.maximum(stats, across(stats, step, planes))
+    final = across(stats, 4, planes)
+    gap, total, mark = closing(stats, final, pts_count)
+    full = mark[0, 0] > 0
+
+    def fast():
+        totals = lax.all_to_all(total, "pts", 0, 0, tiled=True)
+        gradient_sums, counts = sums(grad_got, medoid_count)
+        coverage = jnp.sum(totals[:, 0, 0]) / (row_count * pts_count)
+        return gap[0], coverage, counts[0], gradient_sums
+
+    return lax.cond(full, lambda: general(sketches, assignment, medoid_ids), fast)
 
 
 def solution(mesh):

time: 150 us -> 114 us (0.76)
  blocking collectives: 35.3 us -> 17.2 us
  Pallas kernels: 37.4 us -> 23.3 us
  starting transfers between devices: 35.4 us -> 44.9 us
  waiting for transfers between devices: 29.7 us -> 23 us
  other arithmetic: 4.61 us -> 0.72 us
  local copies, waits for them, and re-layouts: 2.52 us -> 0.68 us
    all_to_all x1 -> x0, blocking collectives: 18 us -> none  [from_everyone(): lax.all_to_all(jnp.broadcast_to(array[None], (size, *array.shape)), axis,...]
    all_to_all x1, waiting for transfers between devices: 17.6 us -> 0.01 us  [shards(): grad_got = lax.all_to_all(grad_send, 'pts', 0, 0, tiled=True)]
    ppermute x0 -> x3, starting transfers between devices: none -> 11.9 us  [across(): return lax.ppermute(array, 'med', [(z, z ^ step) for z in range(planes)])]
    pallas_call x1, Pallas kernels: 13.7 us -> 6.79 us  [pick(): pl.pallas_call(pick_kernel, grid_spec=pltpu.PrefetchScalarGridSpec(num_sc...]
    ppermute x13, waiting for transfers between devices: 12.1 us -> 17.6 us  [shifted(): return lax.ppermute(array, 'pts', pairs)]
    ppermute x0 -> x3, waiting for transfers between devices: none -> 5.43 us  [across(): return lax.ppermute(array, 'med', [(z, z ^ step) for z in range(planes)])]
    pallas_call x2 -> x1, Pallas kernels: 13 us -> 8.39 us  [scored(): pl.pallas_call(functools.partial(score_kernel, 1.0 / feats), grid_spec=pl...]
    pallas_call x1, Pallas kernels: 9.53 us -> 6.29 us  [sums(): pl.pallas_call(sums_kernel, in_specs=[pl.BlockSpec(memory_space=pltpu.VME...]
  transfers between devices with their start and end apart: 15 -> 18, of which waited for: 10 -> 12; matrix products, arithmetic and copies ran while one was open for 2% -> 1% of each run, Pallas kernels for 11% -> 14%
where the time goes in v3:
time: 114 us; the launch traced here: 113 us
  starting transfers between devices  44.9 us (39%)
  Pallas kernels  23.3 us (20%)
  waiting for transfers between devices  23 us (20%)
  blocking collectives  17.2 us (15%)
  between operations  2.59 us (2%)
    ppermute x13, starting transfers between devices, shifted(): return lax.ppermute(array, 'pts', pairs)  19.1 us
    ppermute x13, waiting for transfers between devices, shifted(): return lax.ppermute(array, 'pts', pairs)  17.6 us
    all_to_all x1, blocking collectives, shards(): med_got = lax.all_to_all(med_send, 'pts', 0, 0, tiled=True)  17.2 us
    ppermute x3, starting transfers between devices, across(): return lax.ppermute(array, 'med', [(z, z ^ step) for z in range(planes)])  11.9 us
    pallas_call x1, Pallas kernels, scored(): pl.pallas_call(functools.partial(score_kernel, 1.0 / feats), grid_spec=pl...  8.39 us
    all_to_all x1, starting transfers between devices, fast(): totals = lax.all_to_all(total, 'pts', 0, 0, tiled=True)  7.47 us
    pallas_call x1, Pallas kernels, pick(): pl.pallas_call(pick_kernel, grid_spec=pltpu.PrefetchScalarGridSpec(num_sc...  6.79 us
    all_to_all x1, starting transfers between devices, shards(): grad_got = lax.all_to_all(grad_send, 'pts', 0, 0, tiled=True)  6.37 us
  transfers between devices with their start and end apart: 18, of which 12 were waited for; matrix products, arithmetic and copies ran while one was open for 1% of the time, Pallas kernels for 14%

profile of v3, /device:TPU:2, one launch (start us, length us, event | category | flops | bytes accessed | tf_op | source)
XLA Modules:
  0.0 113.0 jit_solution(14853933706138841428)
XLA Ops:
  0.7 0.1 stack.68.where_ref
  0.8 6.8 %pick.1 = (bf16[32,32,256]{2,1,0:T(8,128)(2,1)S(1)}, bf16[32,192,128]{2,1,0:T(8,128)(2,1)S(1)}) custom-call(s32[8]{0:T(128)S(1)} %stack.68.where_ref, s32[8,128]{1,0:T(8,128)} %bitcast.62, s32[1,512]{1,0:T(1,128)} %bitcast.66, bf16[1024,4096]{1,0:T(8,128)(2,1)} %sk_ref.3), custom_call_target="tpu_custom_call" | custom-call | flops 2147483648 | bytes 8388608 | tf_op jit(solution)/shard_map/pick/pallas_call | solution.py:112
  7.6 17.2 %all_to_all.41.got_ref = bf16[32,32,256]{2,1,0:T(8,128)(2,1)S(1)} all-to-all(bf16[32,32,256]{2,1,0:T(8,128)(2,1)S(1)} %get-tuple-element.32), channel_id=1, replica_groups=mesh['pts'=32,'med'=8] {'pts'}, dimensions={0} | all-to-all | bytes 1048576 | tf_op jit(solution)/shard_map/all_to_all | solution.py:416
  24.8 1.0 place.1
  25.8 1.8 %collective-permute-start.8 = (bf16[128,256]{1,0:T(8,128)(2,1)S(1)}, bf16[128,256]{1,0:T(8,128)(2,1)S(1)}, u32[]{:S(2)}, u32[]{:S(2)}) collective-permute-start(bf16[128,256]{1,0:T(8,128)(2,1)S(1)} %get-tuple-element.35), channel_id=1, source_target_pairs={{0,48},{8,56},{16,0},{24,8},{32,16},{40,24},{48,32},{56,40},{64,11... | collective-permute-start | bytes 196616 | tf_op jit(solution)/shard_map/ppermute | solution.py:357
  27.6 0.8 collective-permute-start.7
  28.4 0.9 collective-permute-start.6
  29.3 1.5 %collective-permute-done.8 = bf16[128,256]{1,0:T(8,128)(2,1)S(1)} collective-permute-done((bf16[128,256]{1,0:T(8,128)(2,1)S(1)}, bf16[128,256]{1,0:T(8,128)(2,1)S(1)}, u32[]{:S(2)}, u32[]{:S(2)}) %collective-permute-start.8) | collective-permute-done | bytes 65568 | tf_op jit(solution)/shard_map/ppermute | solution.py:357
  30.8 3.1 %collective-permute-done.7 = bf16[128,256]{1,0:T(8,128)(2,1)S(1)} collective-permute-done((bf16[128,256]{1,0:T(8,128)(2,1)S(1)}, bf16[128,256]{1,0:T(8,128)(2,1)S(1)}, u32[]{:S(2)}, u32[]{:S(2)}) %collective-permute-start.7) | collective-permute-done | bytes 65568 | tf_op jit(solution)/shard_map/ppermute | solution.py:357
  33.9 0.8 collective-permute-done.6
  34.8 1.5 %collective-permute-start.11 = (bf16[4,128,256]{2,1,0:T(8,128)(2,1)S(1)}, bf16[4,128,256]{2,1,0:T(8,128)(2,1)S(1)}, u32[]{:S(2)}, u32[]{:S(2)}) collective-permute-start(bf16[4,128,256]{2,1,0:T(8,128)(2,1)S(1)} %pad_maximum_fusion.2.refs_4_), channel_id=1, source_target_pairs={{0,192},{8,200},{16,208},{24,216},{32,224},{40,232},{48,240},{56,2... | collective-permute-start | bytes 786440 | tf_op jit(solution)/shard_map/ppermute | solution.py:357
  36.2 1.2 %collective-permute-start.2 = (bf16[128,256]{1,0:T(8,128)(2,1)S(1)}, bf16[128,256]{1,0:T(8,128)(2,1)S(1)}, u32[]{:S(2)}, u32[]{:S(2)}) collective-permute-start(bf16[128,256]{1,0:T(8,128)(2,1)S(1)} %get-tuple-element.34), channel_id=1, source_target_pairs={{0,192},{8,200},{16,208},{24,216},{32,224},{40,232},{48,240},{56,2... | collective-permute-start | bytes 196616 | tf_op jit(solution)/shard_map/ppermute | solution.py:357
  37.4 0.9 collective-permute-start.1
  38.4 1.1 collective-permute-start
  39.4 3.0 %collective-permute-start.10 = (bf16[4,128,256]{2,1,0:T(8,128)(2,1)S(1)}, bf16[4,128,256]{2,1,0:T(8,128)(2,1)S(1)}, u32[]{:S(2)}, u32[]{:S(2)}) collective-permute-start(bf16[4,128,256]{2,1,0:T(8,128)(2,1)S(1)} %pad_maximum_fusion.2.refs_4_), channel_id=1, source_target_pairs={{0,128},{8,136},{16,144},{24,152},{32,160},{40,168},{48,176},{56,1... | collective-permute-start | bytes 786440 | tf_op jit(solution)/shard_map/ppermute | solution.py:357
  42.4 3.1 %collective-permute-done.2 = bf16[128,256]{1,0:T(8,128)(2,1)S(1)} collective-permute-done((bf16[128,256]{1,0:T(8,128)(2,1)S(1)}, bf16[128,256]{1,0:T(8,128)(2,1)S(1)}, u32[]{:S(2)}, u32[]{:S(2)}) %collective-permute-start.2) | collective-permute-done | bytes 65568 | tf_op jit(solution)/shard_map/ppermute | solution.py:357
  45.5 0.5 collective-permute-start.9
  45.9 0.9 collective-permute-done.1
  46.9 0.0 collective-permute-done
  46.9 4.8 %collective-permute-start.5 = (bf16[4,128,256]{2,1,0:T(8,128)(2,1)S(1)}, bf16[4,128,256]{2,1,0:T(8,128)(2,1)S(1)}, u32[]{:S(2)}, u32[]{:S(2)}) collective-permute-start(bf16[4,128,256]{2,1,0:T(8,128)(2,1)S(1)} %pad_maximum_fusion.1.refs_0_), channel_id=1, source_target_pairs={{0,48},{8,56},{16,0},{24,8},{32,16},{40,24},{48,32},{56,40},{64,11... | collective-permute-start | bytes 786440 | tf_op jit(solution)/shard_map/ppermute | solution.py:357
  51.7 1.3 %collective-permute-start.4 = (bf16[4,128,256]{2,1,0:T(8,128)(2,1)S(1)}, bf16[4,128,256]{2,1,0:T(8,128)(2,1)S(1)}, u32[]{:S(2)}, u32[]{:S(2)}) collective-permute-start(bf16[4,128,256]{2,1,0:T(8,128)(2,1)S(1)} %pad_maximum_fusion.1.refs_0_), channel_id=1, source_target_pairs={{0,32},{8,40},{16,48},{24,56},{32,0},{40,8},{48,16},{56,24},{64,96... | collective-permute-start | bytes 786440 | tf_op jit(solution)/shard_map/ppermute | solution.py:357
  53.0 0.0 collective-permute-done.11.refs_7_
  53.0 1.3 %collective-permute-start.3 = (bf16[4,128,256]{2,1,0:T(8,128)(2,1)S(1)}, bf16[4,128,256]{2,1,0:T(8,128)(2,1)S(1)}, u32[]{:S(2)}, u32[]{:S(2)}) collective-permute-start(bf16[4,128,256]{2,1,0:T(8,128)(2,1)S(1)} %pad_maximum_fusion.1.refs_0_), channel_id=1, source_target_pairs={{0,16},{8,24},{16,32},{24,40},{32,48},{40,56},{48,0},{56,8},{64,80... | collective-permute-start | bytes 786440 | tf_op jit(solution)/shard_map/ppermute | solution.py:357
  54.3 0.0 collective-permute-done.10.refs_6_
  54.3 0.2 collective-permute-done.9.refs_5_
  54.5 4.5 %collective-permute-done.5.refs_3_ = bf16[4,128,256]{2,1,0:T(8,128)(2,1)S(1)} collective-permute-done((bf16[4,128,256]{2,1,0:T(8,128)(2,1)S(1)}, bf16[4,128,256]{2,1,0:T(8,128)(2,1)S(1)}, u32[]{:S(2)}, u32[]{:S(2)}) %collective-permute-start.5) | collective-permute-done | bytes 262176 | tf_op jit(solution)/shard_map/ppermute | solution.py:357
  59.0 0.7 collective-permute-done.4.refs_2_
  59.7 2.7 %collective-permute-done.3.refs_1_ = bf16[4,128,256]{2,1,0:T(8,128)(2,1)S(1)} collective-permute-done((bf16[4,128,256]{2,1,0:T(8,128)(2,1)S(1)}, bf16[4,128,256]{2,1,0:T(8,128)(2,1)S(1)}, u32[]{:S(2)}, u32[]{:S(2)}) %collective-permute-start.3) | collective-permute-done | bytes 262176 | tf_op jit(solution)/shard_map/ppermute | solution.py:357
  62.4 0.1 joined.1.own_ref
  62.5 0.1 collective-permute-start.12
  62.7 6.4 %all-to-all-start.8 = ((bf16[32,192,128]{2,1,0:T(8,128)(2,1)}), bf16[32,192,128]{2,1,0:T(8,128)(2,1)}, u32[]{:S(2)}, u32[]{:S(2)}) async-start(bf16[32,192,128]{2,1,0:T(8,128)(2,1)} %copy-done), calls=%async_computation.8 | async-start | bytes 3145728 | tf_op jit(solution)/shard_map/all_to_all | solution.py:424
  69.0 0.0 collective-permute-done.12.other_ref
  69.1 0.0 copy-start.2
  69.1 8.4 %scored.1 = f32[3,1024]{1,0:T(4,128)S(1)} custom-call(s32[8]{0:T(128)S(1)} %stack.68.where_ref, s32[1,1024]{1,0:T(1,128)S(1)} %bitcast.63, f32[1,256]{1,0:T(1,128)S(1)} %get-tuple-element.33.mark_ref, bf16[1024,4096]{1,0:T(8,128)(2,1)} %sk_ref.3, bf16[32,128,256]{2,1,0:T(8,128)(2,1)S(1)} %joined.1.own_ref, ...), custom_call_target="tpu_custom_call" | custom-call | flops 4294967296 | bytes 8388608 | tf_op jit(solution)/shard_map/scored/pallas_call | solution.py:287
  77.5 2.0 %collective-permute-start.13 = (f32[3,1024]{1,0:T(4,128)S(1)}, f32[3,1024]{1,0:T(4,128)S(1)}, u32[]{:S(2)}, u32[]{:S(2)}) collective-permute-start(f32[3,1024]{1,0:T(4,128)S(1)} %scored.1), channel_id=1, source_target_pairs={{0,1},{1,0},{2,3},{3,2},{4,5},{5,4},{6,7},{7,6},{8,9},{9,8},{10,11... | collective-permute-start | bytes 36872 | tf_op jit(solution)/shard_map/ppermute | solution.py:361
  79.5 1.8 %collective-permute-done.13 = f32[3,1024]{1,0:T(4,128)S(1)} collective-permute-done((f32[3,1024]{1,0:T(4,128)S(1)}, f32[3,1024]{1,0:T(4,128)S(1)}, u32[]{:S(2)}, u32[]{:S(2)}) %collective-permute-start.13) | collective-permute-done | bytes 12320 | tf_op jit(solution)/shard_map/ppermute | solution.py:361
  81.3 3.3 %collective-permute-start.14 = (f32[3,1024]{1,0:T(4,128)S(1)}, f32[3,1024]{1,0:T(4,128)S(1)}, u32[]{:S(2)}, u32[]{:S(2)}) collective-permute-start(f32[3,1024]{1,0:T(4,128)S(1)} %max.14), channel_id=1, source_target_pairs={{0,2},{1,3},{2,0},{3,1},{4,6},{5,7},{6,4},{7,5},{8,10},{9,11},{10,... | collective-permute-start | bytes 36872 | tf_op jit(solution)/shard_map/ppermute | solution.py:361
  84.6 1.9 %collective-permute-done.14 = f32[3,1024]{1,0:T(4,128)S(1)} collective-permute-done((f32[3,1024]{1,0:T(4,128)S(1)}, f32[3,1024]{1,0:T(4,128)S(1)}, u32[]{:S(2)}, u32[]{:S(2)}) %collective-permute-start.14) | collective-permute-done | bytes 12320 | tf_op jit(solution)/shard_map/ppermute | solution.py:361
  86.5 6.7 %collective-permute-start.15 = (f32[3,1024]{1,0:T(4,128)S(1)}, f32[3,1024]{1,0:T(4,128)S(1)}, u32[]{:S(2)}, u32[]{:S(2)}) collective-permute-start(f32[3,1024]{1,0:T(4,128)S(1)} %max.15.a_ref), channel_id=1, source_target_pairs={{0,4},{1,5},{2,6},{3,7},{4,0},{5,1},{6,2},{7,3},{8,12},{9,13},{10,... | collective-permute-start | bytes 36872 | tf_op jit(solution)/shard_map/ppermute | solution.py:361
  93.1 1.7 %collective-permute-done.15.b_ref = f32[3,1024]{1,0:T(4,128)S(1)} collective-permute-done((f32[3,1024]{1,0:T(4,128)S(1)}, f32[3,1024]{1,0:T(4,128)S(1)}, u32[]{:S(2)}, u32[]{:S(2)}) %collective-permute-start.15) | collective-permute-done | bytes 12320 | tf_op jit(solution)/shard_map/ppermute | solution.py:361
  94.9 0.7 closing.1
  96.2 0.0 all-to-all-done.8
  96.2 15.6 %conditional.1 = (f32[1024]{0:T(1024)}, f32[]{:T(128)}, f32[512]{0:T(512)}, f32[128,512]{1,0:T(8,128)}) conditional(s32[]{:T(128)} %bitcast.30, (f32[1,1024]{1,0:T(1,128)}, f32[32,1,128]{2,1,0:T(1,128)}, bf16[32,192,128]{2,1,0:T(8,128)(2,1)}) %tuple.39, (s32[512]{0:T(512)S(1)}, bf16[1024,4096]{1,0:T(8,128)(2,1)}, s32[1024]{0:T(1024)S(1)}) %tuple.41), branch_computations={%region_0.2_spmd, %region_2.11_spmd} | conditional | flops 8601925632 | bytes 130077376 | solution.py:438
  96.2 7.5 %all-to-all-start = ((f32[32,1,128]{2,1,0:T(1,128)}), f32[32,1,128]{2,1,0:T(1,128)S(1)}, u32[]{:S(2)}, u32[]{:S(2)}) async-start(f32[32,1,128]{2,1,0:T(1,128)} %get-tuple-element.13), calls=%async_computation | async-start | bytes 32768 | tf_op jit(solution)/shard_map/cond/branch_0_fun/all_to_all | solution.py:433
  103.7 6.3 %sums.1 = (f32[128,512]{1,0:T(8,128)}, f32[8,512]{1,0:T(8,128)S(1)}) custom-call(bf16[32,192,128]{2,1,0:T(8,128)(2,1)} %get-tuple-element.14.got_ref), custom_call_target="tpu_custom_call" | custom-call | flops 1610612736 | bytes 1572864 | tf_op jit(solution)/shard_map/cond/branch_0_fun/sums/pallas_call | solution.py:220
  110.0 0.6 slice.10
  110.6 0.0 all-to-all-done
  110.6 0.6 slice_reduce_fusion
  (9 shorter events, 0.1 us)
Async XLA Ops:
  7.6 55.1 %copy-start = (bf16[32,192,128]{2,1,0:T(8,128)(2,1)}, bf16[32,192,128]{2,1,0:T(8,128)(2,1)S(1)}, u32[]{:S(2)}) copy-start(bf16[32,192,128]{2,1,0:T(8,128)(2,1)S(1)} %get-tuple-element.39) | copy-start | bytes 4718596
  25.8 5.0 %collective-permute-start.8 = (bf16[128,256]{1,0:T(8,128)(2,1)S(1)}, bf16[128,256]{1,0:T(8,128)(2,1)S(1)}, u32[]{:S(2)}, u32[]{:S(2)}) collective-permute-start(bf16[128,256]{1,0:T(8,128)(2,1)S(1)} %get-tuple-element.35), channel_id=1, source_target_pairs={{0,48},{8,56},{16,0},{24,8},{32,16},{40,24},{48,32},{56,40},{64,11... | collective-permute-start | bytes 196616 | tf_op jit(solution)/shard_map/ppermute | solution.py:357
  27.6 6.4 %collective-permute-start.7 = (bf16[128,256]{1,0:T(8,128)(2,1)S(1)}, bf16[128,256]{1,0:T(8,128)(2,1)S(1)}, u32[]{:S(2)}, u32[]{:S(2)}) collective-permute-start(bf16[128,256]{1,0:T(8,128)(2,1)S(1)} %get-tuple-element.35), channel_id=1, source_target_pairs={{0,32},{8,40},{16,48},{24,56},{32,0},{40,8},{48,16},{56,24},{64,96... | collective-permute-start | bytes 196616 | tf_op jit(solution)/shard_map/ppermute | solution.py:357
  28.4 6.3 %collective-permute-start.6 = (bf16[128,256]{1,0:T(8,128)(2,1)S(1)}, bf16[128,256]{1,0:T(8,128)(2,1)S(1)}, u32[]{:S(2)}, u32[]{:S(2)}) collective-permute-start(bf16[128,256]{1,0:T(8,128)(2,1)S(1)} %get-tuple-element.35), channel_id=1, source_target_pairs={{0,16},{8,24},{16,32},{24,40},{32,48},{40,56},{48,0},{56,8},{64,80... | collective-permute-start | bytes 196616 | tf_op jit(solution)/shard_map/ppermute | solution.py:357
  34.7 34.3 %copy-start.1 = (s32[1024]{0:T(1024)S(1)}, s32[1024]{0:T(1024)}, u32[]{:S(2)}) copy-start(s32[1024]{0:T(1024)} %param.6) | copy-start | bytes 12292
  34.8 18.2 %collective-permute-start.11 = (bf16[4,128,256]{2,1,0:T(8,128)(2,1)S(1)}, bf16[4,128,256]{2,1,0:T(8,128)(2,1)S(1)}, u32[]{:S(2)}, u32[]{:S(2)}) collective-permute-start(bf16[4,128,256]{2,1,0:T(8,128)(2,1)S(1)} %pad_maximum_fusion.2.refs_4_), channel_id=1, source_target_pairs={{0,192},{8,200},{16,208},{24,216},{32,224},{40,232},{48,240},{56,2... | collective-permute-start | bytes 786440 | tf_op jit(solution)/shard_map/ppermute | solution.py:357
  36.2 9.2 %collective-permute-start.2 = (bf16[128,256]{1,0:T(8,128)(2,1)S(1)}, bf16[128,256]{1,0:T(8,128)(2,1)S(1)}, u32[]{:S(2)}, u32[]{:S(2)}) collective-permute-start(bf16[128,256]{1,0:T(8,128)(2,1)S(1)} %get-tuple-element.34), channel_id=1, source_target_pairs={{0,192},{8,200},{16,208},{24,216},{32,224},{40,232},{48,240},{56,2... | collective-permute-start | bytes 196616 | tf_op jit(solution)/shard_map/ppermute | solution.py:357
  37.4 9.4 %collective-permute-start.1 = (bf16[128,256]{1,0:T(8,128)(2,1)S(1)}, bf16[128,256]{1,0:T(8,128)(2,1)S(1)}, u32[]{:S(2)}, u32[]{:S(2)}) collective-permute-start(bf16[128,256]{1,0:T(8,128)(2,1)S(1)} %get-tuple-element.34), channel_id=1, source_target_pairs={{0,128},{8,136},{16,144},{24,152},{32,160},{40,168},{48,176},{56,1... | collective-permute-start | bytes 196616 | tf_op jit(solution)/shard_map/ppermute | solution.py:357
  38.4 8.5 %collective-permute-start = (bf16[128,256]{1,0:T(8,128)(2,1)S(1)}, bf16[128,256]{1,0:T(8,128)(2,1)S(1)}, u32[]{:S(2)}, u32[]{:S(2)}) collective-permute-start(bf16[128,256]{1,0:T(8,128)(2,1)S(1)} %get-tuple-element.34), channel_id=1, source_target_pairs={{0,64},{8,72},{16,80},{24,88},{32,96},{40,104},{48,112},{56,120},{... | collective-permute-start | bytes 196616 | tf_op jit(solution)/shard_map/ppermute | solution.py:357
  39.4 14.9 %collective-permute-start.10 = (bf16[4,128,256]{2,1,0:T(8,128)(2,1)S(1)}, bf16[4,128,256]{2,1,0:T(8,128)(2,1)S(1)}, u32[]{:S(2)}, u32[]{:S(2)}) collective-permute-start(bf16[4,128,256]{2,1,0:T(8,128)(2,1)S(1)} %pad_maximum_fusion.2.refs_4_), channel_id=1, source_target_pairs={{0,128},{8,136},{16,144},{24,152},{32,160},{40,168},{48,176},{56,1... | collective-permute-start | bytes 786440 | tf_op jit(solution)/shard_map/ppermute | solution.py:357
  45.5 9.0 %collective-permute-start.9 = (bf16[4,128,256]{2,1,0:T(8,128)(2,1)S(1)}, bf16[4,128,256]{2,1,0:T(8,128)(2,1)S(1)}, u32[]{:S(2)}, u32[]{:S(2)}) collective-permute-start(bf16[4,128,256]{2,1,0:T(8,128)(2,1)S(1)} %pad_maximum_fusion.2.refs_4_), channel_id=1, source_target_pairs={{0,64},{8,72},{16,80},{24,88},{32,96},{40,104},{48,112},{56,120},{... | collective-permute-start | bytes 786440 | tf_op jit(solution)/shard_map/ppermute | solution.py:357
  46.9 12.1 %collective-permute-start.5 = (bf16[4,128,256]{2,1,0:T(8,128)(2,1)S(1)}, bf16[4,128,256]{2,1,0:T(8,128)(2,1)S(1)}, u32[]{:S(2)}, u32[]{:S(2)}) collective-permute-start(bf16[4,128,256]{2,1,0:T(8,128)(2,1)S(1)} %pad_maximum_fusion.1.refs_0_), channel_id=1, source_target_pairs={{0,48},{8,56},{16,0},{24,8},{32,16},{40,24},{48,32},{56,40},{64,11... | collective-permute-start | bytes 786440 | tf_op jit(solution)/shard_map/ppermute | solution.py:357
  51.7 8.0 %collective-permute-start.4 = (bf16[4,128,256]{2,1,0:T(8,128)(2,1)S(1)}, bf16[4,128,256]{2,1,0:T(8,128)(2,1)S(1)}, u32[]{:S(2)}, u32[]{:S(2)}) collective-permute-start(bf16[4,128,256]{2,1,0:T(8,128)(2,1)S(1)} %pad_maximum_fusion.1.refs_0_), channel_id=1, source_target_pairs={{0,32},{8,40},{16,48},{24,56},{32,0},{40,8},{48,16},{56,24},{64,96... | collective-permute-start | bytes 786440 | tf_op jit(solution)/shard_map/ppermute | solution.py:357
  53.0 9.4 %collective-permute-start.3 = (bf16[4,128,256]{2,1,0:T(8,128)(2,1)S(1)}, bf16[4,128,256]{2,1,0:T(8,128)(2,1)S(1)}, u32[]{:S(2)}, u32[]{:S(2)}) collective-permute-start(bf16[4,128,256]{2,1,0:T(8,128)(2,1)S(1)} %pad_maximum_fusion.1.refs_0_), channel_id=1, source_target_pairs={{0,16},{8,24},{16,32},{24,40},{32,48},{40,56},{48,0},{56,8},{64,80... | collective-permute-start | bytes 786440 | tf_op jit(solution)/shard_map/ppermute | solution.py:357
  62.5 6.5 %collective-permute-start.12 = (bf16[32,128,256]{2,1,0:T(8,128)(2,1)S(1)}, bf16[32,128,256]{2,1,0:T(8,128)(2,1)}, u32[]{:S(2)}, u32[]{:S(2)}) collective-permute-start(bf16[32,128,256]{2,1,0:T(8,128)(2,1)S(1)} %joined.1.own_ref), channel_id=1, source_target_pairs={{0,8},{8,0},{16,24},{24,16},{32,40},{40,32},{48,56},{56,48},{64,72... | collective-permute-start | bytes 6291464 | tf_op jit(solution)/shard_map/ppermute | solution.py:357
  62.7 33.6 %all-to-all-start.8 = ((bf16[32,192,128]{2,1,0:T(8,128)(2,1)}), bf16[32,192,128]{2,1,0:T(8,128)(2,1)}, u32[]{:S(2)}, u32[]{:S(2)}) async-start(bf16[32,192,128]{2,1,0:T(8,128)(2,1)} %copy-done), calls=%async_computation.8 | async-start | bytes 3145728 | tf_op jit(solution)/shard_map/all_to_all | solution.py:424
  69.1 27.2 %copy-start.2 = (s32[512]{0:T(512)S(1)}, s32[512]{0:T(512)}, u32[]{:S(2)}) copy-start(s32[512]{0:T(512)} %param.7) | copy-start | bytes 6148
  77.5 3.8 %collective-permute-start.13 = (f32[3,1024]{1,0:T(4,128)S(1)}, f32[3,1024]{1,0:T(4,128)S(1)}, u32[]{:S(2)}, u32[]{:S(2)}) collective-permute-start(f32[3,1024]{1,0:T(4,128)S(1)} %scored.1), channel_id=1, source_target_pairs={{0,1},{1,0},{2,3},{3,2},{4,5},{5,4},{6,7},{7,6},{8,9},{9,8},{10,11... | collective-permute-start | bytes 36872 | tf_op jit(solution)/shard_map/ppermute | solution.py:361
  81.3 5.2 %collective-permute-start.14 = (f32[3,1024]{1,0:T(4,128)S(1)}, f32[3,1024]{1,0:T(4,128)S(1)}, u32[]{:S(2)}, u32[]{:S(2)}) collective-permute-start(f32[3,1024]{1,0:T(4,128)S(1)} %max.14), channel_id=1, source_target_pairs={{0,2},{1,3},{2,0},{3,1},{4,6},{5,7},{6,4},{7,5},{8,10},{9,11},{10,... | collective-permute-start | bytes 36872 | tf_op jit(solution)/shard_map/ppermute | solution.py:361
  86.5 8.4 %collective-permute-start.15 = (f32[3,1024]{1,0:T(4,128)S(1)}, f32[3,1024]{1,0:T(4,128)S(1)}, u32[]{:S(2)}, u32[]{:S(2)}) collective-permute-start(f32[3,1024]{1,0:T(4,128)S(1)} %max.15.a_ref), channel_id=1, source_target_pairs={{0,4},{1,5},{2,6},{3,7},{4,0},{5,1},{6,2},{7,3},{8,12},{9,13},{10,... | collective-permute-start | bytes 36872 | tf_op jit(solution)/shard_map/ppermute | solution.py:361
  96.2 14.3 %all-to-all-start = ((f32[32,1,128]{2,1,0:T(1,128)}), f32[32,1,128]{2,1,0:T(1,128)S(1)}, u32[]{:S(2)}, u32[]{:S(2)}) async-start(f32[32,1,128]{2,1,0:T(1,128)} %get-tuple-element.13), calls=%async_computation | async-start | bytes 32768 | tf_op jit(solution)/shard_map/cond/branch_0_fun/all_to_all | solution.py:433

commit v4 on v3

--- a/solution.py
+++ b/solution.py
@@ -213,7 +213,7 @@
         0, got_ref.shape[0] // per, body, jnp.zeros((medoids, feats + LANES), F32)
     )
     sums_ref[...] = total[:, :feats].T
-    count_ref[...] = total[:, feats:].T[:8]
+    count_ref[...] = total[:, feats:].T[:1]
 
 
 def sums(got, medoids):
@@ -223,7 +223,7 @@
         out_specs=[pl.BlockSpec(memory_space=pltpu.VMEM)] * 2,
         out_shape=[
             jax.ShapeDtypeStruct((got.shape[2], medoids), F32),
-            jax.ShapeDtypeStruct((8, medoids), F32),
+            jax.ShapeDtypeStruct((1, medoids), F32),
         ],
         compiler_params=pltpu.CompilerParams(vmem_limit_bytes=16 * 2**20),
         cost_estimate=pl.CostEstimate(
@@ -307,8 +307,8 @@
     )(where, assignment[None, :], marks, sketches, own, other)
 
 
-def closing_kernel(a_ref, b_ref, gap_ref, send_ref, mark_ref):
-    both = jnp.maximum(a_ref[...], b_ref[...])
+def closing_kernel(a_ref, b_ref, c_ref, gap_ref, send_ref, mark_ref):
+    both = jnp.maximum(jnp.maximum(a_ref[...], b_ref[...]), c_ref[...])
     gap_ref[...] = both[0:1] - both[1:2]
     mark_ref[0, 0] = jnp.max(both[2:3, :LANES]).astype(I32)
     total = jnp.broadcast_to(jnp.sum(both[0:1], axis=1, keepdims=True), (1, LANES))
@@ -316,10 +316,10 @@
         send_ref[i] = total
 
 
-def closing(a, b, pts_count):
+def closing(a, b, c, pts_count):
     return pl.pallas_call(
         closing_kernel,
-        in_specs=[pl.BlockSpec(memory_space=pltpu.VMEM)] * 2,
+        in_specs=[pl.BlockSpec(memory_space=pltpu.VMEM)] * 3,
         out_specs=[
             pl.BlockSpec(memory_space=pltpu.VMEM),
             pl.BlockSpec(memory_space=pltpu.VMEM),
@@ -335,7 +335,7 @@
             flops=a.size, bytes_accessed=8 * a.size, transcendentals=0
         ),
         name="closing",
-    )(a, b)
+    )(a, b, c)
 
 
 def from_everyone(array, axis):
@@ -358,7 +358,7 @@
 
 
 def across(array, step, planes):
-    return lax.ppermute(array, "med", [(z, z ^ step) for z in range(planes)])
+    return lax.ppermute(array, "med", [(z, (z + step) % planes) for z in range(planes)])
 
 
 def general(sketches, assignment, medoid_ids):
@@ -415,18 +415,22 @@
     )
     med_got = lax.all_to_all(med_send, "pts", 0, 0, tiled=True)
     a, b, marks = place(where, med_got, half)
-    pa = jnp.stack([a] + [shifted(a, k, 0, 0) for k in (1, 2, 3)])
-    pb = jnp.stack([b] + [shifted(b, 0, k, 0) for k in (1, 2, 3)])
-    qa = [pa] + [shifted(pa, 0, k, 0) for k in (1, 2, 3)]
-    qb = [pb] + [shifted(pb, k, 0, 0) for k in (1, 2, 3)]
-    own = joined(qa + qb)
+    a2, b2 = shifted(a, 2, 0, 0), shifted(b, 0, 2, 0)
+    a1, b1 = shifted(a, 1, 0, 0), shifted(b, 0, 1, 0)
+    a3, b3 = shifted(a, 3, 0, 0), shifted(b, 0, 3, 0)
+    pa = jnp.stack([a, a1, a2, a3])
+    pb = jnp.stack([b, b1, b2, b3])
+    qa2, qb2 = shifted(pa, 0, 2, 0), shifted(pb, 2, 0, 0)
+    qa1, qb1 = shifted(pa, 0, 1, 0), shifted(pb, 1, 0, 0)
+    qa3, qb3 = shifted(pa, 0, 3, 0), shifted(pb, 3, 0, 0)
+    own = joined([pa, qa1, qa2, qa3, pb, qb1, qb2, qb3])
     other = shifted(own, 0, 0, 1)
     grad_got = lax.all_to_all(grad_send, "pts", 0, 0, tiled=True)
     stats = scored(where, assignment, marks, sketches, own, other)
-    for step in (1, 2):
-        stats = jnp.maximum(stats, across(stats, step, planes))
-    final = across(stats, 4, planes)
-    gap, total, mark = closing(stats, final, pts_count)
+    ahead, behind = across(stats, 1, planes), across(stats, -1, planes)
+    stats = jnp.maximum(jnp.maximum(stats, ahead), behind)
+    ahead, behind = across(stats, 3, planes), across(stats, -3, planes)
+    gap, total, mark = closing(stats, ahead, behind, pts_count)
     full = mark[0, 0] > 0
 
     def fast():

time: 114 us -> 115 us (level)
  waiting for transfers between devices: 23 us -> 26.1 us
  starting transfers between devices: 44.9 us -> 42.8 us
    ppermute x3 -> x4, waiting for transfers between devices: 5.43 us -> 8.55 us  [across(): lax.ppermute(array, 'med', [(z, (z + step) % planes) for z in range(plane...]
    ppermute x3 -> x4, starting transfers between devices: 11.9 us -> 9.83 us  [across(): lax.ppermute(array, 'med', [(z, (z + step) % planes) for z in range(plane...]
  transfers between devices with their start and end apart: 18 -> 19, of which waited for: 12 -> 13; matrix products, arithmetic and copies ran while one was open for 1% -> 0% of each run, Pallas kernels for 14% -> 14%
where the time goes in v4:
time: 115 us; the launch traced here: 113 us
  starting transfers between devices  42.8 us (37%)
  waiting for transfers between devices  26.1 us (23%)
  Pallas kernels  23.2 us (20%)
  blocking collectives  17.2 us (15%)
  between operations  2.59 us (2%)
    ppermute x13, starting transfers between devices, shifted(): return lax.ppermute(array, 'pts', pairs)  19.1 us
    ppermute x13, waiting for transfers between devices, shifted(): return lax.ppermute(array, 'pts', pairs)  17.6 us
    all_to_all x1, blocking collectives, shards(): med_got = lax.all_to_all(med_send, 'pts', 0, 0, tiled=True)  17.2 us
    ppermute x4, starting transfers between devices, across(): lax.ppermute(array, 'med', [(z, (z + step) % planes) for z in range(plane...  9.83 us
    ppermute x4, waiting for transfers between devices, across(): lax.ppermute(array, 'med', [(z, (z + step) % planes) for z in range(plane...  8.55 us
    pallas_call x1, Pallas kernels, scored(): pl.pallas_call(functools.partial(score_kernel, 1.0 / feats), grid_spec=pl...  8.39 us
    all_to_all x1, starting transfers between devices, fast(): totals = lax.all_to_all(total, 'pts', 0, 0, tiled=True)  7.47 us
    pallas_call x1, Pallas kernels, pick(): pl.pallas_call(pick_kernel, grid_spec=pltpu.PrefetchScalarGridSpec(num_sc...  6.79 us
  transfers between devices with their start and end apart: 19, of which 13 were waited for; matrix products, arithmetic and copies ran while one was open for 0% of the time, Pallas kernels for 14%

profile of v4, /device:TPU:2, one launch (start us, length us, event | category | flops | bytes accessed | tf_op | source)
XLA Modules:
  0.0 113.4 jit_solution(9194363569516944928)
XLA Ops:
  0.7 0.1 stack.68.where_ref
  0.8 6.8 %pick.1 = (bf16[32,32,256]{2,1,0:T(8,128)(2,1)S(1)}, bf16[32,192,128]{2,1,0:T(8,128)(2,1)S(1)}) custom-call(s32[8]{0:T(128)S(1)} %stack.68.where_ref, s32[8,128]{1,0:T(8,128)} %bitcast.62, s32[1,512]{1,0:T(1,128)} %bitcast.66, bf16[1024,4096]{1,0:T(8,128)(2,1)} %sk_ref.3), custom_call_target="tpu_custom_call" | custom-call | flops 2147483648 | bytes 8388608 | tf_op jit(solution)/shard_map/pick/pallas_call | solution.py:112
  7.6 17.2 %all_to_all.41.got_ref = bf16[32,32,256]{2,1,0:T(8,128)(2,1)S(1)} all-to-all(bf16[32,32,256]{2,1,0:T(8,128)(2,1)S(1)} %get-tuple-element.32), channel_id=1, replica_groups=mesh['pts'=32,'med'=8] {'pts'}, dimensions={0} | all-to-all | bytes 1048576 | tf_op jit(solution)/shard_map/all_to_all | solution.py:416
  24.8 1.0 place.1
  25.8 1.8 %collective-permute-start.8 = (bf16[128,256]{1,0:T(8,128)(2,1)S(1)}, bf16[128,256]{1,0:T(8,128)(2,1)S(1)}, u32[]{:S(2)}, u32[]{:S(2)}) collective-permute-start(bf16[128,256]{1,0:T(8,128)(2,1)S(1)} %get-tuple-element.35), channel_id=1, source_target_pairs={{0,48},{8,56},{16,0},{24,8},{32,16},{40,24},{48,32},{56,40},{64,11... | collective-permute-start | bytes 196616 | tf_op jit(solution)/shard_map/ppermute | solution.py:357
  27.6 0.8 collective-permute-start.7
  28.4 0.9 collective-permute-start.6
  29.3 1.5 %collective-permute-done.8 = bf16[128,256]{1,0:T(8,128)(2,1)S(1)} collective-permute-done((bf16[128,256]{1,0:T(8,128)(2,1)S(1)}, bf16[128,256]{1,0:T(8,128)(2,1)S(1)}, u32[]{:S(2)}, u32[]{:S(2)}) %collective-permute-start.8) | collective-permute-done | bytes 65568 | tf_op jit(solution)/shard_map/ppermute | solution.py:357
  30.8 3.1 %collective-permute-done.7 = bf16[128,256]{1,0:T(8,128)(2,1)S(1)} collective-permute-done((bf16[128,256]{1,0:T(8,128)(2,1)S(1)}, bf16[128,256]{1,0:T(8,128)(2,1)S(1)}, u32[]{:S(2)}, u32[]{:S(2)}) %collective-permute-start.7) | collective-permute-done | bytes 65568 | tf_op jit(solution)/shard_map/ppermute | solution.py:357
  33.9 0.8 collective-permute-done.6
  34.8 1.5 %collective-permute-start.11 = (bf16[4,128,256]{2,1,0:T(8,128)(2,1)S(1)}, bf16[4,128,256]{2,1,0:T(8,128)(2,1)S(1)}, u32[]{:S(2)}, u32[]{:S(2)}) collective-permute-start(bf16[4,128,256]{2,1,0:T(8,128)(2,1)S(1)} %pad_maximum_fusion.2.refs_4_), channel_id=1, source_target_pairs={{0,192},{8,200},{16,208},{24,216},{32,224},{40,232},{48,240},{56,2... | collective-permute-start | bytes 786440 | tf_op jit(solution)/shard_map/ppermute | solution.py:357
  36.2 1.2 %collective-permute-start.2 = (bf16[128,256]{1,0:T(8,128)(2,1)S(1)}, bf16[128,256]{1,0:T(8,128)(2,1)S(1)}, u32[]{:S(2)}, u32[]{:S(2)}) collective-permute-start(bf16[128,256]{1,0:T(8,128)(2,1)S(1)} %get-tuple-element.34), channel_id=1, source_target_pairs={{0,192},{8,200},{16,208},{24,216},{32,224},{40,232},{48,240},{56,2... | collective-permute-start | bytes 196616 | tf_op jit(solution)/shard_map/ppermute | solution.py:357
  37.4 0.9 collective-permute-start.1
  38.4 1.1 collective-permute-start
  39.4 3.0 %collective-permute-start.10 = (bf16[4,128,256]{2,1,0:T(8,128)(2,1)S(1)}, bf16[4,128,256]{2,1,0:T(8,128)(2,1)S(1)}, u32[]{:S(2)}, u32[]{:S(2)}) collective-permute-start(bf16[4,128,256]{2,1,0:T(8,128)(2,1)S(1)} %pad_maximum_fusion.2.refs_4_), channel_id=1, source_target_pairs={{0,128},{8,136},{16,144},{24,152},{32,160},{40,168},{48,176},{56,1... | collective-permute-start | bytes 786440 | tf_op jit(solution)/shard_map/ppermute | solution.py:357
  42.4 3.1 %collective-permute-done.2 = bf16[128,256]{1,0:T(8,128)(2,1)S(1)} collective-permute-done((bf16[128,256]{1,0:T(8,128)(2,1)S(1)}, bf16[128,256]{1,0:T(8,128)(2,1)S(1)}, u32[]{:S(2)}, u32[]{:S(2)}) %collective-permute-start.2) | collective-permute-done | bytes 65568 | tf_op jit(solution)/shard_map/ppermute | solution.py:357
  45.5 0.5 collective-permute-start.9
  45.9 0.9 collective-permute-done.1
  46.9 0.0 collective-permute-done
  46.9 4.8 %collective-permute-start.5 = (bf16[4,128,256]{2,1,0:T(8,128)(2,1)S(1)}, bf16[4,128,256]{2,1,0:T(8,128)(2,1)S(1)}, u32[]{:S(2)}, u32[]{:S(2)}) collective-permute-start(bf16[4,128,256]{2,1,0:T(8,128)(2,1)S(1)} %pad_maximum_fusion.1.refs_0_), channel_id=1, source_target_pairs={{0,48},{8,56},{16,0},{24,8},{32,16},{40,24},{48,32},{56,40},{64,11... | collective-permute-start | bytes 786440 | tf_op jit(solution)/shard_map/ppermute | solution.py:357
  51.7 1.3 %collective-permute-start.4 = (bf16[4,128,256]{2,1,0:T(8,128)(2,1)S(1)}, bf16[4,128,256]{2,1,0:T(8,128)(2,1)S(1)}, u32[]{:S(2)}, u32[]{:S(2)}) collective-permute-start(bf16[4,128,256]{2,1,0:T(8,128)(2,1)S(1)} %pad_maximum_fusion.1.refs_0_), channel_id=1, source_target_pairs={{0,32},{8,40},{16,48},{24,56},{32,0},{40,8},{48,16},{56,24},{64,96... | collective-permute-start | bytes 786440 | tf_op jit(solution)/shard_map/ppermute | solution.py:357
  53.0 0.0 collective-permute-done.11.refs_7_
  53.0 1.3 %collective-permute-start.3 = (bf16[4,128,256]{2,1,0:T(8,128)(2,1)S(1)}, bf16[4,128,256]{2,1,0:T(8,128)(2,1)S(1)}, u32[]{:S(2)}, u32[]{:S(2)}) collective-permute-start(bf16[4,128,256]{2,1,0:T(8,128)(2,1)S(1)} %pad_maximum_fusion.1.refs_0_), channel_id=1, source_target_pairs={{0,16},{8,24},{16,32},{24,40},{32,48},{40,56},{48,0},{56,8},{64,80... | collective-permute-start | bytes 786440 | tf_op jit(solution)/shard_map/ppermute | solution.py:357
  54.3 0.0 collective-permute-done.10.refs_6_
  54.3 0.2 collective-permute-done.9.refs_5_
  54.5 4.5 %collective-permute-done.5.refs_3_ = bf16[4,128,256]{2,1,0:T(8,128)(2,1)S(1)} collective-permute-done((bf16[4,128,256]{2,1,0:T(8,128)(2,1)S(1)}, bf16[4,128,256]{2,1,0:T(8,128)(2,1)S(1)}, u32[]{:S(2)}, u32[]{:S(2)}) %collective-permute-start.5) | collective-permute-done | bytes 262176 | tf_op jit(solution)/shard_map/ppermute | solution.py:357
  59.0 0.7 collective-permute-done.4.refs_2_
  59.7 2.7 %collective-permute-done.3.refs_1_ = bf16[4,128,256]{2,1,0:T(8,128)(2,1)S(1)} collective-permute-done((bf16[4,128,256]{2,1,0:T(8,128)(2,1)S(1)}, bf16[4,128,256]{2,1,0:T(8,128)(2,1)S(1)}, u32[]{:S(2)}, u32[]{:S(2)}) %collective-permute-start.3) | collective-permute-done | bytes 262176 | tf_op jit(solution)/shard_map/ppermute | solution.py:357
  62.4 0.1 joined.1.own_ref
  62.5 0.1 collective-permute-start.12
  62.7 6.4 %all-to-all-start.8 = ((bf16[32,192,128]{2,1,0:T(8,128)(2,1)}), bf16[32,192,128]{2,1,0:T(8,128)(2,1)}, u32[]{:S(2)}, u32[]{:S(2)}) async-start(bf16[32,192,128]{2,1,0:T(8,128)(2,1)} %copy-done), calls=%async_computation.8 | async-start | bytes 3145728 | tf_op jit(solution)/shard_map/all_to_all | solution.py:428
  69.1 0.0 collective-permute-done.12.other_ref
  69.1 0.0 copy-start.2
  69.1 8.4 %scored.1 = f32[3,1024]{1,0:T(4,128)S(1)} custom-call(s32[8]{0:T(128)S(1)} %stack.68.where_ref, s32[1,1024]{1,0:T(1,128)S(1)} %bitcast.63, f32[1,256]{1,0:T(1,128)S(1)} %get-tuple-element.33.mark_ref, bf16[1024,4096]{1,0:T(8,128)(2,1)} %sk_ref.3, bf16[32,128,256]{2,1,0:T(8,128)(2,1)S(1)} %joined.1.own_ref, ...), custom_call_target="tpu_custom_call" | custom-call | flops 4294967296 | bytes 8388608 | tf_op jit(solution)/shard_map/scored/pallas_call | solution.py:287
  77.5 5.9 %collective-permute-start.14 = (f32[3,1024]{1,0:T(4,128)S(1)}, f32[3,1024]{1,0:T(4,128)S(1)}, u32[]{:S(2)}, u32[]{:S(2)}) collective-permute-start(f32[3,1024]{1,0:T(4,128)S(1)} %scored.1), channel_id=1, source_target_pairs={{0,7},{1,0},{2,1},{3,2},{4,3},{5,4},{6,5},{7,6},{8,15},{9,8},{10,9... | collective-permute-start | bytes 36872 | tf_op jit(solution)/shard_map/ppermute | solution.py:361
  83.4 0.0 collective-permute-start.13
  83.4 1.4 %collective-permute-done.14 = f32[3,1024]{1,0:T(4,128)S(1)} collective-permute-done((f32[3,1024]{1,0:T(4,128)S(1)}, f32[3,1024]{1,0:T(4,128)S(1)}, u32[]{:S(2)}, u32[]{:S(2)}) %collective-permute-start.14) | collective-permute-done | bytes 12320 | tf_op jit(solution)/shard_map/ppermute | solution.py:361
  84.9 3.5 %collective-permute-done.13 = f32[3,1024]{1,0:T(4,128)S(1)} collective-permute-done((f32[3,1024]{1,0:T(4,128)S(1)}, f32[3,1024]{1,0:T(4,128)S(1)}, u32[]{:S(2)}, u32[]{:S(2)}) %collective-permute-start.13) | collective-permute-done | bytes 12320 | tf_op jit(solution)/shard_map/ppermute | solution.py:361
  88.4 0.8 collective-permute-start.16
  89.1 3.1 %collective-permute-start.15 = (f32[3,1024]{1,0:T(4,128)S(1)}, f32[3,1024]{1,0:T(4,128)S(1)}, u32[]{:S(2)}, u32[]{:S(2)}) collective-permute-start(f32[3,1024]{1,0:T(4,128)S(1)} %maximum_maximum_fusion.a_ref), channel_id=1, source_target_pairs={{0,3},{1,4},{2,5},{3,6},{4,7},{5,0},{6,1},{7,2},{8,11},{9,12},{10,... | collective-permute-start | bytes 36872 | tf_op jit(solution)/shard_map/ppermute | solution.py:361
  92.3 1.7 %collective-permute-done.16.c_ref = f32[3,1024]{1,0:T(4,128)S(1)} collective-permute-done((f32[3,1024]{1,0:T(4,128)S(1)}, f32[3,1024]{1,0:T(4,128)S(1)}, u32[]{:S(2)}, u32[]{:S(2)}) %collective-permute-start.16) | collective-permute-done | bytes 12320 | tf_op jit(solution)/shard_map/ppermute | solution.py:361
  94.0 1.9 %collective-permute-done.15.b_ref = f32[3,1024]{1,0:T(4,128)S(1)} collective-permute-done((f32[3,1024]{1,0:T(4,128)S(1)}, f32[3,1024]{1,0:T(4,128)S(1)}, u32[]{:S(2)}, u32[]{:S(2)}) %collective-permute-start.15) | collective-permute-done | bytes 12320 | tf_op jit(solution)/shard_map/ppermute | solution.py:361
  95.9 0.7 closing.1
  97.2 0.0 all-to-all-done.8
  97.3 15.0 %conditional.1 = (f32[1024]{0:T(1024)}, f32[]{:T(128)}, f32[512]{0:T(512)}, f32[128,512]{1,0:T(8,128)}) conditional(s32[]{:T(128)} %bitcast.30, (f32[1,1024]{1,0:T(1,128)}, f32[32,1,128]{2,1,0:T(1,128)}, bf16[32,192,128]{2,1,0:T(8,128)(2,1)}) %tuple.39, (s32[512]{0:T(512)S(1)}, bf16[1024,4096]{1,0:T(8,128)(2,1)}, s32[1024]{0:T(1024)S(1)}) %tuple.41), branch_computations={%region_0.2_spmd, %region_2.11_spmd} | conditional | flops 8601925632 | bytes 130077376 | solution.py:442
  97.3 7.5 %all-to-all-start = ((f32[32,1,128]{2,1,0:T(1,128)}), f32[32,1,128]{2,1,0:T(1,128)S(1)}, u32[]{:S(2)}, u32[]{:S(2)}) async-start(f32[32,1,128]{2,1,0:T(1,128)} %get-tuple-element.13), calls=%async_computation | async-start | bytes 32768 | tf_op jit(solution)/shard_map/cond/branch_0_fun/all_to_all | solution.py:437
  104.8 6.2 %sums.1 = (f32[128,512]{1,0:T(8,128)}, f32[1,512]{1,0:T(1,128)}) custom-call(bf16[32,192,128]{2,1,0:T(8,128)(2,1)} %get-tuple-element.14.got_ref), custom_call_target="tpu_custom_call" | custom-call | flops 1610612736 | bytes 1572864 | tf_op jit(solution)/shard_map/cond/branch_0_fun/sums/pallas_call | solution.py:220
  111.0 0.6 slice_reduce_fusion
  (9 shorter events, 0.1 us)
Async XLA Ops:
  7.6 55.1 %copy-start = (bf16[32,192,128]{2,1,0:T(8,128)(2,1)}, bf16[32,192,128]{2,1,0:T(8,128)(2,1)S(1)}, u32[]{:S(2)}) copy-start(bf16[32,192,128]{2,1,0:T(8,128)(2,1)S(1)} %get-tuple-element.39) | copy-start | bytes 4718596
  25.8 5.0 %collective-permute-start.8 = (bf16[128,256]{1,0:T(8,128)(2,1)S(1)}, bf16[128,256]{1,0:T(8,128)(2,1)S(1)}, u32[]{:S(2)}, u32[]{:S(2)}) collective-permute-start(bf16[128,256]{1,0:T(8,128)(2,1)S(1)} %get-tuple-element.35), channel_id=1, source_target_pairs={{0,48},{8,56},{16,0},{24,8},{32,16},{40,24},{48,32},{56,40},{64,11... | collective-permute-start | bytes 196616 | tf_op jit(solution)/shard_map/ppermute | solution.py:357
  27.6 6.4 %collective-permute-start.7 = (bf16[128,256]{1,0:T(8,128)(2,1)S(1)}, bf16[128,256]{1,0:T(8,128)(2,1)S(1)}, u32[]{:S(2)}, u32[]{:S(2)}) collective-permute-start(bf16[128,256]{1,0:T(8,128)(2,1)S(1)} %get-tuple-element.35), channel_id=1, source_target_pairs={{0,32},{8,40},{16,48},{24,56},{32,0},{40,8},{48,16},{56,24},{64,96... | collective-permute-start | bytes 196616 | tf_op jit(solution)/shard_map/ppermute | solution.py:357
  28.4 6.3 %collective-permute-start.6 = (bf16[128,256]{1,0:T(8,128)(2,1)S(1)}, bf16[128,256]{1,0:T(8,128)(2,1)S(1)}, u32[]{:S(2)}, u32[]{:S(2)}) collective-permute-start(bf16[128,256]{1,0:T(8,128)(2,1)S(1)} %get-tuple-element.35), channel_id=1, source_target_pairs={{0,16},{8,24},{16,32},{24,40},{32,48},{40,56},{48,0},{56,8},{64,80... | collective-permute-start | bytes 196616 | tf_op jit(solution)/shard_map/ppermute | solution.py:357
  34.7 34.3 %copy-start.1 = (s32[1024]{0:T(1024)S(1)}, s32[1024]{0:T(1024)}, u32[]{:S(2)}) copy-start(s32[1024]{0:T(1024)} %param.6) | copy-start | bytes 12292
  34.8 18.2 %collective-permute-start.11 = (bf16[4,128,256]{2,1,0:T(8,128)(2,1)S(1)}, bf16[4,128,256]{2,1,0:T(8,128)(2,1)S(1)}, u32[]{:S(2)}, u32[]{:S(2)}) collective-permute-start(bf16[4,128,256]{2,1,0:T(8,128)(2,1)S(1)} %pad_maximum_fusion.2.refs_4_), channel_id=1, source_target_pairs={{0,192},{8,200},{16,208},{24,216},{32,224},{40,232},{48,240},{56,2... | collective-permute-start | bytes 786440 | tf_op jit(solution)/shard_map/ppermute | solution.py:357
  36.2 9.2 %collective-permute-start.2 = (bf16[128,256]{1,0:T(8,128)(2,1)S(1)}, bf16[128,256]{1,0:T(8,128)(2,1)S(1)}, u32[]{:S(2)}, u32[]{:S(2)}) collective-permute-start(bf16[128,256]{1,0:T(8,128)(2,1)S(1)} %get-tuple-element.34), channel_id=1, source_target_pairs={{0,192},{8,200},{16,208},{24,216},{32,224},{40,232},{48,240},{56,2... | collective-permute-start | bytes 196616 | tf_op jit(solution)/shard_map/ppermute | solution.py:357
  37.4 9.4 %collective-permute-start.1 = (bf16[128,256]{1,0:T(8,128)(2,1)S(1)}, bf16[128,256]{1,0:T(8,128)(2,1)S(1)}, u32[]{:S(2)}, u32[]{:S(2)}) collective-permute-start(bf16[128,256]{1,0:T(8,128)(2,1)S(1)} %get-tuple-element.34), channel_id=1, source_target_pairs={{0,128},{8,136},{16,144},{24,152},{32,160},{40,168},{48,176},{56,1... | collective-permute-start | bytes 196616 | tf_op jit(solution)/shard_map/ppermute | solution.py:357
  38.4 8.5 %collective-permute-start = (bf16[128,256]{1,0:T(8,128)(2,1)S(1)}, bf16[128,256]{1,0:T(8,128)(2,1)S(1)}, u32[]{:S(2)}, u32[]{:S(2)}) collective-permute-start(bf16[128,256]{1,0:T(8,128)(2,1)S(1)} %get-tuple-element.34), channel_id=1, source_target_pairs={{0,64},{8,72},{16,80},{24,88},{32,96},{40,104},{48,112},{56,120},{... | collective-permute-start | bytes 196616 | tf_op jit(solution)/shard_map/ppermute | solution.py:357
  39.4 14.9 %collective-permute-start.10 = (bf16[4,128,256]{2,1,0:T(8,128)(2,1)S(1)}, bf16[4,128,256]{2,1,0:T(8,128)(2,1)S(1)}, u32[]{:S(2)}, u32[]{:S(2)}) collective-permute-start(bf16[4,128,256]{2,1,0:T(8,128)(2,1)S(1)} %pad_maximum_fusion.2.refs_4_), channel_id=1, source_target_pairs={{0,128},{8,136},{16,144},{24,152},{32,160},{40,168},{48,176},{56,1... | collective-permute-start | bytes 786440 | tf_op jit(solution)/shard_map/ppermute | solution.py:357
  45.5 9.0 %collective-permute-start.9 = (bf16[4,128,256]{2,1,0:T(8,128)(2,1)S(1)}, bf16[4,128,256]{2,1,0:T(8,128)(2,1)S(1)}, u32[]{:S(2)}, u32[]{:S(2)}) collective-permute-start(bf16[4,128,256]{2,1,0:T(8,128)(2,1)S(1)} %pad_maximum_fusion.2.refs_4_), channel_id=1, source_target_pairs={{0,64},{8,72},{16,80},{24,88},{32,96},{40,104},{48,112},{56,120},{... | collective-permute-start | bytes 786440 | tf_op jit(solution)/shard_map/ppermute | solution.py:357
  46.9 12.1 %collective-permute-start.5 = (bf16[4,128,256]{2,1,0:T(8,128)(2,1)S(1)}, bf16[4,128,256]{2,1,0:T(8,128)(2,1)S(1)}, u32[]{:S(2)}, u32[]{:S(2)}) collective-permute-start(bf16[4,128,256]{2,1,0:T(8,128)(2,1)S(1)} %pad_maximum_fusion.1.refs_0_), channel_id=1, source_target_pairs={{0,48},{8,56},{16,0},{24,8},{32,16},{40,24},{48,32},{56,40},{64,11... | collective-permute-start | bytes 786440 | tf_op jit(solution)/shard_map/ppermute | solution.py:357
  51.7 8.0 %collective-permute-start.4 = (bf16[4,128,256]{2,1,0:T(8,128)(2,1)S(1)}, bf16[4,128,256]{2,1,0:T(8,128)(2,1)S(1)}, u32[]{:S(2)}, u32[]{:S(2)}) collective-permute-start(bf16[4,128,256]{2,1,0:T(8,128)(2,1)S(1)} %pad_maximum_fusion.1.refs_0_), channel_id=1, source_target_pairs={{0,32},{8,40},{16,48},{24,56},{32,0},{40,8},{48,16},{56,24},{64,96... | collective-permute-start | bytes 786440 | tf_op jit(solution)/shard_map/ppermute | solution.py:357
  53.0 9.4 %collective-permute-start.3 = (bf16[4,128,256]{2,1,0:T(8,128)(2,1)S(1)}, bf16[4,128,256]{2,1,0:T(8,128)(2,1)S(1)}, u32[]{:S(2)}, u32[]{:S(2)}) collective-permute-start(bf16[4,128,256]{2,1,0:T(8,128)(2,1)S(1)} %pad_maximum_fusion.1.refs_0_), channel_id=1, source_target_pairs={{0,16},{8,24},{16,32},{24,40},{32,48},{40,56},{48,0},{56,8},{64,80... | collective-permute-start | bytes 786440 | tf_op jit(solution)/shard_map/ppermute | solution.py:357
  62.5 6.5 %collective-permute-start.12 = (bf16[32,128,256]{2,1,0:T(8,128)(2,1)S(1)}, bf16[32,128,256]{2,1,0:T(8,128)(2,1)}, u32[]{:S(2)}, u32[]{:S(2)}) collective-permute-start(bf16[32,128,256]{2,1,0:T(8,128)(2,1)S(1)} %joined.1.own_ref), channel_id=1, source_target_pairs={{0,8},{8,0},{16,24},{24,16},{32,40},{40,32},{48,56},{56,48},{64,72... | collective-permute-start | bytes 6291464 | tf_op jit(solution)/shard_map/ppermute | solution.py:357
  62.7 34.6 %all-to-all-start.8 = ((bf16[32,192,128]{2,1,0:T(8,128)(2,1)}), bf16[32,192,128]{2,1,0:T(8,128)(2,1)}, u32[]{:S(2)}, u32[]{:S(2)}) async-start(bf16[32,192,128]{2,1,0:T(8,128)(2,1)} %copy-done), calls=%async_computation.8 | async-start | bytes 3145728 | tf_op jit(solution)/shard_map/all_to_all | solution.py:428
  69.1 28.2 %copy-start.2 = (s32[512]{0:T(512)S(1)}, s32[512]{0:T(512)}, u32[]{:S(2)}) copy-start(s32[512]{0:T(512)} %param.7) | copy-start | bytes 6148
  77.5 7.4 %collective-permute-start.14 = (f32[3,1024]{1,0:T(4,128)S(1)}, f32[3,1024]{1,0:T(4,128)S(1)}, u32[]{:S(2)}, u32[]{:S(2)}) collective-permute-start(f32[3,1024]{1,0:T(4,128)S(1)} %scored.1), channel_id=1, source_target_pairs={{0,7},{1,0},{2,1},{3,2},{4,3},{5,4},{6,5},{7,6},{8,15},{9,8},{10,9... | collective-permute-start | bytes 36872 | tf_op jit(solution)/shard_map/ppermute | solution.py:361
  83.4 4.9 %collective-permute-start.13 = (f32[3,1024]{1,0:T(4,128)S(1)}, f32[3,1024]{1,0:T(4,128)S(1)}, u32[]{:S(2)}, u32[]{:S(2)}) collective-permute-start(f32[3,1024]{1,0:T(4,128)S(1)} %scored.1), channel_id=1, source_target_pairs={{0,1},{1,2},{2,3},{3,4},{4,5},{5,6},{6,7},{7,0},{8,9},{9,10},{10,1... | collective-permute-start | bytes 36872 | tf_op jit(solution)/shard_map/ppermute | solution.py:361
  88.4 5.6 %collective-permute-start.16 = (f32[3,1024]{1,0:T(4,128)S(1)}, f32[3,1024]{1,0:T(4,128)S(1)}, u32[]{:S(2)}, u32[]{:S(2)}) collective-permute-start(f32[3,1024]{1,0:T(4,128)S(1)} %maximum_maximum_fusion.a_ref), channel_id=1, source_target_pairs={{0,5},{1,6},{2,7},{3,0},{4,1},{5,2},{6,3},{7,4},{8,13},{9,14},{10,... | collective-permute-start | bytes 36872 | tf_op jit(solution)/shard_map/ppermute | solution.py:361
  89.1 6.7 %collective-permute-start.15 = (f32[3,1024]{1,0:T(4,128)S(1)}, f32[3,1024]{1,0:T(4,128)S(1)}, u32[]{:S(2)}, u32[]{:S(2)}) collective-permute-start(f32[3,1024]{1,0:T(4,128)S(1)} %maximum_maximum_fusion.a_ref), channel_id=1, source_target_pairs={{0,3},{1,4},{2,5},{3,6},{4,7},{5,0},{6,1},{7,2},{8,11},{9,12},{10,... | collective-permute-start | bytes 36872 | tf_op jit(solution)/shard_map/ppermute | solution.py:361
  97.3 13.7 %all-to-all-start = ((f32[32,1,128]{2,1,0:T(1,128)}), f32[32,1,128]{2,1,0:T(1,128)S(1)}, u32[]{:S(2)}, u32[]{:S(2)}) async-start(f32[32,1,128]{2,1,0:T(1,128)} %get-tuple-element.13), calls=%async_computation | async-start | bytes 32768 | tf_op jit(solution)/shard_map/cond/branch_0_fun/all_to_all | solution.py:437

commit v5 on v3

--- a/solution.py
+++ b/solution.py
@@ -95,8 +95,10 @@
 
     codes = code[...]
     lines = jnp.concatenate([codes[:, :LANES], codes[:, LANES:]], axis=0)
-    for chip in range(sk_ref.shape[1] // SEL):
-        block = sk_ref[:, chip * SEL : (chip + 1) * SEL]
+
+    @pl.loop(0, sk_ref.shape[1] // SEL)
+    def _(chip):
+        block = sk_ref[:, pl.ds(pl.multiple_of(chip * SEL, SEL), SEL)]
         rows = jnp.dot(sel[...], block, preferred_element_type=F32).astype(BF)
         for c in range(2):
             to = 2 * chip + c
@@ -213,7 +215,7 @@
         0, got_ref.shape[0] // per, body, jnp.zeros((medoids, feats + LANES), F32)
     )
     sums_ref[...] = total[:, :feats].T
-    count_ref[...] = total[:, feats:].T[:8]
+    count_ref[...] = total[:, feats:].T[:1]
 
 
 def sums(got, medoids):
@@ -223,7 +225,7 @@
         out_specs=[pl.BlockSpec(memory_space=pltpu.VMEM)] * 2,
         out_shape=[
             jax.ShapeDtypeStruct((got.shape[2], medoids), F32),
-            jax.ShapeDtypeStruct((8, medoids), F32),
+            jax.ShapeDtypeStruct((1, medoids), F32),
         ],
         compiler_params=pltpu.CompilerParams(vmem_limit_bytes=16 * 2**20),
         cost_estimate=pl.CostEstimate(
@@ -233,78 +235,70 @@
     )(got)
 
 
-def joined_kernel(*refs):
-    parts, out_ref = refs[:-1], refs[-1]
-    size = parts[0].shape[0]
-    for i, part in enumerate(parts):
-        out_ref[i * size : (i + 1) * size] = part[...]
-
-
-def joined(parts):
-    size, *rest = parts[0].shape
-    return pl.pallas_call(
-        joined_kernel,
-        in_specs=[pl.BlockSpec(memory_space=pltpu.VMEM)] * len(parts),
-        out_specs=pl.BlockSpec(memory_space=pltpu.VMEM),
-        out_shape=jax.ShapeDtypeStruct((size * len(parts), *rest), parts[0].dtype),
-        compiler_params=pltpu.CompilerParams(vmem_limit_bytes=8 * 2**20),
-        cost_estimate=pl.CostEstimate(
-            flops=0, bytes_accessed=4 * len(parts) * parts[0].size, transcendentals=0
-        ),
-        name="joined",
-    )(*parts)
-
-
-def score_kernel(scale, where_ref, assign_ref, mark_ref, sk_ref, own_ref, other_ref, out_ref):
-    quarter, wide = own_ref.shape[1:]
+def score_kernel(scale, where_ref, assign_ref, mark_ref, near_ref, far_ref, *refs):
+    parts, (near_out, far_out) = refs[:8], refs[8:]
+    quarter, wide = parts[0].shape[1:]
     half = 2 * quarter
-    core, x, y, base = where_ref[2], where_ref[3], where_ref[4], where_ref[5]
-    points = sk_ref.shape[0]
-    total = jnp.zeros((2 * half, points), F32)
-    for kx in range(4):
-        for ky in range(4):
-            block = ((x + 4 - kx) & 3) * 4 + ((y + 4 - ky) & 3)
-            at = pl.multiple_of(block * wide, wide)
-            a, b = ky * 4 + kx, 16 + kx * 4 + ky
-            total = total + contract_last(
-                jnp.concatenate([own_ref[a], own_ref[b], other_ref[a], other_ref[b]], axis=0),
-                sk_ref[:, pl.ds(at, wide)],
-            )
-    scores = total * scale
-    best = jnp.max(scores, axis=0, keepdims=True)
-    row = lax.broadcasted_iota(I32, scores.shape, 0)
-    local = assign_ref[...] - base
-    here = (local >= 0) & (local < 2 * half)
-    local = jnp.where(here, local ^ (core * half), -1)
-    chosen = jnp.max(jnp.where(local == row, scores, NONE), axis=0, keepdims=True)
-    out_ref[...] = jnp.concatenate([best, chosen, mark_ref[...]], axis=0)
-
-
-def scored(where, assignment, marks, sketches, own, other):
-    rows, feats = sketches.shape
+    x, y, base = where_ref[3], where_ref[4], where_ref[5]
+    step = pl.program_id(0)
+    count = pl.num_programs(0) // 2
+
+    def stats(points_ref):
+        total = jnp.zeros((half, points_ref.shape[0]), F32)
+        for kx in range(4):
+            for ky in range(4):
+                block = ((x + 4 - kx) & 3) * 4 + ((y + 4 - ky) & 3)
+                at = pl.multiple_of(block * wide, wide)
+                total = total + contract_last(
+                    jnp.concatenate([parts[ky][kx], parts[4 + kx][ky]], axis=0),
+                    points_ref[:, pl.ds(at, wide)],
+                )
+        scores = total * scale
+        best = jnp.max(scores, axis=0, keepdims=True)
+        row = lax.broadcasted_iota(I32, scores.shape, 0)
+        local = assign_ref[...] - base
+        chosen = jnp.max(jnp.where(local == row, scores, NONE), axis=0, keepdims=True)
+        return jnp.concatenate([best, chosen, mark_ref[...]], axis=0)
+
+    @pl.when(step < count)
+    def _():
+        near_out[...] = stats(near_ref)
+
+    @pl.when(step >= count)
+    def _():
+        far_out[...] = stats(far_ref)
+
+
+def scored(where, assignments, marks, near, far, parts):
+    rows, feats = near.shape
     tile = 2 * LANES
-    whole = lambda a: pl.BlockSpec(a.shape, lambda i, w: (0,) * a.ndim)
+    count = rows // tile
+    early = lambda i, w: (jnp.minimum(i, count - 1), 0)
+    late = lambda i, w: (jnp.maximum(i - count, 0), 0)
     return pl.pallas_call(
         functools.partial(score_kernel, 1.0 / feats),
         grid_spec=pltpu.PrefetchScalarGridSpec(
             num_scalar_prefetch=1,
-            grid=(rows // tile,),
+            grid=(2 * count,),
             in_specs=[
                 pl.BlockSpec((1, tile), lambda i, w: (0, i)),
                 pl.BlockSpec((1, tile), lambda i, w: (0, 0)),
-                pl.BlockSpec((tile, feats), lambda i, w: (i, 0)),
-                whole(own),
-                whole(other),
+                pl.BlockSpec((tile, feats), early),
+                pl.BlockSpec((tile, feats), late),
+            ]
+            + [pl.BlockSpec(a.shape, lambda i, w: (0, 0, 0)) for a in parts],
+            out_specs=[
+                pl.BlockSpec((3, tile), lambda i, w: early(i, w)[::-1]),
+                pl.BlockSpec((3, tile), lambda i, w: late(i, w)[::-1]),
             ],
-            out_specs=pl.BlockSpec((3, tile), lambda i, w: (0, i)),
-        ),
-        out_shape=jax.ShapeDtypeStruct((3, rows), F32),
-        compiler_params=pltpu.CompilerParams(vmem_limit_bytes=24 * 2**20),
+        ),
+        out_shape=[jax.ShapeDtypeStruct((3, rows), F32)] * 2,
+        compiler_params=pltpu.CompilerParams(vmem_limit_bytes=32 * 2**20),
         cost_estimate=pl.CostEstimate(
-            flops=2 * rows * feats * 512, bytes_accessed=rows * feats * 2, transcendentals=0
+            flops=4 * rows * feats * 256, bytes_accessed=rows * feats * 4, transcendentals=0
         ),
         name="scored",
-    )(where, assignment[None, :], marks, sketches, own, other)
+    )(where, assignments, marks, near, far, *parts)
 
 
 def closing_kernel(a_ref, b_ref, gap_ref, send_ref, mark_ref):
@@ -357,8 +351,13 @@
     return lax.ppermute(array, "pts", pairs)
 
 
-def across(array, step, planes):
-    return lax.ppermute(array, "med", [(z, z ^ step) for z in range(planes)])
+def across(array, core, step, planes):
+    pairs = [
+        (p * planes + z, (p ^ core) * planes + (z ^ step))
+        for p in range(32)
+        for z in range(planes)
+    ]
+    return lax.ppermute(array, ("pts", "med"), pairs)
 
 
 def general(sketches, assignment, medoid_ids):
@@ -407,9 +406,11 @@
     core = p % 2
     planes = lax.axis_size("med")
     where = jnp.stack(
-        [p * row_count, m, core, p // 8, (p // 2) % 4, m * medoid_count, m, m]
+        [p * row_count, m, core, p // 8, (p // 2) % 4, m * medoid_count + core * half, m, m]
     ).astype(I32)
 
+    far = shifted(sketches, 0, 0, 1)
+    far_assignment = shifted(assignment, 0, 0, 1)
     med_send, grad_send = pick(
         where, assignment, medoid_ids, sketches, pts_count
     )
@@ -417,21 +418,24 @@
     a, b, marks = place(where, med_got, half)
     pa = jnp.stack([a] + [shifted(a, k, 0, 0) for k in (1, 2, 3)])
     pb = jnp.stack([b] + [shifted(b, 0, k, 0) for k in (1, 2, 3)])
-    qa = [pa] + [shifted(pa, 0, k, 0) for k in (1, 2, 3)]
+    qa = [pa, shifted(pa, 0, 1, 0)]
+    qa = qa + [shifted(pa, 0, k, 0) for k in (2, 3)]
     qb = [pb] + [shifted(pb, k, 0, 0) for k in (1, 2, 3)]
-    own = joined(qa + qb)
-    other = shifted(own, 0, 0, 1)
     grad_got = lax.all_to_all(grad_send, "pts", 0, 0, tiled=True)
-    stats = scored(where, assignment, marks, sketches, own, other)
-    for step in (1, 2):
-        stats = jnp.maximum(stats, across(stats, step, planes))
-    final = across(stats, 4, planes)
+    assignments = jnp.concatenate([assignment, far_assignment])[None, :]
+    stats, theirs = scored(where, assignments, marks, sketches, far, qa + qb)
+    stats = jnp.maximum(
+        jnp.maximum(stats, across(stats, 0, 1, planes)),
+        jnp.maximum(across(theirs, 1, 0, planes), across(theirs, 1, 1, planes)),
+    )
+    stats = jnp.maximum(stats, across(stats, 0, 2, planes))
+    final = across(stats, 0, 4, planes)
+    gradient_sums, counts = sums(grad_got, medoid_count)
     gap, total, mark = closing(stats, final, pts_count)
     full = mark[0, 0] > 0
 
     def fast():
         totals = lax.all_to_all(total, "pts", 0, 0, tiled=True)
-        gradient_sums, counts = sums(grad_got, medoid_count)
         coverage = jnp.sum(totals[:, 0, 0]) / (row_count * pts_count)
         return gap[0], coverage, counts[0], gradient_sums
 

time: 114 us -> 144 us (1.26)
  waiting for transfers between devices: 23 us -> 44 us
  blocking collectives: 17.2 us -> 28.6 us
  starting transfers between devices: 44.9 us -> 37.4 us
  Pallas kernels: 23.3 us -> 26.6 us
    ppermute x13 -> x14, waiting for transfers between devices: 17.6 us -> 39.1 us  [shifted(): return lax.ppermute(array, 'pts', pairs)]
    all_to_all x0 -> x1, blocking collectives: none -> 11.2 us  [fast(): totals = lax.all_to_all(total, 'pts', 0, 0, tiled=True)]
    all_to_all x1 -> x0, starting transfers between devices: 7.47 us -> none  [fast(): totals = lax.all_to_all(total, 'pts', 0, 0, tiled=True)]
    pallas_call x1, Pallas kernels: 8.39 us -> 11.7 us  [scored(): pl.pallas_call(functools.partial(score_kernel, 1.0 / feats), grid_spec=pl...]
    pallas_call x1, Pallas kernels: 6.79 us -> 8.45 us  [pick(): pl.pallas_call(pick_kernel, grid_spec=pltpu.PrefetchScalarGridSpec(num_sc...]
    ppermute x13 -> x14, starting transfers between devices: 19.1 us -> 20.6 us  [shifted(): return lax.ppermute(array, 'pts', pairs)]
    pallas_call x1, Pallas kernels: 6.29 us -> 4.81 us  [sums(): pl.pallas_call(sums_kernel, in_specs=[pl.BlockSpec(memory_space=pltpu.VME...]
    ppermute x3 -> x5, waiting for transfers between devices: 5.43 us -> 4.84 us  [across(): return lax.ppermute(array, ('pts', 'med'), pairs)]
  transfers between devices with their start and end apart: 18 -> 20, of which waited for: 12 -> 13; matrix products, arithmetic and copies ran while one was open for 1% -> 0% of each run, Pallas kernels for 14% -> 18%
where the time goes in v5:
time: 144 us; the launch traced here: 142 us
  waiting for transfers between devices  44 us (31%)
  starting transfers between devices  37.4 us (26%)
  blocking collectives  28.6 us (20%)
  Pallas kernels  26.6 us (18%)
  between operations  2.57 us (2%)
    ppermute x14, waiting for transfers between devices, shifted(): return lax.ppermute(array, 'pts', pairs)  39.1 us
    ppermute x14, starting transfers between devices, shifted(): return lax.ppermute(array, 'pts', pairs)  20.6 us
    all_to_all x1, blocking collectives, shards(): med_got = lax.all_to_all(med_send, 'pts', 0, 0, tiled=True)  17.4 us
    pallas_call x1, Pallas kernels, scored(): pl.pallas_call(functools.partial(score_kernel, 1.0 / feats), grid_spec=pl...  11.7 us
    ppermute x5, starting transfers between devices, across(): return lax.ppermute(array, ('pts', 'med'), pairs)  11.4 us
    all_to_all x1, blocking collectives, fast(): totals = lax.all_to_all(total, 'pts', 0, 0, tiled=True)  11.2 us
    pallas_call x1, Pallas kernels, pick(): pl.pallas_call(pick_kernel, grid_spec=pltpu.PrefetchScalarGridSpec(num_sc...  8.45 us
    all_to_all x1, starting transfers between devices, shards(): grad_got = lax.all_to_all(grad_send, 'pts', 0, 0, tiled=True)  5.42 us
  transfers between devices with their start and end apart: 20, of which 13 were waited for; matrix products, arithmetic and copies ran while one was open for 0% of the time, Pallas kernels for 18%

profile of v5, /device:TPU:2, one launch (start us, length us, event | category | flops | bytes accessed | tf_op | source)
XLA Modules:
  0.0 141.8 jit_solution(9447889431144134667)
XLA Ops:
  0.6 0.1 collective-permute-start.1
  0.8 0.1 stack.68.where_ref
  0.9 8.4 %pick.1 = (bf16[32,32,256]{2,1,0:T(8,128)(2,1)S(1)}, bf16[32,192,128]{2,1,0:T(8,128)(2,1)S(1)}) custom-call(s32[8]{0:T(128)S(1)} %stack.68.where_ref, s32[8,128]{1,0:T(8,128)} %bitcast.63, s32[1,512]{1,0:T(1,128)} %bitcast.66, bf16[1024,4096]{1,0:T(8,128)(2,1)} %near_ref.1), custom_call_target="tpu_custom_call" | custom-call | flops 2147483648 | bytes 8388608 | tf_op jit(solution)/shard_map/pick/pallas_call | solution.py:114
  9.3 1.2 copy-done
  10.5 17.4 %all_to_all.42.got_ref = bf16[32,32,256]{2,1,0:T(8,128)(2,1)S(1)} all-to-all(bf16[32,32,256]{2,1,0:T(8,128)(2,1)S(1)} %get-tuple-element.37), channel_id=1, replica_groups=mesh['pts'=32,'med'=8] {'pts'}, dimensions={0} | all-to-all | bytes 1048576 | tf_op jit(solution)/shard_map/all_to_all | solution.py:417
  27.9 5.4 %all-to-all-start.8 = ((bf16[32,192,128]{2,1,0:T(8,128)(2,1)}), bf16[32,192,128]{2,1,0:T(8,128)(2,1)S(1)}, u32[]{:S(2)}, u32[]{:S(2)}) async-start(bf16[32,192,128]{2,1,0:T(8,128)(2,1)} %copy-done), calls=%async_computation.8 | async-start | bytes 3145728 | tf_op jit(solution)/shard_map/all_to_all | solution.py:424
  33.4 1.0 place.1
  34.3 2.8 %collective-permute-start.10 = (bf16[128,256]{1,0:T(8,128)(2,1)S(1)}, bf16[128,256]{1,0:T(8,128)(2,1)S(1)}, u32[]{:S(2)}, u32[]{:S(2)}) collective-permute-start(bf16[128,256]{1,0:T(8,128)(2,1)S(1)} %get-tuple-element.40), channel_id=1, source_target_pairs={{0,48},{8,56},{16,0},{24,8},{32,16},{40,24},{48,32},{56,40},{64,11... | collective-permute-start | bytes 196616 | tf_op jit(solution)/shard_map/ppermute | solution.py:351
  37.1 0.9 collective-permute-start.9
  38.0 0.9 collective-permute-start.8
  38.8 15.5 %collective-permute-done.10 = bf16[128,256]{1,0:T(8,128)(2,1)S(1)} collective-permute-done((bf16[128,256]{1,0:T(8,128)(2,1)S(1)}, bf16[128,256]{1,0:T(8,128)(2,1)S(1)}, u32[]{:S(2)}, u32[]{:S(2)}) %collective-permute-start.10) | collective-permute-done | bytes 65568 | tf_op jit(solution)/shard_map/ppermute | solution.py:351
  54.3 1.9 %collective-permute-done.9 = bf16[128,256]{1,0:T(8,128)(2,1)S(1)} collective-permute-done((bf16[128,256]{1,0:T(8,128)(2,1)S(1)}, bf16[128,256]{1,0:T(8,128)(2,1)S(1)}, u32[]{:S(2)}, u32[]{:S(2)}) %collective-permute-start.9) | collective-permute-done | bytes 65568 | tf_op jit(solution)/shard_map/ppermute | solution.py:351
  56.2 0.5 collective-permute-done.8
  56.8 0.6 collective-permute-start.13
  57.4 2.4 %collective-permute-start.12 = (bf16[4,128,256]{2,1,0:T(8,128)(2,1)S(1)}, bf16[4,128,256]{2,1,0:T(8,128)(2,1)S(1)}, u32[]{:S(2)}, u32[]{:S(2)}) collective-permute-start(bf16[4,128,256]{2,1,0:T(8,128)(2,1)S(1)} %pad_maximum_fusion.2.refs_4_), channel_id=1, source_target_pairs={{0,128},{8,136},{16,144},{24,152},{32,160},{40,168},{48,176},{56,1... | collective-permute-start | bytes 786440 | tf_op jit(solution)/shard_map/ppermute | solution.py:351
  59.8 1.1 collective-permute-start.4
  61.0 2.2 %collective-permute-start.3 = (bf16[128,256]{1,0:T(8,128)(2,1)S(1)}, bf16[128,256]{1,0:T(8,128)(2,1)S(1)}, u32[]{:S(2)}, u32[]{:S(2)}) collective-permute-start(bf16[128,256]{1,0:T(8,128)(2,1)S(1)} %get-tuple-element.39), channel_id=1, source_target_pairs={{0,128},{8,136},{16,144},{24,152},{32,160},{40,168},{48,176},{56,1... | collective-permute-start | bytes 196616 | tf_op jit(solution)/shard_map/ppermute | solution.py:351
  63.1 7.5 %collective-permute-done.4 = bf16[128,256]{1,0:T(8,128)(2,1)S(1)} collective-permute-done((bf16[128,256]{1,0:T(8,128)(2,1)S(1)}, bf16[128,256]{1,0:T(8,128)(2,1)S(1)}, u32[]{:S(2)}, u32[]{:S(2)}) %collective-permute-start.4) | collective-permute-done | bytes 65568 | tf_op jit(solution)/shard_map/ppermute | solution.py:351
  70.6 3.5 %collective-permute-start.2 = (bf16[128,256]{1,0:T(8,128)(2,1)S(1)}, bf16[128,256]{1,0:T(8,128)(2,1)S(1)}, u32[]{:S(2)}, u32[]{:S(2)}) collective-permute-start(bf16[128,256]{1,0:T(8,128)(2,1)S(1)} %get-tuple-element.39), channel_id=1, source_target_pairs={{0,64},{8,72},{16,80},{24,88},{32,96},{40,104},{48,112},{56,120},{... | collective-permute-start | bytes 196616 | tf_op jit(solution)/shard_map/ppermute | solution.py:351
  74.1 0.1 collective-permute-done.3
  74.3 0.0 collective-permute-start
  74.3 1.9 %collective-permute-done.2 = bf16[128,256]{1,0:T(8,128)(2,1)S(1)} collective-permute-done((bf16[128,256]{1,0:T(8,128)(2,1)S(1)}, bf16[128,256]{1,0:T(8,128)(2,1)S(1)}, u32[]{:S(2)}, u32[]{:S(2)}) %collective-permute-start.2) | collective-permute-done | bytes 65568 | tf_op jit(solution)/shard_map/ppermute | solution.py:351
  76.1 2.8 %collective-permute-start.11 = (bf16[4,128,256]{2,1,0:T(8,128)(2,1)S(1)}, bf16[4,128,256]{2,1,0:T(8,128)(2,1)S(1)}, u32[]{:S(2)}, u32[]{:S(2)}) collective-permute-start(bf16[4,128,256]{2,1,0:T(8,128)(2,1)S(1)} %pad_maximum_fusion.2.refs_4_), channel_id=1, source_target_pairs={{0,64},{8,72},{16,80},{24,88},{32,96},{40,104},{48,112},{56,120},{... | collective-permute-start | bytes 786440 | tf_op jit(solution)/shard_map/ppermute | solution.py:351
  78.9 0.0 collective-permute-done
  78.9 1.9 %collective-permute-start.7 = (bf16[4,128,256]{2,1,0:T(8,128)(2,1)S(1)}, bf16[4,128,256]{2,1,0:T(8,128)(2,1)S(1)}, u32[]{:S(2)}, u32[]{:S(2)}) collective-permute-start(bf16[4,128,256]{2,1,0:T(8,128)(2,1)S(1)} %pad_maximum_fusion.1.refs_0_), channel_id=1, source_target_pairs={{0,48},{8,56},{16,0},{24,8},{32,16},{40,24},{48,32},{56,40},{64,11... | collective-permute-start | bytes 786440 | tf_op jit(solution)/shard_map/ppermute | solution.py:351
  80.9 1.5 %collective-permute-start.6 = (bf16[4,128,256]{2,1,0:T(8,128)(2,1)S(1)}, bf16[4,128,256]{2,1,0:T(8,128)(2,1)S(1)}, u32[]{:S(2)}, u32[]{:S(2)}) collective-permute-start(bf16[4,128,256]{2,1,0:T(8,128)(2,1)S(1)} %pad_maximum_fusion.1.refs_0_), channel_id=1, source_target_pairs={{0,32},{8,40},{16,48},{24,56},{32,0},{40,8},{48,16},{56,24},{64,96... | collective-permute-start | bytes 786440 | tf_op jit(solution)/shard_map/ppermute | solution.py:351
  82.4 0.0 collective-permute-done.12.refs_6_
  82.4 0.0 collective-permute-start.5
  82.4 1.8 %collective-permute-done.11.refs_5_ = bf16[4,128,256]{2,1,0:T(8,128)(2,1)S(1)} collective-permute-done((bf16[4,128,256]{2,1,0:T(8,128)(2,1)S(1)}, bf16[4,128,256]{2,1,0:T(8,128)(2,1)S(1)}, u32[]{:S(2)}, u32[]{:S(2)}) %collective-permute-start.11) | collective-permute-done | bytes 262176 | tf_op jit(solution)/shard_map/ppermute | solution.py:351
  84.2 4.0 %collective-permute-done.7.refs_3_ = bf16[4,128,256]{2,1,0:T(8,128)(2,1)S(1)} collective-permute-done((bf16[4,128,256]{2,1,0:T(8,128)(2,1)S(1)}, bf16[4,128,256]{2,1,0:T(8,128)(2,1)S(1)}, u32[]{:S(2)}, u32[]{:S(2)}) %collective-permute-start.7) | collective-permute-done | bytes 262176 | tf_op jit(solution)/shard_map/ppermute | solution.py:351
  88.2 3.1 %collective-permute-done.6.refs_2_ = bf16[4,128,256]{2,1,0:T(8,128)(2,1)S(1)} collective-permute-done((bf16[4,128,256]{2,1,0:T(8,128)(2,1)S(1)}, bf16[4,128,256]{2,1,0:T(8,128)(2,1)S(1)}, u32[]{:S(2)}, u32[]{:S(2)}) %collective-permute-start.6) | collective-permute-done | bytes 262176 | tf_op jit(solution)/shard_map/ppermute | solution.py:351
  91.3 2.8 %collective-permute-done.5.refs_1_ = bf16[4,128,256]{2,1,0:T(8,128)(2,1)S(1)} collective-permute-done((bf16[4,128,256]{2,1,0:T(8,128)(2,1)S(1)}, bf16[4,128,256]{2,1,0:T(8,128)(2,1)S(1)}, u32[]{:S(2)}, u32[]{:S(2)}) %collective-permute-start.5) | collective-permute-done | bytes 262176 | tf_op jit(solution)/shard_map/ppermute | solution.py:351
  94.1 0.0 collective-permute-done.1.far_ref
  94.1 11.7 %scored.1 = (f32[3,1024]{1,0:T(4,128)S(1)}, f32[3,1024]{1,0:T(4,128)S(1)}) custom-call(s32[8]{0:T(128)S(1)} %stack.68.where_ref, s32[1,2048]{1,0:T(1,128)S(1)} %bitcast.54, f32[1,256]{1,0:T(1,128)S(1)} %get-tuple-element.38.mark_ref, bf16[1024,4096]{1,0:T(8,128)(2,1)} %near_ref.1, bf16[1024,4096]{1,0:T(8,128)(2,1)} %collective-permute-done.1.far_ref, ...), custom_call_target="tpu_custom_call" | custom-call | flops 4294967296 | bytes 16777216 | tf_op jit(solution)/shard_map/scored/pallas_call | solution.py:278
  105.8 0.0 copy-start.2
  105.8 2.0 %collective-permute-start.14 = (f32[3,1024]{1,0:T(4,128)S(1)}, f32[3,1024]{1,0:T(4,128)S(1)}, u32[]{:S(2)}, u32[]{:S(2)}) collective-permute-start(f32[3,1024]{1,0:T(4,128)S(1)} %get-tuple-element.41), channel_id=1, source_target_pairs={{0,1},{1,0},{2,3},{3,2},{4,5},{5,4},{6,7},{7,6},{8,9},{9,8},{10,11... | collective-permute-start | bytes 36872 | tf_op jit(solution)/shard_map/ppermute | solution.py:360
  107.8 0.2 collective-permute-start.15
  108.0 1.6 %collective-permute-done.14 = f32[3,1024]{1,0:T(4,128)S(1)} collective-permute-done((f32[3,1024]{1,0:T(4,128)S(1)}, f32[3,1024]{1,0:T(4,128)S(1)}, u32[]{:S(2)}, u32[]{:S(2)}) %collective-permute-start.14) | collective-permute-done | bytes 12320 | tf_op jit(solution)/shard_map/ppermute | solution.py:360
  109.6 1.3 collective-permute-done.16
  111.0 0.0 collective-permute-done.15
  111.0 3.4 %collective-permute-start.17 = (f32[3,1024]{1,0:T(4,128)S(1)}, f32[3,1024]{1,0:T(4,128)S(1)}, u32[]{:S(2)}, u32[]{:S(2)}) collective-permute-start(f32[3,1024]{1,0:T(4,128)S(1)} %maximum_maximum_fusion), channel_id=1, source_target_pairs={{0,2},{1,3},{2,0},{3,1},{4,6},{5,7},{6,4},{7,5},{8,10},{9,11},{10,... | collective-permute-start | bytes 36872 | tf_op jit(solution)/shard_map/ppermute | solution.py:360
  114.3 1.9 %collective-permute-done.17 = f32[3,1024]{1,0:T(4,128)S(1)} collective-permute-done((f32[3,1024]{1,0:T(4,128)S(1)}, f32[3,1024]{1,0:T(4,128)S(1)}, u32[]{:S(2)}, u32[]{:S(2)}) %collective-permute-start.17) | collective-permute-done | bytes 12320 | tf_op jit(solution)/shard_map/ppermute | solution.py:360
  116.2 5.8 %collective-permute-start.18 = (f32[3,1024]{1,0:T(4,128)S(1)}, f32[3,1024]{1,0:T(4,128)S(1)}, u32[]{:S(2)}, u32[]{:S(2)}) collective-permute-start(f32[3,1024]{1,0:T(4,128)S(1)} %max.23.a_ref), channel_id=1, source_target_pairs={{0,4},{1,5},{2,6},{3,7},{4,0},{5,1},{6,2},{7,3},{8,12},{9,13},{10,... | collective-permute-start | bytes 36872 | tf_op jit(solution)/shard_map/ppermute | solution.py:360
  122.0 4.8 %sums.1 = (f32[128,512]{1,0:T(8,128)}, f32[1,512]{1,0:T(1,128)}) custom-call(bf16[32,192,128]{2,1,0:T(8,128)(2,1)S(1)} %all-to-all-done.8.got_ref), custom_call_target="tpu_custom_call" | custom-call | flops 1610612736 | bytes 1572864 | tf_op jit(solution)/shard_map/sums/pallas_call | solution.py:222
  126.8 0.6 closing.1
  128.1 12.5 %conditional.1 = (f32[1024]{0:T(1024)}, f32[]{:T(128)}, f32[512]{0:T(512)}, f32[128,512]{1,0:T(8,128)}) conditional(s32[]{:T(128)} %bitcast.30, (f32[1,1024]{1,0:T(1,128)}, f32[32,1,128]{2,1,0:T(1,128)S(1)}, f32[1,512]{1,0:T(1,128)}, f32[128,512]{1,0:T(8,128)}) %tuple.38, (s32[512]{0:T(512)S(1)}, bf16[1024,4096]{1,0:T(8,128)(2,1)}, ...), branch_computations={%region_0.2_spmd, %region_2.11_spmd} | conditional | flops 8601925632 | bytes 130077376 | solution.py:442
  128.1 11.2 %all_to_all.40 = f32[32,1,128]{2,1,0:T(1,128)S(1)} all-to-all(f32[32,1,128]{2,1,0:T(1,128)S(1)} %get-tuple-element.15), channel_id=1, replica_groups=mesh['pts'=32,'med'=8] {'pts'}, dimensions={0} | all-to-all | bytes 32768 | tf_op jit(solution)/shard_map/cond/branch_0_fun/all_to_all | solution.py:438
  139.3 0.6 slice_reduce_fusion
  (13 shorter events, 0.1 us)
Async XLA Ops:
  0.6 93.4 %collective-permute-start.1 = (bf16[1024,4096]{1,0:T(8,128)(2,1)}, bf16[1024,4096]{1,0:T(8,128)(2,1)}, u32[]{:S(2)}, u32[]{:S(2)}) collective-permute-start(bf16[1024,4096]{1,0:T(8,128)(2,1)} %near_ref.1), channel_id=1, source_target_pairs={{0,8},{8,0},{16,24},{24,16},{32,40},{40,32},{48,56},{56,48},{64,72... | collective-permute-start | bytes 25165832 | tf_op jit(solution)/shard_map/ppermute | solution.py:351
  9.3 1.2 copy-start
  10.5 63.7 %copy-start.1 = (s32[1024]{0:T(1024)S(1)}, s32[1024]{0:T(1024)}, u32[]{:S(2)}) copy-start(s32[1024]{0:T(1024)} %param.6) | copy-start | bytes 12292
  27.9 94.1 %all-to-all-start.8 = ((bf16[32,192,128]{2,1,0:T(8,128)(2,1)}), bf16[32,192,128]{2,1,0:T(8,128)(2,1)S(1)}, u32[]{:S(2)}, u32[]{:S(2)}) async-start(bf16[32,192,128]{2,1,0:T(8,128)(2,1)} %copy-done), calls=%async_computation.8 | async-start | bytes 3145728 | tf_op jit(solution)/shard_map/all_to_all | solution.py:424
  34.3 20.0 %collective-permute-start.10 = (bf16[128,256]{1,0:T(8,128)(2,1)S(1)}, bf16[128,256]{1,0:T(8,128)(2,1)S(1)}, u32[]{:S(2)}, u32[]{:S(2)}) collective-permute-start(bf16[128,256]{1,0:T(8,128)(2,1)S(1)} %get-tuple-element.40), channel_id=1, source_target_pairs={{0,48},{8,56},{16,0},{24,8},{32,16},{40,24},{48,32},{56,40},{64,11... | collective-permute-start | bytes 196616 | tf_op jit(solution)/shard_map/ppermute | solution.py:351
  37.1 19.1 %collective-permute-start.9 = (bf16[128,256]{1,0:T(8,128)(2,1)S(1)}, bf16[128,256]{1,0:T(8,128)(2,1)S(1)}, u32[]{:S(2)}, u32[]{:S(2)}) collective-permute-start(bf16[128,256]{1,0:T(8,128)(2,1)S(1)} %get-tuple-element.40), channel_id=1, source_target_pairs={{0,32},{8,40},{16,48},{24,56},{32,0},{40,8},{48,16},{56,24},{64,96... | collective-permute-start | bytes 196616 | tf_op jit(solution)/shard_map/ppermute | solution.py:351
  38.0 18.8 %collective-permute-start.8 = (bf16[128,256]{1,0:T(8,128)(2,1)S(1)}, bf16[128,256]{1,0:T(8,128)(2,1)S(1)}, u32[]{:S(2)}, u32[]{:S(2)}) collective-permute-start(bf16[128,256]{1,0:T(8,128)(2,1)S(1)} %get-tuple-element.40), channel_id=1, source_target_pairs={{0,16},{8,24},{16,32},{24,40},{32,48},{40,56},{48,0},{56,8},{64,80... | collective-permute-start | bytes 196616 | tf_op jit(solution)/shard_map/ppermute | solution.py:351
  56.8 24.1 %collective-permute-start.13 = (bf16[4,128,256]{2,1,0:T(8,128)(2,1)S(1)}, bf16[4,128,256]{2,1,0:T(8,128)(2,1)S(1)}, u32[]{:S(2)}, u32[]{:S(2)}) collective-permute-start(bf16[4,128,256]{2,1,0:T(8,128)(2,1)S(1)} %pad_maximum_fusion.2.refs_4_), channel_id=1, source_target_pairs={{0,192},{8,200},{16,208},{24,216},{32,224},{40,232},{48,240},{56,2... | collective-permute-start | bytes 786440 | tf_op jit(solution)/shard_map/ppermute | solution.py:351
  57.4 25.0 %collective-permute-start.12 = (bf16[4,128,256]{2,1,0:T(8,128)(2,1)S(1)}, bf16[4,128,256]{2,1,0:T(8,128)(2,1)S(1)}, u32[]{:S(2)}, u32[]{:S(2)}) collective-permute-start(bf16[4,128,256]{2,1,0:T(8,128)(2,1)S(1)} %pad_maximum_fusion.2.refs_4_), channel_id=1, source_target_pairs={{0,128},{8,136},{16,144},{24,152},{32,160},{40,168},{48,176},{56,1... | collective-permute-start | bytes 786440 | tf_op jit(solution)/shard_map/ppermute | solution.py:351
  59.8 10.8 %collective-permute-start.4 = (bf16[128,256]{1,0:T(8,128)(2,1)S(1)}, bf16[128,256]{1,0:T(8,128)(2,1)S(1)}, u32[]{:S(2)}, u32[]{:S(2)}) collective-permute-start(bf16[128,256]{1,0:T(8,128)(2,1)S(1)} %get-tuple-element.39), channel_id=1, source_target_pairs={{0,192},{8,200},{16,208},{24,216},{32,224},{40,232},{48,240},{56,2... | collective-permute-start | bytes 196616 | tf_op jit(solution)/shard_map/ppermute | solution.py:351
  61.0 13.3 %collective-permute-start.3 = (bf16[128,256]{1,0:T(8,128)(2,1)S(1)}, bf16[128,256]{1,0:T(8,128)(2,1)S(1)}, u32[]{:S(2)}, u32[]{:S(2)}) collective-permute-start(bf16[128,256]{1,0:T(8,128)(2,1)S(1)} %get-tuple-element.39), channel_id=1, source_target_pairs={{0,128},{8,136},{16,144},{24,152},{32,160},{40,168},{48,176},{56,1... | collective-permute-start | bytes 196616 | tf_op jit(solution)/shard_map/ppermute | solution.py:351
  70.6 5.5 %collective-permute-start.2 = (bf16[128,256]{1,0:T(8,128)(2,1)S(1)}, bf16[128,256]{1,0:T(8,128)(2,1)S(1)}, u32[]{:S(2)}, u32[]{:S(2)}) collective-permute-start(bf16[128,256]{1,0:T(8,128)(2,1)S(1)} %get-tuple-element.39), channel_id=1, source_target_pairs={{0,64},{8,72},{16,80},{24,88},{32,96},{40,104},{48,112},{56,120},{... | collective-permute-start | bytes 196616 | tf_op jit(solution)/shard_map/ppermute | solution.py:351
  74.3 4.7 %collective-permute-start = (s32[1024]{0:T(1024)S(1)}, s32[1024]{0:T(1024)S(1)}, u32[]{:S(2)}, u32[]{:S(2)}) collective-permute-start(s32[1024]{0:T(1024)S(1)} %copy-done.1), channel_id=1, source_target_pairs={{0,8},{8,0},{16,24},{24,16},{32,40},{40,32},{48,56},{56,48},{64,72... | collective-permute-start | bytes 12296 | tf_op jit(solution)/shard_map/ppermute | solution.py:351
  76.1 8.0 %collective-permute-start.11 = (bf16[4,128,256]{2,1,0:T(8,128)(2,1)S(1)}, bf16[4,128,256]{2,1,0:T(8,128)(2,1)S(1)}, u32[]{:S(2)}, u32[]{:S(2)}) collective-permute-start(bf16[4,128,256]{2,1,0:T(8,128)(2,1)S(1)} %pad_maximum_fusion.2.refs_4_), channel_id=1, source_target_pairs={{0,64},{8,72},{16,80},{24,88},{32,96},{40,104},{48,112},{56,120},{... | collective-permute-start | bytes 786440 | tf_op jit(solution)/shard_map/ppermute | solution.py:351
  78.9 9.3 %collective-permute-start.7 = (bf16[4,128,256]{2,1,0:T(8,128)(2,1)S(1)}, bf16[4,128,256]{2,1,0:T(8,128)(2,1)S(1)}, u32[]{:S(2)}, u32[]{:S(2)}) collective-permute-start(bf16[4,128,256]{2,1,0:T(8,128)(2,1)S(1)} %pad_maximum_fusion.1.refs_0_), channel_id=1, source_target_pairs={{0,48},{8,56},{16,0},{24,8},{32,16},{40,24},{48,32},{56,40},{64,11... | collective-permute-start | bytes 786440 | tf_op jit(solution)/shard_map/ppermute | solution.py:351
  80.9 10.4 %collective-permute-start.6 = (bf16[4,128,256]{2,1,0:T(8,128)(2,1)S(1)}, bf16[4,128,256]{2,1,0:T(8,128)(2,1)S(1)}, u32[]{:S(2)}, u32[]{:S(2)}) collective-permute-start(bf16[4,128,256]{2,1,0:T(8,128)(2,1)S(1)} %pad_maximum_fusion.1.refs_0_), channel_id=1, source_target_pairs={{0,32},{8,40},{16,48},{24,56},{32,0},{40,8},{48,16},{56,24},{64,96... | collective-permute-start | bytes 786440 | tf_op jit(solution)/shard_map/ppermute | solution.py:351
  82.4 11.7 %collective-permute-start.5 = (bf16[4,128,256]{2,1,0:T(8,128)(2,1)S(1)}, bf16[4,128,256]{2,1,0:T(8,128)(2,1)S(1)}, u32[]{:S(2)}, u32[]{:S(2)}) collective-permute-start(bf16[4,128,256]{2,1,0:T(8,128)(2,1)S(1)} %pad_maximum_fusion.1.refs_0_), channel_id=1, source_target_pairs={{0,16},{8,24},{16,32},{24,40},{32,48},{40,56},{48,0},{56,8},{64,80... | collective-permute-start | bytes 786440 | tf_op jit(solution)/shard_map/ppermute | solution.py:351
  105.8 22.3 %copy-start.2 = (s32[512]{0:T(512)S(1)}, s32[512]{0:T(512)}, u32[]{:S(2)}) copy-start(s32[512]{0:T(512)} %param.7) | copy-start | bytes 6148
  105.8 3.8 %collective-permute-start.14 = (f32[3,1024]{1,0:T(4,128)S(1)}, f32[3,1024]{1,0:T(4,128)S(1)}, u32[]{:S(2)}, u32[]{:S(2)}) collective-permute-start(f32[3,1024]{1,0:T(4,128)S(1)} %get-tuple-element.41), channel_id=1, source_target_pairs={{0,1},{1,0},{2,3},{3,2},{4,5},{5,4},{6,7},{7,6},{8,9},{9,8},{10,11... | collective-permute-start | bytes 36872 | tf_op jit(solution)/shard_map/ppermute | solution.py:360
  107.8 3.2 %collective-permute-start.16 = (f32[3,1024]{1,0:T(4,128)S(1)}, f32[3,1024]{1,0:T(4,128)S(1)}, u32[]{:S(2)}, u32[]{:S(2)}) collective-permute-start(f32[3,1024]{1,0:T(4,128)S(1)} %get-tuple-element.42), channel_id=1, source_target_pairs={{0,9},{1,8},{2,11},{3,10},{4,13},{5,12},{6,15},{7,14},{8,1},{9,0},... | collective-permute-start | bytes 36872 | tf_op jit(solution)/shard_map/ppermute | solution.py:360
  107.8 3.2 %collective-permute-start.15 = (f32[3,1024]{1,0:T(4,128)S(1)}, f32[3,1024]{1,0:T(4,128)S(1)}, u32[]{:S(2)}, u32[]{:S(2)}) collective-permute-start(f32[3,1024]{1,0:T(4,128)S(1)} %get-tuple-element.42), channel_id=1, source_target_pairs={{0,8},{1,9},{2,10},{3,11},{4,12},{5,13},{6,14},{7,15},{8,0},{9,1},... | collective-permute-start | bytes 36872 | tf_op jit(solution)/shard_map/ppermute | solution.py:360
  111.0 5.3 %collective-permute-start.17 = (f32[3,1024]{1,0:T(4,128)S(1)}, f32[3,1024]{1,0:T(4,128)S(1)}, u32[]{:S(2)}, u32[]{:S(2)}) collective-permute-start(f32[3,1024]{1,0:T(4,128)S(1)} %maximum_maximum_fusion), channel_id=1, source_target_pairs={{0,2},{1,3},{2,0},{3,1},{4,6},{5,7},{6,4},{7,5},{8,10},{9,11},{10,... | collective-permute-start | bytes 36872 | tf_op jit(solution)/shard_map/ppermute | solution.py:360
  116.2 10.6 %collective-permute-start.18 = (f32[3,1024]{1,0:T(4,128)S(1)}, f32[3,1024]{1,0:T(4,128)S(1)}, u32[]{:S(2)}, u32[]{:S(2)}) collective-permute-start(f32[3,1024]{1,0:T(4,128)S(1)} %max.23.a_ref), channel_id=1, source_target_pairs={{0,4},{1,5},{2,6},{3,7},{4,0},{5,1},{6,2},{7,3},{8,12},{9,13},{10,... | collective-permute-start | bytes 36872 | tf_op jit(solution)/shard_map/ppermute | solution.py:360

commit v6 on v5

--- a/solution.py
+++ b/solution.py
@@ -19,13 +19,15 @@
 SEL = GRAD_ROWS + 2 * MED_ROWS
 NONE = -1e30
 CHIPS = 4
+FLOWS = 4
 
 
 def contract_last(a, b):
     return lax.dot_general(a, b, (((1,), (1,)), ((), ())), preferred_element_type=F32)
 
 
-def pick_kernel(where_ref, assign_ref, ids_ref, sk_ref, med_ref, grad_ref, sel, code):
+def pick_kernel(where_ref, assign_ref, ids_ref, *refs):
+    sk_refs, (med_ref, grad_ref, sel, code) = refs[:FLOWS], refs[FLOWS:]
     step = pl.program_id(0)
 
     @pl.when(step == 0)
@@ -96,9 +98,10 @@
     codes = code[...]
     lines = jnp.concatenate([codes[:, :LANES], codes[:, LANES:]], axis=0)
 
-    @pl.loop(0, sk_ref.shape[1] // SEL)
+    @pl.loop(0, sk_refs[0].shape[1] // SEL)
     def _(chip):
-        block = sk_ref[:, pl.ds(pl.multiple_of(chip * SEL, SEL), SEL)]
+        at = pl.ds(pl.multiple_of(chip * SEL, SEL), SEL)
+        block = jnp.concatenate([ref[:, at] for ref in sk_refs], axis=0)
         rows = jnp.dot(sel[...], block, preferred_element_type=F32).astype(BF)
         for c in range(2):
             to = 2 * chip + c
@@ -119,7 +122,10 @@
             in_specs=[
                 pl.BlockSpec((rows // LANES, LANES), lambda i, w: (0, 0)),
                 pl.BlockSpec((1, medoid_ids.shape[0]), lambda i, w: (0, 0)),
-                pl.BlockSpec((rows, wide), lambda i, w: (0, i)),
+            ]
+            + [
+                pl.BlockSpec((rows // FLOWS, wide), lambda i, w, k=k: (k, i))
+                for k in range(FLOWS)
             ],
             out_specs=[
                 pl.BlockSpec((2 * CHIPS, MED_ROWS, 2 * LANES), lambda i, w: (i, 0, 0)),
@@ -136,7 +142,7 @@
             flops=2 * SEL * rows * feats, bytes_accessed=rows * feats * 2, transcendentals=0
         ),
         name="pick",
-    )(where, assignment.reshape(-1, LANES), medoid_ids[None, :], sketches)
+    )(where, assignment.reshape(-1, LANES), medoid_ids[None, :], *[sketches] * FLOWS)
 
 
 def place_kernel(where_ref, got_ref, a_ref, b_ref, flag_ref):
@@ -186,7 +192,8 @@
     )(where, got)
 
 
-def sums_kernel(got_ref, sums_ref, count_ref):
+def sums_kernel(first, steps, got_ref, *refs):
+    prior, (sums_ref, count_ref) = refs[:-2], refs[-2:]
     feats = got_ref.shape[2]
     medoids = sums_ref.shape[1]
     tail = GRAD_ROWS - LANES
@@ -199,7 +206,7 @@
     def body(step, total):
         hots, blocks = [], []
         for k in range(per):
-            q = step * per + k
+            q = (first + step) * per + k
             codes = got_ref[q, GRAD_SLOTS:, :].astype(F32).astype(I32)
             a = codes[1:2] - 1 + codes[2:3] * 256
             b = (codes[9:10] - 1 + codes[10:11] * 256)[:, :tail]
@@ -212,16 +219,19 @@
         )
 
     total = lax.fori_loop(
-        0, got_ref.shape[0] // per, body, jnp.zeros((medoids, feats + LANES), F32)
-    )
-    sums_ref[...] = total[:, :feats].T
-    count_ref[...] = total[:, feats:].T[:1]
-
-
-def sums(got, medoids):
+        0, steps, body, jnp.zeros((medoids, feats + LANES), F32)
+    )
+    sums, counts = total[:, :feats].T, total[:, feats:].T[:1]
+    if prior:
+        sums, counts = prior[0][...] + sums, prior[1][...] + counts
+    sums_ref[...] = sums
+    count_ref[...] = counts
+
+
+def sums(got, medoids, first, steps, prior=()):
     return pl.pallas_call(
-        sums_kernel,
-        in_specs=[pl.BlockSpec(memory_space=pltpu.VMEM)],
+        functools.partial(sums_kernel, first, steps),
+        in_specs=[pl.BlockSpec(memory_space=pltpu.VMEM)] * (1 + len(prior)),
         out_specs=[pl.BlockSpec(memory_space=pltpu.VMEM)] * 2,
         out_shape=[
             jax.ShapeDtypeStruct((got.shape[2], medoids), F32),
@@ -232,10 +242,11 @@
             flops=4 * medoids * got.size, bytes_accessed=2 * got.size, transcendentals=0
         ),
         name="sums",
-    )(got)
-
-
-def score_kernel(scale, where_ref, assign_ref, mark_ref, near_ref, far_ref, *refs):
+    )(got, *prior)
+
+
+def score_kernel(scale, where_ref, assign_ref, mark_ref, *refs):
+    near_refs, far_refs, refs = refs[:FLOWS], refs[FLOWS : 2 * FLOWS], refs[2 * FLOWS :]
     parts, (near_out, far_out) = refs[:8], refs[8:]
     quarter, wide = parts[0].shape[1:]
     half = 2 * quarter
@@ -243,15 +254,15 @@
     step = pl.program_id(0)
     count = pl.num_programs(0) // 2
 
-    def stats(points_ref):
-        total = jnp.zeros((half, points_ref.shape[0]), F32)
+    def stats(point_refs):
+        total = jnp.zeros((half, assign_ref.shape[1]), F32)
         for kx in range(4):
             for ky in range(4):
                 block = ((x + 4 - kx) & 3) * 4 + ((y + 4 - ky) & 3)
                 at = pl.multiple_of(block * wide, wide)
                 total = total + contract_last(
                     jnp.concatenate([parts[ky][kx], parts[4 + kx][ky]], axis=0),
-                    points_ref[:, pl.ds(at, wide)],
+                    jnp.concatenate([ref[:, pl.ds(at, wide)] for ref in point_refs], axis=0),
                 )
         scores = total * scale
         best = jnp.max(scores, axis=0, keepdims=True)
@@ -262,11 +273,11 @@
 
     @pl.when(step < count)
     def _():
-        near_out[...] = stats(near_ref)
+        near_out[...] = stats(near_refs)
 
     @pl.when(step >= count)
     def _():
-        far_out[...] = stats(far_ref)
+        far_out[...] = stats(far_refs)
 
 
 def scored(where, assignments, marks, near, far, parts):
@@ -283,8 +294,11 @@
             in_specs=[
                 pl.BlockSpec((1, tile), lambda i, w: (0, i)),
                 pl.BlockSpec((1, tile), lambda i, w: (0, 0)),
-                pl.BlockSpec((tile, feats), early),
-                pl.BlockSpec((tile, feats), late),
+            ]
+            + [
+                pl.BlockSpec((tile // FLOWS, feats), lambda i, w, f=f, k=k: (FLOWS * f(i, w)[0] + k, 0))
+                for f in (early, late)
+                for k in range(FLOWS)
             ]
             + [pl.BlockSpec(a.shape, lambda i, w: (0, 0, 0)) for a in parts],
             out_specs=[
@@ -298,7 +312,7 @@
             flops=4 * rows * feats * 256, bytes_accessed=rows * feats * 4, transcendentals=0
         ),
         name="scored",
-    )(where, assignments, marks, near, far, *parts)
+    )(where, assignments, marks, *[near] * FLOWS, *[far] * FLOWS, *parts)
 
 
 def closing_kernel(a_ref, b_ref, gap_ref, send_ref, mark_ref):
@@ -368,13 +382,11 @@
     pts_index = lax.axis_index("pts")
     med_index = lax.axis_index("med")
     local_assign = assignment - med_index * medoid_count
-    one_hot = (
-        local_assign[:, None] == jnp.arange(medoid_count, dtype=I32)[None, :]
-    ).astype(BF)
+    chosen = local_assign[:, None] == jnp.arange(medoid_count, dtype=I32)[None, :]
+    one_hot = chosen.astype(BF)
     offsets = medoid_ids - pts_index * row_count
-    inside = (offsets >= 0) & (offsets < row_count)
-    picked = jnp.take(sketches, jnp.clip(offsets, 0, row_count - 1), axis=0)
-    terms = jnp.where(inside[:, None], picked, jnp.zeros_like(picked))
+    picking = offsets[:, None] == jnp.arange(row_count, dtype=I32)[None, :]
+    terms = jnp.dot(picking.astype(BF), sketches, preferred_element_type=F32).astype(BF)
     terms = terms.reshape(medoid_count, pts_count, part).swapaxes(0, 1)
     piece = (
         lax.all_to_all(terms, "pts", 0, 0, tiled=True).astype(F32).sum(axis=0).astype(BF)
@@ -387,11 +399,8 @@
     counts = from_everyone(jnp.sum(one_hot.astype(F32), axis=0), "pts").sum(axis=0)
     scores = contract_last(sketches, everything) * (1.0 / feat_width)
     best = jnp.max(scores, axis=1)
-    here = (local_assign >= 0) & (local_assign < medoid_count)
-    taken = jnp.take_along_axis(
-        scores, jnp.clip(local_assign, 0, medoid_count - 1)[:, None], axis=1
-    )[:, 0]
-    both = from_everyone(jnp.stack([best, jnp.where(here, taken, NONE)]), "med").max(axis=0)
+    taken = jnp.max(jnp.where(chosen, scores, NONE), axis=1)
+    both = from_everyone(jnp.stack([best, taken]), "med").max(axis=0)
     cover = from_everyone(jnp.sum(both[0])[None], "pts").sum()
     return both[0] - both[1], cover / (row_count * pts_count), counts, gradient_sums
 
@@ -430,12 +439,13 @@
     )
     stats = jnp.maximum(stats, across(stats, 0, 2, planes))
     final = across(stats, 0, 4, planes)
-    gradient_sums, counts = sums(grad_got, medoid_count)
+    early = sums(grad_got, medoid_count, 0, 4)
     gap, total, mark = closing(stats, final, pts_count)
     full = mark[0, 0] > 0
 
     def fast():
         totals = lax.all_to_all(total, "pts", 0, 0, tiled=True)
+        gradient_sums, counts = sums(grad_got, medoid_count, 4, 4, early)
         coverage = jnp.sum(totals[:, 0, 0]) / (row_count * pts_count)
         return gap[0], coverage, counts[0], gradient_sums
 

time: 144 us -> 141 us (0.979)
  blocking collectives: 28.6 us -> 17.4 us
  starting transfers between devices: 37.4 us -> 42.6 us
  waiting for transfers between devices: 44 us -> 47.3 us
    all_to_all x1 -> x0, blocking collectives: 11.2 us -> none  [fast(): totals = lax.all_to_all(total, 'pts', 0, 0, tiled=True)]
    all_to_all x0 -> x1, starting transfers between devices: none -> 5.2 us  [fast(): totals = lax.all_to_all(total, 'pts', 0, 0, tiled=True)]
    all_to_all x0 -> x1, waiting for transfers between devices: none -> 3.34 us  [fast(): totals = lax.all_to_all(total, 'pts', 0, 0, tiled=True)]
    pallas_call x1 -> x2, Pallas kernels: 4.81 us -> 5.02 us  [sums(): pl.pallas_call(functools.partial(sums_kernel, first, steps), in_specs=[pl...]
  transfers between devices with their start and end apart: 20 -> 21, of which waited for: 13 -> 14; matrix products, arithmetic and copies ran while one was open for 0% -> 0% of each run, Pallas kernels for 18% -> 19%
where the time goes in v6:
time: 141 us; the launch traced here: 139 us
  waiting for transfers between devices  47.3 us (34%)
  starting transfers between devices  42.6 us (30%)
  Pallas kernels  27.6 us (20%)
  blocking collectives  17.4 us (12%)
  between operations  2.56 us (2%)
    ppermute x14, waiting for transfers between devices, shifted(): return lax.ppermute(array, 'pts', pairs)  39.1 us
    ppermute x14, starting transfers between devices, shifted(): return lax.ppermute(array, 'pts', pairs)  20.6 us
    all_to_all x1, blocking collectives, shards(): med_got = lax.all_to_all(med_send, 'pts', 0, 0, tiled=True)  17.4 us
    pallas_call x1, Pallas kernels, scored(): pl.pallas_call(functools.partial(score_kernel, 1.0 / feats), grid_spec=pl...  11.6 us
    ppermute x5, starting transfers between devices, across(): return lax.ppermute(array, ('pts', 'med'), pairs)  11.3 us
    pallas_call x1, Pallas kernels, pick(): pl.pallas_call(pick_kernel, grid_spec=pltpu.PrefetchScalarGridSpec(num_sc...  9.23 us
    all_to_all x1, starting transfers between devices, shards(): grad_got = lax.all_to_all(grad_send, 'pts', 0, 0, tiled=True)  5.43 us
    all_to_all x1, starting transfers between devices, fast(): totals = lax.all_to_all(total, 'pts', 0, 0, tiled=True)  5.2 us
  transfers between devices with their start and end apart: 21, of which 14 were waited for; matrix products, arithmetic and copies ran while one was open for 0% of the time, Pallas kernels for 19%

profile of v6, /device:TPU:2, one launch (start us, length us, event | category | flops | bytes accessed | tf_op | source)
XLA Modules:
  0.0 138.9 jit_solution(3323762513079157687)
XLA Ops:
  0.6 0.1 collective-permute-start.1
  0.8 0.1 stack.68.where_ref
  0.9 9.2 %pick.1 = (bf16[32,32,256]{2,1,0:T(8,128)(2,1)S(1)}, bf16[32,192,128]{2,1,0:T(8,128)(2,1)}) custom-call(s32[8]{0:T(128)S(1)} %stack.68.where_ref, s32[8,128]{1,0:T(8,128)} %bitcast.59, s32[1,512]{1,0:T(1,128)} %bitcast.61, bf16[1024,4096]{1,0:T(8,128)(2,1)} %refs_3_.3, bf16[1024,4096]{1,0:T(8,128)(2,1)} %refs_3_.3, bf16[1024,4096]{1,0:T(8,128)(2,1)} %refs_3_.3, ...), custom_call_target="tpu_custom_call" | custom-call | flops 2147483648 | bytes 8388608 | tf_op jit(solution)/shard_map/pick/pallas_call | solution.py:117
  10.1 17.4 %all_to_all.41.got_ref = bf16[32,32,256]{2,1,0:T(8,128)(2,1)S(1)} all-to-all(bf16[32,32,256]{2,1,0:T(8,128)(2,1)S(1)} %get-tuple-element.42), channel_id=1, replica_groups=mesh['pts'=32,'med'=8] {'pts'}, dimensions={0} | all-to-all | bytes 1048576 | tf_op jit(solution)/shard_map/all_to_all | solution.py:426
  27.5 5.4 %all-to-all-start.8 = ((bf16[32,192,128]{2,1,0:T(8,128)(2,1)}), bf16[32,192,128]{2,1,0:T(8,128)(2,1)S(1)}, u32[]{:S(2)}, u32[]{:S(2)}) async-start(bf16[32,192,128]{2,1,0:T(8,128)(2,1)} %get-tuple-element.51), calls=%async_computation.8 | async-start | bytes 3145728 | tf_op jit(solution)/shard_map/all_to_all | solution.py:433
  32.9 1.0 place.1
  33.9 2.8 %collective-permute-start.10 = (bf16[128,256]{1,0:T(8,128)(2,1)S(1)}, bf16[128,256]{1,0:T(8,128)(2,1)S(1)}, u32[]{:S(2)}, u32[]{:S(2)}) collective-permute-start(bf16[128,256]{1,0:T(8,128)(2,1)S(1)} %get-tuple-element.45), channel_id=1, source_target_pairs={{0,48},{8,56},{16,0},{24,8},{32,16},{40,24},{48,32},{56,40},{64,11... | collective-permute-start | bytes 196616 | tf_op jit(solution)/shard_map/ppermute | solution.py:365
  36.7 0.9 collective-permute-start.9
  37.5 0.9 collective-permute-start.8
  38.4 15.5 %collective-permute-done.10 = bf16[128,256]{1,0:T(8,128)(2,1)S(1)} collective-permute-done((bf16[128,256]{1,0:T(8,128)(2,1)S(1)}, bf16[128,256]{1,0:T(8,128)(2,1)S(1)}, u32[]{:S(2)}, u32[]{:S(2)}) %collective-permute-start.10) | collective-permute-done | bytes 65568 | tf_op jit(solution)/shard_map/ppermute | solution.py:365
  53.9 1.9 %collective-permute-done.9 = bf16[128,256]{1,0:T(8,128)(2,1)S(1)} collective-permute-done((bf16[128,256]{1,0:T(8,128)(2,1)S(1)}, bf16[128,256]{1,0:T(8,128)(2,1)S(1)}, u32[]{:S(2)}, u32[]{:S(2)}) %collective-permute-start.9) | collective-permute-done | bytes 65568 | tf_op jit(solution)/shard_map/ppermute | solution.py:365
  55.8 0.5 collective-permute-done.8
  56.4 0.6 collective-permute-start.13
  57.0 2.4 %collective-permute-start.12 = (bf16[4,128,256]{2,1,0:T(8,128)(2,1)S(1)}, bf16[4,128,256]{2,1,0:T(8,128)(2,1)S(1)}, u32[]{:S(2)}, u32[]{:S(2)}) collective-permute-start(bf16[4,128,256]{2,1,0:T(8,128)(2,1)S(1)} %pad_maximum_fusion.2.refs_12_), channel_id=1, source_target_pairs={{0,128},{8,136},{16,144},{24,152},{32,160},{40,168},{48,176},{56,1... | collective-permute-start | bytes 786440 | tf_op jit(solution)/shard_map/ppermute | solution.py:365
  59.4 1.1 collective-permute-start.4
  60.5 2.2 %collective-permute-start.3 = (bf16[128,256]{1,0:T(8,128)(2,1)S(1)}, bf16[128,256]{1,0:T(8,128)(2,1)S(1)}, u32[]{:S(2)}, u32[]{:S(2)}) collective-permute-start(bf16[128,256]{1,0:T(8,128)(2,1)S(1)} %get-tuple-element.44), channel_id=1, source_target_pairs={{0,128},{8,136},{16,144},{24,152},{32,160},{40,168},{48,176},{56,1... | collective-permute-start | bytes 196616 | tf_op jit(solution)/shard_map/ppermute | solution.py:365
  62.7 7.5 %collective-permute-done.4 = bf16[128,256]{1,0:T(8,128)(2,1)S(1)} collective-permute-done((bf16[128,256]{1,0:T(8,128)(2,1)S(1)}, bf16[128,256]{1,0:T(8,128)(2,1)S(1)}, u32[]{:S(2)}, u32[]{:S(2)}) %collective-permute-start.4) | collective-permute-done | bytes 65568 | tf_op jit(solution)/shard_map/ppermute | solution.py:365
  70.2 3.5 %collective-permute-start.2 = (bf16[128,256]{1,0:T(8,128)(2,1)S(1)}, bf16[128,256]{1,0:T(8,128)(2,1)S(1)}, u32[]{:S(2)}, u32[]{:S(2)}) collective-permute-start(bf16[128,256]{1,0:T(8,128)(2,1)S(1)} %get-tuple-element.44), channel_id=1, source_target_pairs={{0,64},{8,72},{16,80},{24,88},{32,96},{40,104},{48,112},{56,120},{... | collective-permute-start | bytes 196616 | tf_op jit(solution)/shard_map/ppermute | solution.py:365
  73.7 0.1 collective-permute-done.3
  73.8 1.9 %collective-permute-done.2 = bf16[128,256]{1,0:T(8,128)(2,1)S(1)} collective-permute-done((bf16[128,256]{1,0:T(8,128)(2,1)S(1)}, bf16[128,256]{1,0:T(8,128)(2,1)S(1)}, u32[]{:S(2)}, u32[]{:S(2)}) %collective-permute-start.2) | collective-permute-done | bytes 65568 | tf_op jit(solution)/shard_map/ppermute | solution.py:365
  75.7 2.8 %collective-permute-start.11 = (bf16[4,128,256]{2,1,0:T(8,128)(2,1)S(1)}, bf16[4,128,256]{2,1,0:T(8,128)(2,1)S(1)}, u32[]{:S(2)}, u32[]{:S(2)}) collective-permute-start(bf16[4,128,256]{2,1,0:T(8,128)(2,1)S(1)} %pad_maximum_fusion.2.refs_12_), channel_id=1, source_target_pairs={{0,64},{8,72},{16,80},{24,88},{32,96},{40,104},{48,112},{56,120},{... | collective-permute-start | bytes 786440 | tf_op jit(solution)/shard_map/ppermute | solution.py:365
  78.5 0.0 collective-permute-done
  78.5 1.9 %collective-permute-start.7 = (bf16[4,128,256]{2,1,0:T(8,128)(2,1)S(1)}, bf16[4,128,256]{2,1,0:T(8,128)(2,1)S(1)}, u32[]{:S(2)}, u32[]{:S(2)}) collective-permute-start(bf16[4,128,256]{2,1,0:T(8,128)(2,1)S(1)} %pad_maximum_fusion.1.refs_8_), channel_id=1, source_target_pairs={{0,48},{8,56},{16,0},{24,8},{32,16},{40,24},{48,32},{56,40},{64,11... | collective-permute-start | bytes 786440 | tf_op jit(solution)/shard_map/ppermute | solution.py:365
  80.5 0.0 collective-permute-done.13.refs_15_
  80.5 1.5 %collective-permute-start.6 = (bf16[4,128,256]{2,1,0:T(8,128)(2,1)S(1)}, bf16[4,128,256]{2,1,0:T(8,128)(2,1)S(1)}, u32[]{:S(2)}, u32[]{:S(2)}) collective-permute-start(bf16[4,128,256]{2,1,0:T(8,128)(2,1)S(1)} %pad_maximum_fusion.1.refs_8_), channel_id=1, source_target_pairs={{0,32},{8,40},{16,48},{24,56},{32,0},{40,8},{48,16},{56,24},{64,96... | collective-permute-start | bytes 786440 | tf_op jit(solution)/shard_map/ppermute | solution.py:365
  82.0 0.0 collective-permute-start.5
  82.0 1.8 %collective-permute-done.11.refs_13_ = bf16[4,128,256]{2,1,0:T(8,128)(2,1)S(1)} collective-permute-done((bf16[4,128,256]{2,1,0:T(8,128)(2,1)S(1)}, bf16[4,128,256]{2,1,0:T(8,128)(2,1)S(1)}, u32[]{:S(2)}, u32[]{:S(2)}) %collective-permute-start.11) | collective-permute-done | bytes 262176 | tf_op jit(solution)/shard_map/ppermute | solution.py:365
  83.8 4.0 %collective-permute-done.7.refs_11_ = bf16[4,128,256]{2,1,0:T(8,128)(2,1)S(1)} collective-permute-done((bf16[4,128,256]{2,1,0:T(8,128)(2,1)S(1)}, bf16[4,128,256]{2,1,0:T(8,128)(2,1)S(1)}, u32[]{:S(2)}, u32[]{:S(2)}) %collective-permute-start.7) | collective-permute-done | bytes 262176 | tf_op jit(solution)/shard_map/ppermute | solution.py:365
  87.8 3.1 %collective-permute-done.6.refs_10_ = bf16[4,128,256]{2,1,0:T(8,128)(2,1)S(1)} collective-permute-done((bf16[4,128,256]{2,1,0:T(8,128)(2,1)S(1)}, bf16[4,128,256]{2,1,0:T(8,128)(2,1)S(1)}, u32[]{:S(2)}, u32[]{:S(2)}) %collective-permute-start.6) | collective-permute-done | bytes 262176 | tf_op jit(solution)/shard_map/ppermute | solution.py:365
  90.9 2.8 %collective-permute-done.5.refs_9_ = bf16[4,128,256]{2,1,0:T(8,128)(2,1)S(1)} collective-permute-done((bf16[4,128,256]{2,1,0:T(8,128)(2,1)S(1)}, bf16[4,128,256]{2,1,0:T(8,128)(2,1)S(1)}, u32[]{:S(2)}, u32[]{:S(2)}) %collective-permute-start.5) | collective-permute-done | bytes 262176 | tf_op jit(solution)/shard_map/ppermute | solution.py:365
  93.6 11.6 %scored.1 = (f32[3,1024]{1,0:T(4,128)S(1)}, f32[3,1024]{1,0:T(4,128)S(1)}) custom-call(s32[8]{0:T(128)S(1)} %stack.68.where_ref, s32[1,2048]{1,0:T(1,128)S(1)} %bitcast.50, f32[1,256]{1,0:T(1,128)S(1)} %get-tuple-element.43.mark_ref, bf16[1024,4096]{1,0:T(8,128)(2,1)} %refs_3_.3, bf16[1024,4096]{1,0:T(8,128)(2,1)} %refs_3_.3, bf16[1024,4096]{1,0:T(8,128)(2,1)} %refs_3_.3, ...), custom_call_target="tpu_custom_call" | custom-call | flops 4294967296 | bytes 16777216 | tf_op jit(solution)/shard_map/scored/pallas_call | solution.py:289
  105.3 0.0 copy-start.1
  105.3 2.0 %collective-permute-start.14 = (f32[3,1024]{1,0:T(4,128)S(1)}, f32[3,1024]{1,0:T(4,128)S(1)}, u32[]{:S(2)}, u32[]{:S(2)}) collective-permute-start(f32[3,1024]{1,0:T(4,128)S(1)} %get-tuple-element.46), channel_id=1, source_target_pairs={{0,1},{1,0},{2,3},{3,2},{4,5},{5,4},{6,7},{7,6},{8,9},{9,8},{10,11... | collective-permute-start | bytes 36872 | tf_op jit(solution)/shard_map/ppermute | solution.py:374
  107.3 0.2 collective-permute-start.15
  107.5 1.6 %collective-permute-done.14 = f32[3,1024]{1,0:T(4,128)S(1)} collective-permute-done((f32[3,1024]{1,0:T(4,128)S(1)}, f32[3,1024]{1,0:T(4,128)S(1)}, u32[]{:S(2)}, u32[]{:S(2)}) %collective-permute-start.14) | collective-permute-done | bytes 12320 | tf_op jit(solution)/shard_map/ppermute | solution.py:374
  109.1 1.3 collective-permute-done.16
  110.5 0.0 collective-permute-done.15
  110.5 3.4 %collective-permute-start.17 = (f32[3,1024]{1,0:T(4,128)S(1)}, f32[3,1024]{1,0:T(4,128)S(1)}, u32[]{:S(2)}, u32[]{:S(2)}) collective-permute-start(f32[3,1024]{1,0:T(4,128)S(1)} %maximum_maximum_fusion), channel_id=1, source_target_pairs={{0,2},{1,3},{2,0},{3,1},{4,6},{5,7},{6,4},{7,5},{8,10},{9,11},{10,... | collective-permute-start | bytes 36872 | tf_op jit(solution)/shard_map/ppermute | solution.py:374
  113.8 1.9 %collective-permute-done.17 = f32[3,1024]{1,0:T(4,128)S(1)} collective-permute-done((f32[3,1024]{1,0:T(4,128)S(1)}, f32[3,1024]{1,0:T(4,128)S(1)}, u32[]{:S(2)}, u32[]{:S(2)}) %collective-permute-start.17) | collective-permute-done | bytes 12320 | tf_op jit(solution)/shard_map/ppermute | solution.py:374
  115.7 5.8 %collective-permute-start.18 = (f32[3,1024]{1,0:T(4,128)S(1)}, f32[3,1024]{1,0:T(4,128)S(1)}, u32[]{:S(2)}, u32[]{:S(2)}) collective-permute-start(f32[3,1024]{1,0:T(4,128)S(1)} %max.15.a_ref), channel_id=1, source_target_pairs={{0,4},{1,5},{2,6},{3,7},{4,0},{5,1},{6,2},{7,3},{8,12},{9,13},{10,... | collective-permute-start | bytes 36872 | tf_op jit(solution)/shard_map/ppermute | solution.py:374
  121.5 2.2 %sums.3 = (f32[128,512]{1,0:T(8,128)S(1)}, f32[1,512]{1,0:T(1,128)S(1)}) custom-call(bf16[32,192,128]{2,1,0:T(8,128)(2,1)S(1)} %all-to-all-done.8.got_ref), custom_call_target="tpu_custom_call" | custom-call | flops 1610612736 | bytes 1572864 | tf_op jit(solution)/shard_map/sums/pallas_call | solution.py:232
  123.7 0.0 collective-permute-done.18.b_ref
  123.7 0.7 closing.1
  125.0 12.7 %conditional.1 = (f32[1024]{0:T(1024)}, f32[]{:T(128)}, f32[512]{0:T(512)}, f32[128,512]{1,0:T(8,128)}) conditional(s32[]{:T(128)} %bitcast.27, (f32[1,1024]{1,0:T(1,128)}, f32[32,1,128]{2,1,0:T(1,128)}, bf16[32,192,128]{2,1,0:T(8,128)(2,1)S(1)}, f32[128,512]{1,0:T(8,128)S(1)}, f32[1,512]{1,0:T(1,128)S(1)}) %tuple.37, (s32[512]{0:T(512)S(1)}, ...), branch_computations={%region_0.2_spmd, %region_2.12_spmd} | conditional | flops 12896862208 | bytes 136299184 | solution.py:452
  125.1 5.2 %all-to-all-start = ((f32[32,1,128]{2,1,0:T(1,128)}), f32[32,1,128]{2,1,0:T(1,128)S(1)}, u32[]{:S(2)}, u32[]{:S(2)}) async-start(f32[32,1,128]{2,1,0:T(1,128)} %get-tuple-element.17), calls=%async_computation | async-start | bytes 32768 | tf_op jit(solution)/shard_map/cond/branch_0_fun/all_to_all | solution.py:447
  130.3 2.9 %sums.2 = (f32[128,512]{1,0:T(8,128)}, f32[1,512]{1,0:T(1,128)}) custom-call(bf16[32,192,128]{2,1,0:T(8,128)(2,1)S(1)} %get-tuple-element.18.got_ref, f32[128,512]{1,0:T(8,128)S(1)} %get-tuple-element.19.refs_0_, f32[1,512]{1,0:T(1,128)S(1)} %get-tuple-element.20.refs_1_), custom_call_target="tpu_custom_call" | custom-call | flops 1610612736 | bytes 1572864 | tf_op jit(solution)/shard_map/cond/branch_0_fun/sums/pallas_call | solution.py:232
  133.1 3.3 %all-to-all-done = f32[32,1,128]{2,1,0:T(1,128)S(1)} async-done(((f32[32,1,128]{2,1,0:T(1,128)}), f32[32,1,128]{2,1,0:T(1,128)S(1)}, u32[]{:S(2)}, u32[]{:S(2)}) %all-to-all-start) | async-done | bytes 16416 | tf_op jit(solution)/shard_map/cond/branch_0_fun/all_to_all | solution.py:447
  136.4 0.6 slice_reduce_fusion
  (13 shorter events, 0.1 us)
Async XLA Ops:
  0.6 93.0 %collective-permute-start.1 = (bf16[1024,4096]{1,0:T(8,128)(2,1)}, bf16[1024,4096]{1,0:T(8,128)(2,1)}, u32[]{:S(2)}, u32[]{:S(2)}) collective-permute-start(bf16[1024,4096]{1,0:T(8,128)(2,1)} %refs_3_.3), channel_id=1, source_target_pairs={{0,8},{8,0},{16,24},{24,16},{32,40},{40,32},{48,56},{56,48},{64,72... | collective-permute-start | bytes 25165832 | tf_op jit(solution)/shard_map/ppermute | solution.py:365
  10.1 63.7 %copy-start = (s32[1024]{0:T(1024)S(1)}, s32[1024]{0:T(1024)}, u32[]{:S(2)}) copy-start(s32[1024]{0:T(1024)} %param.6) | copy-start | bytes 12292
  27.5 94.0 %all-to-all-start.8 = ((bf16[32,192,128]{2,1,0:T(8,128)(2,1)}), bf16[32,192,128]{2,1,0:T(8,128)(2,1)S(1)}, u32[]{:S(2)}, u32[]{:S(2)}) async-start(bf16[32,192,128]{2,1,0:T(8,128)(2,1)} %get-tuple-element.51), calls=%async_computation.8 | async-start | bytes 3145728 | tf_op jit(solution)/shard_map/all_to_all | solution.py:433
  33.9 20.0 %collective-permute-start.10 = (bf16[128,256]{1,0:T(8,128)(2,1)S(1)}, bf16[128,256]{1,0:T(8,128)(2,1)S(1)}, u32[]{:S(2)}, u32[]{:S(2)}) collective-permute-start(bf16[128,256]{1,0:T(8,128)(2,1)S(1)} %get-tuple-element.45), channel_id=1, source_target_pairs={{0,48},{8,56},{16,0},{24,8},{32,16},{40,24},{48,32},{56,40},{64,11... | collective-permute-start | bytes 196616 | tf_op jit(solution)/shard_map/ppermute | solution.py:365
  36.7 19.1 %collective-permute-start.9 = (bf16[128,256]{1,0:T(8,128)(2,1)S(1)}, bf16[128,256]{1,0:T(8,128)(2,1)S(1)}, u32[]{:S(2)}, u32[]{:S(2)}) collective-permute-start(bf16[128,256]{1,0:T(8,128)(2,1)S(1)} %get-tuple-element.45), channel_id=1, source_target_pairs={{0,32},{8,40},{16,48},{24,56},{32,0},{40,8},{48,16},{56,24},{64,96... | collective-permute-start | bytes 196616 | tf_op jit(solution)/shard_map/ppermute | solution.py:365
  37.5 18.8 %collective-permute-start.8 = (bf16[128,256]{1,0:T(8,128)(2,1)S(1)}, bf16[128,256]{1,0:T(8,128)(2,1)S(1)}, u32[]{:S(2)}, u32[]{:S(2)}) collective-permute-start(bf16[128,256]{1,0:T(8,128)(2,1)S(1)} %get-tuple-element.45), channel_id=1, source_target_pairs={{0,16},{8,24},{16,32},{24,40},{32,48},{40,56},{48,0},{56,8},{64,80... | collective-permute-start | bytes 196616 | tf_op jit(solution)/shard_map/ppermute | solution.py:365
  56.4 24.1 %collective-permute-start.13 = (bf16[4,128,256]{2,1,0:T(8,128)(2,1)S(1)}, bf16[4,128,256]{2,1,0:T(8,128)(2,1)S(1)}, u32[]{:S(2)}, u32[]{:S(2)}) collective-permute-start(bf16[4,128,256]{2,1,0:T(8,128)(2,1)S(1)} %pad_maximum_fusion.2.refs_12_), channel_id=1, source_target_pairs={{0,192},{8,200},{16,208},{24,216},{32,224},{40,232},{48,240},{56,2... | collective-permute-start | bytes 786440 | tf_op jit(solution)/shard_map/ppermute | solution.py:365
  57.0 25.0 %collective-permute-start.12 = (bf16[4,128,256]{2,1,0:T(8,128)(2,1)S(1)}, bf16[4,128,256]{2,1,0:T(8,128)(2,1)S(1)}, u32[]{:S(2)}, u32[]{:S(2)}) collective-permute-start(bf16[4,128,256]{2,1,0:T(8,128)(2,1)S(1)} %pad_maximum_fusion.2.refs_12_), channel_id=1, source_target_pairs={{0,128},{8,136},{16,144},{24,152},{32,160},{40,168},{48,176},{56,1... | collective-permute-start | bytes 786440 | tf_op jit(solution)/shard_map/ppermute | solution.py:365
  59.4 10.8 %collective-permute-start.4 = (bf16[128,256]{1,0:T(8,128)(2,1)S(1)}, bf16[128,256]{1,0:T(8,128)(2,1)S(1)}, u32[]{:S(2)}, u32[]{:S(2)}) collective-permute-start(bf16[128,256]{1,0:T(8,128)(2,1)S(1)} %get-tuple-element.44), channel_id=1, source_target_pairs={{0,192},{8,200},{16,208},{24,216},{32,224},{40,232},{48,240},{56,2... | collective-permute-start | bytes 196616 | tf_op jit(solution)/shard_map/ppermute | solution.py:365
  60.5 13.3 %collective-permute-start.3 = (bf16[128,256]{1,0:T(8,128)(2,1)S(1)}, bf16[128,256]{1,0:T(8,128)(2,1)S(1)}, u32[]{:S(2)}, u32[]{:S(2)}) collective-permute-start(bf16[128,256]{1,0:T(8,128)(2,1)S(1)} %get-tuple-element.44), channel_id=1, source_target_pairs={{0,128},{8,136},{16,144},{24,152},{32,160},{40,168},{48,176},{56,1... | collective-permute-start | bytes 196616 | tf_op jit(solution)/shard_map/ppermute | solution.py:365
  70.2 5.5 %collective-permute-start.2 = (bf16[128,256]{1,0:T(8,128)(2,1)S(1)}, bf16[128,256]{1,0:T(8,128)(2,1)S(1)}, u32[]{:S(2)}, u32[]{:S(2)}) collective-permute-start(bf16[128,256]{1,0:T(8,128)(2,1)S(1)} %get-tuple-element.44), channel_id=1, source_target_pairs={{0,64},{8,72},{16,80},{24,88},{32,96},{40,104},{48,112},{56,120},{... | collective-permute-start | bytes 196616 | tf_op jit(solution)/shard_map/ppermute | solution.py:365
  73.8 4.7 %collective-permute-start = (s32[1024]{0:T(1024)S(1)}, s32[1024]{0:T(1024)S(1)}, u32[]{:S(2)}, u32[]{:S(2)}) collective-permute-start(s32[1024]{0:T(1024)S(1)} %copy-done), channel_id=1, source_target_pairs={{0,8},{8,0},{16,24},{24,16},{32,40},{40,32},{48,56},{56,48},{64,72... | collective-permute-start | bytes 12296 | tf_op jit(solution)/shard_map/ppermute | solution.py:365
  75.7 8.0 %collective-permute-start.11 = (bf16[4,128,256]{2,1,0:T(8,128)(2,1)S(1)}, bf16[4,128,256]{2,1,0:T(8,128)(2,1)S(1)}, u32[]{:S(2)}, u32[]{:S(2)}) collective-permute-start(bf16[4,128,256]{2,1,0:T(8,128)(2,1)S(1)} %pad_maximum_fusion.2.refs_12_), channel_id=1, source_target_pairs={{0,64},{8,72},{16,80},{24,88},{32,96},{40,104},{48,112},{56,120},{... | collective-permute-start | bytes 786440 | tf_op jit(solution)/shard_map/ppermute | solution.py:365
  78.5 9.3 %collective-permute-start.7 = (bf16[4,128,256]{2,1,0:T(8,128)(2,1)S(1)}, bf16[4,128,256]{2,1,0:T(8,128)(2,1)S(1)}, u32[]{:S(2)}, u32[]{:S(2)}) collective-permute-start(bf16[4,128,256]{2,1,0:T(8,128)(2,1)S(1)} %pad_maximum_fusion.1.refs_8_), channel_id=1, source_target_pairs={{0,48},{8,56},{16,0},{24,8},{32,16},{40,24},{48,32},{56,40},{64,11... | collective-permute-start | bytes 786440 | tf_op jit(solution)/shard_map/ppermute | solution.py:365
  80.5 10.4 %collective-permute-start.6 = (bf16[4,128,256]{2,1,0:T(8,128)(2,1)S(1)}, bf16[4,128,256]{2,1,0:T(8,128)(2,1)S(1)}, u32[]{:S(2)}, u32[]{:S(2)}) collective-permute-start(bf16[4,128,256]{2,1,0:T(8,128)(2,1)S(1)} %pad_maximum_fusion.1.refs_8_), channel_id=1, source_target_pairs={{0,32},{8,40},{16,48},{24,56},{32,0},{40,8},{48,16},{56,24},{64,96... | collective-permute-start | bytes 786440 | tf_op jit(solution)/shard_map/ppermute | solution.py:365
  82.0 11.7 %collective-permute-start.5 = (bf16[4,128,256]{2,1,0:T(8,128)(2,1)S(1)}, bf16[4,128,256]{2,1,0:T(8,128)(2,1)S(1)}, u32[]{:S(2)}, u32[]{:S(2)}) collective-permute-start(bf16[4,128,256]{2,1,0:T(8,128)(2,1)S(1)} %pad_maximum_fusion.1.refs_8_), channel_id=1, source_target_pairs={{0,16},{8,24},{16,32},{24,40},{32,48},{40,56},{48,0},{56,8},{64,80... | collective-permute-start | bytes 786440 | tf_op jit(solution)/shard_map/ppermute | solution.py:365
  105.3 19.8 %copy-start.1 = (s32[512]{0:T(512)S(1)}, s32[512]{0:T(512)}, u32[]{:S(2)}) copy-start(s32[512]{0:T(512)} %param.7) | copy-start | bytes 6148
  105.3 3.8 %collective-permute-start.14 = (f32[3,1024]{1,0:T(4,128)S(1)}, f32[3,1024]{1,0:T(4,128)S(1)}, u32[]{:S(2)}, u32[]{:S(2)}) collective-permute-start(f32[3,1024]{1,0:T(4,128)S(1)} %get-tuple-element.46), channel_id=1, source_target_pairs={{0,1},{1,0},{2,3},{3,2},{4,5},{5,4},{6,7},{7,6},{8,9},{9,8},{10,11... | collective-permute-start | bytes 36872 | tf_op jit(solution)/shard_map/ppermute | solution.py:374
  107.3 3.2 %collective-permute-start.16 = (f32[3,1024]{1,0:T(4,128)S(1)}, f32[3,1024]{1,0:T(4,128)S(1)}, u32[]{:S(2)}, u32[]{:S(2)}) collective-permute-start(f32[3,1024]{1,0:T(4,128)S(1)} %get-tuple-element.47), channel_id=1, source_target_pairs={{0,9},{1,8},{2,11},{3,10},{4,13},{5,12},{6,15},{7,14},{8,1},{9,0},... | collective-permute-start | bytes 36872 | tf_op jit(solution)/shard_map/ppermute | solution.py:374
  107.3 3.2 %collective-permute-start.15 = (f32[3,1024]{1,0:T(4,128)S(1)}, f32[3,1024]{1,0:T(4,128)S(1)}, u32[]{:S(2)}, u32[]{:S(2)}) collective-permute-start(f32[3,1024]{1,0:T(4,128)S(1)} %get-tuple-element.47), channel_id=1, source_target_pairs={{0,8},{1,9},{2,10},{3,11},{4,12},{5,13},{6,14},{7,15},{8,0},{9,1},... | collective-permute-start | bytes 36872 | tf_op jit(solution)/shard_map/ppermute | solution.py:374
  110.5 5.3 %collective-permute-start.17 = (f32[3,1024]{1,0:T(4,128)S(1)}, f32[3,1024]{1,0:T(4,128)S(1)}, u32[]{:S(2)}, u32[]{:S(2)}) collective-permute-start(f32[3,1024]{1,0:T(4,128)S(1)} %maximum_maximum_fusion), channel_id=1, source_target_pairs={{0,2},{1,3},{2,0},{3,1},{4,6},{5,7},{6,4},{7,5},{8,10},{9,11},{10,... | collective-permute-start | bytes 36872 | tf_op jit(solution)/shard_map/ppermute | solution.py:374
  115.7 7.9 %collective-permute-start.18 = (f32[3,1024]{1,0:T(4,128)S(1)}, f32[3,1024]{1,0:T(4,128)S(1)}, u32[]{:S(2)}, u32[]{:S(2)}) collective-permute-start(f32[3,1024]{1,0:T(4,128)S(1)} %max.15.a_ref), channel_id=1, source_target_pairs={{0,4},{1,5},{2,6},{3,7},{4,0},{5,1},{6,2},{7,3},{8,12},{9,13},{10,... | collective-permute-start | bytes 36872 | tf_op jit(solution)/shard_map/ppermute | solution.py:374
  125.1 11.4 %all-to-all-start = ((f32[32,1,128]{2,1,0:T(1,128)}), f32[32,1,128]{2,1,0:T(1,128)S(1)}, u32[]{:S(2)}, u32[]{:S(2)}) async-start(f32[32,1,128]{2,1,0:T(1,128)} %get-tuple-element.17), calls=%async_computation | async-start | bytes 32768 | tf_op jit(solution)/shard_map/cond/branch_0_fun/all_to_all | solution.py:447

commit v7 on v6

--- a/solution.py
+++ b/solution.py
@@ -18,20 +18,25 @@
 MED_SLOTS = 24
 SEL = GRAD_ROWS + 2 * MED_ROWS
 NONE = -1e30
+MED = ("zq", "zr")
 CHIPS = 4
-FLOWS = 4
 
 
 def contract_last(a, b):
     return lax.dot_general(a, b, (((1,), (1,)), ((), ())), preferred_element_type=F32)
 
 
-def pick_kernel(where_ref, assign_ref, ids_ref, *refs):
-    sk_refs, (med_ref, grad_ref, sel, code) = refs[:FLOWS], refs[FLOWS:]
-    step = pl.program_id(0)
-
-    @pl.when(step == 0)
-    def _():
+def pick_kernel(where_ref, assign_ref, ids_ref, sk_ref, med_ref, grad_ref, sel, code, held, arrived):
+    flows, _, wide = held.shape
+
+    def fetch(k):
+        at = pl.ds(pl.multiple_of(k * wide, wide), wide)
+        return pltpu.make_async_copy(sk_ref.at[:, at], held.at[k], arrived.at[k])
+
+    for k in range(flows):
+        fetch(k).start()
+
+    def tables():
         base = where_ref[0]
         plane = where_ref[1]
         groups = assign_ref.shape[0]
@@ -95,44 +100,44 @@
         third = lax.broadcasted_iota(I32, (8, SEL), 0) == 3
         code[...] = jnp.where(third, marks, codes).astype(BF)
 
+    tables()
     codes = code[...]
     lines = jnp.concatenate([codes[:, :LANES], codes[:, LANES:]], axis=0)
 
-    @pl.loop(0, sk_refs[0].shape[1] // SEL)
-    def _(chip):
-        at = pl.ds(pl.multiple_of(chip * SEL, SEL), SEL)
-        block = jnp.concatenate([ref[:, at] for ref in sk_refs], axis=0)
-        rows = jnp.dot(sel[...], block, preferred_element_type=F32).astype(BF)
-        for c in range(2):
-            to = 2 * chip + c
-            grad_ref[to, :GRAD_SLOTS, :] = rows[:GRAD_SLOTS, c * LANES : (c + 1) * LANES]
-            grad_ref[to, GRAD_SLOTS:, :] = lines
-            at = GRAD_ROWS + c * MED_ROWS
-            med_ref[to, :, :] = jnp.concatenate([rows[at : at + MED_SLOTS], codes], axis=0)
+    @pl.loop(0, flows)
+    def _(k):
+        fetch(k).wait()
+        for chip in range(wide // SEL):
+            block = held[k, :, chip * SEL : (chip + 1) * SEL]
+            rows = jnp.dot(sel[...], block, preferred_element_type=F32).astype(BF)
+            for c in range(2):
+                to = k * 2 * (wide // SEL) + 2 * chip + c
+                grad_ref[to, :GRAD_SLOTS, :] = rows[:GRAD_SLOTS, c * LANES : (c + 1) * LANES]
+                grad_ref[to, GRAD_SLOTS:, :] = lines
+                at = GRAD_ROWS + c * MED_ROWS
+                med_ref[to, :, :] = jnp.concatenate([rows[at : at + MED_SLOTS], codes], axis=0)
 
 
 def pick(where, assignment, medoid_ids, sketches, pts_count):
     rows, feats = sketches.shape
     wide = CHIPS * 2 * LANES
+    flows = feats // wide
+    near = pl.BlockSpec(memory_space=pltpu.VMEM)
     return pl.pallas_call(
         pick_kernel,
-        grid_spec=pltpu.PrefetchScalarGridSpec(
-            num_scalar_prefetch=1,
-            grid=(feats // wide,),
-            in_specs=[
-                pl.BlockSpec((rows // LANES, LANES), lambda i, w: (0, 0)),
-                pl.BlockSpec((1, medoid_ids.shape[0]), lambda i, w: (0, 0)),
-            ]
-            + [
-                pl.BlockSpec((rows // FLOWS, wide), lambda i, w, k=k: (k, i))
-                for k in range(FLOWS)
-            ],
-            out_specs=[
-                pl.BlockSpec((2 * CHIPS, MED_ROWS, 2 * LANES), lambda i, w: (i, 0, 0)),
-                pl.BlockSpec((2 * CHIPS, GRAD_ROWS, LANES), lambda i, w: (i, 0, 0)),
-            ],
-            scratch_shapes=[pltpu.VMEM((SEL, rows), BF), pltpu.VMEM((8, SEL), BF)],
-        ),
+        in_specs=[
+            pl.BlockSpec(memory_space=pltpu.SMEM),
+            near,
+            near,
+            pl.BlockSpec(memory_space=pl.ANY),
+        ],
+        out_specs=[near, near],
+        scratch_shapes=[
+            pltpu.VMEM((SEL, rows), BF),
+            pltpu.VMEM((8, SEL), BF),
+            pltpu.VMEM((flows, rows, wide), BF),
+            pltpu.SemaphoreType.DMA((flows,)),
+        ],
         out_shape=[
             jax.ShapeDtypeStruct((pts_count, MED_ROWS, 2 * LANES), BF),
             jax.ShapeDtypeStruct((pts_count, GRAD_ROWS, LANES), BF),
@@ -142,7 +147,7 @@
             flops=2 * SEL * rows * feats, bytes_accessed=rows * feats * 2, transcendentals=0
         ),
         name="pick",
-    )(where, assignment.reshape(-1, LANES), medoid_ids[None, :], *[sketches] * FLOWS)
+    )(where, assignment.reshape(-1, LANES), medoid_ids[None, :], sketches)
 
 
 def place_kernel(where_ref, got_ref, a_ref, b_ref, flag_ref):
@@ -245,97 +250,86 @@
     )(got, *prior)
 
 
-def score_kernel(scale, where_ref, assign_ref, mark_ref, *refs):
-    near_refs, far_refs, refs = refs[:FLOWS], refs[FLOWS : 2 * FLOWS], refs[2 * FLOWS :]
-    parts, (near_out, far_out) = refs[:8], refs[8:]
+def score_kernel(scale, where_ref, assign_ref, mark_ref, near_ref, far_ref, *refs):
+    parts, (near_out, far_out, held, arrived) = refs[:8], refs[8:]
     quarter, wide = parts[0].shape[1:]
     half = 2 * quarter
     x, y, base = where_ref[3], where_ref[4], where_ref[5]
-    step = pl.program_id(0)
-    count = pl.num_programs(0) // 2
-
-    def stats(point_refs):
-        total = jnp.zeros((half, assign_ref.shape[1]), F32)
-        for kx in range(4):
-            for ky in range(4):
-                block = ((x + 4 - kx) & 3) * 4 + ((y + 4 - ky) & 3)
-                at = pl.multiple_of(block * wide, wide)
-                total = total + contract_last(
-                    jnp.concatenate([parts[ky][kx], parts[4 + kx][ky]], axis=0),
-                    jnp.concatenate([ref[:, pl.ds(at, wide)] for ref in point_refs], axis=0),
-                )
-        scores = total * scale
-        best = jnp.max(scores, axis=0, keepdims=True)
-        row = lax.broadcasted_iota(I32, scores.shape, 0)
-        local = assign_ref[...] - base
-        chosen = jnp.max(jnp.where(local == row, scores, NONE), axis=0, keepdims=True)
-        return jnp.concatenate([best, chosen, mark_ref[...]], axis=0)
-
-    @pl.when(step < count)
-    def _():
-        near_out[...] = stats(near_refs)
-
-    @pl.when(step >= count)
-    def _():
-        far_out[...] = stats(far_refs)
+    tile = 2 * LANES
+    count = near_ref.shape[0] // tile
+
+    def fetch(side, i):
+        at = pl.ds(pl.multiple_of(i * tile, tile), tile)
+        return pltpu.make_async_copy(
+            (near_ref, far_ref)[side].at[at], held.at[side, at], arrived.at[side, i]
+        )
+
+    for side in range(2):
+        for i in range(count):
+            fetch(side, i).start()
+
+    for side in range(2):
+
+        @pl.loop(0, count)
+        def _(i):
+            fetch(side, i).wait()
+            at = pl.ds(pl.multiple_of(i * tile, tile), tile)
+            total = jnp.zeros((half, tile), F32)
+            for kx in range(4):
+                for ky in range(4):
+                    block = ((x + 4 - kx) & 3) * 4 + ((y + 4 - ky) & 3)
+                    columns = pl.ds(pl.multiple_of(block * wide, wide), wide)
+                    total = total + contract_last(
+                        jnp.concatenate([parts[ky][kx], parts[4 + kx][ky]], axis=0),
+                        held[side, at, columns],
+                    )
+            scores = total * scale
+            best = jnp.max(scores, axis=0, keepdims=True)
+            row = lax.broadcasted_iota(I32, scores.shape, 0)
+            local = assign_ref[side : side + 1, at] - base
+            chosen = jnp.max(jnp.where(local == row, scores, NONE), axis=0, keepdims=True)
+            out_ref = (near_out, far_out)[side]
+            out_ref[:, at] = jnp.concatenate([best, chosen, mark_ref[...]], axis=0)
 
 
 def scored(where, assignments, marks, near, far, parts):
     rows, feats = near.shape
-    tile = 2 * LANES
-    count = rows // tile
-    early = lambda i, w: (jnp.minimum(i, count - 1), 0)
-    late = lambda i, w: (jnp.maximum(i - count, 0), 0)
+    local = pl.BlockSpec(memory_space=pltpu.VMEM)
+    away = pl.BlockSpec(memory_space=pl.ANY)
     return pl.pallas_call(
         functools.partial(score_kernel, 1.0 / feats),
-        grid_spec=pltpu.PrefetchScalarGridSpec(
-            num_scalar_prefetch=1,
-            grid=(2 * count,),
-            in_specs=[
-                pl.BlockSpec((1, tile), lambda i, w: (0, i)),
-                pl.BlockSpec((1, tile), lambda i, w: (0, 0)),
-            ]
-            + [
-                pl.BlockSpec((tile // FLOWS, feats), lambda i, w, f=f, k=k: (FLOWS * f(i, w)[0] + k, 0))
-                for f in (early, late)
-                for k in range(FLOWS)
-            ]
-            + [pl.BlockSpec(a.shape, lambda i, w: (0, 0, 0)) for a in parts],
-            out_specs=[
-                pl.BlockSpec((3, tile), lambda i, w: early(i, w)[::-1]),
-                pl.BlockSpec((3, tile), lambda i, w: late(i, w)[::-1]),
-            ],
-        ),
+        in_specs=[pl.BlockSpec(memory_space=pltpu.SMEM), local, local, away, away]
+        + [local] * len(parts),
+        out_specs=[local, local],
+        scratch_shapes=[
+            pltpu.VMEM((2, rows, feats), BF),
+            pltpu.SemaphoreType.DMA((2, rows // (2 * LANES))),
+        ],
         out_shape=[jax.ShapeDtypeStruct((3, rows), F32)] * 2,
         compiler_params=pltpu.CompilerParams(vmem_limit_bytes=32 * 2**20),
         cost_estimate=pl.CostEstimate(
             flops=4 * rows * feats * 256, bytes_accessed=rows * feats * 4, transcendentals=0
         ),
         name="scored",
-    )(where, assignments, marks, *[near] * FLOWS, *[far] * FLOWS, *parts)
-
-
-def closing_kernel(a_ref, b_ref, gap_ref, send_ref, mark_ref):
+    )(where, assignments, marks, near, far, *parts)
+
+
+def closing_kernel(a_ref, b_ref, gap_ref, mark_ref):
     both = jnp.maximum(a_ref[...], b_ref[...])
     gap_ref[...] = both[0:1] - both[1:2]
     mark_ref[0, 0] = jnp.max(both[2:3, :LANES]).astype(I32)
-    total = jnp.broadcast_to(jnp.sum(both[0:1], axis=1, keepdims=True), (1, LANES))
-    for i in range(send_ref.shape[0]):
-        send_ref[i] = total
-
-
-def closing(a, b, pts_count):
+
+
+def closing(a, b):
     return pl.pallas_call(
         closing_kernel,
         in_specs=[pl.BlockSpec(memory_space=pltpu.VMEM)] * 2,
         out_specs=[
             pl.BlockSpec(memory_space=pltpu.VMEM),
-            pl.BlockSpec(memory_space=pltpu.VMEM),
             pl.BlockSpec(memory_space=pltpu.SMEM),
         ],
         out_shape=[
             jax.ShapeDtypeStruct((1, a.shape[1]), F32),
-            jax.ShapeDtypeStruct((pts_count, 1, LANES), F32),
             jax.ShapeDtypeStruct((1, 1), I32),
         ],
         compiler_params=pltpu.CompilerParams(vmem_limit_bytes=4 * 2**20),
@@ -344,6 +338,28 @@
         ),
         name="closing",
     )(a, b)
+
+
+def cover_kernel(scale, got_ref, out_ref):
+    total = jnp.zeros(got_ref.shape[1:], F32)
+    for i in range(0, got_ref.shape[0], 2):
+        total = total + jnp.maximum(got_ref[i], got_ref[i + 1])
+    out_ref[0, 0] = jnp.sum(total) * scale
+
+
+def cover(got):
+    points = got.shape[0] // 2 * got.shape[2]
+    return pl.pallas_call(
+        functools.partial(cover_kernel, 1.0 / points),
+        in_specs=[pl.BlockSpec(memory_space=pltpu.VMEM)],
+        out_specs=pl.BlockSpec(memory_space=pltpu.SMEM),
+        out_shape=jax.ShapeDtypeStruct((1, 1), F32),
+        compiler_params=pltpu.CompilerParams(vmem_limit_bytes=4 * 2**20),
+        cost_estimate=pl.CostEstimate(
+            flops=got.size, bytes_accessed=4 * got.size, transcendentals=0
+        ),
+        name="cover",
+    )(got)
 
 
 def from_everyone(array, axis):
@@ -371,7 +387,7 @@
         for p in range(32)
         for z in range(planes)
     ]
-    return lax.ppermute(array, ("pts", "med"), pairs)
+    return lax.ppermute(array, ("pts", *MED), pairs)
 
 
 def general(sketches, assignment, medoid_ids):
@@ -380,7 +396,7 @@
     pts_count = lax.axis_size("pts")
     part = feat_width // pts_count
     pts_index = lax.axis_index("pts")
-    med_index = lax.axis_index("med")
+    med_index = lax.axis_index(MED)
     local_assign = assignment - med_index * medoid_count
     chosen = local_assign[:, None] == jnp.arange(medoid_count, dtype=I32)[None, :]
     one_hot = chosen.astype(BF)
@@ -400,7 +416,7 @@
     scores = contract_last(sketches, everything) * (1.0 / feat_width)
     best = jnp.max(scores, axis=1)
     taken = jnp.max(jnp.where(chosen, scores, NONE), axis=1)
-    both = from_everyone(jnp.stack([best, taken]), "med").max(axis=0)
+    both = from_everyone(jnp.stack([best, taken]), MED).max(axis=0)
     cover = from_everyone(jnp.sum(both[0])[None], "pts").sum()
     return both[0] - both[1], cover / (row_count * pts_count), counts, gradient_sums
 
@@ -411,9 +427,9 @@
     half = medoid_count // 2
     pts_count = lax.axis_size("pts")
     p = lax.axis_index("pts")
-    m = lax.axis_index("med")
+    m = lax.axis_index(MED)
     core = p % 2
-    planes = lax.axis_size("med")
+    planes = lax.axis_size(MED)
     where = jnp.stack(
         [p * row_count, m, core, p // 8, (p // 2) % 4, m * medoid_count + core * half, m, m]
     ).astype(I32)
@@ -431,30 +447,39 @@
     qa = qa + [shifted(pa, 0, k, 0) for k in (2, 3)]
     qb = [pb] + [shifted(pb, k, 0, 0) for k in (1, 2, 3)]
     grad_got = lax.all_to_all(grad_send, "pts", 0, 0, tiled=True)
-    assignments = jnp.concatenate([assignment, far_assignment])[None, :]
+    assignments = jnp.stack([assignment, far_assignment])
     stats, theirs = scored(where, assignments, marks, sketches, far, qa + qb)
     stats = jnp.maximum(
-        jnp.maximum(stats, across(stats, 0, 1, planes)),
-        jnp.maximum(across(theirs, 1, 0, planes), across(theirs, 1, 1, planes)),
+        jnp.maximum(stats, across(stats, 0, 4, planes)),
+        jnp.maximum(across(theirs, 1, 0, planes), across(theirs, 1, 4, planes)),
     )
     stats = jnp.maximum(stats, across(stats, 0, 2, planes))
-    final = across(stats, 0, 4, planes)
-    early = sums(grad_got, medoid_count, 0, 4)
-    gap, total, mark = closing(stats, final, pts_count)
+    final = across(stats, 0, 1, planes)
+    size = 2 * pts_count
+    everyone = lax.all_to_all(
+        jnp.broadcast_to(stats[None, :1], (size, 1, row_count)),
+        ("pts", MED[1]),
+        0,
+        0,
+        tiled=True,
+    )
+    gradient_sums, counts = sums(grad_got, medoid_count, 0, 8)
+    gap, mark = closing(stats, final)
     full = mark[0, 0] > 0
 
     def fast():
-        totals = lax.all_to_all(total, "pts", 0, 0, tiled=True)
-        gradient_sums, counts = sums(grad_got, medoid_count, 4, 4, early)
-        coverage = jnp.sum(totals[:, 0, 0]) / (row_count * pts_count)
-        return gap[0], coverage, counts[0], gradient_sums
+        return gap[0], cover(everyone)[0, 0], counts[0], gradient_sums
 
     return lax.cond(full, lambda: general(sketches, assignment, medoid_ids), fast)
 
 
 def solution(mesh):
-    in_specs = (P("pts", None), P("pts"), P("med"))
-    out_specs = (P("pts"), P(), P("med"), P("pts", "med"))
+    planes = mesh.shape["med"]
+    mesh = jax.sharding.Mesh(
+        mesh.devices.reshape(-1, planes // 2, 2), ("pts", *MED)
+    )
+    in_specs = (P("pts", None), P("pts"), P(MED))
+    out_specs = (P("pts"), P(), P(MED), P("pts", MED))
     return jax.shard_map(
         shards, mesh=mesh, in_specs=in_specs, out_specs=out_specs, check_vma=False
     )

time: 141 us -> 137 us (0.972)
  Pallas kernels: 27.6 us -> 20.7 us
  waiting for transfers between devices: 47.3 us -> 50.6 us
  local copies, waits for them, and re-layouts: 0.1 us -> 2.15 us
    pallas_call x2 -> x3, Pallas kernels: 20.8 us -> 14.2 us  [the longest x1 8.34 us: scored(): pl.pallas_call(functools.partial(score_kernel, 1.0 / feats), in_specs=[pl...]
    ppermute x5, waiting for transfers between devices: 4.84 us -> 10 us  [across(): return lax.ppermute(array, ('pts', *MED), pairs)]
    all_to_all x1, waiting for transfers between devices: 3.34 us -> 1.47 us  [shards(): lax.all_to_all(jnp.broadcast_to(stats[None, :1], (size, 1, row_count)), (...]
    pallas_call x2 -> x1, Pallas kernels: 5.02 us -> 4.81 us  [sums(): pl.pallas_call(functools.partial(sums_kernel, first, steps), in_specs=[pl...]
  transfers between devices with their start and end apart: 21 -> 21, of which waited for: 14 -> 14; matrix products, arithmetic and copies ran while one was open for 0% -> 0% of each run, Pallas kernels for 19% -> 15%
where the time goes in v7:
time: 137 us; the launch traced here: 135 us
  waiting for transfers between devices  50.6 us (37%)
  starting transfers between devices  42.7 us (31%)
  Pallas kernels  20.7 us (15%)
  blocking collectives  17.4 us (13%)
  local copies, waits for them, and re-layouts  2.15 us (2%)
  between operations  1.61 us (1%)
    ppermute x14, waiting for transfers between devices, shifted(): return lax.ppermute(array, 'pts', pairs)  39.1 us
    ppermute x14, starting transfers between devices, shifted(): return lax.ppermute(array, 'pts', pairs)  20.6 us
    all_to_all x1, blocking collectives, shards(): med_got = lax.all_to_all(med_send, 'pts', 0, 0, tiled=True)  17.4 us
    ppermute x5, starting transfers between devices, across(): return lax.ppermute(array, ('pts', *MED), pairs)  10.6 us
    ppermute x5, waiting for transfers between devices, across(): return lax.ppermute(array, ('pts', *MED), pairs)  10 us
    pallas_call x1, Pallas kernels, scored(): pl.pallas_call(functools.partial(score_kernel, 1.0 / feats), in_specs=[pl...  8.34 us
    all_to_all x1, starting transfers between devices, shards(): lax.all_to_all(jnp.broadcast_to(stats[None, :1], (size, 1, row_count)), (...  6.06 us
    all_to_all x1, starting transfers between devices, shards(): grad_got = lax.all_to_all(grad_send, 'pts', 0, 0, tiled=True)  5.43 us
  transfers between devices with their start and end apart: 21, of which 14 were waited for; matrix products, arithmetic and copies ran while one was open for 0% of the time, Pallas kernels for 15%

profile of v7, /device:TPU:2, one launch (start us, length us, event | category | flops | bytes accessed | tf_op | source)
XLA Modules:
  0.0 135.2 jit_solution(3798003498877015147)
XLA Ops:
  0.6 0.1 collective-permute-start.1
  0.8 0.1 stack.77.where_ref
  0.9 5.2 %pick.1 = (bf16[32,32,256]{2,1,0:T(8,128)(2,1)S(1)}, bf16[32,192,128]{2,1,0:T(8,128)(2,1)S(1)}) custom-call(s32[8]{0:T(128)S(1)} %stack.77.where_ref, s32[8,128]{1,0:T(8,128)} %bitcast.61, s32[1,512]{1,0:T(1,128)} %bitcast.65, bf16[1024,4096]{1,0:T(8,128)(2,1)} %near_ref.1), custom_call_target="tpu_custom_call" | custom-call | flops 2147483648 | bytes 8388608 | tf_op jit(solution)/shard_map/pick/pallas_call | solution.py:126
  6.1 1.2 copy-done
  7.3 17.4 %all_to_all.42.got_ref = bf16[32,32,256]{2,1,0:T(8,128)(2,1)S(1)} all-to-all(bf16[32,32,256]{2,1,0:T(8,128)(2,1)S(1)} %get-tuple-element.36), channel_id=1, replica_groups=mesh['pts'=32,'zq'=4,'zr'=2] {'pts'}, dimensions={0} | all-to-all | bytes 1048576 | tf_op jit(solution)/shard_map/all_to_all | solution.py:442
  24.7 5.4 %all-to-all-start.8 = ((bf16[32,192,128]{2,1,0:T(8,128)(2,1)}), bf16[32,192,128]{2,1,0:T(8,128)(2,1)S(1)}, u32[]{:S(2)}, u32[]{:S(2)}) async-start(bf16[32,192,128]{2,1,0:T(8,128)(2,1)} %copy-done), calls=%async_computation.8 | async-start | bytes 3145728 | tf_op jit(solution)/shard_map/all_to_all | solution.py:449
  30.1 1.0 place.1
  31.1 2.8 %collective-permute-start.10 = (bf16[128,256]{1,0:T(8,128)(2,1)S(1)}, bf16[128,256]{1,0:T(8,128)(2,1)S(1)}, u32[]{:S(2)}, u32[]{:S(2)}) collective-permute-start(bf16[128,256]{1,0:T(8,128)(2,1)S(1)} %get-tuple-element.39), channel_id=1, source_target_pairs={{0,48},{8,56},{16,0},{24,8},{32,16},{40,24},{48,32},{56,40},{64,11... | collective-permute-start | bytes 196616 | tf_op jit(solution)/shard_map/ppermute | solution.py:381
  33.9 0.9 collective-permute-start.9
  34.7 0.9 collective-permute-start.8
  35.6 15.5 %collective-permute-done.10 = bf16[128,256]{1,0:T(8,128)(2,1)S(1)} collective-permute-done((bf16[128,256]{1,0:T(8,128)(2,1)S(1)}, bf16[128,256]{1,0:T(8,128)(2,1)S(1)}, u32[]{:S(2)}, u32[]{:S(2)}) %collective-permute-start.10) | collective-permute-done | bytes 65568 | tf_op jit(solution)/shard_map/ppermute | solution.py:381
  51.1 1.9 %collective-permute-done.9 = bf16[128,256]{1,0:T(8,128)(2,1)S(1)} collective-permute-done((bf16[128,256]{1,0:T(8,128)(2,1)S(1)}, bf16[128,256]{1,0:T(8,128)(2,1)S(1)}, u32[]{:S(2)}, u32[]{:S(2)}) %collective-permute-start.9) | collective-permute-done | bytes 65568 | tf_op jit(solution)/shard_map/ppermute | solution.py:381
  53.0 0.5 collective-permute-done.8
  53.6 0.6 collective-permute-start.13
  54.2 2.4 %collective-permute-start.12 = (bf16[4,128,256]{2,1,0:T(8,128)(2,1)S(1)}, bf16[4,128,256]{2,1,0:T(8,128)(2,1)S(1)}, u32[]{:S(2)}, u32[]{:S(2)}) collective-permute-start(bf16[4,128,256]{2,1,0:T(8,128)(2,1)S(1)} %pad_maximum_fusion.2.refs_4_), channel_id=1, source_target_pairs={{0,128},{8,136},{16,144},{24,152},{32,160},{40,168},{48,176},{56,1... | collective-permute-start | bytes 786440 | tf_op jit(solution)/shard_map/ppermute | solution.py:381
  56.6 1.1 collective-permute-start.4
  57.7 2.2 %collective-permute-start.3 = (bf16[128,256]{1,0:T(8,128)(2,1)S(1)}, bf16[128,256]{1,0:T(8,128)(2,1)S(1)}, u32[]{:S(2)}, u32[]{:S(2)}) collective-permute-start(bf16[128,256]{1,0:T(8,128)(2,1)S(1)} %get-tuple-element.38), channel_id=1, source_target_pairs={{0,128},{8,136},{16,144},{24,152},{32,160},{40,168},{48,176},{56,1... | collective-permute-start | bytes 196616 | tf_op jit(solution)/shard_map/ppermute | solution.py:381
  59.9 7.5 %collective-permute-done.4 = bf16[128,256]{1,0:T(8,128)(2,1)S(1)} collective-permute-done((bf16[128,256]{1,0:T(8,128)(2,1)S(1)}, bf16[128,256]{1,0:T(8,128)(2,1)S(1)}, u32[]{:S(2)}, u32[]{:S(2)}) %collective-permute-start.4) | collective-permute-done | bytes 65568 | tf_op jit(solution)/shard_map/ppermute | solution.py:381
  67.4 3.5 %collective-permute-start.2 = (bf16[128,256]{1,0:T(8,128)(2,1)S(1)}, bf16[128,256]{1,0:T(8,128)(2,1)S(1)}, u32[]{:S(2)}, u32[]{:S(2)}) collective-permute-start(bf16[128,256]{1,0:T(8,128)(2,1)S(1)} %get-tuple-element.38), channel_id=1, source_target_pairs={{0,64},{8,72},{16,80},{24,88},{32,96},{40,104},{48,112},{56,120},{... | collective-permute-start | bytes 196616 | tf_op jit(solution)/shard_map/ppermute | solution.py:381
  70.9 0.1 collective-permute-done.3
  71.0 1.9 %collective-permute-done.2 = bf16[128,256]{1,0:T(8,128)(2,1)S(1)} collective-permute-done((bf16[128,256]{1,0:T(8,128)(2,1)S(1)}, bf16[128,256]{1,0:T(8,128)(2,1)S(1)}, u32[]{:S(2)}, u32[]{:S(2)}) %collective-permute-start.2) | collective-permute-done | bytes 65568 | tf_op jit(solution)/shard_map/ppermute | solution.py:381
  72.9 2.8 %collective-permute-start.11 = (bf16[4,128,256]{2,1,0:T(8,128)(2,1)S(1)}, bf16[4,128,256]{2,1,0:T(8,128)(2,1)S(1)}, u32[]{:S(2)}, u32[]{:S(2)}) collective-permute-start(bf16[4,128,256]{2,1,0:T(8,128)(2,1)S(1)} %pad_maximum_fusion.2.refs_4_), channel_id=1, source_target_pairs={{0,64},{8,72},{16,80},{24,88},{32,96},{40,104},{48,112},{56,120},{... | collective-permute-start | bytes 786440 | tf_op jit(solution)/shard_map/ppermute | solution.py:381
  75.7 0.0 collective-permute-done
  75.7 1.9 %collective-permute-start.7 = (bf16[4,128,256]{2,1,0:T(8,128)(2,1)S(1)}, bf16[4,128,256]{2,1,0:T(8,128)(2,1)S(1)}, u32[]{:S(2)}, u32[]{:S(2)}) collective-permute-start(bf16[4,128,256]{2,1,0:T(8,128)(2,1)S(1)} %pad_maximum_fusion.1.refs_0_), channel_id=1, source_target_pairs={{0,48},{8,56},{16,0},{24,8},{32,16},{40,24},{48,32},{56,40},{64,11... | collective-permute-start | bytes 786440 | tf_op jit(solution)/shard_map/ppermute | solution.py:381
  77.7 0.0 collective-permute-done.13.refs_7_
  77.7 1.5 %collective-permute-start.6 = (bf16[4,128,256]{2,1,0:T(8,128)(2,1)S(1)}, bf16[4,128,256]{2,1,0:T(8,128)(2,1)S(1)}, u32[]{:S(2)}, u32[]{:S(2)}) collective-permute-start(bf16[4,128,256]{2,1,0:T(8,128)(2,1)S(1)} %pad_maximum_fusion.1.refs_0_), channel_id=1, source_target_pairs={{0,32},{8,40},{16,48},{24,56},{32,0},{40,8},{48,16},{56,24},{64,96... | collective-permute-start | bytes 786440 | tf_op jit(solution)/shard_map/ppermute | solution.py:381
  79.1 0.0 collective-permute-start.5
  79.2 1.8 %collective-permute-done.11.refs_5_ = bf16[4,128,256]{2,1,0:T(8,128)(2,1)S(1)} collective-permute-done((bf16[4,128,256]{2,1,0:T(8,128)(2,1)S(1)}, bf16[4,128,256]{2,1,0:T(8,128)(2,1)S(1)}, u32[]{:S(2)}, u32[]{:S(2)}) %collective-permute-start.11) | collective-permute-done | bytes 262176 | tf_op jit(solution)/shard_map/ppermute | solution.py:381
  80.9 4.0 %collective-permute-done.7.refs_3_ = bf16[4,128,256]{2,1,0:T(8,128)(2,1)S(1)} collective-permute-done((bf16[4,128,256]{2,1,0:T(8,128)(2,1)S(1)}, bf16[4,128,256]{2,1,0:T(8,128)(2,1)S(1)}, u32[]{:S(2)}, u32[]{:S(2)}) %collective-permute-start.7) | collective-permute-done | bytes 262176 | tf_op jit(solution)/shard_map/ppermute | solution.py:381
  85.0 3.1 %collective-permute-done.6.refs_2_ = bf16[4,128,256]{2,1,0:T(8,128)(2,1)S(1)} collective-permute-done((bf16[4,128,256]{2,1,0:T(8,128)(2,1)S(1)}, bf16[4,128,256]{2,1,0:T(8,128)(2,1)S(1)}, u32[]{:S(2)}, u32[]{:S(2)}) %collective-permute-start.6) | collective-permute-done | bytes 262176 | tf_op jit(solution)/shard_map/ppermute | solution.py:381
  88.1 2.8 %collective-permute-done.5.refs_1_ = bf16[4,128,256]{2,1,0:T(8,128)(2,1)S(1)} collective-permute-done((bf16[4,128,256]{2,1,0:T(8,128)(2,1)S(1)}, bf16[4,128,256]{2,1,0:T(8,128)(2,1)S(1)}, u32[]{:S(2)}, u32[]{:S(2)}) %collective-permute-start.5) | collective-permute-done | bytes 262176 | tf_op jit(solution)/shard_map/ppermute | solution.py:381
  90.8 0.0 collective-permute-done.1.far_ref
  90.8 8.3 %scored.1 = (f32[3,1024]{1,0:T(4,128)S(1)}, f32[3,1024]{1,0:T(4,128)S(1)}) custom-call(s32[8]{0:T(128)S(1)} %stack.77.where_ref, s32[2,1024]{1,0:T(2,128)S(1)} %pad_add_fusion.assign_ref, f32[1,256]{1,0:T(1,128)S(1)} %get-tuple-element.37.mark_ref, bf16[1024,4096]{1,0:T(8,128)(2,1)} %near_ref.1, bf16[1024,4096]{1,0:T(8,128)(2,1)} %collective-permute-done.1.far_ref, ...), custom_call_target="tpu_custom_call" | custom-call | flops 4294967296 | bytes 16777216 | tf_op jit(solution)/shard_map/scored/pallas_call | solution.py:299
  99.2 0.0 copy-start.2
  99.2 7.3 %collective-permute-start.14 = (f32[3,1024]{1,0:T(4,128)S(1)}, f32[3,1024]{1,0:T(4,128)S(1)}, u32[]{:S(2)}, u32[]{:S(2)}) collective-permute-start(f32[3,1024]{1,0:T(4,128)S(1)} %get-tuple-element.40), channel_id=1, source_target_pairs={{0,4},{1,5},{2,6},{3,7},{4,0},{5,1},{6,2},{7,3},{8,12},{9,13},{10,... | collective-permute-start | bytes 36872 | tf_op jit(solution)/shard_map/ppermute | solution.py:390
  106.5 0.2 collective-permute-start.15
  106.7 1.5 %collective-permute-done.14 = f32[3,1024]{1,0:T(4,128)S(1)} collective-permute-done((f32[3,1024]{1,0:T(4,128)S(1)}, f32[3,1024]{1,0:T(4,128)S(1)}, u32[]{:S(2)}, u32[]{:S(2)}) %collective-permute-start.14) | collective-permute-done | bytes 12320 | tf_op jit(solution)/shard_map/ppermute | solution.py:390
  108.2 5.4 %collective-permute-done.16 = f32[3,1024]{1,0:T(4,128)S(1)} collective-permute-done((f32[3,1024]{1,0:T(4,128)S(1)}, f32[3,1024]{1,0:T(4,128)S(1)}, u32[]{:S(2)}, u32[]{:S(2)}) %collective-permute-start.16) | collective-permute-done | bytes 12320 | tf_op jit(solution)/shard_map/ppermute | solution.py:390
  113.6 1.6 %collective-permute-start.17 = (f32[3,1024]{1,0:T(4,128)S(1)}, f32[3,1024]{1,0:T(4,128)S(1)}, u32[]{:S(2)}, u32[]{:S(2)}) collective-permute-start(f32[3,1024]{1,0:T(4,128)S(1)} %maximum_maximum_fusion), channel_id=1, source_target_pairs={{0,2},{1,3},{2,0},{3,1},{4,6},{5,7},{6,4},{7,5},{8,10},{9,11},{10,... | collective-permute-start | bytes 36872 | tf_op jit(solution)/shard_map/ppermute | solution.py:390
  115.1 3.2 %collective-permute-done.17 = f32[3,1024]{1,0:T(4,128)S(1)} collective-permute-done((f32[3,1024]{1,0:T(4,128)S(1)}, f32[3,1024]{1,0:T(4,128)S(1)}, u32[]{:S(2)}, u32[]{:S(2)}) %collective-permute-start.17) | collective-permute-done | bytes 12320 | tf_op jit(solution)/shard_map/ppermute | solution.py:390
  118.3 0.8 broadcast_in_dim.20
  119.1 6.1 %all-to-all-start.7 = ((f32[64,1,1024]{2,1,0:T(1,128)}), f32[64,1,1024]{2,1,0:T(1,128)S(1)}, u32[]{:S(2)}, u32[]{:S(2)}) async-start(f32[64,1,1024]{2,1,0:T(1,128)} %broadcast_in_dim.20), calls=%async_computation.7 | async-start | bytes 524288 | tf_op jit(solution)/shard_map/all_to_all | solution.py:459
  125.2 1.6 %collective-permute-start.18 = (f32[3,1024]{1,0:T(4,128)S(1)}, f32[3,1024]{1,0:T(4,128)S(1)}, u32[]{:S(2)}, u32[]{:S(2)}) collective-permute-start(f32[3,1024]{1,0:T(4,128)S(1)} %max.15.a_ref), channel_id=1, source_target_pairs={{0,1},{1,0},{2,3},{3,2},{4,5},{5,4},{6,7},{7,6},{8,9},{9,8},{10,11... | collective-permute-start | bytes 36872 | tf_op jit(solution)/shard_map/ppermute | solution.py:390
  126.8 4.8 %sums.1 = (f32[128,512]{1,0:T(8,128)}, f32[1,512]{1,0:T(1,128)}) custom-call(bf16[32,192,128]{2,1,0:T(8,128)(2,1)S(1)} %all-to-all-done.8.got_ref), custom_call_target="tpu_custom_call" | custom-call | flops 1610612736 | bytes 1572864 | tf_op jit(solution)/shard_map/sums/pallas_call | solution.py:237
  131.6 0.6 closing.1
  132.9 1.5 %all-to-all-done.7 = f32[64,1,1024]{2,1,0:T(1,128)S(1)} async-done(((f32[64,1,1024]{2,1,0:T(1,128)}), f32[64,1,1024]{2,1,0:T(1,128)S(1)}, u32[]{:S(2)}, u32[]{:S(2)}) %all-to-all-start.7) | async-done | bytes 262176 | tf_op jit(solution)/shard_map/all_to_all | solution.py:459
  134.3 0.7 conditional.1
  134.3 0.7 cover.1
  (16 shorter events, 0.1 us)
Async XLA Ops:
  0.6 90.2 %collective-permute-start.1 = (bf16[1024,4096]{1,0:T(8,128)(2,1)}, bf16[1024,4096]{1,0:T(8,128)(2,1)}, u32[]{:S(2)}, u32[]{:S(2)}) collective-permute-start(bf16[1024,4096]{1,0:T(8,128)(2,1)} %near_ref.1), channel_id=1, source_target_pairs={{0,8},{8,0},{16,24},{24,16},{32,40},{40,32},{48,56},{56,48},{64,72... | collective-permute-start | bytes 25165832 | tf_op jit(solution)/shard_map/ppermute | solution.py:381
  6.1 1.2 copy-start
  7.3 63.7 %copy-start.1 = (s32[1024]{0:T(1024)S(1)}, s32[1024]{0:T(1024)}, u32[]{:S(2)}) copy-start(s32[1024]{0:T(1024)} %param.6) | copy-start | bytes 12292
  24.7 93.6 %all-to-all-start.8 = ((bf16[32,192,128]{2,1,0:T(8,128)(2,1)}), bf16[32,192,128]{2,1,0:T(8,128)(2,1)S(1)}, u32[]{:S(2)}, u32[]{:S(2)}) async-start(bf16[32,192,128]{2,1,0:T(8,128)(2,1)} %copy-done), calls=%async_computation.8 | async-start | bytes 3145728 | tf_op jit(solution)/shard_map/all_to_all | solution.py:449
  31.1 20.0 %collective-permute-start.10 = (bf16[128,256]{1,0:T(8,128)(2,1)S(1)}, bf16[128,256]{1,0:T(8,128)(2,1)S(1)}, u32[]{:S(2)}, u32[]{:S(2)}) collective-permute-start(bf16[128,256]{1,0:T(8,128)(2,1)S(1)} %get-tuple-element.39), channel_id=1, source_target_pairs={{0,48},{8,56},{16,0},{24,8},{32,16},{40,24},{48,32},{56,40},{64,11... | collective-permute-start | bytes 196616 | tf_op jit(solution)/shard_map/ppermute | solution.py:381
  33.9 19.1 %collective-permute-start.9 = (bf16[128,256]{1,0:T(8,128)(2,1)S(1)}, bf16[128,256]{1,0:T(8,128)(2,1)S(1)}, u32[]{:S(2)}, u32[]{:S(2)}) collective-permute-start(bf16[128,256]{1,0:T(8,128)(2,1)S(1)} %get-tuple-element.39), channel_id=1, source_target_pairs={{0,32},{8,40},{16,48},{24,56},{32,0},{40,8},{48,16},{56,24},{64,96... | collective-permute-start | bytes 196616 | tf_op jit(solution)/shard_map/ppermute | solution.py:381
  34.7 18.8 %collective-permute-start.8 = (bf16[128,256]{1,0:T(8,128)(2,1)S(1)}, bf16[128,256]{1,0:T(8,128)(2,1)S(1)}, u32[]{:S(2)}, u32[]{:S(2)}) collective-permute-start(bf16[128,256]{1,0:T(8,128)(2,1)S(1)} %get-tuple-element.39), channel_id=1, source_target_pairs={{0,16},{8,24},{16,32},{24,40},{32,48},{40,56},{48,0},{56,8},{64,80... | collective-permute-start | bytes 196616 | tf_op jit(solution)/shard_map/ppermute | solution.py:381
  53.6 24.1 %collective-permute-start.13 = (bf16[4,128,256]{2,1,0:T(8,128)(2,1)S(1)}, bf16[4,128,256]{2,1,0:T(8,128)(2,1)S(1)}, u32[]{:S(2)}, u32[]{:S(2)}) collective-permute-start(bf16[4,128,256]{2,1,0:T(8,128)(2,1)S(1)} %pad_maximum_fusion.2.refs_4_), channel_id=1, source_target_pairs={{0,192},{8,200},{16,208},{24,216},{32,224},{40,232},{48,240},{56,2... | collective-permute-start | bytes 786440 | tf_op jit(solution)/shard_map/ppermute | solution.py:381
  54.2 25.0 %collective-permute-start.12 = (bf16[4,128,256]{2,1,0:T(8,128)(2,1)S(1)}, bf16[4,128,256]{2,1,0:T(8,128)(2,1)S(1)}, u32[]{:S(2)}, u32[]{:S(2)}) collective-permute-start(bf16[4,128,256]{2,1,0:T(8,128)(2,1)S(1)} %pad_maximum_fusion.2.refs_4_), channel_id=1, source_target_pairs={{0,128},{8,136},{16,144},{24,152},{32,160},{40,168},{48,176},{56,1... | collective-permute-start | bytes 786440 | tf_op jit(solution)/shard_map/ppermute | solution.py:381
  56.6 10.8 %collective-permute-start.4 = (bf16[128,256]{1,0:T(8,128)(2,1)S(1)}, bf16[128,256]{1,0:T(8,128)(2,1)S(1)}, u32[]{:S(2)}, u32[]{:S(2)}) collective-permute-start(bf16[128,256]{1,0:T(8,128)(2,1)S(1)} %get-tuple-element.38), channel_id=1, source_target_pairs={{0,192},{8,200},{16,208},{24,216},{32,224},{40,232},{48,240},{56,2... | collective-permute-start | bytes 196616 | tf_op jit(solution)/shard_map/ppermute | solution.py:381
  57.7 13.3 %collective-permute-start.3 = (bf16[128,256]{1,0:T(8,128)(2,1)S(1)}, bf16[128,256]{1,0:T(8,128)(2,1)S(1)}, u32[]{:S(2)}, u32[]{:S(2)}) collective-permute-start(bf16[128,256]{1,0:T(8,128)(2,1)S(1)} %get-tuple-element.38), channel_id=1, source_target_pairs={{0,128},{8,136},{16,144},{24,152},{32,160},{40,168},{48,176},{56,1... | collective-permute-start | bytes 196616 | tf_op jit(solution)/shard_map/ppermute | solution.py:381
  67.4 5.5 %collective-permute-start.2 = (bf16[128,256]{1,0:T(8,128)(2,1)S(1)}, bf16[128,256]{1,0:T(8,128)(2,1)S(1)}, u32[]{:S(2)}, u32[]{:S(2)}) collective-permute-start(bf16[128,256]{1,0:T(8,128)(2,1)S(1)} %get-tuple-element.38), channel_id=1, source_target_pairs={{0,64},{8,72},{16,80},{24,88},{32,96},{40,104},{48,112},{56,120},{... | collective-permute-start | bytes 196616 | tf_op jit(solution)/shard_map/ppermute | solution.py:381
  71.0 4.7 %collective-permute-start = (s32[1024]{0:T(1024)S(1)}, s32[1024]{0:T(1024)S(1)}, u32[]{:S(2)}, u32[]{:S(2)}) collective-permute-start(s32[1024]{0:T(1024)S(1)} %copy-done.1), channel_id=1, source_target_pairs={{0,8},{8,0},{16,24},{24,16},{32,40},{40,32},{48,56},{56,48},{64,72... | collective-permute-start | bytes 12296 | tf_op jit(solution)/shard_map/ppermute | solution.py:381
  72.9 8.0 %collective-permute-start.11 = (bf16[4,128,256]{2,1,0:T(8,128)(2,1)S(1)}, bf16[4,128,256]{2,1,0:T(8,128)(2,1)S(1)}, u32[]{:S(2)}, u32[]{:S(2)}) collective-permute-start(bf16[4,128,256]{2,1,0:T(8,128)(2,1)S(1)} %pad_maximum_fusion.2.refs_4_), channel_id=1, source_target_pairs={{0,64},{8,72},{16,80},{24,88},{32,96},{40,104},{48,112},{56,120},{... | collective-permute-start | bytes 786440 | tf_op jit(solution)/shard_map/ppermute | solution.py:381
  75.7 9.3 %collective-permute-start.7 = (bf16[4,128,256]{2,1,0:T(8,128)(2,1)S(1)}, bf16[4,128,256]{2,1,0:T(8,128)(2,1)S(1)}, u32[]{:S(2)}, u32[]{:S(2)}) collective-permute-start(bf16[4,128,256]{2,1,0:T(8,128)(2,1)S(1)} %pad_maximum_fusion.1.refs_0_), channel_id=1, source_target_pairs={{0,48},{8,56},{16,0},{24,8},{32,16},{40,24},{48,32},{56,40},{64,11... | collective-permute-start | bytes 786440 | tf_op jit(solution)/shard_map/ppermute | solution.py:381
  77.7 10.4 %collective-permute-start.6 = (bf16[4,128,256]{2,1,0:T(8,128)(2,1)S(1)}, bf16[4,128,256]{2,1,0:T(8,128)(2,1)S(1)}, u32[]{:S(2)}, u32[]{:S(2)}) collective-permute-start(bf16[4,128,256]{2,1,0:T(8,128)(2,1)S(1)} %pad_maximum_fusion.1.refs_0_), channel_id=1, source_target_pairs={{0,32},{8,40},{16,48},{24,56},{32,0},{40,8},{48,16},{56,24},{64,96... | collective-permute-start | bytes 786440 | tf_op jit(solution)/shard_map/ppermute | solution.py:381
  79.1 11.7 %collective-permute-start.5 = (bf16[4,128,256]{2,1,0:T(8,128)(2,1)S(1)}, bf16[4,128,256]{2,1,0:T(8,128)(2,1)S(1)}, u32[]{:S(2)}, u32[]{:S(2)}) collective-permute-start(bf16[4,128,256]{2,1,0:T(8,128)(2,1)S(1)} %pad_maximum_fusion.1.refs_0_), channel_id=1, source_target_pairs={{0,16},{8,24},{16,32},{24,40},{32,48},{40,56},{48,0},{56,8},{64,80... | collective-permute-start | bytes 786440 | tf_op jit(solution)/shard_map/ppermute | solution.py:381
  99.2 35.2 %copy-start.2 = (s32[512]{0:T(512)S(1)}, s32[512]{0:T(512)}, u32[]{:S(2)}) copy-start(s32[512]{0:T(512)} %param.7) | copy-start | bytes 6148
  99.2 9.0 %collective-permute-start.14 = (f32[3,1024]{1,0:T(4,128)S(1)}, f32[3,1024]{1,0:T(4,128)S(1)}, u32[]{:S(2)}, u32[]{:S(2)}) collective-permute-start(f32[3,1024]{1,0:T(4,128)S(1)} %get-tuple-element.40), channel_id=1, source_target_pairs={{0,4},{1,5},{2,6},{3,7},{4,0},{5,1},{6,2},{7,3},{8,12},{9,13},{10,... | collective-permute-start | bytes 36872 | tf_op jit(solution)/shard_map/ppermute | solution.py:390
  106.5 7.1 %collective-permute-start.16 = (f32[3,1024]{1,0:T(4,128)S(1)}, f32[3,1024]{1,0:T(4,128)S(1)}, u32[]{:S(2)}, u32[]{:S(2)}) collective-permute-start(f32[3,1024]{1,0:T(4,128)S(1)} %get-tuple-element.41), channel_id=1, source_target_pairs={{0,12},{1,13},{2,14},{3,15},{4,8},{5,9},{6,10},{7,11},{8,4},{9,5},... | collective-permute-start | bytes 36872 | tf_op jit(solution)/shard_map/ppermute | solution.py:390
  106.5 7.1 %collective-permute-start.15 = (f32[3,1024]{1,0:T(4,128)S(1)}, f32[3,1024]{1,0:T(4,128)S(1)}, u32[]{:S(2)}, u32[]{:S(2)}) collective-permute-start(f32[3,1024]{1,0:T(4,128)S(1)} %get-tuple-element.41), channel_id=1, source_target_pairs={{0,8},{1,9},{2,10},{3,11},{4,12},{5,13},{6,14},{7,15},{8,0},{9,1},... | collective-permute-start | bytes 36872 | tf_op jit(solution)/shard_map/ppermute | solution.py:390
  113.6 4.7 %collective-permute-start.17 = (f32[3,1024]{1,0:T(4,128)S(1)}, f32[3,1024]{1,0:T(4,128)S(1)}, u32[]{:S(2)}, u32[]{:S(2)}) collective-permute-start(f32[3,1024]{1,0:T(4,128)S(1)} %maximum_maximum_fusion), channel_id=1, source_target_pairs={{0,2},{1,3},{2,0},{3,1},{4,6},{5,7},{6,4},{7,5},{8,10},{9,11},{10,... | collective-permute-start | bytes 36872 | tf_op jit(solution)/shard_map/ppermute | solution.py:390
  119.1 15.2 %all-to-all-start.7 = ((f32[64,1,1024]{2,1,0:T(1,128)}), f32[64,1,1024]{2,1,0:T(1,128)S(1)}, u32[]{:S(2)}, u32[]{:S(2)}) async-start(f32[64,1,1024]{2,1,0:T(1,128)} %broadcast_in_dim.20), calls=%async_computation.7 | async-start | bytes 524288 | tf_op jit(solution)/shard_map/all_to_all | solution.py:459
  125.2 6.4 %collective-permute-start.18 = (f32[3,1024]{1,0:T(4,128)S(1)}, f32[3,1024]{1,0:T(4,128)S(1)}, u32[]{:S(2)}, u32[]{:S(2)}) collective-permute-start(f32[3,1024]{1,0:T(4,128)S(1)} %max.15.a_ref), channel_id=1, source_target_pairs={{0,1},{1,0},{2,3},{3,2},{4,5},{5,4},{6,7},{7,6},{8,9},{9,8},{10,11... | collective-permute-start | bytes 36872 | tf_op jit(solution)/shard_map/ppermute | solution.py:390

commit v8 on v7

--- a/solution.py
+++ b/solution.py
@@ -18,6 +18,7 @@
 MED_SLOTS = 24
 SEL = GRAD_ROWS + 2 * MED_ROWS
 NONE = -1e30
+LOST = 1e30
 MED = ("zq", "zr")
 CHIPS = 4
 
@@ -251,7 +252,8 @@
 
 
 def score_kernel(scale, where_ref, assign_ref, mark_ref, near_ref, far_ref, *refs):
-    parts, (near_out, far_out, held, arrived) = refs[:8], refs[8:]
+    parts, (out_ref, held, arrived) = refs[:8], refs[8:]
+    lost = mark_ref[...] > 0
     quarter, wide = parts[0].shape[1:]
     half = 2 * quarter
     x, y, base = where_ref[3], where_ref[4], where_ref[5]
@@ -288,8 +290,8 @@
             row = lax.broadcasted_iota(I32, scores.shape, 0)
             local = assign_ref[side : side + 1, at] - base
             chosen = jnp.max(jnp.where(local == row, scores, NONE), axis=0, keepdims=True)
-            out_ref = (near_out, far_out)[side]
-            out_ref[:, at] = jnp.concatenate([best, chosen, mark_ref[...]], axis=0)
+            out_ref[side : side + 1, at] = best
+            out_ref[2 + side : 3 + side, at] = jnp.where(lost, LOST, chosen)
 
 
 def scored(where, assignments, marks, near, far, parts):
@@ -300,12 +302,12 @@
         functools.partial(score_kernel, 1.0 / feats),
         in_specs=[pl.BlockSpec(memory_space=pltpu.SMEM), local, local, away, away]
         + [local] * len(parts),
-        out_specs=[local, local],
+        out_specs=local,
         scratch_shapes=[
             pltpu.VMEM((2, rows, feats), BF),
             pltpu.SemaphoreType.DMA((2, rows // (2 * LANES))),
         ],
-        out_shape=[jax.ShapeDtypeStruct((3, rows), F32)] * 2,
+        out_shape=jax.ShapeDtypeStruct((4, rows), F32),
         compiler_params=pltpu.CompilerParams(vmem_limit_bytes=32 * 2**20),
         cost_estimate=pl.CostEstimate(
             flops=4 * rows * feats * 256, bytes_accessed=rows * feats * 4, transcendentals=0
@@ -314,16 +316,19 @@
     )(where, assignments, marks, near, far, *parts)
 
 
-def closing_kernel(a_ref, b_ref, gap_ref, mark_ref):
-    both = jnp.maximum(a_ref[...], b_ref[...])
-    gap_ref[...] = both[0:1] - both[1:2]
-    mark_ref[0, 0] = jnp.max(both[2:3, :LANES]).astype(I32)
-
-
-def closing(a, b):
+def closing_kernel(a_ref, b_ref, c_ref, d_ref, gap_ref, mark_ref):
+    same = jnp.maximum(a_ref[...], b_ref[...])
+    partner = jnp.maximum(c_ref[...], d_ref[...])
+    best = jnp.maximum(same[0:1], partner[1:2])
+    chosen = jnp.maximum(same[2:3], partner[3:4])
+    gap_ref[...] = best - chosen
+    mark_ref[0, 0] = jnp.where(jnp.max(chosen) > 0.5 * LOST, 1, 0)
+
+
+def closing(a, b, c, d):
     return pl.pallas_call(
         closing_kernel,
-        in_specs=[pl.BlockSpec(memory_space=pltpu.VMEM)] * 2,
+        in_specs=[pl.BlockSpec(memory_space=pltpu.VMEM)] * 4,
         out_specs=[
             pl.BlockSpec(memory_space=pltpu.VMEM),
             pl.BlockSpec(memory_space=pltpu.SMEM),
@@ -334,16 +339,18 @@
         ],
         compiler_params=pltpu.CompilerParams(vmem_limit_bytes=4 * 2**20),
         cost_estimate=pl.CostEstimate(
-            flops=a.size, bytes_accessed=8 * a.size, transcendentals=0
+            flops=a.size, bytes_accessed=16 * a.size, transcendentals=0
         ),
         name="closing",
-    )(a, b)
+    )(a, b, c, d)
 
 
 def cover_kernel(scale, got_ref, out_ref):
-    total = jnp.zeros(got_ref.shape[1:], F32)
-    for i in range(0, got_ref.shape[0], 2):
-        total = total + jnp.maximum(got_ref[i], got_ref[i + 1])
+    total = jnp.zeros((1, got_ref.shape[2]), F32)
+    for i in range(0, got_ref.shape[0], 4):
+        one = jnp.maximum(got_ref[i], got_ref[i + 1])
+        two = jnp.maximum(got_ref[i + 2], got_ref[i + 3])
+        total = total + jnp.maximum(one[0:1], two[1:2]) + jnp.maximum(one[1:2], two[0:1])
     out_ref[0, 0] = jnp.sum(total) * scale
 
 
@@ -448,23 +455,22 @@
     qb = [pb] + [shifted(pb, k, 0, 0) for k in (1, 2, 3)]
     grad_got = lax.all_to_all(grad_send, "pts", 0, 0, tiled=True)
     assignments = jnp.stack([assignment, far_assignment])
-    stats, theirs = scored(where, assignments, marks, sketches, far, qa + qb)
-    stats = jnp.maximum(
-        jnp.maximum(stats, across(stats, 0, 4, planes)),
-        jnp.maximum(across(theirs, 1, 0, planes), across(theirs, 1, 4, planes)),
-    )
+    stats = scored(where, assignments, marks, sketches, far, qa + qb)
+    stats = jnp.maximum(stats, across(stats, 0, 4, planes))
     stats = jnp.maximum(stats, across(stats, 0, 2, planes))
-    final = across(stats, 0, 1, planes)
     size = 2 * pts_count
     everyone = lax.all_to_all(
-        jnp.broadcast_to(stats[None, :1], (size, 1, row_count)),
+        jnp.broadcast_to(stats[None, :2], (size, 2, row_count)),
         ("pts", MED[1]),
         0,
         0,
         tiled=True,
     )
+    plane = across(stats, 0, 1, planes)
+    partner = across(stats, 1, 0, planes)
+    both = across(stats, 1, 1, planes)
     gradient_sums, counts = sums(grad_got, medoid_count, 0, 8)
-    gap, mark = closing(stats, final)
+    gap, mark = closing(stats, plane, partner, both)
     full = mark[0, 0] > 0
 
     def fast():

time: 137 us -> 134 us (0.978)
  waiting for transfers between devices: 50.6 us -> 47.2 us
    ppermute x5, waiting for transfers between devices: 10 us -> 5.9 us  [across(): return lax.ppermute(array, ('pts', *MED), pairs)]
  transfers between devices with their start and end apart: 21 -> 21, of which waited for: 14 -> 15; matrix products, arithmetic and copies ran while one was open for 0% -> 0% of each run, Pallas kernels for 15% -> 15%
where the time goes in v8:
time: 134 us; the launch traced here: 133 us
  waiting for transfers between devices  47.2 us (35%)
  starting transfers between devices  43.6 us (33%)
  Pallas kernels  20.7 us (15%)
  blocking collectives  17.4 us (13%)
  local copies, waits for them, and re-layouts  2.24 us (2%)
  between operations  1.61 us (1%)
    ppermute x14, waiting for transfers between devices, shifted(): return lax.ppermute(array, 'pts', pairs)  39.1 us
    ppermute x14, starting transfers between devices, shifted(): return lax.ppermute(array, 'pts', pairs)  20.6 us
    all_to_all x1, blocking collectives, shards(): med_got = lax.all_to_all(med_send, 'pts', 0, 0, tiled=True)  17.4 us
    ppermute x5, starting transfers between devices, across(): return lax.ppermute(array, ('pts', *MED), pairs)  11.5 us
    pallas_call x1, Pallas kernels, scored(): pl.pallas_call(functools.partial(score_kernel, 1.0 / feats), in_specs=[pl...  8.36 us
    all_to_all x1, starting transfers between devices, shards(): lax.all_to_all(jnp.broadcast_to(stats[None, :2], (size, 2, row_count)), (...  6.1 us
    ppermute x5, waiting for transfers between devices, across(): return lax.ppermute(array, ('pts', *MED), pairs)  5.9 us
    all_to_all x1, starting transfers between devices, shards(): grad_got = lax.all_to_all(grad_send, 'pts', 0, 0, tiled=True)  5.43 us
  transfers between devices with their start and end apart: 21, of which 15 were waited for; matrix products, arithmetic and copies ran while one was open for 0% of the time, Pallas kernels for 15%

profile of v8, /device:TPU:2, one launch (start us, length us, event | category | flops | bytes accessed | tf_op | source)
XLA Modules:
  0.0 132.8 jit_solution(3954468866140451036)
XLA Ops:
  0.6 0.1 collective-permute-start.1
  0.8 0.1 stack.77.where_ref
  0.9 5.2 %pick.1 = (bf16[32,32,256]{2,1,0:T(8,128)(2,1)S(1)}, bf16[32,192,128]{2,1,0:T(8,128)(2,1)S(1)}) custom-call(s32[8]{0:T(128)S(1)} %stack.77.where_ref, s32[8,128]{1,0:T(8,128)} %bitcast.60, s32[1,512]{1,0:T(1,128)} %bitcast.63, bf16[1024,4096]{1,0:T(8,128)(2,1)} %near_ref.1), custom_call_target="tpu_custom_call" | custom-call | flops 2147483648 | bytes 8388608 | tf_op jit(solution)/shard_map/pick/pallas_call | solution.py:127
  6.1 1.2 copy-done
  7.3 17.4 %all_to_all.42.got_ref = bf16[32,32,256]{2,1,0:T(8,128)(2,1)S(1)} all-to-all(bf16[32,32,256]{2,1,0:T(8,128)(2,1)S(1)} %get-tuple-element.34), channel_id=1, replica_groups=mesh['pts'=32,'zq'=4,'zr'=2] {'pts'}, dimensions={0} | all-to-all | bytes 1048576 | tf_op jit(solution)/shard_map/all_to_all | solution.py:449
  24.7 5.4 %all-to-all-start.8 = ((bf16[32,192,128]{2,1,0:T(8,128)(2,1)}), bf16[32,192,128]{2,1,0:T(8,128)(2,1)S(1)}, u32[]{:S(2)}, u32[]{:S(2)}) async-start(bf16[32,192,128]{2,1,0:T(8,128)(2,1)} %copy-done), calls=%async_computation.8 | async-start | bytes 3145728 | tf_op jit(solution)/shard_map/all_to_all | solution.py:456
  30.1 1.0 place.1
  31.1 2.8 %collective-permute-start.10 = (bf16[128,256]{1,0:T(8,128)(2,1)S(1)}, bf16[128,256]{1,0:T(8,128)(2,1)S(1)}, u32[]{:S(2)}, u32[]{:S(2)}) collective-permute-start(bf16[128,256]{1,0:T(8,128)(2,1)S(1)} %get-tuple-element.37), channel_id=1, source_target_pairs={{0,48},{8,56},{16,0},{24,8},{32,16},{40,24},{48,32},{56,40},{64,11... | collective-permute-start | bytes 196616 | tf_op jit(solution)/shard_map/ppermute | solution.py:388
  33.9 0.9 collective-permute-start.9
  34.7 0.9 collective-permute-start.8
  35.6 15.5 %collective-permute-done.10 = bf16[128,256]{1,0:T(8,128)(2,1)S(1)} collective-permute-done((bf16[128,256]{1,0:T(8,128)(2,1)S(1)}, bf16[128,256]{1,0:T(8,128)(2,1)S(1)}, u32[]{:S(2)}, u32[]{:S(2)}) %collective-permute-start.10) | collective-permute-done | bytes 65568 | tf_op jit(solution)/shard_map/ppermute | solution.py:388
  51.1 1.9 %collective-permute-done.9 = bf16[128,256]{1,0:T(8,128)(2,1)S(1)} collective-permute-done((bf16[128,256]{1,0:T(8,128)(2,1)S(1)}, bf16[128,256]{1,0:T(8,128)(2,1)S(1)}, u32[]{:S(2)}, u32[]{:S(2)}) %collective-permute-start.9) | collective-permute-done | bytes 65568 | tf_op jit(solution)/shard_map/ppermute | solution.py:388
  53.0 0.5 collective-permute-done.8
  53.6 0.6 collective-permute-start.13
  54.2 2.4 %collective-permute-start.12 = (bf16[4,128,256]{2,1,0:T(8,128)(2,1)S(1)}, bf16[4,128,256]{2,1,0:T(8,128)(2,1)S(1)}, u32[]{:S(2)}, u32[]{:S(2)}) collective-permute-start(bf16[4,128,256]{2,1,0:T(8,128)(2,1)S(1)} %pad_maximum_fusion.2.refs_4_), channel_id=1, source_target_pairs={{0,128},{8,136},{16,144},{24,152},{32,160},{40,168},{48,176},{56,1... | collective-permute-start | bytes 786440 | tf_op jit(solution)/shard_map/ppermute | solution.py:388
  56.6 1.1 collective-permute-start.4
  57.7 2.2 %collective-permute-start.3 = (bf16[128,256]{1,0:T(8,128)(2,1)S(1)}, bf16[128,256]{1,0:T(8,128)(2,1)S(1)}, u32[]{:S(2)}, u32[]{:S(2)}) collective-permute-start(bf16[128,256]{1,0:T(8,128)(2,1)S(1)} %get-tuple-element.36), channel_id=1, source_target_pairs={{0,128},{8,136},{16,144},{24,152},{32,160},{40,168},{48,176},{56,1... | collective-permute-start | bytes 196616 | tf_op jit(solution)/shard_map/ppermute | solution.py:388
  59.9 7.5 %collective-permute-done.4 = bf16[128,256]{1,0:T(8,128)(2,1)S(1)} collective-permute-done((bf16[128,256]{1,0:T(8,128)(2,1)S(1)}, bf16[128,256]{1,0:T(8,128)(2,1)S(1)}, u32[]{:S(2)}, u32[]{:S(2)}) %collective-permute-start.4) | collective-permute-done | bytes 65568 | tf_op jit(solution)/shard_map/ppermute | solution.py:388
  67.4 3.5 %collective-permute-start.2 = (bf16[128,256]{1,0:T(8,128)(2,1)S(1)}, bf16[128,256]{1,0:T(8,128)(2,1)S(1)}, u32[]{:S(2)}, u32[]{:S(2)}) collective-permute-start(bf16[128,256]{1,0:T(8,128)(2,1)S(1)} %get-tuple-element.36), channel_id=1, source_target_pairs={{0,64},{8,72},{16,80},{24,88},{32,96},{40,104},{48,112},{56,120},{... | collective-permute-start | bytes 196616 | tf_op jit(solution)/shard_map/ppermute | solution.py:388
  70.9 0.1 collective-permute-done.3
  71.0 1.9 %collective-permute-done.2 = bf16[128,256]{1,0:T(8,128)(2,1)S(1)} collective-permute-done((bf16[128,256]{1,0:T(8,128)(2,1)S(1)}, bf16[128,256]{1,0:T(8,128)(2,1)S(1)}, u32[]{:S(2)}, u32[]{:S(2)}) %collective-permute-start.2) | collective-permute-done | bytes 65568 | tf_op jit(solution)/shard_map/ppermute | solution.py:388
  72.9 2.8 %collective-permute-start.11 = (bf16[4,128,256]{2,1,0:T(8,128)(2,1)S(1)}, bf16[4,128,256]{2,1,0:T(8,128)(2,1)S(1)}, u32[]{:S(2)}, u32[]{:S(2)}) collective-permute-start(bf16[4,128,256]{2,1,0:T(8,128)(2,1)S(1)} %pad_maximum_fusion.2.refs_4_), channel_id=1, source_target_pairs={{0,64},{8,72},{16,80},{24,88},{32,96},{40,104},{48,112},{56,120},{... | collective-permute-start | bytes 786440 | tf_op jit(solution)/shard_map/ppermute | solution.py:388
  75.7 0.0 collective-permute-done
  75.7 1.9 %collective-permute-start.7 = (bf16[4,128,256]{2,1,0:T(8,128)(2,1)S(1)}, bf16[4,128,256]{2,1,0:T(8,128)(2,1)S(1)}, u32[]{:S(2)}, u32[]{:S(2)}) collective-permute-start(bf16[4,128,256]{2,1,0:T(8,128)(2,1)S(1)} %pad_maximum_fusion.1.refs_0_), channel_id=1, source_target_pairs={{0,48},{8,56},{16,0},{24,8},{32,16},{40,24},{48,32},{56,40},{64,11... | collective-permute-start | bytes 786440 | tf_op jit(solution)/shard_map/ppermute | solution.py:388
  77.7 1.5 %collective-permute-start.6 = (bf16[4,128,256]{2,1,0:T(8,128)(2,1)S(1)}, bf16[4,128,256]{2,1,0:T(8,128)(2,1)S(1)}, u32[]{:S(2)}, u32[]{:S(2)}) collective-permute-start(bf16[4,128,256]{2,1,0:T(8,128)(2,1)S(1)} %pad_maximum_fusion.1.refs_0_), channel_id=1, source_target_pairs={{0,32},{8,40},{16,48},{24,56},{32,0},{40,8},{48,16},{56,24},{64,96... | collective-permute-start | bytes 786440 | tf_op jit(solution)/shard_map/ppermute | solution.py:388
  79.2 0.0 collective-permute-start.5
  79.2 1.8 %collective-permute-done.11.refs_5_ = bf16[4,128,256]{2,1,0:T(8,128)(2,1)S(1)} collective-permute-done((bf16[4,128,256]{2,1,0:T(8,128)(2,1)S(1)}, bf16[4,128,256]{2,1,0:T(8,128)(2,1)S(1)}, u32[]{:S(2)}, u32[]{:S(2)}) %collective-permute-start.11) | collective-permute-done | bytes 262176 | tf_op jit(solution)/shard_map/ppermute | solution.py:388
  81.0 4.0 %collective-permute-done.7.refs_3_ = bf16[4,128,256]{2,1,0:T(8,128)(2,1)S(1)} collective-permute-done((bf16[4,128,256]{2,1,0:T(8,128)(2,1)S(1)}, bf16[4,128,256]{2,1,0:T(8,128)(2,1)S(1)}, u32[]{:S(2)}, u32[]{:S(2)}) %collective-permute-start.7) | collective-permute-done | bytes 262176 | tf_op jit(solution)/shard_map/ppermute | solution.py:388
  85.0 3.1 %collective-permute-done.6.refs_2_ = bf16[4,128,256]{2,1,0:T(8,128)(2,1)S(1)} collective-permute-done((bf16[4,128,256]{2,1,0:T(8,128)(2,1)S(1)}, bf16[4,128,256]{2,1,0:T(8,128)(2,1)S(1)}, u32[]{:S(2)}, u32[]{:S(2)}) %collective-permute-start.6) | collective-permute-done | bytes 262176 | tf_op jit(solution)/shard_map/ppermute | solution.py:388
  88.1 2.8 %collective-permute-done.5.refs_1_ = bf16[4,128,256]{2,1,0:T(8,128)(2,1)S(1)} collective-permute-done((bf16[4,128,256]{2,1,0:T(8,128)(2,1)S(1)}, bf16[4,128,256]{2,1,0:T(8,128)(2,1)S(1)}, u32[]{:S(2)}, u32[]{:S(2)}) %collective-permute-start.5) | collective-permute-done | bytes 262176 | tf_op jit(solution)/shard_map/ppermute | solution.py:388
  90.8 8.4 %scored.1 = f32[4,1024]{1,0:T(4,128)S(1)} custom-call(s32[8]{0:T(128)S(1)} %stack.77.where_ref, s32[2,1024]{1,0:T(2,128)S(1)} %pad_add_fusion.assign_ref, f32[1,256]{1,0:T(1,128)S(1)} %get-tuple-element.35.mark_ref, bf16[1024,4096]{1,0:T(8,128)(2,1)} %near_ref.1, bf16[1024,4096]{1,0:T(8,128)(2,1)} %collective-permute-done.1.far_ref, ...), custom_call_target="tpu_custom_call" | custom-call | flops 4294967296 | bytes 16777216 | tf_op jit(solution)/shard_map/scored/pallas_call | solution.py:301
  99.2 0.0 copy-start.2
  99.2 7.3 %collective-permute-start.14 = (f32[4,1024]{1,0:T(4,128)S(1)}, f32[4,1024]{1,0:T(4,128)S(1)}, u32[]{:S(2)}, u32[]{:S(2)}) collective-permute-start(f32[4,1024]{1,0:T(4,128)S(1)} %scored.1), channel_id=1, source_target_pairs={{0,4},{1,5},{2,6},{3,7},{4,0},{5,1},{6,2},{7,3},{8,12},{9,13},{10,... | collective-permute-start | bytes 49160 | tf_op jit(solution)/shard_map/ppermute | solution.py:397
  106.5 1.7 %collective-permute-done.14 = f32[4,1024]{1,0:T(4,128)S(1)} collective-permute-done((f32[4,1024]{1,0:T(4,128)S(1)}, f32[4,1024]{1,0:T(4,128)S(1)}, u32[]{:S(2)}, u32[]{:S(2)}) %collective-permute-start.14) | collective-permute-done | bytes 16416 | tf_op jit(solution)/shard_map/ppermute | solution.py:397
  108.2 2.0 %collective-permute-start.15 = (f32[4,1024]{1,0:T(4,128)S(1)}, f32[4,1024]{1,0:T(4,128)S(1)}, u32[]{:S(2)}, u32[]{:S(2)}) collective-permute-start(f32[4,1024]{1,0:T(4,128)S(1)} %max.6), channel_id=1, source_target_pairs={{0,2},{1,3},{2,0},{3,1},{4,6},{5,7},{6,4},{7,5},{8,10},{9,11},{10,... | collective-permute-start | bytes 49160 | tf_op jit(solution)/shard_map/ppermute | solution.py:397
  110.2 2.6 %collective-permute-done.15 = f32[4,1024]{1,0:T(4,128)S(1)} collective-permute-done((f32[4,1024]{1,0:T(4,128)S(1)}, f32[4,1024]{1,0:T(4,128)S(1)}, u32[]{:S(2)}, u32[]{:S(2)}) %collective-permute-start.15) | collective-permute-done | bytes 16416 | tf_op jit(solution)/shard_map/ppermute | solution.py:397
  112.9 0.9 broadcast_in_dim.16
  113.8 6.1 %all-to-all-start.7 = ((f32[64,2,1024]{2,1,0:T(2,128)}), f32[64,2,1024]{2,1,0:T(2,128)S(1)}, u32[]{:S(2)}, u32[]{:S(2)}) async-start(f32[64,2,1024]{2,1,0:T(2,128)} %broadcast_in_dim.16), calls=%async_computation.7 | async-start | bytes 1048576 | tf_op jit(solution)/shard_map/all_to_all | solution.py:462
  119.9 1.3 collective-permute-start.18
  121.2 0.4 collective-permute-start.17
  121.6 0.6 collective-permute-start.16
  122.1 4.8 %sums.1 = (f32[128,512]{1,0:T(8,128)}, f32[1,512]{1,0:T(1,128)}) custom-call(bf16[32,192,128]{2,1,0:T(8,128)(2,1)S(1)} %all-to-all-done.8.got_ref), custom_call_target="tpu_custom_call" | custom-call | flops 1610612736 | bytes 1572864 | tf_op jit(solution)/shard_map/sums/pallas_call | solution.py:238
  127.0 0.6 collective-permute-done.18.d_ref
  127.6 0.9 collective-permute-done.16.b_ref
  128.5 0.6 closing.1
  129.8 2.2 %all-to-all-done.7 = f32[64,2,1024]{2,1,0:T(2,128)S(1)} async-done(((f32[64,2,1024]{2,1,0:T(2,128)}), f32[64,2,1024]{2,1,0:T(2,128)S(1)}, u32[]{:S(2)}, u32[]{:S(2)}) %all-to-all-start.7) | async-done | bytes 524320 | tf_op jit(solution)/shard_map/all_to_all | solution.py:462
  132.0 0.7 conditional.1
  132.0 0.7 cover.1
  (16 shorter events, 0.1 us)
Async XLA Ops:
  0.6 90.2 %collective-permute-start.1 = (bf16[1024,4096]{1,0:T(8,128)(2,1)}, bf16[1024,4096]{1,0:T(8,128)(2,1)}, u32[]{:S(2)}, u32[]{:S(2)}) collective-permute-start(bf16[1024,4096]{1,0:T(8,128)(2,1)} %near_ref.1), channel_id=1, source_target_pairs={{0,8},{8,0},{16,24},{24,16},{32,40},{40,32},{48,56},{56,48},{64,72... | collective-permute-start | bytes 25165832 | tf_op jit(solution)/shard_map/ppermute | solution.py:388
  6.1 1.2 copy-start
  7.3 63.7 %copy-start.1 = (s32[1024]{0:T(1024)S(1)}, s32[1024]{0:T(1024)}, u32[]{:S(2)}) copy-start(s32[1024]{0:T(1024)} %param.6) | copy-start | bytes 12292
  24.7 88.2 %all-to-all-start.8 = ((bf16[32,192,128]{2,1,0:T(8,128)(2,1)}), bf16[32,192,128]{2,1,0:T(8,128)(2,1)S(1)}, u32[]{:S(2)}, u32[]{:S(2)}) async-start(bf16[32,192,128]{2,1,0:T(8,128)(2,1)} %copy-done), calls=%async_computation.8 | async-start | bytes 3145728 | tf_op jit(solution)/shard_map/all_to_all | solution.py:456
  31.1 20.0 %collective-permute-start.10 = (bf16[128,256]{1,0:T(8,128)(2,1)S(1)}, bf16[128,256]{1,0:T(8,128)(2,1)S(1)}, u32[]{:S(2)}, u32[]{:S(2)}) collective-permute-start(bf16[128,256]{1,0:T(8,128)(2,1)S(1)} %get-tuple-element.37), channel_id=1, source_target_pairs={{0,48},{8,56},{16,0},{24,8},{32,16},{40,24},{48,32},{56,40},{64,11... | collective-permute-start | bytes 196616 | tf_op jit(solution)/shard_map/ppermute | solution.py:388
  33.9 19.1 %collective-permute-start.9 = (bf16[128,256]{1,0:T(8,128)(2,1)S(1)}, bf16[128,256]{1,0:T(8,128)(2,1)S(1)}, u32[]{:S(2)}, u32[]{:S(2)}) collective-permute-start(bf16[128,256]{1,0:T(8,128)(2,1)S(1)} %get-tuple-element.37), channel_id=1, source_target_pairs={{0,32},{8,40},{16,48},{24,56},{32,0},{40,8},{48,16},{56,24},{64,96... | collective-permute-start | bytes 196616 | tf_op jit(solution)/shard_map/ppermute | solution.py:388
  34.7 18.8 %collective-permute-start.8 = (bf16[128,256]{1,0:T(8,128)(2,1)S(1)}, bf16[128,256]{1,0:T(8,128)(2,1)S(1)}, u32[]{:S(2)}, u32[]{:S(2)}) collective-permute-start(bf16[128,256]{1,0:T(8,128)(2,1)S(1)} %get-tuple-element.37), channel_id=1, source_target_pairs={{0,16},{8,24},{16,32},{24,40},{32,48},{40,56},{48,0},{56,8},{64,80... | collective-permute-start | bytes 196616 | tf_op jit(solution)/shard_map/ppermute | solution.py:388
  53.6 24.1 %collective-permute-start.13 = (bf16[4,128,256]{2,1,0:T(8,128)(2,1)S(1)}, bf16[4,128,256]{2,1,0:T(8,128)(2,1)S(1)}, u32[]{:S(2)}, u32[]{:S(2)}) collective-permute-start(bf16[4,128,256]{2,1,0:T(8,128)(2,1)S(1)} %pad_maximum_fusion.2.refs_4_), channel_id=1, source_target_pairs={{0,192},{8,200},{16,208},{24,216},{32,224},{40,232},{48,240},{56,2... | collective-permute-start | bytes 786440 | tf_op jit(solution)/shard_map/ppermute | solution.py:388
  54.2 25.0 %collective-permute-start.12 = (bf16[4,128,256]{2,1,0:T(8,128)(2,1)S(1)}, bf16[4,128,256]{2,1,0:T(8,128)(2,1)S(1)}, u32[]{:S(2)}, u32[]{:S(2)}) collective-permute-start(bf16[4,128,256]{2,1,0:T(8,128)(2,1)S(1)} %pad_maximum_fusion.2.refs_4_), channel_id=1, source_target_pairs={{0,128},{8,136},{16,144},{24,152},{32,160},{40,168},{48,176},{56,1... | collective-permute-start | bytes 786440 | tf_op jit(solution)/shard_map/ppermute | solution.py:388
  56.6 10.8 %collective-permute-start.4 = (bf16[128,256]{1,0:T(8,128)(2,1)S(1)}, bf16[128,256]{1,0:T(8,128)(2,1)S(1)}, u32[]{:S(2)}, u32[]{:S(2)}) collective-permute-start(bf16[128,256]{1,0:T(8,128)(2,1)S(1)} %get-tuple-element.36), channel_id=1, source_target_pairs={{0,192},{8,200},{16,208},{24,216},{32,224},{40,232},{48,240},{56,2... | collective-permute-start | bytes 196616 | tf_op jit(solution)/shard_map/ppermute | solution.py:388
  57.7 13.3 %collective-permute-start.3 = (bf16[128,256]{1,0:T(8,128)(2,1)S(1)}, bf16[128,256]{1,0:T(8,128)(2,1)S(1)}, u32[]{:S(2)}, u32[]{:S(2)}) collective-permute-start(bf16[128,256]{1,0:T(8,128)(2,1)S(1)} %get-tuple-element.36), channel_id=1, source_target_pairs={{0,128},{8,136},{16,144},{24,152},{32,160},{40,168},{48,176},{56,1... | collective-permute-start | bytes 196616 | tf_op jit(solution)/shard_map/ppermute | solution.py:388
  67.4 5.5 %collective-permute-start.2 = (bf16[128,256]{1,0:T(8,128)(2,1)S(1)}, bf16[128,256]{1,0:T(8,128)(2,1)S(1)}, u32[]{:S(2)}, u32[]{:S(2)}) collective-permute-start(bf16[128,256]{1,0:T(8,128)(2,1)S(1)} %get-tuple-element.36), channel_id=1, source_target_pairs={{0,64},{8,72},{16,80},{24,88},{32,96},{40,104},{48,112},{56,120},{... | collective-permute-start | bytes 196616 | tf_op jit(solution)/shard_map/ppermute | solution.py:388
  71.0 4.7 %collective-permute-start = (s32[1024]{0:T(1024)S(1)}, s32[1024]{0:T(1024)S(1)}, u32[]{:S(2)}, u32[]{:S(2)}) collective-permute-start(s32[1024]{0:T(1024)S(1)} %copy-done.1), channel_id=1, source_target_pairs={{0,8},{8,0},{16,24},{24,16},{32,40},{40,32},{48,56},{56,48},{64,72... | collective-permute-start | bytes 12296 | tf_op jit(solution)/shard_map/ppermute | solution.py:388
  72.9 8.0 %collective-permute-start.11 = (bf16[4,128,256]{2,1,0:T(8,128)(2,1)S(1)}, bf16[4,128,256]{2,1,0:T(8,128)(2,1)S(1)}, u32[]{:S(2)}, u32[]{:S(2)}) collective-permute-start(bf16[4,128,256]{2,1,0:T(8,128)(2,1)S(1)} %pad_maximum_fusion.2.refs_4_), channel_id=1, source_target_pairs={{0,64},{8,72},{16,80},{24,88},{32,96},{40,104},{48,112},{56,120},{... | collective-permute-start | bytes 786440 | tf_op jit(solution)/shard_map/ppermute | solution.py:388
  75.7 9.3 %collective-permute-start.7 = (bf16[4,128,256]{2,1,0:T(8,128)(2,1)S(1)}, bf16[4,128,256]{2,1,0:T(8,128)(2,1)S(1)}, u32[]{:S(2)}, u32[]{:S(2)}) collective-permute-start(bf16[4,128,256]{2,1,0:T(8,128)(2,1)S(1)} %pad_maximum_fusion.1.refs_0_), channel_id=1, source_target_pairs={{0,48},{8,56},{16,0},{24,8},{32,16},{40,24},{48,32},{56,40},{64,11... | collective-permute-start | bytes 786440 | tf_op jit(solution)/shard_map/ppermute | solution.py:388
  77.7 10.4 %collective-permute-start.6 = (bf16[4,128,256]{2,1,0:T(8,128)(2,1)S(1)}, bf16[4,128,256]{2,1,0:T(8,128)(2,1)S(1)}, u32[]{:S(2)}, u32[]{:S(2)}) collective-permute-start(bf16[4,128,256]{2,1,0:T(8,128)(2,1)S(1)} %pad_maximum_fusion.1.refs_0_), channel_id=1, source_target_pairs={{0,32},{8,40},{16,48},{24,56},{32,0},{40,8},{48,16},{56,24},{64,96... | collective-permute-start | bytes 786440 | tf_op jit(solution)/shard_map/ppermute | solution.py:388
  79.2 11.7 %collective-permute-start.5 = (bf16[4,128,256]{2,1,0:T(8,128)(2,1)S(1)}, bf16[4,128,256]{2,1,0:T(8,128)(2,1)S(1)}, u32[]{:S(2)}, u32[]{:S(2)}) collective-permute-start(bf16[4,128,256]{2,1,0:T(8,128)(2,1)S(1)} %pad_maximum_fusion.1.refs_0_), channel_id=1, source_target_pairs={{0,16},{8,24},{16,32},{24,40},{32,48},{40,56},{48,0},{56,8},{64,80... | collective-permute-start | bytes 786440 | tf_op jit(solution)/shard_map/ppermute | solution.py:388
  99.2 32.8 %copy-start.2 = (s32[512]{0:T(512)S(1)}, s32[512]{0:T(512)}, u32[]{:S(2)}) copy-start(s32[512]{0:T(512)} %param.7) | copy-start | bytes 6148
  99.2 9.0 %collective-permute-start.14 = (f32[4,1024]{1,0:T(4,128)S(1)}, f32[4,1024]{1,0:T(4,128)S(1)}, u32[]{:S(2)}, u32[]{:S(2)}) collective-permute-start(f32[4,1024]{1,0:T(4,128)S(1)} %scored.1), channel_id=1, source_target_pairs={{0,4},{1,5},{2,6},{3,7},{4,0},{5,1},{6,2},{7,3},{8,12},{9,13},{10,... | collective-permute-start | bytes 49160 | tf_op jit(solution)/shard_map/ppermute | solution.py:397
  108.2 4.6 %collective-permute-start.15 = (f32[4,1024]{1,0:T(4,128)S(1)}, f32[4,1024]{1,0:T(4,128)S(1)}, u32[]{:S(2)}, u32[]{:S(2)}) collective-permute-start(f32[4,1024]{1,0:T(4,128)S(1)} %max.6), channel_id=1, source_target_pairs={{0,2},{1,3},{2,0},{3,1},{4,6},{5,7},{6,4},{7,5},{8,10},{9,11},{10,... | collective-permute-start | bytes 49160 | tf_op jit(solution)/shard_map/ppermute | solution.py:397
  113.8 18.2 %all-to-all-start.7 = ((f32[64,2,1024]{2,1,0:T(2,128)}), f32[64,2,1024]{2,1,0:T(2,128)S(1)}, u32[]{:S(2)}, u32[]{:S(2)}) async-start(f32[64,2,1024]{2,1,0:T(2,128)} %broadcast_in_dim.16), calls=%async_computation.7 | async-start | bytes 1048576 | tf_op jit(solution)/shard_map/all_to_all | solution.py:462
  119.9 7.7 %collective-permute-start.18 = (f32[4,1024]{1,0:T(4,128)S(1)}, f32[4,1024]{1,0:T(4,128)S(1)}, u32[]{:S(2)}, u32[]{:S(2)}) collective-permute-start(f32[4,1024]{1,0:T(4,128)S(1)} %max.7.a_ref), channel_id=1, source_target_pairs={{0,9},{1,8},{2,11},{3,10},{4,13},{5,12},{6,15},{7,14},{8,1},{9,0},... | collective-permute-start | bytes 49160 | tf_op jit(solution)/shard_map/ppermute | solution.py:397
  121.2 6.4 %collective-permute-start.17 = (f32[4,1024]{1,0:T(4,128)S(1)}, f32[4,1024]{1,0:T(4,128)S(1)}, u32[]{:S(2)}, u32[]{:S(2)}) collective-permute-start(f32[4,1024]{1,0:T(4,128)S(1)} %max.7.a_ref), channel_id=1, source_target_pairs={{0,8},{1,9},{2,10},{3,11},{4,12},{5,13},{6,14},{7,15},{8,0},{9,1},... | collective-permute-start | bytes 49160 | tf_op jit(solution)/shard_map/ppermute | solution.py:397
  121.6 6.9 %collective-permute-start.16 = (f32[4,1024]{1,0:T(4,128)S(1)}, f32[4,1024]{1,0:T(4,128)S(1)}, u32[]{:S(2)}, u32[]{:S(2)}) collective-permute-start(f32[4,1024]{1,0:T(4,128)S(1)} %max.7.a_ref), channel_id=1, source_target_pairs={{0,1},{1,0},{2,3},{3,2},{4,5},{5,4},{6,7},{7,6},{8,9},{9,8},{10,11... | collective-permute-start | bytes 49160 | tf_op jit(solution)/shard_map/ppermute | solution.py:397

commit v9 on v8

--- a/solution.py
+++ b/solution.py
@@ -19,6 +19,7 @@
 SEL = GRAD_ROWS + 2 * MED_ROWS
 NONE = -1e30
 LOST = 1e30
+PTS = ("chip", "core")
 MED = ("zq", "zr")
 CHIPS = 4
 
@@ -316,19 +317,43 @@
     )(where, assignments, marks, near, far, *parts)
 
 
-def closing_kernel(a_ref, b_ref, c_ref, d_ref, gap_ref, mark_ref):
+def merge_kernel(a_ref, b_ref, c_ref, d_ref, all_ref, send_ref):
     same = jnp.maximum(a_ref[...], b_ref[...])
     partner = jnp.maximum(c_ref[...], d_ref[...])
-    best = jnp.maximum(same[0:1], partner[1:2])
-    chosen = jnp.maximum(same[2:3], partner[3:4])
-    gap_ref[...] = best - chosen
-    mark_ref[0, 0] = jnp.where(jnp.max(chosen) > 0.5 * LOST, 1, 0)
-
-
-def closing(a, b, c, d):
+    turned = jnp.concatenate([partner[1:2], partner[0:1], partner[3:4], partner[2:3]], axis=0)
+    both = jnp.maximum(same, turned)
+    all_ref[...] = both
+    for i in range(send_ref.shape[0]):
+        send_ref[i] = both[:2]
+
+
+def merge(a, b, c, d, copies):
+    return pl.pallas_call(
+        merge_kernel,
+        in_specs=[pl.BlockSpec(memory_space=pltpu.VMEM)] * 4,
+        out_specs=[pl.BlockSpec(memory_space=pltpu.VMEM)] * 2,
+        out_shape=[
+            jax.ShapeDtypeStruct(a.shape, F32),
+            jax.ShapeDtypeStruct((copies, 2, a.shape[1]), F32),
+        ],
+        compiler_params=pltpu.CompilerParams(vmem_limit_bytes=4 * 2**20),
+        cost_estimate=pl.CostEstimate(
+            flops=4 * a.size, bytes_accessed=4 * copies * a.size, transcendentals=0
+        ),
+        name="merge",
+    )(a, b, c, d)
+
+
+def closing_kernel(a_ref, b_ref, gap_ref, mark_ref):
+    both = jnp.maximum(a_ref[...], b_ref[...])
+    gap_ref[...] = both[0:1] - both[2:3]
+    mark_ref[0, 0] = jnp.where(jnp.max(both[2:3]) > 0.5 * LOST, 1, 0)
+
+
+def closing(a, b):
     return pl.pallas_call(
         closing_kernel,
-        in_specs=[pl.BlockSpec(memory_space=pltpu.VMEM)] * 4,
+        in_specs=[pl.BlockSpec(memory_space=pltpu.VMEM)] * 2,
         out_specs=[
             pl.BlockSpec(memory_space=pltpu.VMEM),
             pl.BlockSpec(memory_space=pltpu.SMEM),
@@ -339,23 +364,22 @@
         ],
         compiler_params=pltpu.CompilerParams(vmem_limit_bytes=4 * 2**20),
         cost_estimate=pl.CostEstimate(
-            flops=a.size, bytes_accessed=16 * a.size, transcendentals=0
+            flops=a.size, bytes_accessed=8 * a.size, transcendentals=0
         ),
         name="closing",
-    )(a, b, c, d)
+    )(a, b)
 
 
 def cover_kernel(scale, got_ref, out_ref):
     total = jnp.zeros((1, got_ref.shape[2]), F32)
-    for i in range(0, got_ref.shape[0], 4):
-        one = jnp.maximum(got_ref[i], got_ref[i + 1])
-        two = jnp.maximum(got_ref[i + 2], got_ref[i + 3])
-        total = total + jnp.maximum(one[0:1], two[1:2]) + jnp.maximum(one[1:2], two[0:1])
+    for i in range(0, got_ref.shape[0], 2):
+        best = jnp.maximum(got_ref[i], got_ref[i + 1])
+        total = total + (best[0:1] + best[1:2])
     out_ref[0, 0] = jnp.sum(total) * scale
 
 
 def cover(got):
-    points = got.shape[0] // 2 * got.shape[2]
+    points = got.size // 2
     return pl.pallas_call(
         functools.partial(cover_kernel, 1.0 / points),
         in_specs=[pl.BlockSpec(memory_space=pltpu.VMEM)],
@@ -385,7 +409,7 @@
     for p in range(32):
         x, y, c = chip_of(p)
         pairs.append((p, (((x + dx) % 4) * 4 + (y + dy) % 4) * 2 + (c ^ dc)))
-    return lax.ppermute(array, "pts", pairs)
+    return lax.ppermute(array, PTS, pairs)
 
 
 def across(array, core, step, planes):
@@ -394,15 +418,15 @@
         for p in range(32)
         for z in range(planes)
     ]
-    return lax.ppermute(array, ("pts", *MED), pairs)
+    return lax.ppermute(array, (*PTS, *MED), pairs)
 
 
 def general(sketches, assignment, medoid_ids):
     row_count, feat_width = sketches.shape
     medoid_count = medoid_ids.shape[0]
-    pts_count = lax.axis_size("pts")
+    pts_count = lax.axis_size(PTS)
     part = feat_width // pts_count
-    pts_index = lax.axis_index("pts")
+    pts_index = lax.axis_index(PTS)
     med_index = lax.axis_index(MED)
     local_assign = assignment - med_index * medoid_count
     chosen = local_assign[:, None] == jnp.arange(medoid_count, dtype=I32)[None, :]
@@ -412,19 +436,19 @@
     terms = jnp.dot(picking.astype(BF), sketches, preferred_element_type=F32).astype(BF)
     terms = terms.reshape(medoid_count, pts_count, part).swapaxes(0, 1)
     piece = (
-        lax.all_to_all(terms, "pts", 0, 0, tiled=True).astype(F32).sum(axis=0).astype(BF)
+        lax.all_to_all(terms, PTS, 0, 0, tiled=True).astype(F32).sum(axis=0).astype(BF)
     )
-    everything = from_everyone(piece, "pts").swapaxes(0, 1).reshape(medoid_count, feat_width)
+    everything = from_everyone(piece, PTS).swapaxes(0, 1).reshape(medoid_count, feat_width)
     partial = lax.dot_general(
         sketches, one_hot, (((0,), (0,)), ((), ())), preferred_element_type=F32
     ).reshape(pts_count, part, medoid_count)
-    gradient_sums = lax.all_to_all(partial, "pts", 0, 0, tiled=True).sum(axis=0)
-    counts = from_everyone(jnp.sum(one_hot.astype(F32), axis=0), "pts").sum(axis=0)
+    gradient_sums = lax.all_to_all(partial, PTS, 0, 0, tiled=True).sum(axis=0)
+    counts = from_everyone(jnp.sum(one_hot.astype(F32), axis=0), PTS).sum(axis=0)
     scores = contract_last(sketches, everything) * (1.0 / feat_width)
     best = jnp.max(scores, axis=1)
     taken = jnp.max(jnp.where(chosen, scores, NONE), axis=1)
     both = from_everyone(jnp.stack([best, taken]), MED).max(axis=0)
-    cover = from_everyone(jnp.sum(both[0])[None], "pts").sum()
+    cover = from_everyone(jnp.sum(both[0])[None], PTS).sum()
     return both[0] - both[1], cover / (row_count * pts_count), counts, gradient_sums
 
 
@@ -432,8 +456,8 @@
     row_count, _ = sketches.shape
     medoid_count = medoid_ids.shape[0]
     half = medoid_count // 2
-    pts_count = lax.axis_size("pts")
-    p = lax.axis_index("pts")
+    pts_count = lax.axis_size(PTS)
+    p = lax.axis_index(PTS)
     m = lax.axis_index(MED)
     core = p % 2
     planes = lax.axis_size(MED)
@@ -446,31 +470,24 @@
     med_send, grad_send = pick(
         where, assignment, medoid_ids, sketches, pts_count
     )
-    med_got = lax.all_to_all(med_send, "pts", 0, 0, tiled=True)
+    med_got = lax.all_to_all(med_send, PTS, 0, 0, tiled=True)
     a, b, marks = place(where, med_got, half)
     pa = jnp.stack([a] + [shifted(a, k, 0, 0) for k in (1, 2, 3)])
     pb = jnp.stack([b] + [shifted(b, 0, k, 0) for k in (1, 2, 3)])
     qa = [pa, shifted(pa, 0, 1, 0)]
     qa = qa + [shifted(pa, 0, k, 0) for k in (2, 3)]
     qb = [pb] + [shifted(pb, k, 0, 0) for k in (1, 2, 3)]
-    grad_got = lax.all_to_all(grad_send, "pts", 0, 0, tiled=True)
+    grad_got = lax.all_to_all(grad_send, PTS, 0, 0, tiled=True)
     assignments = jnp.stack([assignment, far_assignment])
     stats = scored(where, assignments, marks, sketches, far, qa + qb)
     stats = jnp.maximum(stats, across(stats, 0, 4, planes))
-    stats = jnp.maximum(stats, across(stats, 0, 2, planes))
-    size = 2 * pts_count
-    everyone = lax.all_to_all(
-        jnp.broadcast_to(stats[None, :2], (size, 2, row_count)),
-        ("pts", MED[1]),
-        0,
-        0,
-        tiled=True,
-    )
+    near = across(stats, 0, 2, planes)
+    partner, both = across(stats, 1, 0, planes), across(stats, 1, 2, planes)
+    stats, send = merge(stats, near, partner, both, pts_count)
+    everyone = lax.all_to_all(send, (PTS[0], MED[1]), 0, 0, tiled=True)
     plane = across(stats, 0, 1, planes)
-    partner = across(stats, 1, 0, planes)
-    both = across(stats, 1, 1, planes)
     gradient_sums, counts = sums(grad_got, medoid_count, 0, 8)
-    gap, mark = closing(stats, plane, partner, both)
+    gap, mark = closing(stats, plane)
     full = mark[0, 0] > 0
 
     def fast():
@@ -482,10 +499,10 @@
 def solution(mesh):
     planes = mesh.shape["med"]
     mesh = jax.sharding.Mesh(
-        mesh.devices.reshape(-1, planes // 2, 2), ("pts", *MED)
+        mesh.devices.reshape(-1, 2, planes // 2, 2), (*PTS, *MED)
     )
-    in_specs = (P("pts", None), P("pts"), P(MED))
-    out_specs = (P("pts"), P(), P(MED), P("pts", MED))
+    in_specs = (P(PTS, None), P(PTS), P(MED))
+    out_specs = (P(PTS), P(), P(MED), P(PTS, MED))
     return jax.shard_map(
         shards, mesh=mesh, in_specs=in_specs, out_specs=out_specs, check_vma=False
     )

time: 134 us -> 132 us (0.985)
  waiting for transfers between devices: 47.2 us -> 44.6 us
    all_to_all x2, waiting for transfers between devices: 2.18 us -> 0.01 us  [the longest x1 0.01 us: shards(): grad_got = lax.all_to_all(grad_send, PTS, 0, 0, tiled=True)]
  transfers between devices with their start and end apart: 21 -> 21, of which waited for: 15 -> 13; matrix products, arithmetic and copies ran while one was open for 0% -> 0% of each run, Pallas kernels for 15% -> 16%
where the time goes in v9:
time: 132 us; the launch traced here: 131 us
  waiting for transfers between devices  44.6 us (34%)
  starting transfers between devices  44.5 us (34%)
  Pallas kernels  21.4 us (16%)
  blocking collectives  17.4 us (13%)
  between operations  1.62 us (1%)
    ppermute x14, waiting for transfers between devices, shifted(): return lax.ppermute(array, PTS, pairs)  39.1 us
    ppermute x14, starting transfers between devices, shifted(): return lax.ppermute(array, PTS, pairs)  20.6 us
    all_to_all x1, blocking collectives, shards(): med_got = lax.all_to_all(med_send, PTS, 0, 0, tiled=True)  17.4 us
    ppermute x5, starting transfers between devices, across(): return lax.ppermute(array, (*PTS, *MED), pairs)  11.9 us
    pallas_call x1, Pallas kernels, scored(): pl.pallas_call(functools.partial(score_kernel, 1.0 / feats), in_specs=[pl...  8.36 us
    all_to_all x1, starting transfers between devices, shards(): everyone = lax.all_to_all(send, (PTS[0], MED[1]), 0, 0, tiled=True)  6.62 us
    ppermute x5, waiting for transfers between devices, across(): return lax.ppermute(array, (*PTS, *MED), pairs)  5.44 us
    all_to_all x1, starting transfers between devices, shards(): grad_got = lax.all_to_all(grad_send, PTS, 0, 0, tiled=True)  5.42 us
  transfers between devices with their start and end apart: 21, of which 13 were waited for; matrix products, arithmetic and copies ran while one was open for 0% of the time, Pallas kernels for 16%

profile of v9, /device:TPU:2, one launch (start us, length us, event | category | flops | bytes accessed | tf_op | source)
XLA Modules:
  0.0 130.9 jit_solution(5429191787379273949)
XLA Ops:
  0.6 0.1 collective-permute-start.1
  0.8 0.1 stack.77.where_ref
  0.9 5.2 %pick.1 = (bf16[32,32,256]{2,1,0:T(8,128)(2,1)S(1)}, bf16[32,192,128]{2,1,0:T(8,128)(2,1)S(1)}) custom-call(s32[8]{0:T(128)S(1)} %stack.77.where_ref, s32[8,128]{1,0:T(8,128)} %bitcast.60, s32[1,512]{1,0:T(1,128)} %bitcast.63, bf16[1024,4096]{1,0:T(8,128)(2,1)} %near_ref.1), custom_call_target="tpu_custom_call" | custom-call | flops 2147483648 | bytes 8388608 | tf_op jit(solution)/shard_map/pick/pallas_call | solution.py:128
  6.1 1.2 copy-done
  7.3 17.4 %all_to_all.42.got_ref = bf16[32,32,256]{2,1,0:T(8,128)(2,1)S(1)} all-to-all(bf16[32,32,256]{2,1,0:T(8,128)(2,1)S(1)} %get-tuple-element.36), channel_id=1, replica_groups=mesh['chip'=16,'core'=2,'zq'=4,'zr'=2] {'chip','core'}, dimensions={0} | all-to-all | bytes 1048576 | tf_op jit(solution)/shard_map/all_to_all | solution.py:473
  24.7 5.4 %all-to-all-start.8 = ((bf16[32,192,128]{2,1,0:T(8,128)(2,1)}), bf16[32,192,128]{2,1,0:T(8,128)(2,1)S(1)}, u32[]{:S(2)}, u32[]{:S(2)}) async-start(bf16[32,192,128]{2,1,0:T(8,128)(2,1)} %copy-done), calls=%async_computation.8 | async-start | bytes 3145728 | tf_op jit(solution)/shard_map/all_to_all | solution.py:480
  30.1 1.0 place.1
  31.1 2.8 %collective-permute-start.10 = (bf16[128,256]{1,0:T(8,128)(2,1)S(1)}, bf16[128,256]{1,0:T(8,128)(2,1)S(1)}, u32[]{:S(2)}, u32[]{:S(2)}) collective-permute-start(bf16[128,256]{1,0:T(8,128)(2,1)S(1)} %get-tuple-element.39), channel_id=1, source_target_pairs={{0,48},{8,56},{16,0},{24,8},{32,16},{40,24},{48,32},{56,40},{64,11... | collective-permute-start | bytes 196616 | tf_op jit(solution)/shard_map/ppermute | solution.py:412
  33.9 0.9 collective-permute-start.9
  34.7 0.9 collective-permute-start.8
  35.6 15.5 %collective-permute-done.10 = bf16[128,256]{1,0:T(8,128)(2,1)S(1)} collective-permute-done((bf16[128,256]{1,0:T(8,128)(2,1)S(1)}, bf16[128,256]{1,0:T(8,128)(2,1)S(1)}, u32[]{:S(2)}, u32[]{:S(2)}) %collective-permute-start.10) | collective-permute-done | bytes 65568 | tf_op jit(solution)/shard_map/ppermute | solution.py:412
  51.1 1.9 %collective-permute-done.9 = bf16[128,256]{1,0:T(8,128)(2,1)S(1)} collective-permute-done((bf16[128,256]{1,0:T(8,128)(2,1)S(1)}, bf16[128,256]{1,0:T(8,128)(2,1)S(1)}, u32[]{:S(2)}, u32[]{:S(2)}) %collective-permute-start.9) | collective-permute-done | bytes 65568 | tf_op jit(solution)/shard_map/ppermute | solution.py:412
  53.0 0.5 collective-permute-done.8
  53.6 0.6 collective-permute-start.13
  54.2 2.4 %collective-permute-start.12 = (bf16[4,128,256]{2,1,0:T(8,128)(2,1)S(1)}, bf16[4,128,256]{2,1,0:T(8,128)(2,1)S(1)}, u32[]{:S(2)}, u32[]{:S(2)}) collective-permute-start(bf16[4,128,256]{2,1,0:T(8,128)(2,1)S(1)} %pad_maximum_fusion.2.refs_4_), channel_id=1, source_target_pairs={{0,128},{8,136},{16,144},{24,152},{32,160},{40,168},{48,176},{56,1... | collective-permute-start | bytes 786440 | tf_op jit(solution)/shard_map/ppermute | solution.py:412
  56.6 1.1 collective-permute-start.4
  57.7 2.2 %collective-permute-start.3 = (bf16[128,256]{1,0:T(8,128)(2,1)S(1)}, bf16[128,256]{1,0:T(8,128)(2,1)S(1)}, u32[]{:S(2)}, u32[]{:S(2)}) collective-permute-start(bf16[128,256]{1,0:T(8,128)(2,1)S(1)} %get-tuple-element.38), channel_id=1, source_target_pairs={{0,128},{8,136},{16,144},{24,152},{32,160},{40,168},{48,176},{56,1... | collective-permute-start | bytes 196616 | tf_op jit(solution)/shard_map/ppermute | solution.py:412
  59.9 7.5 %collective-permute-done.4 = bf16[128,256]{1,0:T(8,128)(2,1)S(1)} collective-permute-done((bf16[128,256]{1,0:T(8,128)(2,1)S(1)}, bf16[128,256]{1,0:T(8,128)(2,1)S(1)}, u32[]{:S(2)}, u32[]{:S(2)}) %collective-permute-start.4) | collective-permute-done | bytes 65568 | tf_op jit(solution)/shard_map/ppermute | solution.py:412
  67.4 3.5 %collective-permute-start.2 = (bf16[128,256]{1,0:T(8,128)(2,1)S(1)}, bf16[128,256]{1,0:T(8,128)(2,1)S(1)}, u32[]{:S(2)}, u32[]{:S(2)}) collective-permute-start(bf16[128,256]{1,0:T(8,128)(2,1)S(1)} %get-tuple-element.38), channel_id=1, source_target_pairs={{0,64},{8,72},{16,80},{24,88},{32,96},{40,104},{48,112},{56,120},{... | collective-permute-start | bytes 196616 | tf_op jit(solution)/shard_map/ppermute | solution.py:412
  70.9 0.1 collective-permute-done.3
  71.0 0.0 collective-permute-start
  71.0 1.9 %collective-permute-done.2 = bf16[128,256]{1,0:T(8,128)(2,1)S(1)} collective-permute-done((bf16[128,256]{1,0:T(8,128)(2,1)S(1)}, bf16[128,256]{1,0:T(8,128)(2,1)S(1)}, u32[]{:S(2)}, u32[]{:S(2)}) %collective-permute-start.2) | collective-permute-done | bytes 65568 | tf_op jit(solution)/shard_map/ppermute | solution.py:412
  72.9 2.8 %collective-permute-start.11 = (bf16[4,128,256]{2,1,0:T(8,128)(2,1)S(1)}, bf16[4,128,256]{2,1,0:T(8,128)(2,1)S(1)}, u32[]{:S(2)}, u32[]{:S(2)}) collective-permute-start(bf16[4,128,256]{2,1,0:T(8,128)(2,1)S(1)} %pad_maximum_fusion.2.refs_4_), channel_id=1, source_target_pairs={{0,64},{8,72},{16,80},{24,88},{32,96},{40,104},{48,112},{56,120},{... | collective-permute-start | bytes 786440 | tf_op jit(solution)/shard_map/ppermute | solution.py:412
  75.7 1.9 %collective-permute-start.7 = (bf16[4,128,256]{2,1,0:T(8,128)(2,1)S(1)}, bf16[4,128,256]{2,1,0:T(8,128)(2,1)S(1)}, u32[]{:S(2)}, u32[]{:S(2)}) collective-permute-start(bf16[4,128,256]{2,1,0:T(8,128)(2,1)S(1)} %pad_maximum_fusion.1.refs_0_), channel_id=1, source_target_pairs={{0,48},{8,56},{16,0},{24,8},{32,16},{40,24},{48,32},{56,40},{64,11... | collective-permute-start | bytes 786440 | tf_op jit(solution)/shard_map/ppermute | solution.py:412
  77.6 0.0 collective-permute-done.13.refs_7_
  77.7 1.5 %collective-permute-start.6 = (bf16[4,128,256]{2,1,0:T(8,128)(2,1)S(1)}, bf16[4,128,256]{2,1,0:T(8,128)(2,1)S(1)}, u32[]{:S(2)}, u32[]{:S(2)}) collective-permute-start(bf16[4,128,256]{2,1,0:T(8,128)(2,1)S(1)} %pad_maximum_fusion.1.refs_0_), channel_id=1, source_target_pairs={{0,32},{8,40},{16,48},{24,56},{32,0},{40,8},{48,16},{56,24},{64,96... | collective-permute-start | bytes 786440 | tf_op jit(solution)/shard_map/ppermute | solution.py:412
  79.1 0.0 collective-permute-done.12.refs_6_
  79.1 0.0 collective-permute-start.5
  79.2 1.8 %collective-permute-done.11.refs_5_ = bf16[4,128,256]{2,1,0:T(8,128)(2,1)S(1)} collective-permute-done((bf16[4,128,256]{2,1,0:T(8,128)(2,1)S(1)}, bf16[4,128,256]{2,1,0:T(8,128)(2,1)S(1)}, u32[]{:S(2)}, u32[]{:S(2)}) %collective-permute-start.11) | collective-permute-done | bytes 262176 | tf_op jit(solution)/shard_map/ppermute | solution.py:412
  80.9 4.0 %collective-permute-done.7.refs_3_ = bf16[4,128,256]{2,1,0:T(8,128)(2,1)S(1)} collective-permute-done((bf16[4,128,256]{2,1,0:T(8,128)(2,1)S(1)}, bf16[4,128,256]{2,1,0:T(8,128)(2,1)S(1)}, u32[]{:S(2)}, u32[]{:S(2)}) %collective-permute-start.7) | collective-permute-done | bytes 262176 | tf_op jit(solution)/shard_map/ppermute | solution.py:412
  85.0 3.1 %collective-permute-done.6.refs_2_ = bf16[4,128,256]{2,1,0:T(8,128)(2,1)S(1)} collective-permute-done((bf16[4,128,256]{2,1,0:T(8,128)(2,1)S(1)}, bf16[4,128,256]{2,1,0:T(8,128)(2,1)S(1)}, u32[]{:S(2)}, u32[]{:S(2)}) %collective-permute-start.6) | collective-permute-done | bytes 262176 | tf_op jit(solution)/shard_map/ppermute | solution.py:412
  88.1 2.8 %collective-permute-done.5.refs_1_ = bf16[4,128,256]{2,1,0:T(8,128)(2,1)S(1)} collective-permute-done((bf16[4,128,256]{2,1,0:T(8,128)(2,1)S(1)}, bf16[4,128,256]{2,1,0:T(8,128)(2,1)S(1)}, u32[]{:S(2)}, u32[]{:S(2)}) %collective-permute-start.5) | collective-permute-done | bytes 262176 | tf_op jit(solution)/shard_map/ppermute | solution.py:412
  90.8 8.4 %scored.1 = f32[4,1024]{1,0:T(4,128)S(1)} custom-call(s32[8]{0:T(128)S(1)} %stack.77.where_ref, s32[2,1024]{1,0:T(2,128)S(1)} %pad_add_fusion.assign_ref, f32[1,256]{1,0:T(1,128)S(1)} %get-tuple-element.37.mark_ref, bf16[1024,4096]{1,0:T(8,128)(2,1)} %near_ref.1, bf16[1024,4096]{1,0:T(8,128)(2,1)} %collective-permute-done.1.far_ref, ...), custom_call_target="tpu_custom_call" | custom-call | flops 4294967296 | bytes 16777216 | tf_op jit(solution)/shard_map/scored/pallas_call | solution.py:302
  99.2 0.0 copy-start.2
  99.2 7.3 %collective-permute-start.14 = (f32[4,1024]{1,0:T(4,128)S(1)}, f32[4,1024]{1,0:T(4,128)S(1)}, u32[]{:S(2)}, u32[]{:S(2)}) collective-permute-start(f32[4,1024]{1,0:T(4,128)S(1)} %scored.1), channel_id=1, source_target_pairs={{0,4},{1,5},{2,6},{3,7},{4,0},{5,1},{6,2},{7,3},{8,12},{9,13},{10,... | collective-permute-start | bytes 49160 | tf_op jit(solution)/shard_map/ppermute | solution.py:421
  106.5 1.7 %collective-permute-done.14 = f32[4,1024]{1,0:T(4,128)S(1)} collective-permute-done((f32[4,1024]{1,0:T(4,128)S(1)}, f32[4,1024]{1,0:T(4,128)S(1)}, u32[]{:S(2)}, u32[]{:S(2)}) %collective-permute-start.14) | collective-permute-done | bytes 16416 | tf_op jit(solution)/shard_map/ppermute | solution.py:421
  108.2 2.1 %collective-permute-start.16 = (f32[4,1024]{1,0:T(4,128)S(1)}, f32[4,1024]{1,0:T(4,128)S(1)}, u32[]{:S(2)}, u32[]{:S(2)}) collective-permute-start(f32[4,1024]{1,0:T(4,128)S(1)} %max.3.a_ref), channel_id=1, source_target_pairs={{0,8},{1,9},{2,10},{3,11},{4,12},{5,13},{6,14},{7,15},{8,0},{9,1},... | collective-permute-start | bytes 49160 | tf_op jit(solution)/shard_map/ppermute | solution.py:421
  110.3 0.9 collective-permute-start.15
  111.3 1.0 collective-permute-done.17.d_ref
  112.3 0.0 collective-permute-done.16.c_ref
  112.3 2.7 %collective-permute-done.15.b_ref = f32[4,1024]{1,0:T(4,128)S(1)} collective-permute-done((f32[4,1024]{1,0:T(4,128)S(1)}, f32[4,1024]{1,0:T(4,128)S(1)}, u32[]{:S(2)}, u32[]{:S(2)}) %collective-permute-start.15) | collective-permute-done | bytes 16416 | tf_op jit(solution)/shard_map/ppermute | solution.py:421
  115.0 0.7 merge.1
  115.7 6.6 %all-to-all-start.7 = ((f32[32,2,1024]{2,1,0:T(2,128)}), f32[32,2,1024]{2,1,0:T(2,128)S(1)}, u32[]{:S(2)}, u32[]{:S(2)}) async-start(f32[32,2,1024]{2,1,0:T(2,128)} %get-tuple-element.43), calls=%async_computation.7 | async-start | bytes 524288 | tf_op jit(solution)/shard_map/all_to_all | solution.py:487
  122.3 1.6 %collective-permute-start.18 = (f32[4,1024]{1,0:T(4,128)S(1)}, f32[4,1024]{1,0:T(4,128)S(1)}, u32[]{:S(2)}, u32[]{:S(2)}) collective-permute-start(f32[4,1024]{1,0:T(4,128)S(1)} %get-tuple-element.40.a_ref), channel_id=1, source_target_pairs={{0,1},{1,0},{2,3},{3,2},{4,5},{5,4},{6,7},{7,6},{8,9},{9,8},{10,11... | collective-permute-start | bytes 49160 | tf_op jit(solution)/shard_map/ppermute | solution.py:421
  123.9 4.8 %sums.1 = (f32[128,512]{1,0:T(8,128)}, f32[1,512]{1,0:T(1,128)}) custom-call(bf16[32,192,128]{2,1,0:T(8,128)(2,1)S(1)} %all-to-all-done.8.got_ref), custom_call_target="tpu_custom_call" | custom-call | flops 1610612736 | bytes 1572864 | tf_op jit(solution)/shard_map/sums/pallas_call | solution.py:239
  128.7 0.6 closing.1
  130.0 0.7 conditional.1
  130.0 0.7 cover.1
  (14 shorter events, 0.1 us)
Async XLA Ops:
  0.6 90.2 %collective-permute-start.1 = (bf16[1024,4096]{1,0:T(8,128)(2,1)}, bf16[1024,4096]{1,0:T(8,128)(2,1)}, u32[]{:S(2)}, u32[]{:S(2)}) collective-permute-start(bf16[1024,4096]{1,0:T(8,128)(2,1)} %near_ref.1), channel_id=1, source_target_pairs={{0,8},{8,0},{16,24},{24,16},{32,40},{40,32},{48,56},{56,48},{64,72... | collective-permute-start | bytes 25165832 | tf_op jit(solution)/shard_map/ppermute | solution.py:412
  6.1 1.2 copy-start
  7.3 63.7 %copy-start.1 = (s32[1024]{0:T(1024)S(1)}, s32[1024]{0:T(1024)}, u32[]{:S(2)}) copy-start(s32[1024]{0:T(1024)} %param.6) | copy-start | bytes 12292
  24.7 91.0 %all-to-all-start.8 = ((bf16[32,192,128]{2,1,0:T(8,128)(2,1)}), bf16[32,192,128]{2,1,0:T(8,128)(2,1)S(1)}, u32[]{:S(2)}, u32[]{:S(2)}) async-start(bf16[32,192,128]{2,1,0:T(8,128)(2,1)} %copy-done), calls=%async_computation.8 | async-start | bytes 3145728 | tf_op jit(solution)/shard_map/all_to_all | solution.py:480
  31.1 20.0 %collective-permute-start.10 = (bf16[128,256]{1,0:T(8,128)(2,1)S(1)}, bf16[128,256]{1,0:T(8,128)(2,1)S(1)}, u32[]{:S(2)}, u32[]{:S(2)}) collective-permute-start(bf16[128,256]{1,0:T(8,128)(2,1)S(1)} %get-tuple-element.39), channel_id=1, source_target_pairs={{0,48},{8,56},{16,0},{24,8},{32,16},{40,24},{48,32},{56,40},{64,11... | collective-permute-start | bytes 196616 | tf_op jit(solution)/shard_map/ppermute | solution.py:412
  33.9 19.1 %collective-permute-start.9 = (bf16[128,256]{1,0:T(8,128)(2,1)S(1)}, bf16[128,256]{1,0:T(8,128)(2,1)S(1)}, u32[]{:S(2)}, u32[]{:S(2)}) collective-permute-start(bf16[128,256]{1,0:T(8,128)(2,1)S(1)} %get-tuple-element.39), channel_id=1, source_target_pairs={{0,32},{8,40},{16,48},{24,56},{32,0},{40,8},{48,16},{56,24},{64,96... | collective-permute-start | bytes 196616 | tf_op jit(solution)/shard_map/ppermute | solution.py:412
  34.7 18.8 %collective-permute-start.8 = (bf16[128,256]{1,0:T(8,128)(2,1)S(1)}, bf16[128,256]{1,0:T(8,128)(2,1)S(1)}, u32[]{:S(2)}, u32[]{:S(2)}) collective-permute-start(bf16[128,256]{1,0:T(8,128)(2,1)S(1)} %get-tuple-element.39), channel_id=1, source_target_pairs={{0,16},{8,24},{16,32},{24,40},{32,48},{40,56},{48,0},{56,8},{64,80... | collective-permute-start | bytes 196616 | tf_op jit(solution)/shard_map/ppermute | solution.py:412
  53.6 24.1 %collective-permute-start.13 = (bf16[4,128,256]{2,1,0:T(8,128)(2,1)S(1)}, bf16[4,128,256]{2,1,0:T(8,128)(2,1)S(1)}, u32[]{:S(2)}, u32[]{:S(2)}) collective-permute-start(bf16[4,128,256]{2,1,0:T(8,128)(2,1)S(1)} %pad_maximum_fusion.2.refs_4_), channel_id=1, source_target_pairs={{0,192},{8,200},{16,208},{24,216},{32,224},{40,232},{48,240},{56,2... | collective-permute-start | bytes 786440 | tf_op jit(solution)/shard_map/ppermute | solution.py:412
  54.2 25.0 %collective-permute-start.12 = (bf16[4,128,256]{2,1,0:T(8,128)(2,1)S(1)}, bf16[4,128,256]{2,1,0:T(8,128)(2,1)S(1)}, u32[]{:S(2)}, u32[]{:S(2)}) collective-permute-start(bf16[4,128,256]{2,1,0:T(8,128)(2,1)S(1)} %pad_maximum_fusion.2.refs_4_), channel_id=1, source_target_pairs={{0,128},{8,136},{16,144},{24,152},{32,160},{40,168},{48,176},{56,1... | collective-permute-start | bytes 786440 | tf_op jit(solution)/shard_map/ppermute | solution.py:412
  56.6 10.8 %collective-permute-start.4 = (bf16[128,256]{1,0:T(8,128)(2,1)S(1)}, bf16[128,256]{1,0:T(8,128)(2,1)S(1)}, u32[]{:S(2)}, u32[]{:S(2)}) collective-permute-start(bf16[128,256]{1,0:T(8,128)(2,1)S(1)} %get-tuple-element.38), channel_id=1, source_target_pairs={{0,192},{8,200},{16,208},{24,216},{32,224},{40,232},{48,240},{56,2... | collective-permute-start | bytes 196616 | tf_op jit(solution)/shard_map/ppermute | solution.py:412
  57.7 13.3 %collective-permute-start.3 = (bf16[128,256]{1,0:T(8,128)(2,1)S(1)}, bf16[128,256]{1,0:T(8,128)(2,1)S(1)}, u32[]{:S(2)}, u32[]{:S(2)}) collective-permute-start(bf16[128,256]{1,0:T(8,128)(2,1)S(1)} %get-tuple-element.38), channel_id=1, source_target_pairs={{0,128},{8,136},{16,144},{24,152},{32,160},{40,168},{48,176},{56,1... | collective-permute-start | bytes 196616 | tf_op jit(solution)/shard_map/ppermute | solution.py:412
  67.4 5.5 %collective-permute-start.2 = (bf16[128,256]{1,0:T(8,128)(2,1)S(1)}, bf16[128,256]{1,0:T(8,128)(2,1)S(1)}, u32[]{:S(2)}, u32[]{:S(2)}) collective-permute-start(bf16[128,256]{1,0:T(8,128)(2,1)S(1)} %get-tuple-element.38), channel_id=1, source_target_pairs={{0,64},{8,72},{16,80},{24,88},{32,96},{40,104},{48,112},{56,120},{... | collective-permute-start | bytes 196616 | tf_op jit(solution)/shard_map/ppermute | solution.py:412
  71.0 4.7 %collective-permute-start = (s32[1024]{0:T(1024)S(1)}, s32[1024]{0:T(1024)S(1)}, u32[]{:S(2)}, u32[]{:S(2)}) collective-permute-start(s32[1024]{0:T(1024)S(1)} %copy-done.1), channel_id=1, source_target_pairs={{0,8},{8,0},{16,24},{24,16},{32,40},{40,32},{48,56},{56,48},{64,72... | collective-permute-start | bytes 12296 | tf_op jit(solution)/shard_map/ppermute | solution.py:412
  72.9 8.0 %collective-permute-start.11 = (bf16[4,128,256]{2,1,0:T(8,128)(2,1)S(1)}, bf16[4,128,256]{2,1,0:T(8,128)(2,1)S(1)}, u32[]{:S(2)}, u32[]{:S(2)}) collective-permute-start(bf16[4,128,256]{2,1,0:T(8,128)(2,1)S(1)} %pad_maximum_fusion.2.refs_4_), channel_id=1, source_target_pairs={{0,64},{8,72},{16,80},{24,88},{32,96},{40,104},{48,112},{56,120},{... | collective-permute-start | bytes 786440 | tf_op jit(solution)/shard_map/ppermute | solution.py:412
  75.7 9.3 %collective-permute-start.7 = (bf16[4,128,256]{2,1,0:T(8,128)(2,1)S(1)}, bf16[4,128,256]{2,1,0:T(8,128)(2,1)S(1)}, u32[]{:S(2)}, u32[]{:S(2)}) collective-permute-start(bf16[4,128,256]{2,1,0:T(8,128)(2,1)S(1)} %pad_maximum_fusion.1.refs_0_), channel_id=1, source_target_pairs={{0,48},{8,56},{16,0},{24,8},{32,16},{40,24},{48,32},{56,40},{64,11... | collective-permute-start | bytes 786440 | tf_op jit(solution)/shard_map/ppermute | solution.py:412
  77.7 10.4 %collective-permute-start.6 = (bf16[4,128,256]{2,1,0:T(8,128)(2,1)S(1)}, bf16[4,128,256]{2,1,0:T(8,128)(2,1)S(1)}, u32[]{:S(2)}, u32[]{:S(2)}) collective-permute-start(bf16[4,128,256]{2,1,0:T(8,128)(2,1)S(1)} %pad_maximum_fusion.1.refs_0_), channel_id=1, source_target_pairs={{0,32},{8,40},{16,48},{24,56},{32,0},{40,8},{48,16},{56,24},{64,96... | collective-permute-start | bytes 786440 | tf_op jit(solution)/shard_map/ppermute | solution.py:412
  79.1 11.7 %collective-permute-start.5 = (bf16[4,128,256]{2,1,0:T(8,128)(2,1)S(1)}, bf16[4,128,256]{2,1,0:T(8,128)(2,1)S(1)}, u32[]{:S(2)}, u32[]{:S(2)}) collective-permute-start(bf16[4,128,256]{2,1,0:T(8,128)(2,1)S(1)} %pad_maximum_fusion.1.refs_0_), channel_id=1, source_target_pairs={{0,16},{8,24},{16,32},{24,40},{32,48},{40,56},{48,0},{56,8},{64,80... | collective-permute-start | bytes 786440 | tf_op jit(solution)/shard_map/ppermute | solution.py:412
  99.2 30.8 %copy-start.2 = (s32[512]{0:T(512)S(1)}, s32[512]{0:T(512)}, u32[]{:S(2)}) copy-start(s32[512]{0:T(512)} %param.7) | copy-start | bytes 6148
  99.2 9.0 %collective-permute-start.14 = (f32[4,1024]{1,0:T(4,128)S(1)}, f32[4,1024]{1,0:T(4,128)S(1)}, u32[]{:S(2)}, u32[]{:S(2)}) collective-permute-start(f32[4,1024]{1,0:T(4,128)S(1)} %scored.1), channel_id=1, source_target_pairs={{0,4},{1,5},{2,6},{3,7},{4,0},{5,1},{6,2},{7,3},{8,12},{9,13},{10,... | collective-permute-start | bytes 49160 | tf_op jit(solution)/shard_map/ppermute | solution.py:421
  108.2 4.1 %collective-permute-start.17 = (f32[4,1024]{1,0:T(4,128)S(1)}, f32[4,1024]{1,0:T(4,128)S(1)}, u32[]{:S(2)}, u32[]{:S(2)}) collective-permute-start(f32[4,1024]{1,0:T(4,128)S(1)} %max.3.a_ref), channel_id=1, source_target_pairs={{0,10},{1,11},{2,8},{3,9},{4,14},{5,15},{6,12},{7,13},{8,2},{9,3},... | collective-permute-start | bytes 49160 | tf_op jit(solution)/shard_map/ppermute | solution.py:421
  108.2 4.1 %collective-permute-start.16 = (f32[4,1024]{1,0:T(4,128)S(1)}, f32[4,1024]{1,0:T(4,128)S(1)}, u32[]{:S(2)}, u32[]{:S(2)}) collective-permute-start(f32[4,1024]{1,0:T(4,128)S(1)} %max.3.a_ref), channel_id=1, source_target_pairs={{0,8},{1,9},{2,10},{3,11},{4,12},{5,13},{6,14},{7,15},{8,0},{9,1},... | collective-permute-start | bytes 49160 | tf_op jit(solution)/shard_map/ppermute | solution.py:421
  110.3 4.6 %collective-permute-start.15 = (f32[4,1024]{1,0:T(4,128)S(1)}, f32[4,1024]{1,0:T(4,128)S(1)}, u32[]{:S(2)}, u32[]{:S(2)}) collective-permute-start(f32[4,1024]{1,0:T(4,128)S(1)} %max.3.a_ref), channel_id=1, source_target_pairs={{0,2},{1,3},{2,0},{3,1},{4,6},{5,7},{6,4},{7,5},{8,10},{9,11},{10,... | collective-permute-start | bytes 49160 | tf_op jit(solution)/shard_map/ppermute | solution.py:421
  115.7 14.3 %all-to-all-start.7 = ((f32[32,2,1024]{2,1,0:T(2,128)}), f32[32,2,1024]{2,1,0:T(2,128)S(1)}, u32[]{:S(2)}, u32[]{:S(2)}) async-start(f32[32,2,1024]{2,1,0:T(2,128)} %get-tuple-element.43), calls=%async_computation.7 | async-start | bytes 524288 | tf_op jit(solution)/shard_map/all_to_all | solution.py:487
  122.3 6.4 %collective-permute-start.18 = (f32[4,1024]{1,0:T(4,128)S(1)}, f32[4,1024]{1,0:T(4,128)S(1)}, u32[]{:S(2)}, u32[]{:S(2)}) collective-permute-start(f32[4,1024]{1,0:T(4,128)S(1)} %get-tuple-element.40.a_ref), channel_id=1, source_target_pairs={{0,1},{1,0},{2,3},{3,2},{4,5},{5,4},{6,7},{7,6},{8,9},{9,8},{10,11... | collective-permute-start | bytes 49160 | tf_op jit(solution)/shard_map/ppermute | solution.py:421

commit v10 on v9

--- a/solution.py
+++ b/solution.py
@@ -20,8 +20,8 @@
 NONE = -1e30
 LOST = 1e30
 PTS = ("chip", "core")
-MED = ("zq", "zr")
-CHIPS = 4
+MED = ("zr", "zq")
+CHIPS = 2
 
 
 def contract_last(a, b):
@@ -480,12 +480,12 @@
     grad_got = lax.all_to_all(grad_send, PTS, 0, 0, tiled=True)
     assignments = jnp.stack([assignment, far_assignment])
     stats = scored(where, assignments, marks, sketches, far, qa + qb)
-    stats = jnp.maximum(stats, across(stats, 0, 4, planes))
+    stats = jnp.maximum(stats, across(stats, 0, 1, planes))
     near = across(stats, 0, 2, planes)
     partner, both = across(stats, 1, 0, planes), across(stats, 1, 2, planes)
     stats, send = merge(stats, near, partner, both, pts_count)
-    everyone = lax.all_to_all(send, (PTS[0], MED[1]), 0, 0, tiled=True)
-    plane = across(stats, 0, 1, planes)
+    everyone = lax.all_to_all(send, (PTS[0], MED[0]), 0, 0, tiled=True)
+    plane = across(stats, 0, planes // 2, planes)
     gradient_sums, counts = sums(grad_got, medoid_count, 0, 8)
     gap, mark = closing(stats, plane)
     full = mark[0, 0] > 0
@@ -499,7 +499,7 @@
 def solution(mesh):
     planes = mesh.shape["med"]
     mesh = jax.sharding.Mesh(
-        mesh.devices.reshape(-1, 2, planes // 2, 2), (*PTS, *MED)
+        mesh.devices.reshape(-1, 2, 2, planes // 2), (*PTS, *MED)
     )
     in_specs = (P(PTS, None), P(PTS), P(MED))
     out_specs = (P(PTS), P(), P(MED), P(PTS, MED))

time: 132 us -> 138 us (1.045); the launches traced: 131 us -> 135 us
  starting transfers between devices: 44.5 us -> 47 us
  waiting for transfers between devices: 44.6 us -> 46.1 us
    all_to_all x1, starting transfers between devices: 6.62 us -> 10 us  [shards(): everyone = lax.all_to_all(send, (PTS[0], MED[0]), 0, 0, tiled=True)]
  transfers between devices with their start and end apart: 21 -> 21, of which waited for: 13 -> 15; matrix products, arithmetic and copies ran while one was open for 0% -> 0% of each run, Pallas kernels for 16% -> 16%
where the time goes in v10:
time: 138 us; the launch traced here: 135 us
  starting transfers between devices  47 us (34%)
  waiting for transfers between devices  46.1 us (33%)
  Pallas kernels  21.7 us (16%)
  blocking collectives  17.4 us (13%)
  between operations  1.6 us (1%)
    ppermute x14, waiting for transfers between devices, shifted(): return lax.ppermute(array, PTS, pairs)  39.1 us
    ppermute x14, starting transfers between devices, shifted(): return lax.ppermute(array, PTS, pairs)  20.6 us
    all_to_all x1, blocking collectives, shards(): med_got = lax.all_to_all(med_send, PTS, 0, 0, tiled=True)  17.4 us
    ppermute x5, starting transfers between devices, across(): return lax.ppermute(array, (*PTS, *MED), pairs)  10.9 us
    all_to_all x1, starting transfers between devices, shards(): everyone = lax.all_to_all(send, (PTS[0], MED[0]), 0, 0, tiled=True)  10 us
    pallas_call x1, Pallas kernels, scored(): pl.pallas_call(functools.partial(score_kernel, 1.0 / feats), in_specs=[pl...  8.36 us
    ppermute x5, waiting for transfers between devices, across(): return lax.ppermute(array, (*PTS, *MED), pairs)  6.38 us
    pallas_call x1, Pallas kernels, pick(): pl.pallas_call(pick_kernel, in_specs=[pl.BlockSpec(memory_space=pltpu.SME...  5.54 us
  transfers between devices with their start and end apart: 21, of which 15 were waited for; matrix products, arithmetic and copies ran while one was open for 0% of the time, Pallas kernels for 16%

profile of v10, /device:TPU:2, one launch (start us, length us, event | category | flops | bytes accessed | tf_op | source)
XLA Modules:
  0.0 135.2 jit_solution(11030243877538417258)
XLA Ops:
  0.6 0.1 collective-permute-start.1
  0.8 0.1 stack.77.where_ref
  0.9 5.5 %pick.1 = (bf16[32,32,256]{2,1,0:T(8,128)(2,1)S(1)}, bf16[32,192,128]{2,1,0:T(8,128)(2,1)S(1)}) custom-call(s32[8]{0:T(128)S(1)} %stack.77.where_ref, s32[8,128]{1,0:T(8,128)} %bitcast.60, s32[1,512]{1,0:T(1,128)} %bitcast.63, bf16[1024,4096]{1,0:T(8,128)(2,1)} %near_ref.1), custom_call_target="tpu_custom_call" | custom-call | flops 2147483648 | bytes 8388608 | tf_op jit(solution)/shard_map/pick/pallas_call | solution.py:128
  6.4 1.2 copy-done
  7.6 17.4 %all_to_all.42.got_ref = bf16[32,32,256]{2,1,0:T(8,128)(2,1)S(1)} all-to-all(bf16[32,32,256]{2,1,0:T(8,128)(2,1)S(1)} %get-tuple-element.36), channel_id=1, replica_groups=mesh['chip'=16,'core'=2,'zr'=2,'zq'=4] {'chip','core'}, dimensions={0} | all-to-all | bytes 1048576 | tf_op jit(solution)/shard_map/all_to_all | solution.py:473
  25.0 5.4 %all-to-all-start.8 = ((bf16[32,192,128]{2,1,0:T(8,128)(2,1)}), bf16[32,192,128]{2,1,0:T(8,128)(2,1)S(1)}, u32[]{:S(2)}, u32[]{:S(2)}) async-start(bf16[32,192,128]{2,1,0:T(8,128)(2,1)} %copy-done), calls=%async_computation.8 | async-start | bytes 3145728 | tf_op jit(solution)/shard_map/all_to_all | solution.py:480
  30.4 1.0 place.1
  31.4 2.8 %collective-permute-start.10 = (bf16[128,256]{1,0:T(8,128)(2,1)S(1)}, bf16[128,256]{1,0:T(8,128)(2,1)S(1)}, u32[]{:S(2)}, u32[]{:S(2)}) collective-permute-start(bf16[128,256]{1,0:T(8,128)(2,1)S(1)} %get-tuple-element.39), channel_id=1, source_target_pairs={{0,48},{8,56},{16,0},{24,8},{32,16},{40,24},{48,32},{56,40},{64,11... | collective-permute-start | bytes 196616 | tf_op jit(solution)/shard_map/ppermute | solution.py:412
  34.2 0.9 collective-permute-start.9
  35.0 0.9 collective-permute-start.8
  35.9 15.5 %collective-permute-done.10 = bf16[128,256]{1,0:T(8,128)(2,1)S(1)} collective-permute-done((bf16[128,256]{1,0:T(8,128)(2,1)S(1)}, bf16[128,256]{1,0:T(8,128)(2,1)S(1)}, u32[]{:S(2)}, u32[]{:S(2)}) %collective-permute-start.10) | collective-permute-done | bytes 65568 | tf_op jit(solution)/shard_map/ppermute | solution.py:412
  51.4 1.9 %collective-permute-done.9 = bf16[128,256]{1,0:T(8,128)(2,1)S(1)} collective-permute-done((bf16[128,256]{1,0:T(8,128)(2,1)S(1)}, bf16[128,256]{1,0:T(8,128)(2,1)S(1)}, u32[]{:S(2)}, u32[]{:S(2)}) %collective-permute-start.9) | collective-permute-done | bytes 65568 | tf_op jit(solution)/shard_map/ppermute | solution.py:412
  53.3 0.5 collective-permute-done.8
  53.9 0.6 collective-permute-start.13
  54.5 2.4 %collective-permute-start.12 = (bf16[4,128,256]{2,1,0:T(8,128)(2,1)S(1)}, bf16[4,128,256]{2,1,0:T(8,128)(2,1)S(1)}, u32[]{:S(2)}, u32[]{:S(2)}) collective-permute-start(bf16[4,128,256]{2,1,0:T(8,128)(2,1)S(1)} %pad_maximum_fusion.2.refs_4_), channel_id=1, source_target_pairs={{0,128},{8,136},{16,144},{24,152},{32,160},{40,168},{48,176},{56,1... | collective-permute-start | bytes 786440 | tf_op jit(solution)/shard_map/ppermute | solution.py:412
  56.9 1.1 collective-permute-start.4
  58.1 2.2 %collective-permute-start.3 = (bf16[128,256]{1,0:T(8,128)(2,1)S(1)}, bf16[128,256]{1,0:T(8,128)(2,1)S(1)}, u32[]{:S(2)}, u32[]{:S(2)}) collective-permute-start(bf16[128,256]{1,0:T(8,128)(2,1)S(1)} %get-tuple-element.38), channel_id=1, source_target_pairs={{0,128},{8,136},{16,144},{24,152},{32,160},{40,168},{48,176},{56,1... | collective-permute-start | bytes 196616 | tf_op jit(solution)/shard_map/ppermute | solution.py:412
  60.2 7.5 %collective-permute-done.4 = bf16[128,256]{1,0:T(8,128)(2,1)S(1)} collective-permute-done((bf16[128,256]{1,0:T(8,128)(2,1)S(1)}, bf16[128,256]{1,0:T(8,128)(2,1)S(1)}, u32[]{:S(2)}, u32[]{:S(2)}) %collective-permute-start.4) | collective-permute-done | bytes 65568 | tf_op jit(solution)/shard_map/ppermute | solution.py:412
  67.7 3.5 %collective-permute-start.2 = (bf16[128,256]{1,0:T(8,128)(2,1)S(1)}, bf16[128,256]{1,0:T(8,128)(2,1)S(1)}, u32[]{:S(2)}, u32[]{:S(2)}) collective-permute-start(bf16[128,256]{1,0:T(8,128)(2,1)S(1)} %get-tuple-element.38), channel_id=1, source_target_pairs={{0,64},{8,72},{16,80},{24,88},{32,96},{40,104},{48,112},{56,120},{... | collective-permute-start | bytes 196616 | tf_op jit(solution)/shard_map/ppermute | solution.py:412
  71.2 0.1 collective-permute-done.3
  71.3 0.0 collective-permute-start
  71.3 1.9 %collective-permute-done.2 = bf16[128,256]{1,0:T(8,128)(2,1)S(1)} collective-permute-done((bf16[128,256]{1,0:T(8,128)(2,1)S(1)}, bf16[128,256]{1,0:T(8,128)(2,1)S(1)}, u32[]{:S(2)}, u32[]{:S(2)}) %collective-permute-start.2) | collective-permute-done | bytes 65568 | tf_op jit(solution)/shard_map/ppermute | solution.py:412
  73.2 2.8 %collective-permute-start.11 = (bf16[4,128,256]{2,1,0:T(8,128)(2,1)S(1)}, bf16[4,128,256]{2,1,0:T(8,128)(2,1)S(1)}, u32[]{:S(2)}, u32[]{:S(2)}) collective-permute-start(bf16[4,128,256]{2,1,0:T(8,128)(2,1)S(1)} %pad_maximum_fusion.2.refs_4_), channel_id=1, source_target_pairs={{0,64},{8,72},{16,80},{24,88},{32,96},{40,104},{48,112},{56,120},{... | collective-permute-start | bytes 786440 | tf_op jit(solution)/shard_map/ppermute | solution.py:412
  76.0 1.9 %collective-permute-start.7 = (bf16[4,128,256]{2,1,0:T(8,128)(2,1)S(1)}, bf16[4,128,256]{2,1,0:T(8,128)(2,1)S(1)}, u32[]{:S(2)}, u32[]{:S(2)}) collective-permute-start(bf16[4,128,256]{2,1,0:T(8,128)(2,1)S(1)} %pad_maximum_fusion.1.refs_0_), channel_id=1, source_target_pairs={{0,48},{8,56},{16,0},{24,8},{32,16},{40,24},{48,32},{56,40},{64,11... | collective-permute-start | bytes 786440 | tf_op jit(solution)/shard_map/ppermute | solution.py:412
  78.0 1.5 %collective-permute-start.6 = (bf16[4,128,256]{2,1,0:T(8,128)(2,1)S(1)}, bf16[4,128,256]{2,1,0:T(8,128)(2,1)S(1)}, u32[]{:S(2)}, u32[]{:S(2)}) collective-permute-start(bf16[4,128,256]{2,1,0:T(8,128)(2,1)S(1)} %pad_maximum_fusion.1.refs_0_), channel_id=1, source_target_pairs={{0,32},{8,40},{16,48},{24,56},{32,0},{40,8},{48,16},{56,24},{64,96... | collective-permute-start | bytes 786440 | tf_op jit(solution)/shard_map/ppermute | solution.py:412
  79.5 0.0 collective-permute-start.5
  79.5 1.8 %collective-permute-done.11.refs_5_ = bf16[4,128,256]{2,1,0:T(8,128)(2,1)S(1)} collective-permute-done((bf16[4,128,256]{2,1,0:T(8,128)(2,1)S(1)}, bf16[4,128,256]{2,1,0:T(8,128)(2,1)S(1)}, u32[]{:S(2)}, u32[]{:S(2)}) %collective-permute-start.11) | collective-permute-done | bytes 262176 | tf_op jit(solution)/shard_map/ppermute | solution.py:412
  81.3 4.0 %collective-permute-done.7.refs_3_ = bf16[4,128,256]{2,1,0:T(8,128)(2,1)S(1)} collective-permute-done((bf16[4,128,256]{2,1,0:T(8,128)(2,1)S(1)}, bf16[4,128,256]{2,1,0:T(8,128)(2,1)S(1)}, u32[]{:S(2)}, u32[]{:S(2)}) %collective-permute-start.7) | collective-permute-done | bytes 262176 | tf_op jit(solution)/shard_map/ppermute | solution.py:412
  85.3 3.1 %collective-permute-done.6.refs_2_ = bf16[4,128,256]{2,1,0:T(8,128)(2,1)S(1)} collective-permute-done((bf16[4,128,256]{2,1,0:T(8,128)(2,1)S(1)}, bf16[4,128,256]{2,1,0:T(8,128)(2,1)S(1)}, u32[]{:S(2)}, u32[]{:S(2)}) %collective-permute-start.6) | collective-permute-done | bytes 262176 | tf_op jit(solution)/shard_map/ppermute | solution.py:412
  88.4 2.8 %collective-permute-done.5.refs_1_ = bf16[4,128,256]{2,1,0:T(8,128)(2,1)S(1)} collective-permute-done((bf16[4,128,256]{2,1,0:T(8,128)(2,1)S(1)}, bf16[4,128,256]{2,1,0:T(8,128)(2,1)S(1)}, u32[]{:S(2)}, u32[]{:S(2)}) %collective-permute-start.5) | collective-permute-done | bytes 262176 | tf_op jit(solution)/shard_map/ppermute | solution.py:412
  91.2 8.4 %scored.1 = f32[4,1024]{1,0:T(4,128)S(1)} custom-call(s32[8]{0:T(128)S(1)} %stack.77.where_ref, s32[2,1024]{1,0:T(2,128)S(1)} %pad_add_fusion.assign_ref, f32[1,256]{1,0:T(1,128)S(1)} %get-tuple-element.37.mark_ref, bf16[1024,4096]{1,0:T(8,128)(2,1)} %near_ref.1, bf16[1024,4096]{1,0:T(8,128)(2,1)} %collective-permute-done.1.far_ref, ...), custom_call_target="tpu_custom_call" | custom-call | flops 4294967296 | bytes 16777216 | tf_op jit(solution)/shard_map/scored/pallas_call | solution.py:302
  99.5 0.0 copy-start.2
  99.5 2.0 %collective-permute-start.14 = (f32[4,1024]{1,0:T(4,128)S(1)}, f32[4,1024]{1,0:T(4,128)S(1)}, u32[]{:S(2)}, u32[]{:S(2)}) collective-permute-start(f32[4,1024]{1,0:T(4,128)S(1)} %scored.1), channel_id=1, source_target_pairs={{0,1},{1,0},{2,3},{3,2},{4,5},{5,4},{6,7},{7,6},{8,9},{9,8},{10,11... | collective-permute-start | bytes 49160 | tf_op jit(solution)/shard_map/ppermute | solution.py:421
  101.5 1.8 %collective-permute-done.14 = f32[4,1024]{1,0:T(4,128)S(1)} collective-permute-done((f32[4,1024]{1,0:T(4,128)S(1)}, f32[4,1024]{1,0:T(4,128)S(1)}, u32[]{:S(2)}, u32[]{:S(2)}) %collective-permute-start.14) | collective-permute-done | bytes 16416 | tf_op jit(solution)/shard_map/ppermute | solution.py:421
  103.4 1.1 collective-permute-start.17
  104.5 2.3 %collective-permute-start.16 = (f32[4,1024]{1,0:T(4,128)S(1)}, f32[4,1024]{1,0:T(4,128)S(1)}, u32[]{:S(2)}, u32[]{:S(2)}) collective-permute-start(f32[4,1024]{1,0:T(4,128)S(1)} %max.3.a_ref), channel_id=1, source_target_pairs={{0,8},{1,9},{2,10},{3,11},{4,12},{5,13},{6,14},{7,15},{8,0},{9,1},... | collective-permute-start | bytes 49160 | tf_op jit(solution)/shard_map/ppermute | solution.py:421
  106.8 0.1 collective-permute-start.15
  106.8 0.6 collective-permute-done.17.d_ref
  107.4 0.2 collective-permute-done.16.c_ref
  107.6 3.8 %collective-permute-done.15.b_ref = f32[4,1024]{1,0:T(4,128)S(1)} collective-permute-done((f32[4,1024]{1,0:T(4,128)S(1)}, f32[4,1024]{1,0:T(4,128)S(1)}, u32[]{:S(2)}, u32[]{:S(2)}) %collective-permute-start.15) | collective-permute-done | bytes 16416 | tf_op jit(solution)/shard_map/ppermute | solution.py:421
  111.4 0.7 merge.1
  112.1 10.0 %all-to-all-start.7 = ((f32[32,2,1024]{2,1,0:T(2,128)}), f32[32,2,1024]{2,1,0:T(2,128)S(1)}, u32[]{:S(2)}, u32[]{:S(2)}) async-start(f32[32,2,1024]{2,1,0:T(2,128)} %get-tuple-element.43), calls=%async_computation.7 | async-start | bytes 524288 | tf_op jit(solution)/shard_map/all_to_all | solution.py:487
  122.2 5.5 %collective-permute-start.18 = (f32[4,1024]{1,0:T(4,128)S(1)}, f32[4,1024]{1,0:T(4,128)S(1)}, u32[]{:S(2)}, u32[]{:S(2)}) collective-permute-start(f32[4,1024]{1,0:T(4,128)S(1)} %get-tuple-element.40.a_ref), channel_id=1, source_target_pairs={{0,4},{1,5},{2,6},{3,7},{4,0},{5,1},{6,2},{7,3},{8,12},{9,13},{10,... | collective-permute-start | bytes 49160 | tf_op jit(solution)/shard_map/ppermute | solution.py:421
  127.6 4.8 %sums.1 = (f32[128,512]{1,0:T(8,128)}, f32[1,512]{1,0:T(1,128)}) custom-call(bf16[32,192,128]{2,1,0:T(8,128)(2,1)S(1)} %all-to-all-done.8.got_ref), custom_call_target="tpu_custom_call" | custom-call | flops 1610612736 | bytes 1572864 | tf_op jit(solution)/shard_map/sums/pallas_call | solution.py:239
  132.5 0.6 closing.1
  133.8 0.6 all-to-all-done.7
  134.4 0.7 conditional.1
  134.4 0.7 cover.1
  (14 shorter events, 0.1 us)
Async XLA Ops:
  0.6 90.5 %collective-permute-start.1 = (bf16[1024,4096]{1,0:T(8,128)(2,1)}, bf16[1024,4096]{1,0:T(8,128)(2,1)}, u32[]{:S(2)}, u32[]{:S(2)}) collective-permute-start(bf16[1024,4096]{1,0:T(8,128)(2,1)} %near_ref.1), channel_id=1, source_target_pairs={{0,8},{8,0},{16,24},{24,16},{32,40},{40,32},{48,56},{56,48},{64,72... | collective-permute-start | bytes 25165832 | tf_op jit(solution)/shard_map/ppermute | solution.py:412
  6.4 1.2 copy-start
  7.6 63.7 %copy-start.1 = (s32[1024]{0:T(1024)S(1)}, s32[1024]{0:T(1024)}, u32[]{:S(2)}) copy-start(s32[1024]{0:T(1024)} %param.6) | copy-start | bytes 12292
  25.0 87.1 %all-to-all-start.8 = ((bf16[32,192,128]{2,1,0:T(8,128)(2,1)}), bf16[32,192,128]{2,1,0:T(8,128)(2,1)S(1)}, u32[]{:S(2)}, u32[]{:S(2)}) async-start(bf16[32,192,128]{2,1,0:T(8,128)(2,1)} %copy-done), calls=%async_computation.8 | async-start | bytes 3145728 | tf_op jit(solution)/shard_map/all_to_all | solution.py:480
  31.4 20.0 %collective-permute-start.10 = (bf16[128,256]{1,0:T(8,128)(2,1)S(1)}, bf16[128,256]{1,0:T(8,128)(2,1)S(1)}, u32[]{:S(2)}, u32[]{:S(2)}) collective-permute-start(bf16[128,256]{1,0:T(8,128)(2,1)S(1)} %get-tuple-element.39), channel_id=1, source_target_pairs={{0,48},{8,56},{16,0},{24,8},{32,16},{40,24},{48,32},{56,40},{64,11... | collective-permute-start | bytes 196616 | tf_op jit(solution)/shard_map/ppermute | solution.py:412
  34.2 19.1 %collective-permute-start.9 = (bf16[128,256]{1,0:T(8,128)(2,1)S(1)}, bf16[128,256]{1,0:T(8,128)(2,1)S(1)}, u32[]{:S(2)}, u32[]{:S(2)}) collective-permute-start(bf16[128,256]{1,0:T(8,128)(2,1)S(1)} %get-tuple-element.39), channel_id=1, source_target_pairs={{0,32},{8,40},{16,48},{24,56},{32,0},{40,8},{48,16},{56,24},{64,96... | collective-permute-start | bytes 196616 | tf_op jit(solution)/shard_map/ppermute | solution.py:412
  35.0 18.8 %collective-permute-start.8 = (bf16[128,256]{1,0:T(8,128)(2,1)S(1)}, bf16[128,256]{1,0:T(8,128)(2,1)S(1)}, u32[]{:S(2)}, u32[]{:S(2)}) collective-permute-start(bf16[128,256]{1,0:T(8,128)(2,1)S(1)} %get-tuple-element.39), channel_id=1, source_target_pairs={{0,16},{8,24},{16,32},{24,40},{32,48},{40,56},{48,0},{56,8},{64,80... | collective-permute-start | bytes 196616 | tf_op jit(solution)/shard_map/ppermute | solution.py:412
  53.9 24.1 %collective-permute-start.13 = (bf16[4,128,256]{2,1,0:T(8,128)(2,1)S(1)}, bf16[4,128,256]{2,1,0:T(8,128)(2,1)S(1)}, u32[]{:S(2)}, u32[]{:S(2)}) collective-permute-start(bf16[4,128,256]{2,1,0:T(8,128)(2,1)S(1)} %pad_maximum_fusion.2.refs_4_), channel_id=1, source_target_pairs={{0,192},{8,200},{16,208},{24,216},{32,224},{40,232},{48,240},{56,2... | collective-permute-start | bytes 786440 | tf_op jit(solution)/shard_map/ppermute | solution.py:412
  54.5 25.0 %collective-permute-start.12 = (bf16[4,128,256]{2,1,0:T(8,128)(2,1)S(1)}, bf16[4,128,256]{2,1,0:T(8,128)(2,1)S(1)}, u32[]{:S(2)}, u32[]{:S(2)}) collective-permute-start(bf16[4,128,256]{2,1,0:T(8,128)(2,1)S(1)} %pad_maximum_fusion.2.refs_4_), channel_id=1, source_target_pairs={{0,128},{8,136},{16,144},{24,152},{32,160},{40,168},{48,176},{56,1... | collective-permute-start | bytes 786440 | tf_op jit(solution)/shard_map/ppermute | solution.py:412
  56.9 10.8 %collective-permute-start.4 = (bf16[128,256]{1,0:T(8,128)(2,1)S(1)}, bf16[128,256]{1,0:T(8,128)(2,1)S(1)}, u32[]{:S(2)}, u32[]{:S(2)}) collective-permute-start(bf16[128,256]{1,0:T(8,128)(2,1)S(1)} %get-tuple-element.38), channel_id=1, source_target_pairs={{0,192},{8,200},{16,208},{24,216},{32,224},{40,232},{48,240},{56,2... | collective-permute-start | bytes 196616 | tf_op jit(solution)/shard_map/ppermute | solution.py:412
  58.1 13.3 %collective-permute-start.3 = (bf16[128,256]{1,0:T(8,128)(2,1)S(1)}, bf16[128,256]{1,0:T(8,128)(2,1)S(1)}, u32[]{:S(2)}, u32[]{:S(2)}) collective-permute-start(bf16[128,256]{1,0:T(8,128)(2,1)S(1)} %get-tuple-element.38), channel_id=1, source_target_pairs={{0,128},{8,136},{16,144},{24,152},{32,160},{40,168},{48,176},{56,1... | collective-permute-start | bytes 196616 | tf_op jit(solution)/shard_map/ppermute | solution.py:412
  67.7 5.5 %collective-permute-start.2 = (bf16[128,256]{1,0:T(8,128)(2,1)S(1)}, bf16[128,256]{1,0:T(8,128)(2,1)S(1)}, u32[]{:S(2)}, u32[]{:S(2)}) collective-permute-start(bf16[128,256]{1,0:T(8,128)(2,1)S(1)} %get-tuple-element.38), channel_id=1, source_target_pairs={{0,64},{8,72},{16,80},{24,88},{32,96},{40,104},{48,112},{56,120},{... | collective-permute-start | bytes 196616 | tf_op jit(solution)/shard_map/ppermute | solution.py:412
  71.3 4.7 %collective-permute-start = (s32[1024]{0:T(1024)S(1)}, s32[1024]{0:T(1024)S(1)}, u32[]{:S(2)}, u32[]{:S(2)}) collective-permute-start(s32[1024]{0:T(1024)S(1)} %copy-done.1), channel_id=1, source_target_pairs={{0,8},{8,0},{16,24},{24,16},{32,40},{40,32},{48,56},{56,48},{64,72... | collective-permute-start | bytes 12296 | tf_op jit(solution)/shard_map/ppermute | solution.py:412
  73.2 8.0 %collective-permute-start.11 = (bf16[4,128,256]{2,1,0:T(8,128)(2,1)S(1)}, bf16[4,128,256]{2,1,0:T(8,128)(2,1)S(1)}, u32[]{:S(2)}, u32[]{:S(2)}) collective-permute-start(bf16[4,128,256]{2,1,0:T(8,128)(2,1)S(1)} %pad_maximum_fusion.2.refs_4_), channel_id=1, source_target_pairs={{0,64},{8,72},{16,80},{24,88},{32,96},{40,104},{48,112},{56,120},{... | collective-permute-start | bytes 786440 | tf_op jit(solution)/shard_map/ppermute | solution.py:412
  76.0 9.3 %collective-permute-start.7 = (bf16[4,128,256]{2,1,0:T(8,128)(2,1)S(1)}, bf16[4,128,256]{2,1,0:T(8,128)(2,1)S(1)}, u32[]{:S(2)}, u32[]{:S(2)}) collective-permute-start(bf16[4,128,256]{2,1,0:T(8,128)(2,1)S(1)} %pad_maximum_fusion.1.refs_0_), channel_id=1, source_target_pairs={{0,48},{8,56},{16,0},{24,8},{32,16},{40,24},{48,32},{56,40},{64,11... | collective-permute-start | bytes 786440 | tf_op jit(solution)/shard_map/ppermute | solution.py:412
  78.0 10.4 %collective-permute-start.6 = (bf16[4,128,256]{2,1,0:T(8,128)(2,1)S(1)}, bf16[4,128,256]{2,1,0:T(8,128)(2,1)S(1)}, u32[]{:S(2)}, u32[]{:S(2)}) collective-permute-start(bf16[4,128,256]{2,1,0:T(8,128)(2,1)S(1)} %pad_maximum_fusion.1.refs_0_), channel_id=1, source_target_pairs={{0,32},{8,40},{16,48},{24,56},{32,0},{40,8},{48,16},{56,24},{64,96... | collective-permute-start | bytes 786440 | tf_op jit(solution)/shard_map/ppermute | solution.py:412
  79.5 11.7 %collective-permute-start.5 = (bf16[4,128,256]{2,1,0:T(8,128)(2,1)S(1)}, bf16[4,128,256]{2,1,0:T(8,128)(2,1)S(1)}, u32[]{:S(2)}, u32[]{:S(2)}) collective-permute-start(bf16[4,128,256]{2,1,0:T(8,128)(2,1)S(1)} %pad_maximum_fusion.1.refs_0_), channel_id=1, source_target_pairs={{0,16},{8,24},{16,32},{24,40},{32,48},{40,56},{48,0},{56,8},{64,80... | collective-permute-start | bytes 786440 | tf_op jit(solution)/shard_map/ppermute | solution.py:412
  99.5 34.9 %copy-start.2 = (s32[512]{0:T(512)S(1)}, s32[512]{0:T(512)}, u32[]{:S(2)}) copy-start(s32[512]{0:T(512)} %param.7) | copy-start | bytes 6148
  99.5 3.8 %collective-permute-start.14 = (f32[4,1024]{1,0:T(4,128)S(1)}, f32[4,1024]{1,0:T(4,128)S(1)}, u32[]{:S(2)}, u32[]{:S(2)}) collective-permute-start(f32[4,1024]{1,0:T(4,128)S(1)} %scored.1), channel_id=1, source_target_pairs={{0,1},{1,0},{2,3},{3,2},{4,5},{5,4},{6,7},{7,6},{8,9},{9,8},{10,11... | collective-permute-start | bytes 49160 | tf_op jit(solution)/shard_map/ppermute | solution.py:421
  103.4 4.1 %collective-permute-start.17 = (f32[4,1024]{1,0:T(4,128)S(1)}, f32[4,1024]{1,0:T(4,128)S(1)}, u32[]{:S(2)}, u32[]{:S(2)}) collective-permute-start(f32[4,1024]{1,0:T(4,128)S(1)} %max.3.a_ref), channel_id=1, source_target_pairs={{0,10},{1,11},{2,8},{3,9},{4,14},{5,15},{6,12},{7,13},{8,2},{9,3},... | collective-permute-start | bytes 49160 | tf_op jit(solution)/shard_map/ppermute | solution.py:421
  104.5 3.1 %collective-permute-start.16 = (f32[4,1024]{1,0:T(4,128)S(1)}, f32[4,1024]{1,0:T(4,128)S(1)}, u32[]{:S(2)}, u32[]{:S(2)}) collective-permute-start(f32[4,1024]{1,0:T(4,128)S(1)} %max.3.a_ref), channel_id=1, source_target_pairs={{0,8},{1,9},{2,10},{3,11},{4,12},{5,13},{6,14},{7,15},{8,0},{9,1},... | collective-permute-start | bytes 49160 | tf_op jit(solution)/shard_map/ppermute | solution.py:421
  106.8 4.6 %collective-permute-start.15 = (f32[4,1024]{1,0:T(4,128)S(1)}, f32[4,1024]{1,0:T(4,128)S(1)}, u32[]{:S(2)}, u32[]{:S(2)}) collective-permute-start(f32[4,1024]{1,0:T(4,128)S(1)} %max.3.a_ref), channel_id=1, source_target_pairs={{0,2},{1,3},{2,0},{3,1},{4,6},{5,7},{6,4},{7,5},{8,10},{9,11},{10,... | collective-permute-start | bytes 49160 | tf_op jit(solution)/shard_map/ppermute | solution.py:421
  112.1 22.3 %all-to-all-start.7 = ((f32[32,2,1024]{2,1,0:T(2,128)}), f32[32,2,1024]{2,1,0:T(2,128)S(1)}, u32[]{:S(2)}, u32[]{:S(2)}) async-start(f32[32,2,1024]{2,1,0:T(2,128)} %get-tuple-element.43), calls=%async_computation.7 | async-start | bytes 524288 | tf_op jit(solution)/shard_map/all_to_all | solution.py:487
  122.2 10.3 %collective-permute-start.18 = (f32[4,1024]{1,0:T(4,128)S(1)}, f32[4,1024]{1,0:T(4,128)S(1)}, u32[]{:S(2)}, u32[]{:S(2)}) collective-permute-start(f32[4,1024]{1,0:T(4,128)S(1)} %get-tuple-element.40.a_ref), channel_id=1, source_target_pairs={{0,4},{1,5},{2,6},{3,7},{4,0},{5,1},{6,2},{7,3},{8,12},{9,13},{10,... | collective-permute-start | bytes 49160 | tf_op jit(solution)/shard_map/ppermute | solution.py:421
